TPU v7x, 128 devices: a whole 4x4x4 slice. The times are simulated.
128 devices in a mesh: aa: 32 (over z, y, core), ba: 4 (over x).
Axes of the slice: x: 4, y: 4, z: 4, core: 2. Of those that a mesh axis runs over, the one named last changes fastest.
Arguments:
- features: bfloat16 [262144, 256], P(('aa', 'ba')), may hold values from -6 to 6
- tile_ids: int32 [262144, 1], P(('aa', 'ba')), may hold values from 0 to 127; in each aligned block of 2048 rows (0 to 2047, 2048 to 4095, ...) at most 24 rows name the same one
- cell_ids: int32 [262144], P(('aa', 'ba')), may hold values from 0 to 2047
- spread_weight: float32 [262144], P(('aa', 'ba')), may hold values from 0.1 to 0.6
- read_weight: float32 [262144], P(('aa', 'ba')), may hold values from 0.5 to 2
- message_weight: bfloat16 [256, 256], replicated, may hold values from -0.375 to 0.375
- skip_weight: bfloat16 [256, 256], replicated, may hold values from -0.375 to 0.375
- spectral_weight: bfloat16 [16, 256, 256, 256], P('ba', 'aa'), may hold values from -1.5 to 1.5
- hidden_weight: bfloat16 [256, 256], replicated, may hold values from -0.375 to 0.375
- output_weight: bfloat16 [256, 256], replicated, may hold values from -0.75 to 0.75
Outputs:
- point_out: bfloat16 [262144, 256], P(('aa', 'ba'))
Inputs may be any that keep to these rules, and one draw needn't show every extreme that they name: `tile_ids`: among the rows of one device no index appears more than 24 times, and some index appears exactly 24 times.
All inputs are finite; a program needn't handle non-finite values.
Results may differ from a plain program's by a relative error of at most 0.015.
Values may be sent and summed in bfloat16 or wider, within the bound.
No kernel may reach another device: no remote copies, remote signals or barrier semaphores. Data moves between devices by JAX's collectives and lax.ppermute only.
A program may use at most 64 MiB of HBM per device.

v0:
```python
import math

import jax
import jax.numpy as jnp
from jax import lax
from jax.sharding import PartitionSpec as P

G = 64
M = 16


def side_by_side(arrays, axis, split_dim, concat_dim, along):
    ends, at = ([], 0)
    for a in arrays[:-1]:
        at += a.shape[along]
        ends.append(at)
    both = jnp.concatenate(arrays, axis=along)
    return tuple(
        jnp.split(
            lax.all_to_all(both, axis, split_axis=split_dim, concat_axis=concat_dim, tiled=True),
            ends,
            axis=along,
        )
    )


def cut_along(shard, dim, devices):
    before, after = (shard.shape[:dim], shard.shape[dim + 1 :])
    return jnp.moveaxis(shard.reshape(*before, devices, -1, *after), dim, 0)


def sum_at_owner(shard, axis, dim):
    devices = lax.axis_size(axis)
    blocks = lax.all_to_all(cut_along(shard, dim, devices), axis, 0, 0, tiled=True)
    return jnp.sum(blocks.astype(jnp.float32), axis=0)


def from_everyone(shard, axis):
    devices = lax.axis_size(axis)
    return lax.all_to_all(
        jnp.broadcast_to(shard[None], (devices, *shard.shape)), axis, 0, 0, tiled=True
    )


def in_order(blocks, dim):
    dims = list(blocks.shape[1:])
    dims[dim] *= blocks.shape[0]
    return jnp.moveaxis(blocks, 0, dim).reshape(dims)


def gathered_copies(shard, axis, dim):
    blocks = from_everyone(shard, axis)
    return in_order(blocks, dim)


def basis_table(mode_count, grid_length, positions):
    mode_index = jnp.arange(mode_count, dtype=jnp.int32)[:, None]
    half_modes = mode_count // 2
    frequency = jnp.where(mode_index < half_modes, mode_index, mode_index - half_modes + 1).astype(
        jnp.float32
    )
    phase_angle = 2.0 * math.pi * frequency * positions.astype(jnp.float32)[None, :] / grid_length
    waveform = jnp.where(mode_index < half_modes, jnp.cos(phase_angle), jnp.sin(phase_angle))
    norm_scale = jnp.where(
        mode_index == 0, math.sqrt(1.0 / grid_length), math.sqrt(2.0 / grid_length)
    )
    return waveform * norm_scale


def per_device(
    features,
    tile_ids,
    cell_ids,
    spread_weight,
    read_weight,
    message_weight,
    skip_weight,
    spectral_weight,
    hidden_weight,
    output_weight,
):
    point_count, width = features.shape
    axis_first = lax.axis_size("aa")
    axis_second = lax.axis_size("ba")
    device_count = axis_first * axis_second
    capacity = 3 * point_count // (2 * device_count)
    tile_x = G // axis_first
    tile_y = G // axis_second
    cell_count = tile_x * tile_y * G
    modes_y = M // axis_second
    chan_share = width // axis_first
    targets = tile_ids[:, 0]
    one_hot = (targets[:, None] == jnp.arange(device_count, dtype=jnp.int32)[None, :]).astype(
        jnp.int32
    )
    ranks = jnp.sum(jnp.cumsum(one_hot, axis=0) * one_hot, axis=1) - 1
    slots = targets * capacity + ranks
    product = jnp.dot(features, message_weight, preferred_element_type=jnp.float32)
    message = (spread_weight[:, None] * product).astype(jnp.bfloat16)
    placing = jnp.stack([cell_ids // G, cell_ids % G], axis=1).astype(jnp.bfloat16)
    send_rows = jnp.zeros((device_count * capacity, width), jnp.bfloat16).at[slots].set(message)
    send_where = jnp.zeros((device_count * capacity, 2), jnp.bfloat16).at[slots].set(placing)
    recv_rows, recv_where = side_by_side((send_rows, send_where), ("aa", "ba"), 0, 0, 1)
    local_cells = recv_where[:, 0].astype(jnp.int32) * G + recv_where[:, 1].astype(jnp.int32)
    latent_sum = (
        jnp.zeros((cell_count, width), jnp.float32)
        .at[local_cells]
        .add(recv_rows.astype(jnp.float32))
    )
    latent = latent_sum.astype(jnp.bfloat16)
    second_pos = lax.axis_index("ba") * tile_y + jnp.arange(tile_y, dtype=jnp.int32)
    basis_y = basis_table(M, G, second_pos)
    basis_z = basis_table(M, G, jnp.arange(G, dtype=jnp.int32))
    cube = latent.astype(jnp.float32).reshape(tile_x, tile_y, G, width)
    along_z = jnp.einsum("kz,xyzc->xykc", basis_z, cube)
    along_y = jnp.einsum("jy,xykc->jxkc", basis_y, along_z)
    row_part = sum_at_owner(along_y.astype(jnp.bfloat16), "ba", 0)
    lines = lax.all_to_all(
        row_part.astype(jnp.bfloat16), "aa", split_axis=3, concat_axis=1, tiled=True
    ).astype(row_part.dtype)
    full_modes = jnp.einsum("ix,jxkc->jikc", basis_z, lines)
    full_modes = full_modes.reshape(modes_y, M * M, chan_share).astype(jnp.bfloat16)
    spectrum_low = lax.all_to_all(full_modes, "aa", split_axis=1, concat_axis=2, tiled=True)
    mixed = jnp.einsum(
        "jmc,jmco->jmo", spectrum_low, spectral_weight, preferred_element_type=jnp.float32
    ).astype(jnp.bfloat16)
    share_modes = lax.all_to_all(mixed, "aa", split_axis=2, concat_axis=1, tiled=True)
    share_modes = share_modes.reshape(modes_y, M, M, chan_share).astype(jnp.float32)
    line_values = jnp.einsum("ix,jikc->jxkc", basis_z, share_modes)
    slab_values = lax.all_to_all(
        line_values.astype(jnp.bfloat16), "aa", split_axis=1, concat_axis=3, tiled=True
    ).astype(line_values.dtype)
    inv_x = gathered_copies(slab_values.astype(jnp.bfloat16), "ba", 0).astype(slab_values.dtype)
    inv_z = jnp.einsum("kz,jxkc->jxzc", basis_z, inv_x)
    inverse = jnp.einsum("jy,jxzc->xyzc", basis_y, inv_z)
    skip = jnp.dot(latent, skip_weight, preferred_element_type=jnp.float32)
    latent_out = jax.nn.gelu(inverse.reshape(cell_count, width) + skip).astype(jnp.bfloat16)
    back_rows = latent_out[local_cells]
    returned = lax.all_to_all(back_rows, ("aa", "ba"), split_axis=0, concat_axis=0, tiled=True)
    own_rows = returned[slots]
    gathered = (read_weight[:, None] * own_rows.astype(jnp.float32)).astype(jnp.bfloat16)
    hidden = jax.nn.gelu(
        jnp.dot(gathered, hidden_weight, preferred_element_type=jnp.float32)
    ).astype(jnp.bfloat16)
    return jnp.dot(hidden, output_weight, preferred_element_type=jnp.float32).astype(jnp.bfloat16)


def solution(mesh):
    placed = (
        P(("aa", "ba"), None),
        P(("aa", "ba"), None),
        P(("aa", "ba")),
        P(("aa", "ba")),
        P(("aa", "ba")),
        P(),
        P(),
        P("ba", "aa", None, None),
        P(),
        P(),
    )
    return jax.shard_map(
        per_device, mesh=mesh, in_specs=placed, out_specs=P(("aa", "ba"), None), check_vma=False
    )
```

profile of v0, /device:TPU:1, one launch (start us, length us, event | category | flops | bytes accessed | tf_op | source)
XLA Modules:
  0.0 221.9 jit_solution(2980598704180169572)
XLA Ops:
  0.0 0.8 fusion.46
  0.8 0.8 copy.42
  1.7 0.3 copy.44
  2.0 0.3 fusion.34
  2.4 0.1 broadcast_add_fusion
  2.5 0.0 copy-start.1
  2.5 0.3 copy.43
  2.8 0.2 copy-done.2
  3.1 0.6 fusion.29
  3.7 6.0 %scatter_custom_fusion.1 = bf16[3072,2]{1,0:T(8,128)(2,1)S(1)} fusion(s32[2048]{0:T(1024)S(1)} %bitcast.129, bf16[2048,2]{1,0:T(8,128)(2,1)S(1)} %copy.44, bf16[]{:T(256)} %constant.70.clone.1), kind=kCustom, calls=%fused_computation.66 | custom fusion | bytes 12290 | tf_op jit(solution)/shard_map/scatter | solution.py:102
  9.8 1.4 fusion.2
  11.2 10.1 %scatter_custom_fusion = bf16[3072,256]{1,0:T(8,128)(2,1)S(1)} fusion(s32[2048]{0:T(1024)S(1)} %bitcast.130, bf16[2048,256]{1,0:T(8,128)(2,1)} %fusion.2, bf16[]{:T(256)} %constant.70.clone.1), kind=kCustom, calls=%fused_computation.57 | custom fusion | bytes 1573376 | tf_op jit(solution)/shard_map/scatter | solution.py:101
  21.3 1.7 pad_maximum_fusion
  23.1 11.5 %all-to-all-start = ((bf16[128,24,258]{2,1,0:T(8,128)(2,1)}), bf16[128,24,258]{2,1,0:T(8,128)(2,1)S(1)}, u32[]{:S(2)}, u32[]{:S(2)}) async-start(bf16[128,24,258]{2,1,0:T(8,128)(2,1)} %bitcast.110), calls=%async_computation | async-start | bytes 4718592 | tf_op jit(solution)/shard_map/all_to_all | solution.py:20
  34.6 33.5 %all-to-all-done = bf16[128,24,258]{2,1,0:T(8,128)(2,1)S(1)} async-done(((bf16[128,24,258]{2,1,0:T(8,128)(2,1)}), bf16[128,24,258]{2,1,0:T(8,128)(2,1)S(1)}, u32[]{:S(2)}, u32[]{:S(2)}) %all-to-all-start) | async-done | bytes 1585184 | tf_op jit(solution)/shard_map/all_to_all | solution.py:20
  68.1 1.0 fusion.24
  69.1 18.8 %scatter_custom_fusion.2 = f32[2048,256]{1,0:T(8,128)} fusion(s32[3072]{0:T(1024)S(1)} %fusion.24, bf16[3072,258]{1,0:T(8,128)(2,1)S(1)} %bitcast.109, f32[]{:T(128)} %constant.69.clone.1), kind=kCustom, calls=%fused_computation.8 | custom fusion | flops 1572864 | bytes 3670020 | tf_op jit(solution)/shard_map/scatter-add | solution.py:108
  87.9 1.7 convert_element_type.111
  89.6 0.4 convolution_bitcast_fusion.1
  90.0 0.4 convolution_convert_fusion.1
  90.4 0.1 reshape.88
  90.4 0.1 copy.47
  90.5 8.7 %all_to_all.100 = bf16[4,4,2,16,256]{4,1,3,2,0:T(4,128)(2,1)S(1)} all-to-all(bf16[4,4,2,16,256]{4,1,3,2,0:T(4,128)(2,1)S(1)} %copy.47), channel_id=1, replica_groups=mesh['aa'=32,'ba'=4] {'ba'}, dimensions={0} | all-to-all | bytes 524288 | tf_op jit(solution)/shard_map/all_to_all | solution.py:34
  99.2 0.1 reduce_sum.22
  99.4 0.4 copy.49
  99.8 0.6 reshape.146
  100.4 11.4 %all_to_all.101 = bf16[32,2,512]{2,1,0:T(2,128)(2,1)S(1)} all-to-all(bf16[32,2,512]{2,1,0:T(2,128)(2,1)S(1)} %reshape.146), channel_id=1, replica_groups=mesh['aa'=32,'ba'=4] {'aa'}, dimensions={0} | all-to-all | bytes 131072 | tf_op jit(solution)/shard_map/all_to_all | solution.py:118
  111.8 0.4 reshape.147
  112.1 0.1 copy.94
  112.2 0.1 copy.51
  112.3 0.3 fusion.26
  112.6 0.5 copy.73
  113.2 0.2 reshape.148
  113.4 10.5 %all_to_all.102 = bf16[32,2,128]{2,1,0:T(2,128)(2,1)S(1)} all-to-all(bf16[32,2,128]{2,1,0:T(2,128)(2,1)S(1)} %reshape.148), channel_id=1, replica_groups=mesh['aa'=32,'ba'=4] {'aa'}, dimensions={0} | all-to-all | bytes 32768 | tf_op jit(solution)/shard_map/all_to_all | solution.py:123
  123.9 0.3 reshape.149
  124.3 0.1 copy.96
  124.4 0.2 reshape.138
  124.6 2.8 %fusion.98 = bf16[4,8,1,256]{3,2,1,0:T(2,128)(2,1)S(1)} fusion(bf16[4,8,256,1]{2,3,1,0:T(2,128)(2,1)S(1)} %reshape.138, bf16[4,8,256,256]{3,2,1,0:T(8,128)(2,1)} %param.17), kind=kOutput, calls=%fused_computation.142 | convolution fusion | flops 4194304 | bytes 4227072 | tf_op jit(solution)/shard_map/jmc,jmco->jmo/dot_general | solution.py:124
  127.5 0.2 copy.69
  127.7 0.1 bitcast_bitcast_fusion
  127.8 0.2 reshape.150
  128.0 10.7 %all_to_all.103 = bf16[32,2,128]{2,1,0:T(2,128)(2,1)S(1)} all-to-all(bf16[32,2,128]{2,1,0:T(2,128)(2,1)S(1)} %reshape.150), channel_id=1, replica_groups=mesh['aa'=32,'ba'=4] {'aa'}, dimensions={0} | all-to-all | bytes 32768 | tf_op jit(solution)/shard_map/all_to_all | solution.py:127
  138.7 0.3 reshape.151
  139.0 0.1 copy.95
  139.1 0.1 reshape.89
  139.3 0.3 fusion.27
  139.6 0.8 copy.60
  140.4 0.6 reshape.152
  141.0 11.0 %all_to_all.104 = bf16[32,2,512]{2,1,0:T(2,128)(2,1)S(1)} all-to-all(bf16[32,2,512]{2,1,0:T(2,128)(2,1)S(1)} %reshape.152), channel_id=1, replica_groups=mesh['aa'=32,'ba'=4] {'aa'}, dimensions={0} | all-to-all | bytes 131072 | tf_op jit(solution)/shard_map/all_to_all | solution.py:130
  152.0 0.4 reshape.153
  152.4 0.1 copy.93
  152.5 0.2 copy.63
  152.7 0.7 broadcast_in_dim.69
  153.4 3.6 %all-to-all-start.6 = ((bf16[4,4,2,16,256]{4,3,2,1,0:T(8,128)(2,1)}), bf16[4,4,2,16,256]{4,3,2,1,0:T(8,128)(2,1)S(1)}, u32[]{:S(2)}, u32[]{:S(2)}) async-start(bf16[4,4,2,16,256]{4,3,2,1,0:T(8,128)(2,1)} %broadcast_in_dim.69), calls=%async_computation.6 | async-start | bytes 524288 | tf_op jit(solution)/shard_map/all_to_all | solution.py:40
  157.0 5.8 %all-to-all-done.6 = bf16[4,4,2,16,256]{4,3,2,1,0:T(8,128)(2,1)S(1)} async-done(((bf16[4,4,2,16,256]{4,3,2,1,0:T(8,128)(2,1)}), bf16[4,4,2,16,256]{4,3,2,1,0:T(8,128)(2,1)S(1)}, u32[]{:S(2)}, u32[]{:S(2)}) %all-to-all-start.6) | async-done | bytes 262176 | tf_op jit(solution)/shard_map/all_to_all | solution.py:40
  162.9 0.6 convolution_bitcast_fusion
  163.4 0.8 fusion.21
  164.2 1.2 copy.65
  165.5 0.9 fusion.10
  166.4 13.0 %gather_fusion = bf16[3072,256]{1,0:T(8,128)(2,1)} fusion(bf16[2048,256]{1,0:T(8,128)(2,1)S(1)} %fusion.10, s32[3072]{0:T(1024)S(1)} %broadcast_clamp_fusion), kind=kCustom, calls=%fused_computation | custom fusion | bytes 3158016 | tf_op jit(solution)/shard_map/gather | solution.py:138
  179.4 5.0 %all-to-all-start.7 = ((bf16[128,24,256]{2,1,0:T(8,128)(2,1)}), bf16[128,24,256]{2,1,0:T(8,128)(2,1)S(1)}, u32[]{:S(2)}, u32[]{:S(2)}) async-start(bf16[128,24,256]{2,1,0:T(8,128)(2,1)} %bitcast.111), calls=%async_computation.7 | async-start | bytes 3145728 | tf_op jit(solution)/shard_map/all_to_all | solution.py:139
  184.3 25.3 %all-to-all-done.7 = bf16[128,24,256]{2,1,0:T(8,128)(2,1)S(1)} async-done(((bf16[128,24,256]{2,1,0:T(8,128)(2,1)}), bf16[128,24,256]{2,1,0:T(8,128)(2,1)S(1)}, u32[]{:S(2)}, u32[]{:S(2)}) %all-to-all-start.7) | async-done | bytes 1572896 | tf_op jit(solution)/shard_map/all_to_all | solution.py:139
  209.6 9.0 %gather_fusion.1 = bf16[2048,256]{1,0:T(8,128)(2,1)} fusion(bf16[3072,256]{1,0:T(8,128)(2,1)S(1)} %bitcast.107, s32[2048]{0:T(1024)S(1)} %broadcast_clamp_fusion.1), kind=kCustom, calls=%fused_computation.1 | custom fusion | bytes 2105344 | tf_op jit(solution)/shard_map/gather | solution.py:140
  218.6 3.3 %convolution_convert_fusion = bf16[2048,256]{1,0:T(8,128)(2,1)} fusion(bf16[256,256]{1,0:T(8,128)(2,1)S(1)} %copy-done.5, bf16[256,256]{1,0:T(8,128)(2,1)S(1)} %copy-done.6, bf16[2048,256]{1,0:T(8,128)(2,1)} %gather_fusion.1, f32[2048]{0:T(1024)S(1)} %copy-done.7), kind=kOutput, calls=%fused_computation.13 | convolution fusion | flops 543686656 | bytes 2367488 | tf_op jit(solution)/shard_map/dot_general | solution.py:145
  (28 shorter events, 0.2 us)
Async XLA Ops:
  0.0 9.7 %copy-start = (bf16[2048,256]{1,0:T(8,128)(2,1)S(1)}, bf16[2048,256]{1,0:T(8,128)(2,1)}, u32[]{:S(2)}) copy-start(bf16[2048,256]{1,0:T(8,128)(2,1)} %param.10) | copy-start | bytes 3145732
  2.4 0.7 copy-start.2
  2.5 7.3 %copy-start.1 = (bf16[256,256]{1,0:T(8,128)(2,1)S(1)}, bf16[256,256]{1,0:T(8,128)(2,1)}, u32[]{:S(2)}) copy-start(bf16[256,256]{1,0:T(8,128)(2,1)} %param.15) | copy-start | bytes 393220
  2.5 7.3 %copy-start.3 = (f32[2048]{0:T(1024)S(1)}, f32[2048]{0:T(1024)}, u32[]{:S(2)}) copy-start(f32[2048]{0:T(1024)} %param.13) | copy-start | bytes 24580
  23.1 45.1 %all-to-all-start = ((bf16[128,24,258]{2,1,0:T(8,128)(2,1)}), bf16[128,24,258]{2,1,0:T(8,128)(2,1)S(1)}, u32[]{:S(2)}, u32[]{:S(2)}) async-start(bf16[128,24,258]{2,1,0:T(8,128)(2,1)} %bitcast.110), calls=%async_computation | async-start | bytes 4718592 | tf_op jit(solution)/shard_map/all_to_all | solution.py:20
  153.4 9.5 %all-to-all-start.6 = ((bf16[4,4,2,16,256]{4,3,2,1,0:T(8,128)(2,1)}), bf16[4,4,2,16,256]{4,3,2,1,0:T(8,128)(2,1)S(1)}, u32[]{:S(2)}, u32[]{:S(2)}) async-start(bf16[4,4,2,16,256]{4,3,2,1,0:T(8,128)(2,1)} %broadcast_in_dim.69), calls=%async_computation.6 | async-start | bytes 524288 | tf_op jit(solution)/shard_map/all_to_all | solution.py:40
  164.2 1.2 copy-start.4
  179.4 30.3 %all-to-all-start.7 = ((bf16[128,24,256]{2,1,0:T(8,128)(2,1)}), bf16[128,24,256]{2,1,0:T(8,128)(2,1)S(1)}, u32[]{:S(2)}, u32[]{:S(2)}) async-start(bf16[128,24,256]{2,1,0:T(8,128)(2,1)} %bitcast.111), calls=%async_computation.7 | async-start | bytes 3145728 | tf_op jit(solution)/shard_map/all_to_all | solution.py:139
  209.6 9.0 %copy-start.5 = (bf16[256,256]{1,0:T(8,128)(2,1)S(1)}, bf16[256,256]{1,0:T(8,128)(2,1)}, u32[]{:S(2)}) copy-start(bf16[256,256]{1,0:T(8,128)(2,1)} %param.19) | copy-start | bytes 393220
  209.6 9.0 %copy-start.6 = (bf16[256,256]{1,0:T(8,128)(2,1)S(1)}, bf16[256,256]{1,0:T(8,128)(2,1)}, u32[]{:S(2)}) copy-start(bf16[256,256]{1,0:T(8,128)(2,1)} %param.18) | copy-start | bytes 393220
  209.6 9.0 %copy-start.7 = (f32[2048]{0:T(1024)S(1)}, f32[2048]{0:T(1024)}, u32[]{:S(2)}) copy-start(f32[2048]{0:T(1024)} %param.14) | copy-start | bytes 24580
where the time goes:
time: 223 us; the launch traced here: 222 us
  waiting for transfers between devices  64.6 us (29%)
  blocking collectives  52.3 us (23%)
  local copies, waits for them, and re-layouts  48.1 us (22%)
  other arithmetic  25.3 us (11%)
  starting transfers between devices  20.1 us (9%)
  matrix products  11.2 us (5%)
    all_to_all x1, waiting for transfers between devices, side_by_side(): lax.all_to_all(both, axis, split_axis=split_dim, concat_axis=concat_dim,...  33.5 us
    all_to_all x1, waiting for transfers between devices, per_device(): lax.all_to_all(back_rows, ('aa', 'ba'), split_axis=0, concat_axis=0, tile...  25.3 us
    scatter-add x1, other arithmetic, per_device(): latent_sum = jnp.zeros((cell_count, width), jnp.float32).at[local_cells]....  18.8 us
    gather x1, local copies, waits for them, and re-layouts, per_device(): back_rows = latent_out[local_cells]  13 us
    all_to_all x1, starting transfers between devices, side_by_side(): lax.all_to_all(both, axis, split_axis=split_dim, concat_axis=concat_dim,...  11.5 us
    all_to_all x1, blocking collectives, per_device(): lax.all_to_all(row_part.astype(jnp.bfloat16), 'aa', split_axis=3, concat_...  11.4 us
    all_to_all x1, blocking collectives, per_device(): lax.all_to_all(line_values.astype(jnp.bfloat16), 'aa', split_axis=1, conc...  11 us
    all_to_all x1, blocking collectives, per_device(): lax.all_to_all(mixed, 'aa', split_axis=2, concat_axis=1, tiled=True)  10.7 us
  transfers between devices with their start and end apart: 3, of which 3 were waited for; matrix products, arithmetic and copies ran while one was open for 0% of the time, Pallas kernels for 0%

commit v1 on v0

v1 whole, which is shorter than its diff:
```python
import math

import jax
import jax.numpy as jnp
from jax import lax
from jax.experimental import pallas as pl
from jax.experimental.pallas import tpu as pltpu
from jax.sharding import PartitionSpec as P

G = 64
M = 16
F32 = jnp.float32
BF16 = jnp.bfloat16
VMEM = pl.BlockSpec(memory_space=pltpu.VMEM)
SMEM = pl.BlockSpec(memory_space=pltpu.SMEM)


def iota(shape, dim):
    return lax.broadcasted_iota(jnp.int32, shape, dim)


def mm(a, b):
    return lax.dot_general(a, b, (((1,), (0,)), ((), ())), preferred_element_type=F32)


def mm_nt(a, b):
    return lax.dot_general(a, b, (((1,), (1,)), ((), ())), preferred_element_type=F32)


def as_column(row, lanes):
    n = row.shape[1]
    return jnp.transpose(jnp.broadcast_to(row, (lanes, n)))


def call(body, outs, ins, scratch=(), name=None):
    single = not isinstance(outs, (tuple, list))
    specs = [VMEM if s != "smem" else SMEM for s in ins[1]]
    fn = pl.pallas_call(
        body,
        out_shape=outs,
        in_specs=specs,
        out_specs=VMEM if single else [VMEM] * len(outs),
        scratch_shapes=list(scratch),
        name=name,
    )
    return fn(*ins[0])


def spread_body(feat, tile, cell, spread, weight, send, slots, message, rank_row):
    devices = send.shape[0]
    points = feat.shape[0]
    cap = 24
    upper = (iota((256, 256), 0) < iota((256, 256), 1)).astype(BF16)
    ones = jnp.ones((256, 128), BF16)
    used = jnp.zeros((devices, 256), F32)
    for at in range(0, points, 256):
        hot = tile[:, at : at + 256] == iota((devices, 256), 0)
        hot = hot.astype(F32)
        hot16 = hot.astype(BF16)
        before = mm(hot16, upper) + used
        total = mm(hot16, ones)
        used = used + jnp.concatenate([total, total], axis=1)
        rank = jnp.sum(hot * before, axis=0, keepdims=True).astype(jnp.int32)
        rank_row[:, at : at + 256] = rank
        slots[:, at : at + 256] = tile[:, at : at + 256] * cap + rank
    for at in range(0, points, 128):
        product = mm(feat[at : at + 128, :], weight[...])
        scale = as_column(spread[:, at : at + 128], 128)
        scale = jnp.concatenate([scale, scale], axis=1)
        message[at : at + 128, :] = (scale * product).astype(BF16)
    rank = rank_row[...]
    group = lax.shift_right_logical(rank, 3)
    low = tile[...] * 8 + lax.bitwise_and(rank, 7)
    high_part = lax.shift_right_logical(cell[...], 6).astype(F32)
    low_part = lax.bitwise_and(cell[...], 63).astype(F32)
    lane = iota((128, points), 0)
    where = jnp.where(lane == 2 * group, high_part, 0.0)
    where = jnp.where(lane == 2 * group + 1, low_part, where).astype(BF16)
    slot = slots[...]

    def fill(step, carry):
        base = step * 16
        hot = (slot - base * cap == iota((16 * cap, points), 0)).astype(BF16)
        rows = mm(hot, message[...])
        left = rows[:, :128].reshape(16, cap, 128).astype(BF16)
        right = rows[:, 128:].reshape(16, cap, 128).astype(BF16)
        hot8 = (low - base * 8 == iota((128, points), 0)).astype(BF16)
        placing = mm_nt(hot8, where).reshape(16, 8, 128).astype(BF16)
        send[pl.ds(base, 16), 0:cap, :] = left
        send[pl.ds(base, 16), cap : 2 * cap, :] = right
        send[pl.ds(base, 16), 2 * cap :, :] = placing
        return carry

    lax.fori_loop(0, devices // 16, fill, 0)


def collect_body(recv, basis, latent, places, p0, p1, p2, p3, rows, ids):
    picks = jnp.where(
        iota((8, 128), 1) == 2 * iota((8, 128), 0),
        64.0,
        jnp.where(iota((8, 128), 1) == 2 * iota((8, 128), 0) + 1, 1.0, 0.0),
    ).astype(BF16)

    def unpack(step, carry):
        block = recv[pl.ds(step * 16, 16)].astype(F32)
        place = block[:, 48:56, :].reshape(128, 128).astype(BF16)
        places[pl.ds(step * 128, 128), :] = place
        ids[step] = mm_nt(picks, place).astype(jnp.int32)
        for g in range(3):
            left = block[:, g * 8 : g * 8 + 8, :].reshape(128, 128)
            right = block[:, 24 + g * 8 : 32 + g * 8, :].reshape(128, 128)
            both = jnp.concatenate([left, right], axis=1).astype(BF16)
            rows[pl.ds(step * 384 + g * 128, 128), :] = both
        return carry

    lax.fori_loop(0, 8, unpack, 0)
    tile = 256

    def total(step, carry):
        at = step * tile
        cells = iota((tile, 128), 0) + at
        hot = [
            (ids[i, g : g + 1, :] == cells).astype(BF16) for i in range(8) for g in range(3)
        ]
        latent[pl.ds(at, tile), :] = mm(jnp.concatenate(hot, axis=1), rows[...]).astype(BF16)
        return carry

    lax.fori_loop(0, latent.shape[0] // tile, total, 0)
    for x in range(2):
        part = mm(basis[...], latent[x * 1024 : x * 1024 + 1024, :]).astype(BF16)
        for s, p in enumerate((p0, p1, p2, p3)):
            p[x] = part[s * 64 : s * 64 + 64, :]


def widen_body(a, b, c, d, coef, out):
    total = [
        a[x].astype(F32) + b[x].astype(F32) + c[x].astype(F32) + d[x].astype(F32)
        for x in range(2)
    ]
    halves = [t.reshape(4, 2, 8, 256) for t in total]

    def one(i, carry):
        for h in range(2):
            v = coef[2 * i] * halves[0][:, h] + coef[2 * i + 1] * halves[1][:, h]
            out[2 * i + h] = v.reshape(32, 256).astype(BF16)
        return carry

    lax.fori_loop(0, 16, one, 0)


def mix_body(recv, weight, out):
    spec = jnp.sum(recv[...].astype(F32), axis=0).astype(BF16)
    row = iota((8, 256), 0)
    mixed = jnp.zeros((8, 256), F32)
    for m in range(8):
        mixed = jnp.where(row == m, mm(spec, weight[0, m]), mixed)
    out[...] = jnp.broadcast_to(mixed.astype(BF16)[None], out.shape)


def mix(recv, weight):
    return pl.pallas_call(
        mix_body,
        grid=(4,),
        in_specs=[
            pl.BlockSpec((32, 8, 256), lambda j: (0, j, 0)),
            pl.BlockSpec((1, 8, 256, 256), lambda j: (j, 0, 0, 0)),
        ],
        out_specs=pl.BlockSpec((32, 8, 256), lambda j: (0, j, 0)),
        out_shape=jax.ShapeDtypeStruct((32, 32, 256), BF16),
        name="mix",
    )(recv, weight)


def narrow_body(recv, coef, out):
    for h in range(2):
        acc = [jnp.zeros((4, 8, 256), F32) for x in range(2)]
        for i in range(16):
            v = recv[2 * i + h].astype(F32).reshape(4, 8, 256)
            for x in range(2):
                acc[x] = acc[x] + coef[2 * i + x] * v
        for x in range(2):
            for j in range(4):
                out[x, j * 16 + h * 8 : j * 16 + h * 8 + 8, :] = acc[x][j].astype(BF16)


def finish_body(a, b, c, d, basis, latent, skip, places, out, values):
    for x in range(2):
        modes = jnp.concatenate([a[x], b[x], c[x], d[x]], axis=0)
        for at in range(0, 1024, 256):
            v = mm(basis[at : at + 256, :], modes)
            v = v + mm(latent[x * 1024 + at : x * 1024 + at + 256, :], skip[...])
            values[x * 1024 + at : x * 1024 + at + 256, :] = jax.nn.gelu(v).astype(BF16)

    def back(step, carry):
        place = places[pl.ds(step * 128, 128), :]
        for g in range(3):
            lane = iota((128, 128), 0)
            pick = jnp.where(lane == 2 * g, 64.0, jnp.where(lane == 2 * g + 1, 1.0, 0.0))
            cell = mm(place, pick.astype(BF16)).astype(jnp.int32)
            hot = [
                (cell == iota((128, 128), 1) + 128 * k).astype(BF16) for k in range(16)
            ]
            got = mm(jnp.concatenate(hot, axis=1), values[...])
            out[pl.ds(step * 16, 16), g * 8 : g * 8 + 8, :] = got.reshape(16, 8, 256).astype(BF16)
        return carry

    lax.fori_loop(0, 8, back, 0)


def decode_body(returned, slots, read, hidden_weight, output_weight, out):
    def some(step, carry):
        at = step * 256
        hot = []
        scale = []
        for part in range(2):
            slot = as_column(slots[:, pl.ds(at + part * 128, 128)], 128)
            one = [(slot == iota((128, 128), 1) + 128 * k).astype(BF16) for k in range(24)]
            hot.append(jnp.concatenate(one, axis=1))
            w = as_column(read[:, pl.ds(at + part * 128, 128)], 128)
            scale.append(jnp.concatenate([w, w], axis=1))
        own = mm(jnp.concatenate(hot, axis=0), returned[...])
        gathered = (jnp.concatenate(scale, axis=0) * own).astype(BF16)
        hidden = jax.nn.gelu(mm(gathered, hidden_weight[...])).astype(BF16)
        out[pl.ds(at, 256), :] = mm(hidden, output_weight[...]).astype(BF16)
        return carry

    lax.fori_loop(0, out.shape[0] // 256, some, 0)


def basis_table(mode, position):
    mode = mode[:, None]
    half = M // 2
    frequency = jnp.where(mode < half, mode, mode - half + 1).astype(F32)
    phase = 2.0 * math.pi * frequency * position.astype(F32)[None, :] / G
    wave = jnp.where(mode < half, jnp.cos(phase), jnp.sin(phase))
    return wave * jnp.where(mode == 0, math.sqrt(1.0 / G), math.sqrt(2.0 / G))


def shifted(shard, s):
    return lax.ppermute(shard, "ba", [(i, (i + s) % 4) for i in range(4)])


def per_device(
    features,
    tile_ids,
    cell_ids,
    spread_weight,
    read_weight,
    message_weight,
    skip_weight,
    spectral_weight,
    hidden_weight,
    output_weight,
):
    points, width = features.shape
    devices = lax.axis_size("aa") * lax.axis_size("ba")
    cells = 2048
    shape = jax.ShapeDtypeStruct
    first = lax.axis_index("aa")
    second = lax.axis_index("ba")
    own_y = second * 16 + jnp.arange(16, dtype=jnp.int32)
    modes = jnp.arange(M, dtype=jnp.int32)
    every = jnp.arange(G, dtype=jnp.int32)
    table_z = basis_table(modes, every)
    to_y = basis_table((modes + 4 * second) % M, own_y)
    quarter = modes // 4
    from_y = basis_table(4 * ((second - quarter) % 4) + modes % 4, own_y)
    table_x = basis_table(modes, 2 * first + jnp.arange(2, dtype=jnp.int32))
    table_z, to_y, from_y, table_x = lax.optimization_barrier((table_z, to_y, from_y, table_x))
    coef = table_x.reshape(32)
    basis_to = (to_y[:, None, :, None] * table_z[None, :, None, :]).reshape(256, 1024)
    basis_to = basis_to.astype(BF16)
    basis_from = (jnp.transpose(from_y)[:, None, :, None] * jnp.transpose(table_z)[None, :, None, :])
    basis_from = basis_from.reshape(1024, 256).astype(BF16)

    send, slots = call(
        spread_body,
        (shape((devices, 56, 128), BF16), shape((1, points), jnp.int32)),
        (
            (
                features,
                tile_ids.reshape(1, points),
                cell_ids.reshape(1, points),
                spread_weight.reshape(1, points),
                message_weight,
            ),
            "vvvvv",
        ),
        (pltpu.VMEM((points, width), BF16), pltpu.VMEM((1, points), jnp.int32)),
        "spread",
    )
    recv = lax.all_to_all(send, ("aa", "ba"), 0, 0, tiled=True)
    latent, places, p0, p1, p2, p3 = call(
        collect_body,
        (shape((cells, width), BF16), shape((1024, 128), BF16))
        + (shape((2, 64, width), BF16),) * 4,
        ((recv, basis_to), "vv"),
        (pltpu.VMEM((3072, width), BF16), pltpu.VMEM((8, 8, 128), jnp.int32)),
        "collect",
    )
    wide = call(
        widen_body,
        shape((32, 32, width), BF16),
        ((p0, shifted(p1, 1), shifted(p2, 2), shifted(p3, 3), coef), ["v"] * 4 + ["smem"]),
        (),
        "widen",
    )
    mixed = mix(lax.all_to_all(wide, "aa", 0, 0, tiled=True), spectral_weight)
    lines = call(
        narrow_body,
        shape((2, 64, width), BF16),
        ((lax.all_to_all(mixed, "aa", 0, 0, tiled=True), coef), ["v", "smem"]),
        (),
        "narrow",
    )
    back = call(
        finish_body,
        shape((devices, 24, width), BF16),
        (
            (
                lines,
                shifted(lines, 1),
                shifted(lines, 2),
                shifted(lines, 3),
                basis_from,
                latent,
                skip_weight,
                places,
            ),
            "vvvvvvvv",
        ),
        (pltpu.VMEM((cells, width), BF16),),
        "finish",
    )
    returned = lax.all_to_all(back, ("aa", "ba"), 0, 0, tiled=True)
    return call(
        decode_body,
        shape((points, width), BF16),
        (
            (
                returned.reshape(devices * 24, width),
                slots,
                read_weight.reshape(1, points),
                hidden_weight,
                output_weight,
            ),
            "vvvvv",
        ),
        (),
        "decode",
    )


def solution(mesh):
    placed = (
        P(("aa", "ba"), None),
        P(("aa", "ba"), None),
        P(("aa", "ba")),
        P(("aa", "ba")),
        P(("aa", "ba")),
        P(),
        P(),
        P("ba", "aa", None, None),
        P(),
        P(),
    )
    return jax.shard_map(
        per_device, mesh=mesh, in_specs=placed, out_specs=P(("aa", "ba"), None), check_vma=False
    )
```

time: 223 us -> 170 us (0.76)
  Pallas kernels: 0 us -> 49.3 us
  local copies, waits for them, and re-layouts: 48.1 us -> 6.36 us
  waiting for transfers between devices: 64.6 us -> 30.6 us
  other arithmetic: 25.3 us -> 0.93 us
  blocking collectives: 52.3 us -> 64.6 us
  matrix products: 11.2 us -> 0 us
  starting transfers between devices: 20.1 us -> 17.6 us
    pallas_call x0 -> x7, Pallas kernels: none -> 49.3 us  [the longest x6 44.7 us: call(): return fn(*ins[0])]
    all_to_all x3 -> x1, waiting for transfers between devices: 64.6 us -> 25.7 us  [per_device(): recv = lax.all_to_all(send, ('aa', 'ba'), 0, 0, tiled=True)]
    gather x2 -> x0, local copies, waits for them, and re-layouts: 22 us -> none  [the longest x1 13 us: per_device(): back_rows = latent_out[local_cells]]
    scatter-add x1 -> x0, other arithmetic: 18.8 us -> none  [per_device(): latent_sum = jnp.zeros((cell_count, width), jnp.float32).at[local_cells]....]
    scatter x2 -> x0, local copies, waits for them, and re-layouts: 16.1 us -> none  [the longest x1 10.1 us: per_device(): jnp.zeros((device_count * capacity, width), jnp.bfloat16).at[slots]]
    all_to_all x5 -> x3, blocking collectives: 52.3 us -> 64.6 us  [the longest x1 31.2 us: per_device(): returned = lax.all_to_all(back, ('aa', 'ba'), 0, 0, tiled=True)]
    dot_general x10 -> x0, matrix products: 11.2 us -> none  [the longest x1 3.31 us: per_device(): jnp.dot(hidden, output_weight, preferred_element_type=jnp.float32)]
    all_to_all x3 -> x1, starting transfers between devices: 20.1 us -> 11.5 us  [per_device(): recv = lax.all_to_all(send, ('aa', 'ba'), 0, 0, tiled=True)]
  transfers between devices with their start and end apart: 3 -> 7, of which waited for: 3 -> 6; matrix products, arithmetic and copies ran while one was open for 0% -> 3% of each run, Pallas kernels for 0% -> 0%
where the time goes in v1:
time: 170 us
  blocking collectives  64.6 us (38%)
  Pallas kernels  49.3 us (29%)
  waiting for transfers between devices  30.6 us (18%)
  starting transfers between devices  17.6 us (10%)
  local copies, waits for them, and re-layouts  6.36 us (4%)
    pallas_call x6, Pallas kernels, call(): return fn(*ins[0])  44.7 us
    all_to_all x1, blocking collectives, per_device(): returned = lax.all_to_all(back, ('aa', 'ba'), 0, 0, tiled=True)  31.2 us
    all_to_all x1, waiting for transfers between devices, per_device(): recv = lax.all_to_all(send, ('aa', 'ba'), 0, 0, tiled=True)  25.7 us
    all_to_all x1, blocking collectives, per_device(): mixed = mix(lax.all_to_all(wide, 'aa', 0, 0, tiled=True), spectral_weight)  17.3 us
    all_to_all x1, blocking collectives, per_device(): lax.all_to_all(mixed, 'aa', 0, 0, tiled=True)  16.2 us
    all_to_all x1, starting transfers between devices, per_device(): recv = lax.all_to_all(send, ('aa', 'ba'), 0, 0, tiled=True)  11.5 us
    ppermute x6, starting transfers between devices, shifted(): return lax.ppermute(shard, 'ba', [(i, (i + s) % 4) for i in range(4)])  6.08 us
    ppermute x6, waiting for transfers between devices, shifted(): return lax.ppermute(shard, 'ba', [(i, (i + s) % 4) for i in range(4)])  4.97 us
  transfers between devices with their start and end apart: 7, of which 6 were waited for; matrix products, arithmetic and copies ran while one was open for 3% of the time, Pallas kernels for 0%

profile of v1, /device:TPU:1, one launch (start us, length us, event | category | flops | bytes accessed | tf_op | source)
XLA Modules:
  0.0 169.5 jit_solution(7080736811484541956)
XLA Ops:
  0.0 9.4 %spread.1 = (bf16[128,56,128]{2,1,0:T(8,128)(2,1)}, s32[1,2048]{1,0:T(1,128)}) custom-call(bf16[2048,256]{1,0:T(8,128)(2,1)} %feat.1, s32[1,2048]{1,0:T(1,128)} %bitcast.16, s32[1,2048]{1,0:T(1,128)} %bitcast.17, f32[1,2048]{1,0:T(1,128)} %bitcast.18, bf16[256,256]{1,0:T(8,128)(2,1)} %weight.2), custom_call_target="tpu_custom_call" | custom-call | tf_op jit(solution)/shard_map/spread/pallas_call | solution.py:46
  9.4 11.5 %all-to-all-start = ((bf16[128,56,128]{2,1,0:T(8,128)(2,1)}), bf16[128,56,128]{2,1,0:T(8,128)(2,1)S(1)}, u32[]{:S(2)}, u32[]{:S(2)}) async-start(bf16[128,56,128]{2,1,0:T(8,128)(2,1)} %get-tuple-element.17), calls=%async_computation | async-start | bytes 3670016 | tf_op jit(solution)/shard_map/all_to_all | solution.py:292
  21.1 0.1 select_multiply_fusion.3
  21.2 0.1 select_multiply_fusion
  21.3 0.1 select_multiply_fusion.1
  21.5 0.2 multiply_convert_fusion.1
  21.7 1.5 convert_element_type.66.basis
  23.2 25.7 %all-to-all-done.recv = bf16[128,56,128]{2,1,0:T(8,128)(2,1)S(1)} async-done(((bf16[128,56,128]{2,1,0:T(8,128)(2,1)}), bf16[128,56,128]{2,1,0:T(8,128)(2,1)S(1)}, u32[]{:S(2)}, u32[]{:S(2)}) %all-to-all-start) | async-done | bytes 1835040 | tf_op jit(solution)/shard_map/all_to_all | solution.py:292
  48.9 0.0 copy-start
  48.9 1.3 copy-done
  50.1 8.6 %collect.1 = (bf16[2048,256]{1,0:T(8,128)(2,1)}, bf16[1024,128]{1,0:T(8,128)(2,1)}, bf16[2,64,256]{2,1,0:T(8,128)(2,1)}, bf16[2,64,256]{2,1,0:T(8,128)(2,1)}, bf...) custom-call(bf16[128,56,128]{2,1,0:T(8,128)(2,1)} %copy-done, bf16[256,1024]{1,0:T(8,128)(2,1)} %convert_element_type.66.basis), custom_call_target="tpu_custom_call" | custom-call | tf_op jit(solution)/shard_map/collect/pallas_call | solution.py:46
  58.7 0.3 collective-permute-start
  59.1 1.5 collective-permute-start.1
  60.6 0.9 collective-permute-start.2
  61.5 0.6 reshape.162.coef
  62.1 1.6 collective-permute-done.b
  63.7 0.0 copy-start.1
  63.7 0.9 collective-permute-done.1.c
  64.6 0.0 copy-start.2
  64.6 0.6 collective-permute-done.2.d
  65.2 0.0 copy-start.3
  65.2 0.0 copy-done.1
  65.2 0.0 copy-done.2
  65.2 0.6 copy-done.3
  65.8 2.0 %widen.1 = bf16[32,32,256]{2,1,0:T(8,128)(2,1)} custom-call(bf16[2,64,256]{2,1,0:T(8,128)(2,1)} %get-tuple-element.20.a, bf16[2,64,256]{2,1,0:T(8,128)(2,1)} %copy-done.1, bf16[2,64,256]{2,1,0:T(8,128)(2,1)} %copy-done.2, bf16[2,64,256]{2,1,0:T(8,128)(2,1)} %copy-done.3, f32[32]{0:T(128)} %reshape.162.coef), custom_call_target="tpu_custom_call" | custom-call | tf_op jit(solution)/shard_map/widen/pallas_call | solution.py:46
  67.8 17.3 %all_to_all.20.recv = bf16[32,32,256]{2,1,0:T(8,128)(2,1)} all-to-all(bf16[32,32,256]{2,1,0:T(8,128)(2,1)} %widen.1), channel_id=1, replica_groups=mesh['aa'=32,'ba'=4] {'aa'}, dimensions={0} | all-to-all | bytes 1048576 | tf_op jit(solution)/shard_map/all_to_all | solution.py:308
  85.1 4.6 %mix.1 = bf16[32,32,256]{2,1,0:T(8,128)(2,1)} custom-call(bf16[32,32,256]{2,1,0:T(8,128)(2,1)} %all_to_all.20.recv, bf16[4,8,256,256]{3,2,1,0:T(8,128)(2,1)} %weight.3), custom_call_target="tpu_custom_call" | custom-call | tf_op jit(solution)/shard_map/mix/pallas_call | solution.py:161
  89.6 16.2 %all_to_all.21.recv = bf16[32,32,256]{2,1,0:T(8,128)(2,1)} all-to-all(bf16[32,32,256]{2,1,0:T(8,128)(2,1)} %mix.1), channel_id=1, replica_groups=mesh['aa'=32,'ba'=4] {'aa'}, dimensions={0} | all-to-all | bytes 1048576 | tf_op jit(solution)/shard_map/all_to_all | solution.py:312
  105.8 1.9 %narrow.1.a = bf16[2,64,256]{2,1,0:T(8,128)(2,1)} custom-call(bf16[32,32,256]{2,1,0:T(8,128)(2,1)} %all_to_all.21.recv, f32[32]{0:T(128)} %reshape.162.coef), custom_call_target="tpu_custom_call" | custom-call | tf_op jit(solution)/shard_map/narrow/pallas_call | solution.py:46
  107.7 0.7 collective-permute-start.3
  108.4 2.6 %collective-permute-start.4 = (bf16[2,64,256]{2,1,0:T(8,128)(2,1)}, bf16[2,64,256]{2,1,0:T(8,128)(2,1)S(1)}, u32[]{:S(2)}, u32[]{:S(2)}) collective-permute-start(bf16[2,64,256]{2,1,0:T(8,128)(2,1)} %narrow.1.a), channel_id=1, source_target_pairs={{0,2},{1,3},{2,0},{3,1},{4,6},{5,7},{6,4},{7,5},{8,10},{9,11},{10,... | collective-permute-start | bytes 196616 | tf_op jit(solution)/shard_map/ppermute | solution.py:240
  111.1 0.0 collective-permute-start.5
  111.1 0.2 multiply_convert_fusion
  111.3 0.7 convert_element_type.68
  112.0 1.0 copy.13.basis
  113.0 0.0 collective-permute-done.3.b
  113.1 0.0 copy-start.4
  113.1 1.1 collective-permute-done.4.c
  114.2 0.0 copy-start.5
  114.2 0.8 collective-permute-done.5.d
  115.0 0.0 copy-start.6
  115.0 0.0 copy-done.4
  115.0 0.0 copy-done.5
  115.0 0.6 copy-done.6
  115.6 12.7 %finish.1 = bf16[128,24,256]{2,1,0:T(8,128)(2,1)} custom-call(bf16[2,64,256]{2,1,0:T(8,128)(2,1)} %narrow.1.a, bf16[2,64,256]{2,1,0:T(8,128)(2,1)} %copy-done.4, bf16[2,64,256]{2,1,0:T(8,128)(2,1)} %copy-done.5, bf16[2,64,256]{2,1,0:T(8,128)(2,1)} %copy-done.6, bf16[1024,256]{1,0:T(8,128)(2,1)} %copy.13.basis, bf16[2048,256]{1,0:T(8,128)(2,1)} %get-tuple-element.26.latent, ...), custom_call_target="tpu_custom_call" | custom-call | tf_op jit(solution)/shard_map/finish/pallas_call | solution.py:46
  128.3 31.2 %all_to_all.22 = bf16[128,24,256]{2,1,0:T(8,128)(2,1)} all-to-all(bf16[128,24,256]{2,1,0:T(8,128)(2,1)} %finish.1), channel_id=1, replica_groups=mesh['aa'=32,'ba'=4] {'aa','ba'}, dimensions={0} | all-to-all | bytes 3145728 | tf_op jit(solution)/shard_map/all_to_all | solution.py:335
  159.4 10.1 %decode.1 = bf16[2048,256]{1,0:T(8,128)(2,1)} custom-call(bf16[3072,256]{1,0:T(8,128)(2,1)} %bitcast.13, s32[1,2048]{1,0:T(1,128)} %get-tuple-element.28.slots, f32[1,2048]{1,0:T(1,128)} %bitcast.19, bf16[256,256]{1,0:T(8,128)(2,1)} %hidden_weight.1, bf16[256,256]{1,0:T(8,128)(2,1)} %output_weight.1), custom_call_target="tpu_custom_call" | custom-call | tf_op jit(solution)/shard_map/decode/pallas_call | solution.py:46
  (8 shorter events, 0.1 us)
Async XLA Ops:
  9.4 39.4 %all-to-all-start = ((bf16[128,56,128]{2,1,0:T(8,128)(2,1)}), bf16[128,56,128]{2,1,0:T(8,128)(2,1)S(1)}, u32[]{:S(2)}, u32[]{:S(2)}) async-start(bf16[128,56,128]{2,1,0:T(8,128)(2,1)} %get-tuple-element.17), calls=%async_computation | async-start | bytes 3670016 | tf_op jit(solution)/shard_map/all_to_all | solution.py:292
  48.9 1.3 copy-start
  58.7 5.0 %collective-permute-start = (bf16[2,64,256]{2,1,0:T(8,128)(2,1)}, bf16[2,64,256]{2,1,0:T(8,128)(2,1)S(1)}, u32[]{:S(2)}, u32[]{:S(2)}) collective-permute-start(bf16[2,64,256]{2,1,0:T(8,128)(2,1)} %get-tuple-element.21), channel_id=1, source_target_pairs={{0,1},{1,2},{2,3},{3,0},{4,5},{5,6},{6,7},{7,4},{8,9},{9,10},{10,1... | collective-permute-start | bytes 196616 | tf_op jit(solution)/shard_map/ppermute | solution.py:240
  59.1 5.5 %collective-permute-start.1 = (bf16[2,64,256]{2,1,0:T(8,128)(2,1)}, bf16[2,64,256]{2,1,0:T(8,128)(2,1)S(1)}, u32[]{:S(2)}, u32[]{:S(2)}) collective-permute-start(bf16[2,64,256]{2,1,0:T(8,128)(2,1)} %get-tuple-element.22), channel_id=1, source_target_pairs={{0,2},{1,3},{2,0},{3,1},{4,6},{5,7},{6,4},{7,5},{8,10},{9,11},{10,... | collective-permute-start | bytes 196616 | tf_op jit(solution)/shard_map/ppermute | solution.py:240
  60.6 4.6 %collective-permute-start.2 = (bf16[2,64,256]{2,1,0:T(8,128)(2,1)}, bf16[2,64,256]{2,1,0:T(8,128)(2,1)S(1)}, u32[]{:S(2)}, u32[]{:S(2)}) collective-permute-start(bf16[2,64,256]{2,1,0:T(8,128)(2,1)} %get-tuple-element.23), channel_id=1, source_target_pairs={{0,3},{1,0},{2,1},{3,2},{4,7},{5,4},{6,5},{7,6},{8,11},{9,8},{10,9... | collective-permute-start | bytes 196616 | tf_op jit(solution)/shard_map/ppermute | solution.py:240
  63.7 1.5 copy-start.1
  64.6 0.6 copy-start.2
  65.2 0.6 copy-start.3
  107.7 5.3 %collective-permute-start.3 = (bf16[2,64,256]{2,1,0:T(8,128)(2,1)}, bf16[2,64,256]{2,1,0:T(8,128)(2,1)S(1)}, u32[]{:S(2)}, u32[]{:S(2)}) collective-permute-start(bf16[2,64,256]{2,1,0:T(8,128)(2,1)} %narrow.1.a), channel_id=1, source_target_pairs={{0,1},{1,2},{2,3},{3,0},{4,5},{5,6},{6,7},{7,4},{8,9},{9,10},{10,1... | collective-permute-start | bytes 196616 | tf_op jit(solution)/shard_map/ppermute | solution.py:240
  108.4 5.7 %collective-permute-start.4 = (bf16[2,64,256]{2,1,0:T(8,128)(2,1)}, bf16[2,64,256]{2,1,0:T(8,128)(2,1)S(1)}, u32[]{:S(2)}, u32[]{:S(2)}) collective-permute-start(bf16[2,64,256]{2,1,0:T(8,128)(2,1)} %narrow.1.a), channel_id=1, source_target_pairs={{0,2},{1,3},{2,0},{3,1},{4,6},{5,7},{6,4},{7,5},{8,10},{9,11},{10,... | collective-permute-start | bytes 196616 | tf_op jit(solution)/shard_map/ppermute | solution.py:240
  111.1 3.9 %collective-permute-start.5 = (bf16[2,64,256]{2,1,0:T(8,128)(2,1)}, bf16[2,64,256]{2,1,0:T(8,128)(2,1)S(1)}, u32[]{:S(2)}, u32[]{:S(2)}) collective-permute-start(bf16[2,64,256]{2,1,0:T(8,128)(2,1)} %narrow.1.a), channel_id=1, source_target_pairs={{0,3},{1,0},{2,1},{3,2},{4,7},{5,4},{6,5},{7,6},{8,11},{9,8},{10,9... | collective-permute-start | bytes 196616 | tf_op jit(solution)/shard_map/ppermute | solution.py:240
  113.1 1.9 %copy-start.4 = (bf16[2,64,256]{2,1,0:T(8,128)(2,1)}, bf16[2,64,256]{2,1,0:T(8,128)(2,1)S(1)}, u32[]{:S(2)}) copy-start(bf16[2,64,256]{2,1,0:T(8,128)(2,1)S(1)} %collective-permute-done.3.b) | copy-start | bytes 196612
  114.2 0.8 copy-start.5
  115.0 0.6 copy-start.6

commit v2 on v1

--- a/solution.py
+++ b/solution.py
@@ -42,6 +42,7 @@
         out_specs=VMEM if single else [VMEM] * len(outs),
         scratch_shapes=list(scratch),
         name=name,
+        compiler_params=pltpu.CompilerParams(vmem_limit_bytes=20 * 2**20),
     )
     return fn(*ins[0])
 
@@ -168,6 +169,7 @@
         out_specs=pl.BlockSpec((32, 8, 256), lambda j: (0, j, 0)),
         out_shape=jax.ShapeDtypeStruct((32, 32, 256), BF16),
         name="mix",
+        compiler_params=pltpu.CompilerParams(vmem_limit_bytes=16 * 2**20),
     )(recv, weight)
 
 

time: 170 us -> 159 us (0.935)
  Pallas kernels: 49.3 us -> 35.4 us
  local copies, waits for them, and re-layouts: 6.36 us -> 10.8 us
  blocking collectives: 64.6 us -> 61.6 us
    pallas_call x6, Pallas kernels: 44.7 us -> 34.1 us  [call(): return fn(*ins[0])]
    unnamed x14 -> x28, local copies, waits for them, and re-layouts: 2.49 us -> 8.38 us
    pallas_call x1, Pallas kernels: 4.57 us -> 1.31 us  [mix(): pl.pallas_call(mix_body, grid=(4,), in_specs=[pl.BlockSpec((32, 8, 256),...]
where the time goes in v2:
time: 159 us; the launch traced here: 158 us
  blocking collectives  61.6 us (39%)
  Pallas kernels  35.4 us (22%)
  waiting for transfers between devices  30.8 us (19%)
  starting transfers between devices  17.5 us (11%)
  local copies, waits for them, and re-layouts  10.8 us (7%)
  other arithmetic  2.12 us (1%)
    pallas_call x6, Pallas kernels, call(): return fn(*ins[0])  34.1 us
    all_to_all x1, blocking collectives, per_device(): returned = lax.all_to_all(back, ('aa', 'ba'), 0, 0, tiled=True)  30.9 us
    all_to_all x1, waiting for transfers between devices, per_device(): recv = lax.all_to_all(send, ('aa', 'ba'), 0, 0, tiled=True)  25.3 us
    all_to_all x1, blocking collectives, per_device(): mixed = mix(lax.all_to_all(wide, 'aa', 0, 0, tiled=True), spectral_weight)  15.7 us
    all_to_all x1, blocking collectives, per_device(): lax.all_to_all(mixed, 'aa', 0, 0, tiled=True)  15.1 us
    all_to_all x1, starting transfers between devices, per_device(): recv = lax.all_to_all(send, ('aa', 'ba'), 0, 0, tiled=True)  11.5 us
    unnamed x28, local copies, waits for them, and re-layouts  8.38 us
    ppermute x6, starting transfers between devices, shifted(): return lax.ppermute(shard, 'ba', [(i, (i + s) % 4) for i in range(4)])  6.02 us
  transfers between devices with their start and end apart: 7, of which 6 were waited for; matrix products, arithmetic and copies ran while one was open for 3% of the time, Pallas kernels for 0%

profile of v2, /device:TPU:1, one launch (start us, length us, event | category | flops | bytes accessed | tf_op | source)
XLA Modules:
  0.0 158.4 jit_solution(13300530427132072820)
XLA Ops:
  0.0 0.0 copy-start.2
  0.0 1.2 copy-done.2
  1.2 0.0 copy-start.5
  1.2 0.9 copy-done.5
  2.1 0.0 copy-start.9
  2.1 0.7 copy-done.9
  2.8 0.0 copy-start.10
  2.8 0.7 copy-done.10
  3.5 0.0 copy-start.11
  3.5 0.7 copy-done.11
  4.2 7.0 %spread.1 = (bf16[128,56,128]{2,1,0:T(8,128)(2,1)S(1)}, s32[1,2048]{1,0:T(1,128)S(1)}) custom-call(bf16[2048,256]{1,0:T(8,128)(2,1)S(1)} %copy-done.2, s32[1,2048]{1,0:T(1,128)S(1)} %bitcast.14, s32[1,2048]{1,0:T(1,128)S(1)} %bitcast.15, f32[1,2048]{1,0:T(1,128)S(1)} %bitcast.16, bf16[256,256]{1,0:T(8,128)(2,1)S(1)} %copy-done.5), custom_call_target="tpu_custom_call" | custom-call | tf_op jit(solution)/shard_map/spread/pallas_call | solution.py:47
  11.2 0.0 copy-start.1
  11.2 1.2 copy-done.1
  12.5 11.5 %all-to-all-start = ((bf16[128,56,128]{2,1,0:T(8,128)(2,1)}), bf16[128,56,128]{2,1,0:T(8,128)(2,1)S(1)}, u32[]{:S(2)}, u32[]{:S(2)}) async-start(bf16[128,56,128]{2,1,0:T(8,128)(2,1)} %copy-done.1), calls=%async_computation | async-start | bytes 3670016 | tf_op jit(solution)/shard_map/all_to_all | solution.py:294
  24.1 0.1 select_multiply_fusion.3
  24.2 0.7 select_multiply_fusion
  24.9 0.7 select_multiply_fusion.1
  25.7 0.2 multiply_convert_fusion.1
  25.9 0.7 convert_element_type.66.basis
  26.6 25.3 %all-to-all-done.recv = bf16[128,56,128]{2,1,0:T(8,128)(2,1)S(1)} async-done(((bf16[128,56,128]{2,1,0:T(8,128)(2,1)}), bf16[128,56,128]{2,1,0:T(8,128)(2,1)S(1)}, u32[]{:S(2)}, u32[]{:S(2)}) %all-to-all-start) | async-done | bytes 1835040 | tf_op jit(solution)/shard_map/all_to_all | solution.py:294
  51.9 7.0 %collect.1 = (bf16[2048,256]{1,0:T(8,128)(2,1)S(1)}, bf16[1024,128]{1,0:T(8,128)(2,1)S(1)}, bf16[2,64,256]{2,1,0:T(8,128)(2,1)S(1)}, bf16[2,64,256]{2,1,0:T(8,12...) custom-call(bf16[128,56,128]{2,1,0:T(8,128)(2,1)S(1)} %all-to-all-done.recv, ...), custom_call_target="tpu_custom_call" | custom-call | tf_op jit(solution)/shard_map/collect/pallas_call | solution.py:47
  58.9 0.0 copy-start.3
  58.9 0.7 copy-done.3
  59.6 0.3 collective-permute-start
  59.9 1.5 collective-permute-start.1
  61.5 0.9 collective-permute-start.2
  62.3 0.8 reshape.162.coef
  63.1 1.5 collective-permute-done.b
  64.6 0.9 collective-permute-done.1.c
  65.5 0.6 collective-permute-done.2.d
  66.1 0.8 widen.1
  66.9 15.7 %all_to_all.20.recv = bf16[32,32,256]{2,1,0:T(8,128)(2,1)S(1)} all-to-all(bf16[32,32,256]{2,1,0:T(8,128)(2,1)S(1)} %widen.1), channel_id=1, replica_groups=mesh['aa'=32,'ba'=4] {'aa'}, dimensions={0} | all-to-all | bytes 1048576 | tf_op jit(solution)/shard_map/all_to_all | solution.py:310
  82.5 0.0 copy-start
  82.5 2.2 %copy-done = bf16[4,8,256,256]{3,2,1,0:T(8,128)(2,1)S(1)} copy-done((bf16[4,8,256,256]{3,2,1,0:T(8,128)(2,1)S(1)}, bf16[4,8,256,256]{3,2,1,0:T(8,128)(2,1)}, u32[]{:S(2)}) %copy-start) | copy-done | bytes 4194328
  84.7 0.0 copy-start.13
  84.7 1.3 mix.1
  86.0 15.1 %all_to_all.21.recv = bf16[32,32,256]{2,1,0:T(8,128)(2,1)S(1)} all-to-all(bf16[32,32,256]{2,1,0:T(8,128)(2,1)S(1)} %mix.1), channel_id=1, replica_groups=mesh['aa'=32,'ba'=4] {'aa'}, dimensions={0} | all-to-all | bytes 1048576 | tf_op jit(solution)/shard_map/all_to_all | solution.py:314
  101.1 0.0 copy-start.4
  101.1 0.0 copy-start.8
  101.1 0.8 narrow.1.a
  101.9 0.7 collective-permute-start.3
  102.6 2.6 %collective-permute-start.4 = (bf16[2,64,256]{2,1,0:T(8,128)(2,1)S(1)}, bf16[2,64,256]{2,1,0:T(8,128)(2,1)S(1)}, u32[]{:S(2)}, u32[]{:S(2)}) collective-permute-start(bf16[2,64,256]{2,1,0:T(8,128)(2,1)S(1)} %narrow.1.a), channel_id=1, source_target_pairs={{0,2},{1,3},{2,0},{3,1},{4,6},{5,7},{6,4},{7,5},{8,10},{9,11},{10,... | collective-permute-start | bytes 196616 | tf_op jit(solution)/shard_map/ppermute | solution.py:242
  105.2 0.0 collective-permute-start.5
  105.2 0.0 copy-done.13
  105.2 0.2 multiply_convert_fusion
  105.4 0.7 convert_element_type.68
  106.2 0.2 copy.13.basis
  106.4 0.0 collective-permute-done.3.b
  106.4 1.7 %collective-permute-done.4.c = bf16[2,64,256]{2,1,0:T(8,128)(2,1)S(1)} collective-permute-done((bf16[2,64,256]{2,1,0:T(8,128)(2,1)S(1)}, bf16[2,64,256]{2,1,0:T(8,128)(2,1)S(1)}, u32[]{:S(2)}, u32[]{:S(2)}) %collective-permute-start.4) | collective-permute-done | bytes 65568 | tf_op jit(solution)/shard_map/ppermute | solution.py:242
  108.1 0.9 collective-permute-done.5.d
  109.0 0.0 copy-done.4
  109.0 0.0 copy-done.8
  109.0 9.9 %finish.1 = bf16[128,24,256]{2,1,0:T(8,128)(2,1)S(1)} custom-call(bf16[2,64,256]{2,1,0:T(8,128)(2,1)S(1)} %narrow.1.a, bf16[2,64,256]{2,1,0:T(8,128)(2,1)S(1)} %collective-permute-done.3.b, bf16[2,64,256]{2,1,0:T(8,128)(2,1)S(1)} %collective-permute-done.4.c, bf16[2,64,256]{2,1,0:T(8,128)(2,1)S(1)} %collective-permute-done.5.d, ...), custom_call_target="tpu_custom_call" | custom-call | tf_op jit(solution)/shard_map/finish/pallas_call | solution.py:47
  118.9 0.0 copy-start.6
  118.9 0.0 copy-start.7
  118.9 0.0 copy-start.12
  118.9 30.9 %all_to_all.22 = bf16[128,24,256]{2,1,0:T(8,128)(2,1)S(1)} all-to-all(bf16[128,24,256]{2,1,0:T(8,128)(2,1)S(1)} %finish.1), channel_id=1, replica_groups=mesh['aa'=32,'ba'=4] {'aa','ba'}, dimensions={0} | all-to-all | bytes 3145728 | tf_op jit(solution)/shard_map/all_to_all | solution.py:337
  149.8 0.0 copy-done.6
  149.8 0.0 copy-done.7
  149.8 0.0 copy-done.12
  149.8 8.6 %decode.1 = bf16[2048,256]{1,0:T(8,128)(2,1)} custom-call(bf16[3072,256]{1,0:T(8,128)(2,1)S(1)} %bitcast.13, s32[1,2048]{1,0:T(1,128)S(1)} %get-tuple-element.28.slots, f32[1,2048]{1,0:T(1,128)S(1)} %bitcast.17, bf16[256,256]{1,0:T(8,128)(2,1)S(1)} %copy-done.6, bf16[256,256]{1,0:T(8,128)(2,1)S(1)} %copy-done.7), custom_call_target="tpu_custom_call" | custom-call | tf_op jit(solution)/shard_map/decode/pallas_call | solution.py:47
  (8 shorter events, 0.1 us)
Async XLA Ops:
  0.0 1.2 copy-start.2
  1.2 0.9 copy-start.5
  2.1 0.7 copy-start.9
  2.8 0.7 copy-start.10
  3.5 0.7 copy-start.11
  11.2 1.3 copy-start.1
  12.5 39.4 %all-to-all-start = ((bf16[128,56,128]{2,1,0:T(8,128)(2,1)}), bf16[128,56,128]{2,1,0:T(8,128)(2,1)S(1)}, u32[]{:S(2)}, u32[]{:S(2)}) async-start(bf16[128,56,128]{2,1,0:T(8,128)(2,1)} %copy-done.1), calls=%async_computation | async-start | bytes 3670016 | tf_op jit(solution)/shard_map/all_to_all | solution.py:294
  58.9 0.7 copy-start.3
  59.6 5.0 %collective-permute-start = (bf16[2,64,256]{2,1,0:T(8,128)(2,1)}, bf16[2,64,256]{2,1,0:T(8,128)(2,1)S(1)}, u32[]{:S(2)}, u32[]{:S(2)}) collective-permute-start(bf16[2,64,256]{2,1,0:T(8,128)(2,1)} %get-tuple-element.21), channel_id=1, source_target_pairs={{0,1},{1,2},{2,3},{3,0},{4,5},{5,6},{6,7},{7,4},{8,9},{9,10},{10,1... | collective-permute-start | bytes 196616 | tf_op jit(solution)/shard_map/ppermute | solution.py:242
  59.9 5.5 %collective-permute-start.1 = (bf16[2,64,256]{2,1,0:T(8,128)(2,1)}, bf16[2,64,256]{2,1,0:T(8,128)(2,1)S(1)}, u32[]{:S(2)}, u32[]{:S(2)}) collective-permute-start(bf16[2,64,256]{2,1,0:T(8,128)(2,1)} %get-tuple-element.22), channel_id=1, source_target_pairs={{0,2},{1,3},{2,0},{3,1},{4,6},{5,7},{6,4},{7,5},{8,10},{9,11},{10,... | collective-permute-start | bytes 196616 | tf_op jit(solution)/shard_map/ppermute | solution.py:242
  61.5 4.6 %collective-permute-start.2 = (bf16[2,64,256]{2,1,0:T(8,128)(2,1)S(1)}, bf16[2,64,256]{2,1,0:T(8,128)(2,1)S(1)}, u32[]{:S(2)}, u32[]{:S(2)}) collective-permute-start(bf16[2,64,256]{2,1,0:T(8,128)(2,1)S(1)} %get-tuple-element.23), channel_id=1, source_target_pairs={{0,3},{1,0},{2,1},{3,2},{4,7},{5,4},{6,5},{7,6},{8,11},{9,8},{10,9... | collective-permute-start | bytes 196616 | tf_op jit(solution)/shard_map/ppermute | solution.py:242
  82.5 2.2 %copy-start = (bf16[4,8,256,256]{3,2,1,0:T(8,128)(2,1)S(1)}, bf16[4,8,256,256]{3,2,1,0:T(8,128)(2,1)}, u32[]{:S(2)}) copy-start(bf16[4,8,256,256]{3,2,1,0:T(8,128)(2,1)} %weight.3) | copy-start | bytes 12582916
  84.7 20.5 %copy-start.13 = (f32[16,16]{1,0:T(8,128)S(1)}, f32[16,16]{1,0:T(8,128)}, u32[]{:S(2)}) copy-start(f32[16,16]{1,0:T(8,128)} %get-tuple-element.25) | copy-start | bytes 3076
  101.1 7.9 %copy-start.4 = (bf16[1024,128]{1,0:T(8,128)(2,1)S(1)}, bf16[1024,128]{1,0:T(8,128)(2,1)}, u32[]{:S(2)}) copy-start(bf16[1024,128]{1,0:T(8,128)(2,1)} %copy-done.3) | copy-start | bytes 786436
  101.1 7.9 %copy-start.8 = (bf16[256,256]{1,0:T(8,128)(2,1)S(1)}, bf16[256,256]{1,0:T(8,128)(2,1)}, u32[]{:S(2)}) copy-start(bf16[256,256]{1,0:T(8,128)(2,1)} %skip.1) | copy-start | bytes 393220
  101.9 4.5 %collective-permute-start.3 = (bf16[2,64,256]{2,1,0:T(8,128)(2,1)S(1)}, bf16[2,64,256]{2,1,0:T(8,128)(2,1)S(1)}, u32[]{:S(2)}, u32[]{:S(2)}) collective-permute-start(bf16[2,64,256]{2,1,0:T(8,128)(2,1)S(1)} %narrow.1.a), channel_id=1, source_target_pairs={{0,1},{1,2},{2,3},{3,0},{4,5},{5,6},{6,7},{7,4},{8,9},{9,10},{10,1... | collective-permute-start | bytes 196616 | tf_op jit(solution)/shard_map/ppermute | solution.py:242
  102.6 5.5 %collective-permute-start.4 = (bf16[2,64,256]{2,1,0:T(8,128)(2,1)S(1)}, bf16[2,64,256]{2,1,0:T(8,128)(2,1)S(1)}, u32[]{:S(2)}, u32[]{:S(2)}) collective-permute-start(bf16[2,64,256]{2,1,0:T(8,128)(2,1)S(1)} %narrow.1.a), channel_id=1, source_target_pairs={{0,2},{1,3},{2,0},{3,1},{4,6},{5,7},{6,4},{7,5},{8,10},{9,11},{10,... | collective-permute-start | bytes 196616 | tf_op jit(solution)/shard_map/ppermute | solution.py:242
  105.2 3.8 %collective-permute-start.5 = (bf16[2,64,256]{2,1,0:T(8,128)(2,1)S(1)}, bf16[2,64,256]{2,1,0:T(8,128)(2,1)S(1)}, u32[]{:S(2)}, u32[]{:S(2)}) collective-permute-start(bf16[2,64,256]{2,1,0:T(8,128)(2,1)S(1)} %narrow.1.a), channel_id=1, source_target_pairs={{0,3},{1,0},{2,1},{3,2},{4,7},{5,4},{6,5},{7,6},{8,11},{9,8},{10,9... | collective-permute-start | bytes 196616 | tf_op jit(solution)/shard_map/ppermute | solution.py:242
  118.9 30.9 %copy-start.6 = (bf16[256,256]{1,0:T(8,128)(2,1)S(1)}, bf16[256,256]{1,0:T(8,128)(2,1)}, u32[]{:S(2)}) copy-start(bf16[256,256]{1,0:T(8,128)(2,1)} %hidden_weight.1) | copy-start | bytes 393220
  118.9 30.9 %copy-start.7 = (bf16[256,256]{1,0:T(8,128)(2,1)S(1)}, bf16[256,256]{1,0:T(8,128)(2,1)}, u32[]{:S(2)}) copy-start(bf16[256,256]{1,0:T(8,128)(2,1)} %output_weight.1) | copy-start | bytes 393220
  118.9 30.9 %copy-start.12 = (f32[2048]{0:T(1024)S(1)}, f32[2048]{0:T(1024)}, u32[]{:S(2)}) copy-start(f32[2048]{0:T(1024)} %param.14) | copy-start | bytes 24580

commit v3 on v1

v3 whole, which is shorter than its diff:
```python
import math

import jax
import jax.numpy as jnp
from jax import lax
from jax.experimental import pallas as pl
from jax.experimental.pallas import tpu as pltpu
from jax.sharding import Mesh
from jax.sharding import PartitionSpec as P

G = 64
M = 16
F32 = jnp.float32
BF16 = jnp.bfloat16
VMEM = pl.BlockSpec(memory_space=pltpu.VMEM)


def iota(shape, dim):
    return lax.broadcasted_iota(jnp.int32, shape, dim)


def mm(a, b):
    return lax.dot_general(a, b, (((1,), (0,)), ((), ())), preferred_element_type=F32)


def mm_nt(a, b):
    return lax.dot_general(a, b, (((1,), (1,)), ((), ())), preferred_element_type=F32)


def as_column(row, lanes):
    n = row.shape[1]
    return jnp.transpose(jnp.broadcast_to(row, (lanes, n)))


def call(body, outs, ins, scratch=(), name=None, limit=20, flops=1000000):
    single = not isinstance(outs, (tuple, list))
    fn = pl.pallas_call(
        body,
        out_shape=outs,
        in_specs=[VMEM] * len(ins),
        out_specs=VMEM if single else [VMEM] * len(outs),
        scratch_shapes=list(scratch),
        name=name,
        compiler_params=pltpu.CompilerParams(vmem_limit_bytes=limit * 2**20),
        cost_estimate=pl.CostEstimate(flops=flops, transcendentals=0, bytes_accessed=4000000),
    )
    return fn(*ins)


def spread_body(feat, tile, cell, spread, weight, send, slots, message, rank_row):
    devices = send.shape[0]
    points = feat.shape[0]
    cap = 24
    upper = (iota((256, 256), 0) < iota((256, 256), 1)).astype(BF16)
    ones = jnp.ones((256, 128), BF16)
    used = jnp.zeros((devices, 256), F32)
    for at in range(0, points, 256):
        hot = tile[:, at : at + 256] == iota((devices, 256), 0)
        hot = hot.astype(F32)
        hot16 = hot.astype(BF16)
        before = mm(hot16, upper) + used
        total = mm(hot16, ones)
        used = used + jnp.concatenate([total, total], axis=1)
        rank = jnp.sum(hot * before, axis=0, keepdims=True).astype(jnp.int32)
        rank_row[:, at : at + 256] = rank
        slots[:, at : at + 256] = tile[:, at : at + 256] * cap + rank
    for at in range(0, points, 128):
        product = mm(feat[at : at + 128, :], weight[...])
        scale = as_column(spread[:, at : at + 128], 128)
        scale = jnp.concatenate([scale, scale], axis=1)
        message[at : at + 128, :] = (scale * product).astype(BF16)
    rank = rank_row[...]
    group = lax.shift_right_logical(rank, 3)
    low = tile[...] * 8 + lax.bitwise_and(rank, 7)
    high_part = lax.shift_right_logical(cell[...], 6).astype(F32)
    low_part = lax.bitwise_and(cell[...], 63).astype(F32)
    lane = iota((128, points), 0)
    where = jnp.where(lane == 2 * group, high_part, 0.0)
    where = jnp.where(lane == 2 * group + 1, low_part, where).astype(BF16)
    slot = slots[...]

    def fill(step, carry):
        base = step * 16
        hot = (slot - base * cap == iota((16 * cap, points), 0)).astype(BF16)
        rows = mm(hot, message[...])
        left = rows[:, :128].reshape(16, cap, 128).astype(BF16)
        right = rows[:, 128:].reshape(16, cap, 128).astype(BF16)
        hot8 = (low - base * 8 == iota((128, points), 0)).astype(BF16)
        placing = mm_nt(hot8, where).reshape(16, 8, 128).astype(BF16)
        send[pl.ds(base, 16), 0:cap, :] = left
        send[pl.ds(base, 16), cap : 2 * cap, :] = right
        send[pl.ds(base, 16), 2 * cap :, :] = placing
        return carry

    lax.fori_loop(0, devices // 16, fill, 0)


def positions(tile, cell):
    x = lax.shift_right_logical(tile, 2) * 2 + lax.shift_right_logical(cell, 10)
    y = lax.bitwise_and(tile, 3) * 16 + lax.bitwise_and(lax.shift_right_logical(cell, 6), 15)
    return x, y, lax.bitwise_and(cell, 63)


def spectrum_body(message, tile, cell, table_x, table_y, table_z, out, ys, yz, xs):
    points = message.shape[0]
    x, y, z = positions(tile[...], cell[...])

    def values(table, at):
        hot = (at == iota((64, points), 0)).astype(BF16)
        both = mm(table[...], hot)
        half = both.shape[0] // 2
        return both[:half] + both[half:]

    xs[...] = values(table_x, x)
    ys[...] = values(table_y, y)
    zs = values(table_z, z)

    def some(s, carry):
        for j in range(4):
            yz[j * 8 : j * 8 + 8, :] = zs * ys[pl.ds(s * 4 + j, 1), :]
        rows = [(xs[i : i + 1, :] * yz[...]).astype(BF16) for i in range(16)]
        part = mm(jnp.concatenate(rows, axis=0), message[...])
        out[pl.ds(s * 512, 512), :] = part.astype(BF16)
        return carry

    lax.fori_loop(0, 4, some, 0)


def spectrum(message, tile, cell, table_x, table_y, table_z, name):
    points = message.shape[0]
    return call(
        spectrum_body,
        jax.ShapeDtypeStruct((2048, 256), BF16),
        (message, tile, cell, table_x, table_y, table_z),
        (
            pltpu.VMEM((16, points), F32),
            pltpu.VMEM((32, points), F32),
            pltpu.VMEM((16, points), F32),
        ),
        name,
        flops=2 * 2048 * 2048 * 256,
    )


def add_body(*refs):
    count = len(refs) - 4
    total = refs[0][...].astype(F32)
    for r in refs[1:count]:
        total = total + r[...].astype(F32)
    rows = total.shape[0] // 4
    for s in range(4):
        refs[count + s][...] = total[s * rows : s * rows + rows].astype(BF16)


def add_and_cut(parts, name):
    rows, width = parts[0].shape
    piece = jax.ShapeDtypeStruct((rows // 4, width), BF16)
    return call(add_body, (piece,) * 4, parts, (), name)


def join_body(*refs):
    rows = refs[0].shape[0]
    for s in range(4):
        refs[4][s * rows : s * rows + rows, :] = refs[s][...]


def joined(parts, name):
    rows, width = parts[0].shape
    return call(join_body, jax.ShapeDtypeStruct((rows * 4, width), BF16), parts, (), name)


def collect_body(recv, out, rows, ids, places, latent):
    picks = jnp.where(
        iota((8, 128), 1) == 2 * iota((8, 128), 0),
        64.0,
        jnp.where(iota((8, 128), 1) == 2 * iota((8, 128), 0) + 1, 1.0, 0.0),
    ).astype(BF16)

    def unpack(step, carry):
        block = recv[pl.ds(step * 16, 16)].astype(F32)
        place = block[:, 48:56, :].reshape(128, 128).astype(BF16)
        places[pl.ds(step * 128, 128), :] = place
        ids[step] = mm_nt(picks, place).astype(jnp.int32)
        for g in range(3):
            left = block[:, g * 8 : g * 8 + 8, :].reshape(128, 128)
            right = block[:, 24 + g * 8 : 32 + g * 8, :].reshape(128, 128)
            both = jnp.concatenate([left, right], axis=1).astype(BF16)
            rows[pl.ds(step * 384 + g * 128, 128), :] = both
        return carry

    lax.fori_loop(0, 8, unpack, 0)
    tile = 256

    def total(step, carry):
        at = step * tile
        cells = iota((tile, 128), 0) + at
        hot = [
            (ids[i, g : g + 1, :] == cells).astype(BF16) for i in range(8) for g in range(3)
        ]
        latent[pl.ds(at, tile), :] = mm(jnp.concatenate(hot, axis=1), rows[...]).astype(BF16)
        return carry

    lax.fori_loop(0, latent.shape[0] // tile, total, 0)

    def back(step, carry):
        place = places[pl.ds(step * 128, 128), :]
        for g in range(3):
            lane = iota((128, 128), 0)
            pick = jnp.where(lane == 2 * g, 64.0, jnp.where(lane == 2 * g + 1, 1.0, 0.0))
            cell = mm(place, pick.astype(BF16)).astype(jnp.int32)
            hot = [
                (cell == iota((128, 128), 1) + 128 * k).astype(BF16) for k in range(16)
            ]
            got = mm(jnp.concatenate(hot, axis=1), latent[...])
            out[pl.ds(step * 16, 16), g * 8 : g * 8 + 8, :] = got.reshape(16, 8, 256).astype(BF16)
        return carry

    lax.fori_loop(0, 8, back, 0)


def mix_body(a, b, c, d, weight, out):
    spec = a[...].astype(F32) + b[...].astype(F32) + c[...].astype(F32) + d[...].astype(F32)
    spec = spec.astype(BF16)
    row = iota((8, 256), 0)
    for j in range(4):
        mixed = jnp.zeros((8, 256), F32)
        for m in range(8):
            mixed = jnp.where(row == m, mm(spec[j * 8 : j * 8 + 8], weight[j, m]), mixed)
        out[j * 8 : j * 8 + 8, :] = mixed.astype(BF16)


def own_body(returned, slots, skip, out):
    def some(step, carry):
        at = step * 256
        hot = []
        for part in range(2):
            slot = as_column(slots[:, pl.ds(at + part * 128, 128)], 128)
            one = [(slot == iota((128, 128), 1) + 128 * k).astype(BF16) for k in range(24)]
            hot.append(jnp.concatenate(one, axis=1))
        own = mm(jnp.concatenate(hot, axis=0), returned[...]).astype(BF16)
        out[pl.ds(at, 256), :] = mm(own, skip[...])
        return carry

    lax.fori_loop(0, out.shape[0] // 256, some, 0)


def decode_body(
    m0, m1, m2, m3, m4, m5, m6, m7, tile, cell, wide_x, wide_y, wide_z,
    base, read, hidden_weight, output_weight, out, spots,
):
    x, y, z = positions(tile[...], cell[...])
    spots[0:1, :] = x
    spots[1:2, :] = y
    spots[2:3, :] = z
    modes = (m0, m1, m2, m3, m4, m5, m6, m7)
    lane = lax.bitwise_and(iota((256, 128), 1), 63)

    def some(step, carry):
        at = step * 256

        def column(row):
            return jnp.concatenate(
                [as_column(row(at + 128 * part), 128) for part in range(2)], axis=0
            )

        def values(which, table):
            col = column(lambda lo: spots[which : which + 1, pl.ds(lo, 128)])
            return mm((col == lane).astype(BF16), table[...])

        vx = values(0, wide_x)
        vy = values(1, wide_y)
        vz = values(2, wide_z)
        total = base[pl.ds(at, 256), :]
        for h in range(2):
            for s in range(4):
                yz = vy[:, s * 128 : s * 128 + 128] * vz[:, h * 128 : h * 128 + 128]
                wave = [(yz * vx[:, i * 128 : i * 128 + 128]).astype(BF16) for i in range(4)]
                total = total + mm(jnp.concatenate(wave, axis=1), modes[h * 4 + s][...])
        value = jax.nn.gelu(total).astype(BF16).astype(F32)
        scale = column(lambda lo: read[:, pl.ds(lo, 128)])
        gathered = (jnp.concatenate([scale, scale], axis=1) * value).astype(BF16)
        hidden = jax.nn.gelu(mm(gathered, hidden_weight[...])).astype(BF16)
        out[pl.ds(at, 256), :] = mm(hidden, output_weight[...]).astype(BF16)
        return carry

    lax.fori_loop(0, out.shape[0] // 256, some, 0)


def basis_table(mode, position):
    half = M // 2
    frequency = jnp.where(mode < half, mode, mode - half + 1).astype(F32)
    phase = 2.0 * math.pi * frequency * position.astype(F32) / G
    wave = jnp.where(mode < half, jnp.cos(phase), jnp.sin(phase))
    return wave * jnp.where(mode == 0, math.sqrt(1.0 / G), math.sqrt(2.0 / G))


def two_terms(table):
    high = lax.reduce_precision(table, 8, 7)
    return jnp.concatenate([high, table - high], axis=0).astype(BF16)


def around(shard, axis, s):
    return lax.ppermute(shard, axis, [(i, (i + s) % 4) for i in range(4)])


def from_others(pieces, axis):
    return (pieces[0],) + tuple(around(pieces[s], axis, s) for s in (1, 2, 3))


def swapped(shard):
    return lax.ppermute(shard, "core", [(0, 1), (1, 0)])


def per_device(
    features,
    tile_ids,
    cell_ids,
    spread_weight,
    read_weight,
    message_weight,
    skip_weight,
    spectral_weight,
    hidden_weight,
    output_weight,
):
    points, width = features.shape
    everyone = ("z", "y", "core", "ba")
    devices = lax.axis_size(everyone)
    shape = jax.ShapeDtypeStruct
    at_z, at_y, at_core, at_b = (lax.axis_index(a) for a in everyone)
    tile = tile_ids.reshape(1, points)
    cell = cell_ids.reshape(1, points)
    grid = jnp.arange(G, dtype=jnp.int32)

    def mode_x(i, sign):
        return 4 * ((at_z + sign * (i // 4)) % 4) + (at_y + sign * (i % 4)) % 4

    def mode_y(s, j, sign):
        return 4 * ((at_b + sign * s) % 4) + j

    i16 = jnp.arange(16, dtype=jnp.int32)
    k8 = jnp.arange(8, dtype=jnp.int32)
    to_x = two_terms(basis_table(mode_x(i16, 1)[:, None], grid[None, :]))
    to_y = two_terms(basis_table(mode_y(i16 // 4, i16 % 4, 1)[:, None], grid[None, :]))
    other_z = two_terms(basis_table((8 * (1 - at_core) + k8)[:, None], grid[None, :]))
    own_z = two_terms(basis_table((8 * at_core + k8)[:, None], grid[None, :]))
    lane = jnp.arange(512, dtype=jnp.int32)
    wide_x = two_terms(basis_table(mode_x(lane // 32, -1)[None, :], grid[:, None]))
    wide_y = two_terms(
        basis_table(mode_y(lane // 128, lane // 8 % 4, -1)[None, :], grid[:, None])
    )
    lane = lane[:256]
    wide_z = two_terms(
        basis_table((8 * ((at_core + lane // 128) % 2) + lane % 8)[None, :], grid[:, None])
    )

    send, slots, message = call(
        spread_body,
        (
            shape((devices, 56, 128), BF16),
            shape((1, points), jnp.int32),
            shape((points, width), BF16),
        ),
        (features, tile, cell, spread_weight.reshape(1, points), message_weight),
        (pltpu.VMEM((1, points), jnp.int32),),
        "spread",
        limit=60,
    )
    recv = lax.all_to_all(send, everyone, 0, 0, tiled=True)
    away = spectrum(message, tile, cell, to_x, to_y, other_z, "spectrum_away")
    near = spectrum(message, tile, cell, to_x, to_y, own_z, "spectrum_near")
    parts = add_and_cut((near, swapped(away)), "add_core")
    parts = add_and_cut(from_others(parts, "ba"), "add_ba")
    parts = add_and_cut(from_others(parts, "z"), "add_z")
    mixed = call(
        mix_body,
        shape((32, width), BF16),
        from_others(parts, "y") + (spectral_weight,),
        (),
        "mix",
    )
    line = joined(from_others((mixed,) * 4, "y"), "join_y")
    plane = joined(from_others((line,) * 4, "z"), "join_z")
    modes = from_others((plane,) * 4, "ba")
    modes = modes + tuple(swapped(m) for m in modes)

    back = call(
        collect_body,
        shape((devices, 24, width), BF16),
        (recv,),
        (
            pltpu.VMEM((3072, width), BF16),
            pltpu.VMEM((8, 8, 128), jnp.int32),
            pltpu.VMEM((1024, 128), BF16),
            pltpu.VMEM((2048, width), BF16),
        ),
        "collect",
        flops=4 * 3072 * 2048 * 256,
    )
    returned = lax.all_to_all(back, everyone, 0, 0, tiled=True)
    base = call(
        own_body,
        shape((points, width), F32),
        (returned.reshape(devices * 24, width), slots, skip_weight),
        (),
        "own",
        flops=2 * 3072 * 2048 * 256,
    )
    return call(
        decode_body,
        shape((points, width), BF16),
        modes
        + (
            tile,
            cell,
            wide_x,
            wide_y,
            wide_z,
            base,
            read_weight.reshape(1, points),
            hidden_weight,
            output_weight,
        ),
        (pltpu.VMEM((8, points), jnp.int32),),
        "decode",
        flops=2 * 4096 * 2048 * 256,
    )


def solution(mesh):
    finer = Mesh(mesh.devices.reshape(4, 4, 2, 4), ("z", "y", "core", "ba"))
    rows = P(("z", "y", "core", "ba"))
    every = P()
    placed = (
        P(("z", "y", "core", "ba"), None),
        P(("z", "y", "core", "ba"), None),
        rows,
        rows,
        rows,
        every,
        every,
        P("ba", ("z", "y", "core"), None, None),
        every,
        every,
    )
    return jax.shard_map(
        per_device,
        mesh=finer,
        in_specs=placed,
        out_specs=P(("z", "y", "core", "ba"), None),
        check_vma=False,
    )
```

time: 170 us -> 158 us (0.929)
  blocking collectives: 64.6 us -> 0 us
  starting transfers between devices: 17.6 us -> 55.8 us
  waiting for transfers between devices: 30.6 us -> 40.9 us
  Pallas kernels: 49.3 us -> 56.6 us
  local copies, waits for them, and re-layouts: 6.36 us -> 2.23 us
    all_to_all x3 -> x0, blocking collectives: 64.6 us -> none  [the longest x1 31.2 us: per_device(): returned = lax.all_to_all(back, ('aa', 'ba'), 0, 0, tiled=True)]
    ppermute x6 -> x23, starting transfers between devices: 6.08 us -> 39.7 us  [the longest x18 24 us: around(): return lax.ppermute(shard, axis, [(i, (i + s) % 4) for i in range(4)])]
    ppermute x6 -> x23, waiting for transfers between devices: 4.97 us -> 25.4 us  [the longest x18 25.4 us: around(): return lax.ppermute(shard, axis, [(i, (i + s) % 4) for i in range(4)])]
    all_to_all x1 -> x2, waiting for transfers between devices: 25.7 us -> 15.5 us  [the longest x1 15.5 us: per_device(): recv = lax.all_to_all(send, everyone, 0, 0, tiled=True)]
    pallas_call x7 -> x12, Pallas kernels: 49.3 us -> 56.6 us  [call(): return fn(*ins)]
    all_to_all x1 -> x2, starting transfers between devices: 11.5 us -> 16.1 us  [the longest x1 11.5 us: per_device(): recv = lax.all_to_all(send, everyone, 0, 0, tiled=True)]
    convert_element_type x3 -> x0, local copies, waits for them, and re-layouts: 3.25 us -> none  [the longest x2 1.74 us: per_device(): basis_from = basis_from.reshape(1024, 256).astype(BF16)]
  transfers between devices with their start and end apart: 7 -> 25, of which waited for: 6 -> 10; matrix products, arithmetic and copies ran while one was open for 3% -> 1% of each run, Pallas kernels for 0% -> 19%
where the time goes in v3:
time: 158 us
  Pallas kernels  56.6 us (36%)
  starting transfers between devices  55.8 us (35%)
  waiting for transfers between devices  40.9 us (26%)
  local copies, waits for them, and re-layouts  2.23 us (1%)
  other arithmetic  1.89 us (1%)
    pallas_call x12, Pallas kernels, call(): return fn(*ins)  56.6 us
    ppermute x18, waiting for transfers between devices, around(): return lax.ppermute(shard, axis, [(i, (i + s) % 4) for i in range(4)])  25.4 us
    ppermute x18, starting transfers between devices, around(): return lax.ppermute(shard, axis, [(i, (i + s) % 4) for i in range(4)])  24 us
    ppermute x5, starting transfers between devices, swapped(): return lax.ppermute(shard, 'core', [(0, 1), (1, 0)])  15.8 us
    all_to_all x1, waiting for transfers between devices, per_device(): recv = lax.all_to_all(send, everyone, 0, 0, tiled=True)  15.5 us
    all_to_all x1, starting transfers between devices, per_device(): recv = lax.all_to_all(send, everyone, 0, 0, tiled=True)  11.5 us
    all_to_all x1, starting transfers between devices, per_device(): returned = lax.all_to_all(back, everyone, 0, 0, tiled=True)  4.57 us
  transfers between devices with their start and end apart: 25, of which 10 were waited for; matrix products, arithmetic and copies ran while one was open for 1% of the time, Pallas kernels for 19%

profile of v3, /device:TPU:1, one launch (start us, length us, event | category | flops | bytes accessed | tf_op | source)
XLA Modules:
  0.0 157.7 jit_solution(11344306006932421819)
XLA Ops:
  0.0 9.5 %spread.1 = (bf16[128,56,128]{2,1,0:T(8,128)(2,1)}, s32[1,2048]{1,0:T(1,128)}, bf16[2048,256]{1,0:T(8,128)(2,1)}) custom-call(bf16[2048,256]{1,0:T(8,128)(2,1)} %feat.1, s32[1,2048]{1,0:T(1,128)} %bitcast.6, s32[1,2048]{1,0:T(1,128)} %bitcast.10, f32[1,2048]{1,0:T(1,128)} %bitcast.15, bf16[256,256]{1,0:T(8,128)(2,1)} %weight.2), custom_call_target="tpu_custom_call" | custom-call | flops 1000000 | bytes 4000000 | tf_op jit(solution)/shard_map/spread/pallas_call | solution.py:47
  9.5 11.5 %all-to-all-start = ((bf16[128,56,128]{2,1,0:T(8,128)(2,1)}), bf16[128,56,128]{2,1,0:T(8,128)(2,1)S(1)}, u32[]{:S(2)}, u32[]{:S(2)}) async-start(bf16[128,56,128]{2,1,0:T(8,128)(2,1)} %get-tuple-element.33), calls=%async_computation | async-start | bytes 3670016 | tf_op jit(solution)/shard_map/all_to_all | solution.py:369
  21.1 0.1 reduce-precision_convert_fusion.5
  21.3 0.1 reduce-precision_convert_fusion.3
  21.5 0.0 copy-start.4
  21.5 3.1 %spectrum_away.1 = bf16[2048,256]{1,0:T(8,128)(2,1)S(1)} custom-call(bf16[2048,256]{1,0:T(8,128)(2,1)S(1)} %copy-done.3, s32[1,2048]{1,0:T(1,128)S(1)} %bitcast.7, s32[1,2048]{1,0:T(1,128)S(1)} %bitcast.11, bf16[32,64]{1,0:T(8,128)(2,1)S(1)} %pad_maximum_fusion.3.table_x, bf16[32,64]{1,0:T(8,128)(2,1)S(1)} %pad_maximum_fusion.4.table_y, ...), custom_call_target="tpu_custom_call" | custom-call | flops 2147483648 | bytes 4000000 | tf_op jit(solution)/shard_map/spectrum_away/pallas_call | solution.py:47
  24.6 1.1 collective-permute-start
  25.8 3.1 %spectrum_near.1.refs_0_ = bf16[2048,256]{1,0:T(8,128)(2,1)S(1)} custom-call(bf16[2048,256]{1,0:T(8,128)(2,1)S(1)} %copy-done.4, s32[1,2048]{1,0:T(1,128)S(1)} %bitcast.8, s32[1,2048]{1,0:T(1,128)S(1)} %bitcast.12, bf16[32,64]{1,0:T(8,128)(2,1)S(1)} %pad_maximum_fusion.3.table_x, bf16[32,64]{1,0:T(8,128)(2,1)S(1)} %pad_maximum_fusion.4.table_y, ...), custom_call_target="tpu_custom_call" | custom-call | flops 2147483648 | bytes 4000000 | tf_op jit(solution)/shard_map/spectrum_near/pallas_call | solution.py:47
  28.9 0.0 collective-permute-done.refs_1_
  28.9 0.9 add_core.1
  29.8 0.7 collective-permute-start.1
  30.4 2.4 %collective-permute-start.2 = (bf16[512,256]{1,0:T(8,128)(2,1)S(1)}, bf16[512,256]{1,0:T(8,128)(2,1)S(1)}, u32[]{:S(2)}, u32[]{:S(2)}) collective-permute-start(bf16[512,256]{1,0:T(8,128)(2,1)S(1)} %get-tuple-element.23), channel_id=1, source_target_pairs={{0,2},{1,3},{2,0},{3,1},{4,6},{5,7},{6,4},{7,5},{8,10},{9,11},{10,... | collective-permute-start | bytes 786440 | tf_op jit(solution)/shard_map/ppermute | solution.py:303
  32.8 1.2 collective-permute-start.3
  34.0 15.5 %all-to-all-done.recv = bf16[128,56,128]{2,1,0:T(8,128)(2,1)S(1)} async-done(((bf16[128,56,128]{2,1,0:T(8,128)(2,1)}), bf16[128,56,128]{2,1,0:T(8,128)(2,1)S(1)}, u32[]{:S(2)}, u32[]{:S(2)}) %all-to-all-start) | async-done | bytes 1835040 | tf_op jit(solution)/shard_map/all_to_all | solution.py:369
  49.5 16.1 %collect.1 = bf16[128,24,256]{2,1,0:T(8,128)(2,1)} custom-call(bf16[128,56,128]{2,1,0:T(8,128)(2,1)S(1)} %all-to-all-done.recv), custom_call_target="tpu_custom_call" | custom-call | flops 6442450944 | bytes 4000000 | tf_op jit(solution)/shard_map/collect/pallas_call | solution.py:47
  65.6 4.6 %all-to-all-start.1 = ((bf16[128,24,256]{2,1,0:T(8,128)(2,1)}), bf16[128,24,256]{2,1,0:T(8,128)(2,1)S(1)}, u32[]{:S(2)}, u32[]{:S(2)}) async-start(bf16[128,24,256]{2,1,0:T(8,128)(2,1)} %collect.1), calls=%async_computation.1 | async-start | bytes 3145728 | tf_op jit(solution)/shard_map/all_to_all | solution.py:400
  70.2 0.0 collective-permute-done.1.refs_1_
  70.3 0.0 collective-permute-done.2.refs_2_
  70.3 0.0 collective-permute-done.3.refs_3_
  70.3 0.1 add_ba.1
  70.4 1.6 collective-permute-start.4
  72.0 2.9 %collective-permute-start.5 = (bf16[128,256]{1,0:T(8,128)(2,1)S(1)}, bf16[128,256]{1,0:T(8,128)(2,1)S(1)}, u32[]{:S(2)}, u32[]{:S(2)}) collective-permute-start(bf16[128,256]{1,0:T(8,128)(2,1)S(1)} %get-tuple-element.27), channel_id=1, source_target_pairs={{0,64},{32,96},{64,0},{96,32},{1,65},{33,97},{65,1},{97,33},{2,66}... | collective-permute-start | bytes 196616 | tf_op jit(solution)/shard_map/ppermute | solution.py:303
  74.9 0.9 collective-permute-start.6
  75.8 1.1 reduce-precision_convert_fusion
  76.9 10.9 %collective-permute-done.4.refs_1_ = bf16[128,256]{1,0:T(8,128)(2,1)S(1)} collective-permute-done((bf16[128,256]{1,0:T(8,128)(2,1)S(1)}, bf16[128,256]{1,0:T(8,128)(2,1)S(1)}, u32[]{:S(2)}, u32[]{:S(2)}) %collective-permute-start.4) | collective-permute-done | bytes 65568 | tf_op jit(solution)/shard_map/ppermute | solution.py:303
  87.8 5.4 %collective-permute-done.5.refs_2_ = bf16[128,256]{1,0:T(8,128)(2,1)S(1)} collective-permute-done((bf16[128,256]{1,0:T(8,128)(2,1)S(1)}, bf16[128,256]{1,0:T(8,128)(2,1)S(1)}, u32[]{:S(2)}, u32[]{:S(2)}) %collective-permute-start.5) | collective-permute-done | bytes 65568 | tf_op jit(solution)/shard_map/ppermute | solution.py:303
  93.2 0.0 collective-permute-done.6.refs_3_
  93.2 1.4 collective-permute-start.7
  94.6 2.4 %collective-permute-start.8 = (bf16[32,256]{1,0:T(8,128)(2,1)S(1)}, bf16[32,256]{1,0:T(8,128)(2,1)S(1)}, u32[]{:S(2)}, u32[]{:S(2)}) collective-permute-start(bf16[32,256]{1,0:T(8,128)(2,1)S(1)} %get-tuple-element.31), channel_id=1, source_target_pairs={{0,16},{8,24},{16,0},{24,8},{1,17},{9,25},{17,1},{25,9},{2,18},{10... | collective-permute-start | bytes 49160 | tf_op jit(solution)/shard_map/ppermute | solution.py:303
  97.1 1.0 collective-permute-start.9
  98.1 0.0 collective-permute-done.7.b
  98.1 0.7 collective-permute-done.8.c
  98.8 1.2 collective-permute-done.9.d
  100.0 2.2 %copy-done = bf16[4,8,256,256]{3,2,1,0:T(8,128)(2,1)S(1)} copy-done((bf16[4,8,256,256]{3,2,1,0:T(8,128)(2,1)S(1)}, bf16[4,8,256,256]{3,2,1,0:T(8,128)(2,1)}, u32[]{:S(2)}) %copy-start) | copy-done | bytes 4194328
  102.2 0.7 mix.1.refs_0_
  102.8 2.4 %collective-permute-start.12 = (bf16[32,256]{1,0:T(8,128)(2,1)S(1)}, bf16[32,256]{1,0:T(8,128)(2,1)S(1)}, u32[]{:S(2)}, u32[]{:S(2)}) collective-permute-start(bf16[32,256]{1,0:T(8,128)(2,1)S(1)} %mix.1.refs_0_), channel_id=1, source_target_pairs={{0,24},{8,0},{16,8},{24,16},{1,25},{9,1},{17,9},{25,17},{2,26},{10... | collective-permute-start | bytes 49160 | tf_op jit(solution)/shard_map/ppermute | solution.py:303
  105.2 0.0 collective-permute-start.11
  105.2 0.7 collective-permute-start.10
  105.8 0.2 collective-permute-done.12.refs_3_
  106.0 3.2 %collective-permute-done.11.refs_2_ = bf16[32,256]{1,0:T(8,128)(2,1)S(1)} collective-permute-done((bf16[32,256]{1,0:T(8,128)(2,1)S(1)}, bf16[32,256]{1,0:T(8,128)(2,1)S(1)}, u32[]{:S(2)}, u32[]{:S(2)}) %collective-permute-start.11) | collective-permute-done | bytes 16416 | tf_op jit(solution)/shard_map/ppermute | solution.py:303
  109.3 0.5 collective-permute-start.15
  109.8 1.6 %collective-permute-start.14 = (bf16[128,256]{1,0:T(8,128)(2,1)S(1)}, bf16[128,256]{1,0:T(8,128)(2,1)S(1)}, u32[]{:S(2)}, u32[]{:S(2)}) collective-permute-start(bf16[128,256]{1,0:T(8,128)(2,1)S(1)} %join_y.1.refs_0_), channel_id=1, source_target_pairs={{0,64},{32,96},{64,0},{96,32},{1,65},{33,97},{65,1},{97,33},{2,66}... | collective-permute-start | bytes 196616 | tf_op jit(solution)/shard_map/ppermute | solution.py:303
  111.4 0.1 collective-permute-start.13
  111.5 0.3 reduce-precision_convert_fusion.2
  111.9 0.8 collective-permute-done.15.refs_3_
  112.7 1.7 %collective-permute-done.14.refs_2_ = bf16[128,256]{1,0:T(8,128)(2,1)S(1)} collective-permute-done((bf16[128,256]{1,0:T(8,128)(2,1)S(1)}, bf16[128,256]{1,0:T(8,128)(2,1)S(1)}, u32[]{:S(2)}, u32[]{:S(2)}) %collective-permute-start.14) | collective-permute-done | bytes 65568 | tf_op jit(solution)/shard_map/ppermute | solution.py:303
  114.4 1.3 collective-permute-done.13.refs_1_
  115.7 2.9 %collective-permute-start.18 = (bf16[512,256]{1,0:T(8,128)(2,1)S(1)}, bf16[512,256]{1,0:T(8,128)(2,1)S(1)}, u32[]{:S(2)}, u32[]{:S(2)}) collective-permute-start(bf16[512,256]{1,0:T(8,128)(2,1)S(1)} %join_z.1.m0), channel_id=1, source_target_pairs={{0,3},{1,0},{2,1},{3,2},{4,7},{5,4},{6,5},{7,6},{8,11},{9,8},{10,9... | collective-permute-start | bytes 786440 | tf_op jit(solution)/shard_map/ppermute | solution.py:303
  118.6 0.5 collective-permute-start.17
  119.1 0.8 collective-permute-start.16
  119.9 5.7 %collective-permute-start.19 = (bf16[512,256]{1,0:T(8,128)(2,1)S(1)}, bf16[512,256]{1,0:T(8,128)(2,1)S(1)}, u32[]{:S(2)}, u32[]{:S(2)}) collective-permute-start(bf16[512,256]{1,0:T(8,128)(2,1)S(1)} %join_z.1.m0), channel_id=1, source_target_pairs={{0,4},{4,0},{1,5},{5,1},{2,6},{6,2},{3,7},{7,3},{8,12},{12,8},{9,1... | collective-permute-start | bytes 786440 | tf_op jit(solution)/shard_map/ppermute | solution.py:311
  125.6 0.0 collective-permute-done.18.m3
  125.6 5.1 %collective-permute-start.22 = (bf16[512,256]{1,0:T(8,128)(2,1)S(1)}, bf16[512,256]{1,0:T(8,128)(2,1)}, u32[]{:S(2)}, u32[]{:S(2)}) collective-permute-start(bf16[512,256]{1,0:T(8,128)(2,1)S(1)} %collective-permute-done.18.m3), channel_id=1, source_target_pairs={{0,4},{4,0},{1,5},{5,1},{2,6},{6,2},{3,7},{7,3},{8,12},{12,8},{9,1... | collective-permute-start | bytes 786440 | tf_op jit(solution)/shard_map/ppermute | solution.py:311
  130.8 1.0 collective-permute-start.21
  131.8 0.0 collective-permute-done.16.m1
  131.8 2.7 %collective-permute-start.20 = (bf16[512,256]{1,0:T(8,128)(2,1)S(1)}, bf16[512,256]{1,0:T(8,128)(2,1)}, u32[]{:S(2)}, u32[]{:S(2)}) collective-permute-start(bf16[512,256]{1,0:T(8,128)(2,1)S(1)} %collective-permute-done.16.m1), channel_id=1, source_target_pairs={{0,4},{4,0},{1,5},{5,1},{2,6},{6,2},{3,7},{7,3},{8,12},{12,8},{9,1... | collective-permute-start | bytes 786440 | tf_op jit(solution)/shard_map/ppermute | solution.py:311
  134.5 0.0 all-to-all-done.1
  134.5 0.0 copy-start.6
  134.6 0.0 copy-start.7
  134.6 0.0 copy-start.8
  134.6 6.2 %own.1.base = f32[2048,256]{1,0:T(8,128)S(1)} custom-call(bf16[3072,256]{1,0:T(8,128)(2,1)S(1)} %bitcast.5, s32[1,2048]{1,0:T(1,128)S(1)} %copy-done.9, bf16[256,256]{1,0:T(8,128)(2,1)S(1)} %copy-done.5), custom_call_target="tpu_custom_call" | custom-call | flops 3221225472 | bytes 4000000 | tf_op jit(solution)/shard_map/own/pallas_call | solution.py:47
  140.8 0.0 collective-permute-done.22.m7
  140.8 0.0 collective-permute-done.21.m6
  140.8 16.8 %decode.1 = bf16[2048,256]{1,0:T(8,128)(2,1)} custom-call(bf16[512,256]{1,0:T(8,128)(2,1)S(1)} %join_z.1.m0, bf16[512,256]{1,0:T(8,128)(2,1)S(1)} %collective-permute-done.16.m1, bf16[512,256]{1,0:T(8,128)(2,1)S(1)} %collective-permute-done.17.m2, bf16[512,256]{1,0:T(8,128)(2,1)S(1)} %collective-permute-done.18.m3, ...), custom_call_target="tpu_custom_call" | custom-call | flops 4294967296 | bytes 4000000 | tf_op jit(solution)/shard_map/decode/pallas_call | solution.py:47
  (42 shorter events, 0.3 us)
Async XLA Ops:
  9.5 12.0 %copy-start.1 = (s32[2048,1]{0,1:T(1,128)S(1)}, s32[2048,1]{0,1:T(1,128)}, u32[]{:S(2)}) copy-start(s32[2048,1]{0,1:T(1,128)} %param.11) | copy-start | bytes 24580
  9.5 12.0 %copy-start.2 = (s32[2048]{0:T(1024)S(1)}, s32[2048]{0:T(1024)}, u32[]{:S(2)}) copy-start(s32[2048]{0:T(1024)} %param.12) | copy-start | bytes 24580
  9.5 12.0 %copy-start.3 = (bf16[2048,256]{1,0:T(8,128)(2,1)S(1)}, bf16[2048,256]{1,0:T(8,128)(2,1)}, u32[]{:S(2)}) copy-start(bf16[2048,256]{1,0:T(8,128)(2,1)} %get-tuple-element.20.message) | copy-start | bytes 3145732
  9.5 40.0 %all-to-all-start = ((bf16[128,56,128]{2,1,0:T(8,128)(2,1)}), bf16[128,56,128]{2,1,0:T(8,128)(2,1)S(1)}, u32[]{:S(2)}, u32[]{:S(2)}) async-start(bf16[128,56,128]{2,1,0:T(8,128)(2,1)} %get-tuple-element.33), calls=%async_computation | async-start | bytes 3670016 | tf_op jit(solution)/shard_map/all_to_all | solution.py:369
  21.5 4.3 %copy-start.4 = (bf16[2048,256]{1,0:T(8,128)(2,1)S(1)}, bf16[2048,256]{1,0:T(8,128)(2,1)}, u32[]{:S(2)}) copy-start(bf16[2048,256]{1,0:T(8,128)(2,1)} %get-tuple-element.20.message) | copy-start | bytes 3145732
  24.6 4.3 %collective-permute-start = (bf16[2048,256]{1,0:T(8,128)(2,1)S(1)}, bf16[2048,256]{1,0:T(8,128)(2,1)S(1)}, u32[]{:S(2)}, u32[]{:S(2)}) collective-permute-start(bf16[2048,256]{1,0:T(8,128)(2,1)S(1)} %spectrum_away.1), channel_id=1, source_target_pairs={{0,4},{4,0},{1,5},{5,1},{2,6},{6,2},{3,7},{7,3},{8,12},{12,8},{9,1... | collective-permute-start | bytes 3145736 | tf_op jit(solution)/shard_map/ppermute | solution.py:311
  29.8 40.5 %collective-permute-start.1 = (bf16[512,256]{1,0:T(8,128)(2,1)}, bf16[512,256]{1,0:T(8,128)(2,1)S(1)}, u32[]{:S(2)}, u32[]{:S(2)}) collective-permute-start(bf16[512,256]{1,0:T(8,128)(2,1)} %get-tuple-element.22), channel_id=1, source_target_pairs={{0,1},{1,2},{2,3},{3,0},{4,5},{5,6},{6,7},{7,4},{8,9},{9,10},{10,1... | collective-permute-start | bytes 786440 | tf_op jit(solution)/shard_map/ppermute | solution.py:303
  30.4 39.8 %collective-permute-start.2 = (bf16[512,256]{1,0:T(8,128)(2,1)S(1)}, bf16[512,256]{1,0:T(8,128)(2,1)S(1)}, u32[]{:S(2)}, u32[]{:S(2)}) collective-permute-start(bf16[512,256]{1,0:T(8,128)(2,1)S(1)} %get-tuple-element.23), channel_id=1, source_target_pairs={{0,2},{1,3},{2,0},{3,1},{4,6},{5,7},{6,4},{7,5},{8,10},{9,11},{10,... | collective-permute-start | bytes 786440 | tf_op jit(solution)/shard_map/ppermute | solution.py:303
  32.8 37.4 %collective-permute-start.3 = (bf16[512,256]{1,0:T(8,128)(2,1)S(1)}, bf16[512,256]{1,0:T(8,128)(2,1)S(1)}, u32[]{:S(2)}, u32[]{:S(2)}) collective-permute-start(bf16[512,256]{1,0:T(8,128)(2,1)S(1)} %get-tuple-element.24), channel_id=1, source_target_pairs={{0,3},{1,0},{2,1},{3,2},{4,7},{5,4},{6,5},{7,6},{8,11},{9,8},{10,9... | collective-permute-start | bytes 786440 | tf_op jit(solution)/shard_map/ppermute | solution.py:303
  65.6 68.9 %all-to-all-start.1 = ((bf16[128,24,256]{2,1,0:T(8,128)(2,1)}), bf16[128,24,256]{2,1,0:T(8,128)(2,1)S(1)}, u32[]{:S(2)}, u32[]{:S(2)}) async-start(bf16[128,24,256]{2,1,0:T(8,128)(2,1)} %collect.1), calls=%async_computation.1 | async-start | bytes 3145728 | tf_op jit(solution)/shard_map/all_to_all | solution.py:400
  70.4 17.4 %collective-permute-start.4 = (bf16[128,256]{1,0:T(8,128)(2,1)S(1)}, bf16[128,256]{1,0:T(8,128)(2,1)S(1)}, u32[]{:S(2)}, u32[]{:S(2)}) collective-permute-start(bf16[128,256]{1,0:T(8,128)(2,1)S(1)} %get-tuple-element.26), channel_id=1, source_target_pairs={{0,32},{32,64},{64,96},{96,0},{1,33},{33,65},{65,97},{97,1},{2,34}... | collective-permute-start | bytes 196616 | tf_op jit(solution)/shard_map/ppermute | solution.py:303
  72.0 21.2 %collective-permute-start.5 = (bf16[128,256]{1,0:T(8,128)(2,1)S(1)}, bf16[128,256]{1,0:T(8,128)(2,1)S(1)}, u32[]{:S(2)}, u32[]{:S(2)}) collective-permute-start(bf16[128,256]{1,0:T(8,128)(2,1)S(1)} %get-tuple-element.27), channel_id=1, source_target_pairs={{0,64},{32,96},{64,0},{96,32},{1,65},{33,97},{65,1},{97,33},{2,66}... | collective-permute-start | bytes 196616 | tf_op jit(solution)/shard_map/ppermute | solution.py:303
  74.9 18.3 %collective-permute-start.6 = (bf16[128,256]{1,0:T(8,128)(2,1)S(1)}, bf16[128,256]{1,0:T(8,128)(2,1)S(1)}, u32[]{:S(2)}, u32[]{:S(2)}) collective-permute-start(bf16[128,256]{1,0:T(8,128)(2,1)S(1)} %get-tuple-element.28), channel_id=1, source_target_pairs={{0,96},{32,0},{64,32},{96,64},{1,97},{33,1},{65,33},{97,65},{2,98}... | collective-permute-start | bytes 196616 | tf_op jit(solution)/shard_map/ppermute | solution.py:303
  93.2 4.9 %collective-permute-start.7 = (bf16[32,256]{1,0:T(8,128)(2,1)S(1)}, bf16[32,256]{1,0:T(8,128)(2,1)S(1)}, u32[]{:S(2)}, u32[]{:S(2)}) collective-permute-start(bf16[32,256]{1,0:T(8,128)(2,1)S(1)} %get-tuple-element.30), channel_id=1, source_target_pairs={{0,8},{8,16},{16,24},{24,0},{1,9},{9,17},{17,25},{25,1},{2,10},{10... | collective-permute-start | bytes 49160 | tf_op jit(solution)/shard_map/ppermute | solution.py:303
  94.6 4.1 %collective-permute-start.8 = (bf16[32,256]{1,0:T(8,128)(2,1)S(1)}, bf16[32,256]{1,0:T(8,128)(2,1)S(1)}, u32[]{:S(2)}, u32[]{:S(2)}) collective-permute-start(bf16[32,256]{1,0:T(8,128)(2,1)S(1)} %get-tuple-element.31), channel_id=1, source_target_pairs={{0,16},{8,24},{16,0},{24,8},{1,17},{9,25},{17,1},{25,9},{2,18},{10... | collective-permute-start | bytes 49160 | tf_op jit(solution)/shard_map/ppermute | solution.py:303
  97.1 2.9 %collective-permute-start.9 = (bf16[32,256]{1,0:T(8,128)(2,1)S(1)}, bf16[32,256]{1,0:T(8,128)(2,1)S(1)}, u32[]{:S(2)}, u32[]{:S(2)}) collective-permute-start(bf16[32,256]{1,0:T(8,128)(2,1)S(1)} %get-tuple-element.32), channel_id=1, source_target_pairs={{0,24},{8,0},{16,8},{24,16},{1,25},{9,1},{17,9},{25,17},{2,26},{10... | collective-permute-start | bytes 49160 | tf_op jit(solution)/shard_map/ppermute | solution.py:303
  100.0 2.2 %copy-start = (bf16[4,8,256,256]{3,2,1,0:T(8,128)(2,1)S(1)}, bf16[4,8,256,256]{3,2,1,0:T(8,128)(2,1)}, u32[]{:S(2)}) copy-start(bf16[4,8,256,256]{3,2,1,0:T(8,128)(2,1)} %weight.3) | copy-start | bytes 12582916
  102.1 32.4 %copy-start.5 = (bf16[256,256]{1,0:T(8,128)(2,1)S(1)}, bf16[256,256]{1,0:T(8,128)(2,1)}, u32[]{:S(2)}) copy-start(bf16[256,256]{1,0:T(8,128)(2,1)} %skip.1) | copy-start | bytes 393220
  102.1 32.4 %copy-start.9 = (s32[1,2048]{1,0:T(1,128)S(1)}, s32[1,2048]{1,0:T(1,128)}, u32[]{:S(2)}) copy-start(s32[1,2048]{1,0:T(1,128)} %get-tuple-element.34.slots) | copy-start | bytes 24580
  102.8 3.2 %collective-permute-start.12 = (bf16[32,256]{1,0:T(8,128)(2,1)S(1)}, bf16[32,256]{1,0:T(8,128)(2,1)S(1)}, u32[]{:S(2)}, u32[]{:S(2)}) collective-permute-start(bf16[32,256]{1,0:T(8,128)(2,1)S(1)} %mix.1.refs_0_), channel_id=1, source_target_pairs={{0,24},{8,0},{16,8},{24,16},{1,25},{9,1},{17,9},{25,17},{2,26},{10... | collective-permute-start | bytes 49160 | tf_op jit(solution)/shard_map/ppermute | solution.py:303
  105.2 4.1 %collective-permute-start.11 = (bf16[32,256]{1,0:T(8,128)(2,1)S(1)}, bf16[32,256]{1,0:T(8,128)(2,1)S(1)}, u32[]{:S(2)}, u32[]{:S(2)}) collective-permute-start(bf16[32,256]{1,0:T(8,128)(2,1)S(1)} %mix.1.refs_0_), channel_id=1, source_target_pairs={{0,16},{8,24},{16,0},{24,8},{1,17},{9,25},{17,1},{25,9},{2,18},{10... | collective-permute-start | bytes 49160 | tf_op jit(solution)/shard_map/ppermute | solution.py:303
  105.2 4.1 %collective-permute-start.10 = (bf16[32,256]{1,0:T(8,128)(2,1)S(1)}, bf16[32,256]{1,0:T(8,128)(2,1)S(1)}, u32[]{:S(2)}, u32[]{:S(2)}) collective-permute-start(bf16[32,256]{1,0:T(8,128)(2,1)S(1)} %mix.1.refs_0_), channel_id=1, source_target_pairs={{0,8},{8,16},{16,24},{24,0},{1,9},{9,17},{17,25},{25,1},{2,10},{10... | collective-permute-start | bytes 49160 | tf_op jit(solution)/shard_map/ppermute | solution.py:303
  109.3 3.4 %collective-permute-start.15 = (bf16[128,256]{1,0:T(8,128)(2,1)S(1)}, bf16[128,256]{1,0:T(8,128)(2,1)S(1)}, u32[]{:S(2)}, u32[]{:S(2)}) collective-permute-start(bf16[128,256]{1,0:T(8,128)(2,1)S(1)} %join_y.1.refs_0_), channel_id=1, source_target_pairs={{0,96},{32,0},{64,32},{96,64},{1,97},{33,1},{65,33},{97,65},{2,98}... | collective-permute-start | bytes 196616 | tf_op jit(solution)/shard_map/ppermute | solution.py:303
  109.8 4.6 %collective-permute-start.14 = (bf16[128,256]{1,0:T(8,128)(2,1)S(1)}, bf16[128,256]{1,0:T(8,128)(2,1)S(1)}, u32[]{:S(2)}, u32[]{:S(2)}) collective-permute-start(bf16[128,256]{1,0:T(8,128)(2,1)S(1)} %join_y.1.refs_0_), channel_id=1, source_target_pairs={{0,64},{32,96},{64,0},{96,32},{1,65},{33,97},{65,1},{97,33},{2,66}... | collective-permute-start | bytes 196616 | tf_op jit(solution)/shard_map/ppermute | solution.py:303
  111.4 4.3 %collective-permute-start.13 = (bf16[128,256]{1,0:T(8,128)(2,1)S(1)}, bf16[128,256]{1,0:T(8,128)(2,1)S(1)}, u32[]{:S(2)}, u32[]{:S(2)}) collective-permute-start(bf16[128,256]{1,0:T(8,128)(2,1)S(1)} %join_y.1.refs_0_), channel_id=1, source_target_pairs={{0,32},{32,64},{64,96},{96,0},{1,33},{33,65},{65,97},{97,1},{2,34}... | collective-permute-start | bytes 196616 | tf_op jit(solution)/shard_map/ppermute | solution.py:303
  115.7 9.9 %collective-permute-start.18 = (bf16[512,256]{1,0:T(8,128)(2,1)S(1)}, bf16[512,256]{1,0:T(8,128)(2,1)S(1)}, u32[]{:S(2)}, u32[]{:S(2)}) collective-permute-start(bf16[512,256]{1,0:T(8,128)(2,1)S(1)} %join_z.1.m0), channel_id=1, source_target_pairs={{0,3},{1,0},{2,1},{3,2},{4,7},{5,4},{6,5},{7,6},{8,11},{9,8},{10,9... | collective-permute-start | bytes 786440 | tf_op jit(solution)/shard_map/ppermute | solution.py:303
  118.6 12.1 %collective-permute-start.17 = (bf16[512,256]{1,0:T(8,128)(2,1)S(1)}, bf16[512,256]{1,0:T(8,128)(2,1)S(1)}, u32[]{:S(2)}, u32[]{:S(2)}) collective-permute-start(bf16[512,256]{1,0:T(8,128)(2,1)S(1)} %join_z.1.m0), channel_id=1, source_target_pairs={{0,2},{1,3},{2,0},{3,1},{4,6},{5,7},{6,4},{7,5},{8,10},{9,11},{10,... | collective-permute-start | bytes 786440 | tf_op jit(solution)/shard_map/ppermute | solution.py:303
  119.1 12.7 %collective-permute-start.16 = (bf16[512,256]{1,0:T(8,128)(2,1)S(1)}, bf16[512,256]{1,0:T(8,128)(2,1)S(1)}, u32[]{:S(2)}, u32[]{:S(2)}) collective-permute-start(bf16[512,256]{1,0:T(8,128)(2,1)S(1)} %join_z.1.m0), channel_id=1, source_target_pairs={{0,1},{1,2},{2,3},{3,0},{4,5},{5,6},{6,7},{7,4},{8,9},{9,10},{10,1... | collective-permute-start | bytes 786440 | tf_op jit(solution)/shard_map/ppermute | solution.py:303
  119.9 20.9 %collective-permute-start.19 = (bf16[512,256]{1,0:T(8,128)(2,1)S(1)}, bf16[512,256]{1,0:T(8,128)(2,1)S(1)}, u32[]{:S(2)}, u32[]{:S(2)}) collective-permute-start(bf16[512,256]{1,0:T(8,128)(2,1)S(1)} %join_z.1.m0), channel_id=1, source_target_pairs={{0,4},{4,0},{1,5},{5,1},{2,6},{6,2},{3,7},{7,3},{8,12},{12,8},{9,1... | collective-permute-start | bytes 786440 | tf_op jit(solution)/shard_map/ppermute | solution.py:311
  125.6 15.2 %collective-permute-start.22 = (bf16[512,256]{1,0:T(8,128)(2,1)S(1)}, bf16[512,256]{1,0:T(8,128)(2,1)}, u32[]{:S(2)}, u32[]{:S(2)}) collective-permute-start(bf16[512,256]{1,0:T(8,128)(2,1)S(1)} %collective-permute-done.18.m3), channel_id=1, source_target_pairs={{0,4},{4,0},{1,5},{5,1},{2,6},{6,2},{3,7},{7,3},{8,12},{12,8},{9,1... | collective-permute-start | bytes 786440 | tf_op jit(solution)/shard_map/ppermute | solution.py:311
  130.8 10.0 %collective-permute-start.21 = (bf16[512,256]{1,0:T(8,128)(2,1)S(1)}, bf16[512,256]{1,0:T(8,128)(2,1)}, u32[]{:S(2)}, u32[]{:S(2)}) collective-permute-start(bf16[512,256]{1,0:T(8,128)(2,1)S(1)} %collective-permute-done.17.m2), channel_id=1, source_target_pairs={{0,4},{4,0},{1,5},{5,1},{2,6},{6,2},{3,7},{7,3},{8,12},{12,8},{9,1... | collective-permute-start | bytes 786440 | tf_op jit(solution)/shard_map/ppermute | solution.py:311
  131.8 9.0 %collective-permute-start.20 = (bf16[512,256]{1,0:T(8,128)(2,1)S(1)}, bf16[512,256]{1,0:T(8,128)(2,1)}, u32[]{:S(2)}, u32[]{:S(2)}) collective-permute-start(bf16[512,256]{1,0:T(8,128)(2,1)S(1)} %collective-permute-done.16.m1), channel_id=1, source_target_pairs={{0,4},{4,0},{1,5},{5,1},{2,6},{6,2},{3,7},{7,3},{8,12},{12,8},{9,1... | collective-permute-start | bytes 786440 | tf_op jit(solution)/shard_map/ppermute | solution.py:311
  134.5 6.3 %copy-start.6 = (bf16[256,256]{1,0:T(8,128)(2,1)S(1)}, bf16[256,256]{1,0:T(8,128)(2,1)}, u32[]{:S(2)}) copy-start(bf16[256,256]{1,0:T(8,128)(2,1)} %hidden_weight.1) | copy-start | bytes 393220
  134.6 6.3 %copy-start.7 = (bf16[256,256]{1,0:T(8,128)(2,1)S(1)}, bf16[256,256]{1,0:T(8,128)(2,1)}, u32[]{:S(2)}) copy-start(bf16[256,256]{1,0:T(8,128)(2,1)} %output_weight.1) | copy-start | bytes 393220
  134.6 6.3 %copy-start.8 = (f32[2048]{0:T(1024)S(1)}, f32[2048]{0:T(1024)}, u32[]{:S(2)}) copy-start(f32[2048]{0:T(1024)} %param.14) | copy-start | bytes 24580

commit v4 on v3

--- a/solution.py
+++ b/solution.py
@@ -32,7 +32,7 @@
     return jnp.transpose(jnp.broadcast_to(row, (lanes, n)))
 
 
-def call(body, outs, ins, scratch=(), name=None, limit=20, flops=1000000):
+def call(body, outs, ins, scratch=(), limit=20, flops=1000000):
     single = not isinstance(outs, (tuple, list))
     fn = pl.pallas_call(
         body,
@@ -40,7 +40,6 @@
         in_specs=[VMEM] * len(ins),
         out_specs=VMEM if single else [VMEM] * len(outs),
         scratch_shapes=list(scratch),
-        name=name,
         compiler_params=pltpu.CompilerParams(vmem_limit_bytes=limit * 2**20),
         cost_estimate=pl.CostEstimate(flops=flops, transcendentals=0, bytes_accessed=4000000),
     )
@@ -126,7 +125,7 @@
     lax.fori_loop(0, 4, some, 0)
 
 
-def spectrum(message, tile, cell, table_x, table_y, table_z, name):
+def spectrum(message, tile, cell, table_x, table_y, table_z):
     points = message.shape[0]
     return call(
         spectrum_body,
@@ -137,7 +136,6 @@
             pltpu.VMEM((32, points), F32),
             pltpu.VMEM((16, points), F32),
         ),
-        name,
         flops=2 * 2048 * 2048 * 256,
     )
 
@@ -152,10 +150,10 @@
         refs[count + s][...] = total[s * rows : s * rows + rows].astype(BF16)
 
 
-def add_and_cut(parts, name):
+def add_and_cut(parts):
     rows, width = parts[0].shape
     piece = jax.ShapeDtypeStruct((rows // 4, width), BF16)
-    return call(add_body, (piece,) * 4, parts, (), name)
+    return call(add_body, (piece,) * 4, parts, ())
 
 
 def join_body(*refs):
@@ -164,12 +162,12 @@
         refs[4][s * rows : s * rows + rows, :] = refs[s][...]
 
 
-def joined(parts, name):
+def joined(parts):
     rows, width = parts[0].shape
-    return call(join_body, jax.ShapeDtypeStruct((rows * 4, width), BF16), parts, (), name)
-
-
-def collect_body(recv, out, rows, ids, places, latent):
+    return call(join_body, jax.ShapeDtypeStruct((rows * 4, width), BF16), parts, ())
+
+
+def collect_body(recv, latent, places, rows, ids):
     picks = jnp.where(
         iota((8, 128), 1) == 2 * iota((8, 128), 0),
         64.0,
@@ -202,20 +200,29 @@
 
     lax.fori_loop(0, latent.shape[0] // tile, total, 0)
 
+
+def reply_body(latent, places, weight, out, held, done):
+    copy = pltpu.make_async_copy(weight, held, done)
+    copy.start()
+    lane = iota((128, 128), 0)
+    column = iota((128, 128), 1)
+
     def back(step, carry):
         place = places[pl.ds(step * 128, 128), :]
+        tall = []
         for g in range(3):
-            lane = iota((128, 128), 0)
             pick = jnp.where(lane == 2 * g, 64.0, jnp.where(lane == 2 * g + 1, 1.0, 0.0))
             cell = mm(place, pick.astype(BF16)).astype(jnp.int32)
-            hot = [
-                (cell == iota((128, 128), 1) + 128 * k).astype(BF16) for k in range(16)
-            ]
-            got = mm(jnp.concatenate(hot, axis=1), latent[...])
-            out[pl.ds(step * 16, 16), g * 8 : g * 8 + 8, :] = got.reshape(16, 8, 256).astype(BF16)
+            hot = [(cell == column + 128 * k).astype(BF16) for k in range(16)]
+            tall.append(jnp.concatenate(hot, axis=1))
+        got = mm(jnp.concatenate(tall, axis=0), latent[...])
+        for g in range(3):
+            piece = got[g * 128 : g * 128 + 128].reshape(16, 8, 256).astype(BF16)
+            out[pl.ds(step * 16, 16), g * 8 : g * 8 + 8, :] = piece
         return carry
 
     lax.fori_loop(0, 8, back, 0)
+    copy.wait()
 
 
 def mix_body(a, b, c, d, weight, out):
@@ -244,40 +251,49 @@
     lax.fori_loop(0, out.shape[0] // 256, some, 0)
 
 
-def decode_body(
-    m0, m1, m2, m3, m4, m5, m6, m7, tile, cell, wide_x, wide_y, wide_z,
-    base, read, hidden_weight, output_weight, out, spots,
-):
+def waves_body(tile, cell, wide_x, wide_y, wide_z, out_x, out_yz, spots):
     x, y, z = positions(tile[...], cell[...])
     spots[0:1, :] = x
     spots[1:2, :] = y
     spots[2:3, :] = z
-    modes = (m0, m1, m2, m3, m4, m5, m6, m7)
-    lane = lax.bitwise_and(iota((256, 128), 1), 63)
+    lane = lax.bitwise_and(iota((128, 128), 1), 63)
 
     def some(step, carry):
-        at = step * 256
-
-        def column(row):
-            return jnp.concatenate(
-                [as_column(row(at + 128 * part), 128) for part in range(2)], axis=0
-            )
+        at = step * 128
 
         def values(which, table):
-            col = column(lambda lo: spots[which : which + 1, pl.ds(lo, 128)])
+            col = as_column(spots[which : which + 1, pl.ds(at, 128)], 128)
             return mm((col == lane).astype(BF16), table[...])
 
-        vx = values(0, wide_x)
+        out_x[pl.ds(at, 128), :] = values(0, wide_x).astype(BF16)
         vy = values(1, wide_y)
         vz = values(2, wide_z)
-        total = base[pl.ds(at, 256), :]
         for h in range(2):
             for s in range(4):
                 yz = vy[:, s * 128 : s * 128 + 128] * vz[:, h * 128 : h * 128 + 128]
-                wave = [(yz * vx[:, i * 128 : i * 128 + 128]).astype(BF16) for i in range(4)]
-                total = total + mm(jnp.concatenate(wave, axis=1), modes[h * 4 + s][...])
+                to = (h * 4 + s) * 128
+                out_yz[pl.ds(at, 128), to : to + 128] = yz.astype(BF16)
+        return carry
+
+    lax.fori_loop(0, out_x.shape[0] // 128, some, 0)
+
+
+def decode_body(
+    m0, m1, m2, m3, m4, m5, m6, m7, wave_x, wave_yz, base, read, hidden_weight, output_weight, out
+):
+    modes = (m0, m1, m2, m3, m4, m5, m6, m7)
+
+    def some(step, carry):
+        at = step * 256
+        total = base[pl.ds(at, 256), :]
+        for q in range(8):
+            yz = wave_yz[pl.ds(at, 256), q * 128 : q * 128 + 128]
+            wave = [yz * wave_x[pl.ds(at, 256), i * 128 : i * 128 + 128] for i in range(4)]
+            total = total + mm(jnp.concatenate(wave, axis=1), modes[q][...])
         value = jax.nn.gelu(total).astype(BF16).astype(F32)
-        scale = column(lambda lo: read[:, pl.ds(lo, 128)])
+        scale = jnp.concatenate(
+            [as_column(read[:, pl.ds(at + 128 * part, 128)], 128) for part in range(2)], axis=0
+        )
         gathered = (jnp.concatenate([scale, scale], axis=1) * value).astype(BF16)
         hidden = jax.nn.gelu(mm(gathered, hidden_weight[...])).astype(BF16)
         out[pl.ds(at, 256), :] = mm(hidden, output_weight[...]).astype(BF16)
@@ -304,7 +320,10 @@
 
 
 def from_others(pieces, axis):
-    return (pieces[0],) + tuple(around(pieces[s], axis, s) for s in (1, 2, 3))
+    got = [pieces[0]]
+    for s in (1, 2, 3):
+        got.append(around(pieces[s], axis, s))
+    return tuple(got)
 
 
 def swapped(shard):
@@ -363,66 +382,64 @@
         ),
         (features, tile, cell, spread_weight.reshape(1, points), message_weight),
         (pltpu.VMEM((1, points), jnp.int32),),
-        "spread",
         limit=60,
     )
     recv = lax.all_to_all(send, everyone, 0, 0, tiled=True)
-    away = spectrum(message, tile, cell, to_x, to_y, other_z, "spectrum_away")
-    near = spectrum(message, tile, cell, to_x, to_y, own_z, "spectrum_near")
-    parts = add_and_cut((near, swapped(away)), "add_core")
-    parts = add_and_cut(from_others(parts, "ba"), "add_ba")
-    parts = add_and_cut(from_others(parts, "z"), "add_z")
-    mixed = call(
-        mix_body,
-        shape((32, width), BF16),
-        from_others(parts, "y") + (spectral_weight,),
-        (),
-        "mix",
-    )
-    line = joined(from_others((mixed,) * 4, "y"), "join_y")
-    plane = joined(from_others((line,) * 4, "z"), "join_z")
+    away = spectrum(message, tile, cell, to_x, to_y, other_z)
+    near = spectrum(message, tile, cell, to_x, to_y, own_z)
+    wave_x, wave_yz = call(
+        waves_body,
+        (shape((points, 512), BF16), shape((points, 1024), BF16)),
+        (tile, cell, wide_x, wide_y, wide_z),
+        (pltpu.VMEM((8, points), jnp.int32),),
+        flops=10**9,
+    )
+    parts = add_and_cut((near, swapped(away)))
+    parts = add_and_cut(from_others(parts, "ba"))
+    parts = add_and_cut(from_others(parts, "z"))
+    latent, places = call(
+        collect_body,
+        (shape((2048, width), BF16), shape((1024, 128), BF16)),
+        (recv,),
+        (pltpu.VMEM((3072, width), BF16), pltpu.VMEM((8, 8, 128), jnp.int32)),
+        flops=2 * 3072 * 2048 * 256,
+    )
+    back, weight = pl.pallas_call(
+        reply_body,
+        out_shape=(
+            shape((devices, 24, width), BF16),
+            shape(spectral_weight.shape, BF16),
+        ),
+        in_specs=[VMEM, VMEM, pl.BlockSpec(memory_space=pl.ANY)],
+        out_specs=[VMEM, VMEM],
+        scratch_shapes=[pltpu.SemaphoreType.DMA(())],
+        name="reply",
+        compiler_params=pltpu.CompilerParams(vmem_limit_bytes=20 * 2**20),
+        cost_estimate=pl.CostEstimate(
+            flops=2 * 3072 * 2048 * 256, transcendentals=0, bytes_accessed=4000000
+        ),
+    )(latent, places, spectral_weight)
+    mixed = call(mix_body, shape((32, width), BF16), from_others(parts, "y") + (weight,), ())
+    line = joined(from_others((mixed,) * 4, "y"))
+    plane = joined(from_others((line,) * 4, "z"))
     modes = from_others((plane,) * 4, "ba")
     modes = modes + tuple(swapped(m) for m in modes)
 
-    back = call(
-        collect_body,
-        shape((devices, 24, width), BF16),
-        (recv,),
-        (
-            pltpu.VMEM((3072, width), BF16),
-            pltpu.VMEM((8, 8, 128), jnp.int32),
-            pltpu.VMEM((1024, 128), BF16),
-            pltpu.VMEM((2048, width), BF16),
-        ),
-        "collect",
-        flops=4 * 3072 * 2048 * 256,
-    )
     returned = lax.all_to_all(back, everyone, 0, 0, tiled=True)
     base = call(
         own_body,
         shape((points, width), F32),
         (returned.reshape(devices * 24, width), slots, skip_weight),
         (),
-        "own",
         flops=2 * 3072 * 2048 * 256,
     )
     return call(
         decode_body,
         shape((points, width), BF16),
         modes
-        + (
-            tile,
-            cell,
-            wide_x,
-            wide_y,
-            wide_z,
-            base,
-            read_weight.reshape(1, points),
-            hidden_weight,
-            output_weight,
-        ),
-        (pltpu.VMEM((8, points), jnp.int32),),
-        "decode",
+        + (wave_x, wave_yz, base, read_weight.reshape(1, points), hidden_weight, output_weight),
+        (),
+        limit=32,
         flops=2 * 4096 * 2048 * 256,
     )
 
@@ -443,6 +460,7 @@
         every,
         every,
     )
+
     return jax.shard_map(
         per_device,
         mesh=finer,

time: 158 us -> 166 us (1.051)
  waiting for transfers between devices: 40.9 us -> 53.3 us
  starting transfers between devices: 55.8 us -> 47.5 us
  local copies, waits for them, and re-layouts: 2.23 us -> 9.75 us
  Pallas kernels: 56.6 us -> 52.8 us
    pallas_call x12 -> x13, Pallas kernels: 56.6 us -> 45.7 us  [call(): return fn(*ins)]
    ppermute x18, waiting for transfers between devices: 25.4 us -> 35.2 us  [around(): return lax.ppermute(shard, axis, [(i, (i + s) % 4) for i in range(4)])]
    unnamed x20 -> x36, local copies, waits for them, and re-layouts: 2.23 us -> 9.75 us
    pallas_call x0 -> x1, Pallas kernels: none -> 7.07 us  [per_device(): pl.pallas_call(reply_body, out_shape=(shape((devices, 24, width), BF16),...]
    ppermute x5, starting transfers between devices: 15.8 us -> 9.33 us  [swapped(): return lax.ppermute(shard, 'core', [(0, 1), (1, 0)])]
    all_to_all x1, waiting for transfers between devices: 15.5 us -> 18.1 us  [per_device(): recv = lax.all_to_all(send, everyone, 0, 0, tiled=True)]
  transfers between devices with their start and end apart: 25 -> 25, of which waited for: 10 -> 11; matrix products, arithmetic and copies ran while one was open for 1% -> 1% of each run, Pallas kernels for 19% -> 20%
where the time goes in v4:
time: 166 us
  waiting for transfers between devices  53.3 us (32%)
  Pallas kernels  52.8 us (32%)
  starting transfers between devices  47.5 us (29%)
  local copies, waits for them, and re-layouts  9.75 us (6%)
  other arithmetic  1.89 us (1%)
    pallas_call x13, Pallas kernels, call(): return fn(*ins)  45.7 us
    ppermute x18, waiting for transfers between devices, around(): return lax.ppermute(shard, axis, [(i, (i + s) % 4) for i in range(4)])  35.2 us
    ppermute x18, starting transfers between devices, around(): return lax.ppermute(shard, axis, [(i, (i + s) % 4) for i in range(4)])  22.9 us
    all_to_all x1, waiting for transfers between devices, per_device(): recv = lax.all_to_all(send, everyone, 0, 0, tiled=True)  18.1 us
    all_to_all x1, starting transfers between devices, per_device(): recv = lax.all_to_all(send, everyone, 0, 0, tiled=True)  11.5 us
    unnamed x36, local copies, waits for them, and re-layouts  9.75 us
    ppermute x5, starting transfers between devices, swapped(): return lax.ppermute(shard, 'core', [(0, 1), (1, 0)])  9.33 us
    pallas_call x1, Pallas kernels, per_device(): pl.pallas_call(reply_body, out_shape=(shape((devices, 24, width), BF16),...  7.07 us
  transfers between devices with their start and end apart: 25, of which 11 were waited for; matrix products, arithmetic and copies ran while one was open for 1% of the time, Pallas kernels for 20%

profile of v4, /device:TPU:1, one launch (start us, length us, event | category | flops | bytes accessed | tf_op | source)
XLA Modules:
  0.0 165.7 jit_solution(6563165631775523073)
XLA Ops:
  0.0 9.4 %shard_map.100 = (bf16[128,56,128]{2,1,0:T(8,128)(2,1)}, s32[1,2048]{1,0:T(1,128)}, bf16[2048,256]{1,0:T(8,128)(2,1)}) custom-call(bf16[2048,256]{1,0:T(8,128)(2,1)} %feat.1, s32[1,2048]{1,0:T(1,128)} %bitcast.6, s32[1,2048]{1,0:T(1,128)} %bitcast.10, f32[1,2048]{1,0:T(1,128)} %bitcast.15, bf16[256,256]{1,0:T(8,128)(2,1)} %weight.2), custom_call_target="tpu_custom_call" | custom-call | flops 1000000 | bytes 4000000 | tf_op jit(solution)/shard_map/pallas_call | solution.py:46
  9.4 11.5 %all-to-all-start = ((bf16[128,56,128]{2,1,0:T(8,128)(2,1)}), bf16[128,56,128]{2,1,0:T(8,128)(2,1)S(1)}, u32[]{:S(2)}, u32[]{:S(2)}) async-start(bf16[128,56,128]{2,1,0:T(8,128)(2,1)} %get-tuple-element.39), calls=%async_computation | async-start | bytes 3670016 | tf_op jit(solution)/shard_map/all_to_all | solution.py:387
  21.1 0.1 reduce-precision_convert_fusion.5
  21.2 0.1 reduce-precision_convert_fusion.3
  21.4 0.0 copy-start.8
  21.4 4.1 %shard_map.102 = bf16[2048,256]{1,0:T(8,128)(2,1)} custom-call(bf16[2048,256]{1,0:T(8,128)(2,1)S(1)} %copy-done.7, s32[1,2048]{1,0:T(1,128)S(1)} %bitcast.7, s32[1,2048]{1,0:T(1,128)S(1)} %bitcast.11, bf16[32,64]{1,0:T(8,128)(2,1)S(1)} %pad_maximum_fusion.3.table_x, bf16[32,64]{1,0:T(8,128)(2,1)S(1)} %pad_maximum_fusion.4.table_y, ...), custom_call_target="tpu_custom_call" | custom-call | flops 2147483648 | bytes 4000000 | tf_op jit(solution)/shard_map/pallas_call | solution.py:46
  25.6 1.1 collective-permute-start
  26.7 3.1 %shard_map.101.refs_0_ = bf16[2048,256]{1,0:T(8,128)(2,1)S(1)} custom-call(bf16[2048,256]{1,0:T(8,128)(2,1)S(1)} %copy-done.8, s32[1,2048]{1,0:T(1,128)S(1)} %bitcast.8, s32[1,2048]{1,0:T(1,128)S(1)} %bitcast.12, bf16[32,64]{1,0:T(8,128)(2,1)S(1)} %pad_maximum_fusion.3.table_x, bf16[32,64]{1,0:T(8,128)(2,1)S(1)} %pad_maximum_fusion.4.table_y, ...), custom_call_target="tpu_custom_call" | custom-call | flops 2147483648 | bytes 4000000 | tf_op jit(solution)/shard_map/pallas_call | solution.py:46
  29.8 0.0 copy-start.2
  29.8 1.0 copy-done.2
  30.8 18.1 %all-to-all-done.recv = bf16[128,56,128]{2,1,0:T(8,128)(2,1)S(1)} async-done(((bf16[128,56,128]{2,1,0:T(8,128)(2,1)}), bf16[128,56,128]{2,1,0:T(8,128)(2,1)S(1)}, u32[]{:S(2)}, u32[]{:S(2)}) %all-to-all-start) | async-done | bytes 1835040 | tf_op jit(solution)/shard_map/all_to_all | solution.py:387
  48.9 5.9 %shard_map.106 = (bf16[2048,256]{1,0:T(8,128)(2,1)S(1)}, bf16[1024,128]{1,0:T(8,128)(2,1)S(1)}) custom-call(bf16[128,56,128]{2,1,0:T(8,128)(2,1)S(1)} %all-to-all-done.recv), custom_call_target="tpu_custom_call" | custom-call | flops 3221225472 | bytes 4000000 | tf_op jit(solution)/shard_map/pallas_call | solution.py:46
  54.8 7.1 %reply.1 = (bf16[128,24,256]{2,1,0:T(8,128)(2,1)}, bf16[4,8,256,256]{3,2,1,0:T(8,128)(2,1)S(1)}) custom-call(bf16[2048,256]{1,0:T(8,128)(2,1)S(1)} %get-tuple-element.40.latent, bf16[1024,128]{1,0:T(8,128)(2,1)S(1)} %get-tuple-element.41.places, bf16[4,8,256,256]{3,2,1,0:T(8,128)(2,1)S(1)} %copy-done.6), custom_call_target="tpu_custom_call" | custom-call | flops 3221225472 | bytes 4000000 | tf_op jit(solution)/shard_map/reply/pallas_call | solution.py:407
  61.9 2.0 %copy-done = bf16[4,8,256,256]{3,2,1,0:T(8,128)(2,1)} copy-done((bf16[4,8,256,256]{3,2,1,0:T(8,128)(2,1)}, bf16[4,8,256,256]{3,2,1,0:T(8,128)(2,1)S(1)}, u32[]{:S(2)}) %copy-start) | copy-done | bytes 4194328
  63.9 3.8 %all-to-all-start.1 = ((bf16[128,24,256]{2,1,0:T(8,128)(2,1)}), bf16[128,24,256]{2,1,0:T(8,128)(2,1)S(1)}, u32[]{:S(2)}, u32[]{:S(2)}) async-start(bf16[128,24,256]{2,1,0:T(8,128)(2,1)} %get-tuple-element.45), calls=%async_computation.1 | async-start | bytes 3145728 | tf_op jit(solution)/shard_map/all_to_all | solution.py:428
  67.7 0.0 copy-start.3
  67.7 1.2 copy-done.3
  69.0 0.2 shard_map.103
  69.2 1.4 collective-permute-start.1
  70.6 2.4 %collective-permute-start.2 = (bf16[512,256]{1,0:T(8,128)(2,1)S(1)}, bf16[512,256]{1,0:T(8,128)(2,1)S(1)}, u32[]{:S(2)}, u32[]{:S(2)}) collective-permute-start(bf16[512,256]{1,0:T(8,128)(2,1)S(1)} %get-tuple-element.29), channel_id=1, source_target_pairs={{0,2},{1,3},{2,0},{3,1},{4,6},{5,7},{6,4},{7,5},{8,10},{9,11},{10,... | collective-permute-start | bytes 786440 | tf_op jit(solution)/shard_map/ppermute | solution.py:319
  73.1 1.2 collective-permute-start.3
  74.2 1.1 reduce-precision_convert_fusion
  75.3 17.5 %collective-permute-done.1.refs_1_ = bf16[512,256]{1,0:T(8,128)(2,1)S(1)} collective-permute-done((bf16[512,256]{1,0:T(8,128)(2,1)S(1)}, bf16[512,256]{1,0:T(8,128)(2,1)S(1)}, u32[]{:S(2)}, u32[]{:S(2)}) %collective-permute-start.1) | collective-permute-done | bytes 262176 | tf_op jit(solution)/shard_map/ppermute | solution.py:319
  92.8 5.9 %collective-permute-done.2.refs_2_ = bf16[512,256]{1,0:T(8,128)(2,1)S(1)} collective-permute-done((bf16[512,256]{1,0:T(8,128)(2,1)S(1)}, bf16[512,256]{1,0:T(8,128)(2,1)S(1)}, u32[]{:S(2)}, u32[]{:S(2)}) %collective-permute-start.2) | collective-permute-done | bytes 262176 | tf_op jit(solution)/shard_map/ppermute | solution.py:319
  98.7 0.1 shard_map.104
  98.8 1.5 collective-permute-start.4
  100.3 2.9 %collective-permute-start.5 = (bf16[128,256]{1,0:T(8,128)(2,1)S(1)}, bf16[128,256]{1,0:T(8,128)(2,1)S(1)}, u32[]{:S(2)}, u32[]{:S(2)}) collective-permute-start(bf16[128,256]{1,0:T(8,128)(2,1)S(1)} %get-tuple-element.33), channel_id=1, source_target_pairs={{0,64},{32,96},{64,0},{96,32},{1,65},{33,97},{65,1},{97,33},{2,66}... | collective-permute-start | bytes 196616 | tf_op jit(solution)/shard_map/ppermute | solution.py:319
  103.3 0.9 collective-permute-start.6
  104.2 0.0 collective-permute-done.4.refs_1_
  104.2 1.4 collective-permute-done.5.refs_2_
  105.6 1.2 collective-permute-done.6.refs_3_
  106.9 1.3 collective-permute-start.7
  108.2 2.5 %collective-permute-start.8 = (bf16[32,256]{1,0:T(8,128)(2,1)S(1)}, bf16[32,256]{1,0:T(8,128)(2,1)S(1)}, u32[]{:S(2)}, u32[]{:S(2)}) collective-permute-start(bf16[32,256]{1,0:T(8,128)(2,1)S(1)} %get-tuple-element.37), channel_id=1, source_target_pairs={{0,16},{8,24},{16,0},{24,8},{1,17},{9,25},{17,1},{25,9},{2,18},{10... | collective-permute-start | bytes 49160 | tf_op jit(solution)/shard_map/ppermute | solution.py:319
  110.7 1.1 collective-permute-start.9
  111.8 0.4 collective-permute-done.8.c
  112.3 1.3 collective-permute-done.9.d
  113.6 2.2 %copy-done.1 = bf16[4,8,256,256]{3,2,1,0:T(8,128)(2,1)S(1)} copy-done((bf16[4,8,256,256]{3,2,1,0:T(8,128)(2,1)S(1)}, bf16[4,8,256,256]{3,2,1,0:T(8,128)(2,1)}, u32[]{:S(2)}) %copy-start.1) | copy-done | bytes 4194328
  115.8 0.7 shard_map.107.refs_0_
  116.4 2.2 %collective-permute-start.12 = (bf16[32,256]{1,0:T(8,128)(2,1)S(1)}, bf16[32,256]{1,0:T(8,128)(2,1)S(1)}, u32[]{:S(2)}, u32[]{:S(2)}) collective-permute-start(bf16[32,256]{1,0:T(8,128)(2,1)S(1)} %shard_map.107.refs_0_), channel_id=1, source_target_pairs={{0,24},{8,0},{16,8},{24,16},{1,25},{9,1},{17,9},{25,17},{2,26},{10... | collective-permute-start | bytes 49160 | tf_op jit(solution)/shard_map/ppermute | solution.py:319
  118.7 0.7 collective-permute-start.10
  119.3 0.3 reduce-precision_convert_fusion.2
  119.7 3.1 %collective-permute-done.11.refs_2_ = bf16[32,256]{1,0:T(8,128)(2,1)S(1)} collective-permute-done((bf16[32,256]{1,0:T(8,128)(2,1)S(1)}, bf16[32,256]{1,0:T(8,128)(2,1)S(1)}, u32[]{:S(2)}, u32[]{:S(2)}) %collective-permute-start.11) | collective-permute-done | bytes 16416 | tf_op jit(solution)/shard_map/ppermute | solution.py:319
  122.7 0.0 collective-permute-done.10.refs_1_
  122.8 2.2 %collective-permute-start.15 = (bf16[128,256]{1,0:T(8,128)(2,1)S(1)}, bf16[128,256]{1,0:T(8,128)(2,1)S(1)}, u32[]{:S(2)}, u32[]{:S(2)}) collective-permute-start(bf16[128,256]{1,0:T(8,128)(2,1)S(1)} %shard_map.108.refs_0_), channel_id=1, source_target_pairs={{0,96},{32,0},{64,32},{96,64},{1,97},{33,1},{65,33},{97,65},{2,98}... | collective-permute-start | bytes 196616 | tf_op jit(solution)/shard_map/ppermute | solution.py:319
  124.9 0.7 collective-permute-start.13
  125.6 1.2 collective-permute-done.15.refs_3_
  126.8 2.8 %collective-permute-done.14.refs_2_ = bf16[128,256]{1,0:T(8,128)(2,1)S(1)} collective-permute-done((bf16[128,256]{1,0:T(8,128)(2,1)S(1)}, bf16[128,256]{1,0:T(8,128)(2,1)S(1)}, u32[]{:S(2)}, u32[]{:S(2)}) %collective-permute-start.14) | collective-permute-done | bytes 65568 | tf_op jit(solution)/shard_map/ppermute | solution.py:319
  129.6 0.3 collective-permute-done.13.refs_1_
  130.0 0.0 copy-start.9
  130.0 0.1 collective-permute-start.18
  130.1 1.4 collective-permute-start.17
  131.5 0.3 collective-permute-start.16
  131.9 4.9 %shard_map.110 = (bf16[2048,512]{1,0:T(8,128)(2,1)S(1)}, bf16[2048,1024]{1,0:T(8,128)(2,1)S(1)}) custom-call(s32[1,2048]{1,0:T(1,128)S(1)} %bitcast.9, s32[1,2048]{1,0:T(1,128)S(1)} %bitcast.13, bf16[128,512]{1,0:T(8,128)(2,1)S(1)} %pad_maximum_fusion.wide_x, bf16[128,512]{1,0:T(8,128)(2,1)S(1)} %pad_maximum_fusion.1.wide_y, ...), custom_call_target="tpu_custom_call" | custom-call | flops 1000000000 | bytes 4000000 | tf_op jit(solution)/shard_map/pallas_call | solution.py:46
  136.8 2.0 %copy-done.14 = bf16[2048,1024]{1,0:T(8,128)(2,1)} copy-done((bf16[2048,1024]{1,0:T(8,128)(2,1)}, bf16[2048,1024]{1,0:T(8,128)(2,1)S(1)}, u32[]{:S(2)}) %copy-start.14) | copy-done | bytes 4194328
  138.8 1.4 copy-done.16
  140.1 7.7 %collective-permute-start.19 = (bf16[512,256]{1,0:T(8,128)(2,1)S(1)}, bf16[512,256]{1,0:T(8,128)(2,1)S(1)}, u32[]{:S(2)}, u32[]{:S(2)}) collective-permute-start(bf16[512,256]{1,0:T(8,128)(2,1)S(1)} %shard_map.109.m0), channel_id=1, source_target_pairs={{0,4},{4,0},{1,5},{5,1},{2,6},{6,2},{3,7},{7,3},{8,12},{12,8},{9,1... | collective-permute-start | bytes 786440 | tf_op jit(solution)/shard_map/ppermute | solution.py:330
  147.8 0.0 collective-permute-start.22
  147.8 0.5 collective-permute-start.21
  148.3 0.1 collective-permute-start.20
  148.4 0.0 copy-start.10
  148.4 0.0 copy-start.11
  148.4 0.0 copy-start.12
  148.5 6.2 %shard_map.111.base = f32[2048,256]{1,0:T(8,128)S(1)} custom-call(bf16[3072,256]{1,0:T(8,128)(2,1)S(1)} %bitcast.5, s32[1,2048]{1,0:T(1,128)S(1)} %copy-done.13, bf16[256,256]{1,0:T(8,128)(2,1)S(1)} %copy-done.9), custom_call_target="tpu_custom_call" | custom-call | flops 3221225472 | bytes 4000000 | tf_op jit(solution)/shard_map/pallas_call | solution.py:46
  154.8 10.9 %shard_map.112 = bf16[2048,256]{1,0:T(8,128)(2,1)} custom-call(bf16[512,256]{1,0:T(8,128)(2,1)S(1)} %shard_map.109.m0, bf16[512,256]{1,0:T(8,128)(2,1)S(1)} %collective-permute-done.16.m1, bf16[512,256]{1,0:T(8,128)(2,1)S(1)} %collective-permute-done.17.m2, bf16[512,256]{1,0:T(8,128)(2,1)S(1)} %collective-permute-done.18.m3, ...), custom_call_target="tpu_custom_call" | custom-call | flops 4294967296 | bytes 4000000 | tf_op jit(solution)/shard_map/pallas_call | solution.py:46
  (60 shorter events, 0.4 us)
Async XLA Ops:
  9.4 12.0 %copy-start.4 = (s32[2048,1]{0,1:T(1,128)S(1)}, s32[2048,1]{0,1:T(1,128)}, u32[]{:S(2)}) copy-start(s32[2048,1]{0,1:T(1,128)} %param.11) | copy-start | bytes 24580
  9.4 12.0 %copy-start.5 = (s32[2048]{0:T(1024)S(1)}, s32[2048]{0:T(1024)}, u32[]{:S(2)}) copy-start(s32[2048]{0:T(1024)} %param.12) | copy-start | bytes 24580
  9.4 12.0 %copy-start.7 = (bf16[2048,256]{1,0:T(8,128)(2,1)S(1)}, bf16[2048,256]{1,0:T(8,128)(2,1)}, u32[]{:S(2)}) copy-start(bf16[2048,256]{1,0:T(8,128)(2,1)} %get-tuple-element.26.message) | copy-start | bytes 3145732
  9.4 39.4 %all-to-all-start = ((bf16[128,56,128]{2,1,0:T(8,128)(2,1)}), bf16[128,56,128]{2,1,0:T(8,128)(2,1)S(1)}, u32[]{:S(2)}, u32[]{:S(2)}) async-start(bf16[128,56,128]{2,1,0:T(8,128)(2,1)} %get-tuple-element.39), calls=%async_computation | async-start | bytes 3670016 | tf_op jit(solution)/shard_map/all_to_all | solution.py:387
  21.4 5.2 %copy-start.8 = (bf16[2048,256]{1,0:T(8,128)(2,1)S(1)}, bf16[2048,256]{1,0:T(8,128)(2,1)}, u32[]{:S(2)}) copy-start(bf16[2048,256]{1,0:T(8,128)(2,1)} %get-tuple-element.26.message) | copy-start | bytes 3145732
  25.6 42.2 %collective-permute-start = (bf16[2048,256]{1,0:T(8,128)(2,1)}, bf16[2048,256]{1,0:T(8,128)(2,1)S(1)}, u32[]{:S(2)}, u32[]{:S(2)}) collective-permute-start(bf16[2048,256]{1,0:T(8,128)(2,1)} %shard_map.102), channel_id=1, source_target_pairs={{0,4},{4,0},{1,5},{5,1},{2,6},{6,2},{3,7},{7,3},{8,12},{12,8},{9,1... | collective-permute-start | bytes 3145736 | tf_op jit(solution)/shard_map/ppermute | solution.py:330
  29.8 1.0 copy-start.2
  48.9 5.9 %copy-start.6 = (bf16[4,8,256,256]{3,2,1,0:T(8,128)(2,1)S(1)}, bf16[4,8,256,256]{3,2,1,0:T(8,128)(2,1)}, u32[]{:S(2)}) copy-start(bf16[4,8,256,256]{3,2,1,0:T(8,128)(2,1)} %weight.3) | copy-start | bytes 12582916
  61.9 2.0 %copy-start = (bf16[4,8,256,256]{3,2,1,0:T(8,128)(2,1)}, bf16[4,8,256,256]{3,2,1,0:T(8,128)(2,1)S(1)}, u32[]{:S(2)}) copy-start(bf16[4,8,256,256]{3,2,1,0:T(8,128)(2,1)S(1)} %get-tuple-element.42.weight) | copy-start | bytes 12582916
  63.9 84.5 %all-to-all-start.1 = ((bf16[128,24,256]{2,1,0:T(8,128)(2,1)}), bf16[128,24,256]{2,1,0:T(8,128)(2,1)S(1)}, u32[]{:S(2)}, u32[]{:S(2)}) async-start(bf16[128,24,256]{2,1,0:T(8,128)(2,1)} %get-tuple-element.45), calls=%async_computation.1 | async-start | bytes 3145728 | tf_op jit(solution)/shard_map/all_to_all | solution.py:428
  67.7 1.2 copy-start.3
  69.2 23.6 %collective-permute-start.1 = (bf16[512,256]{1,0:T(8,128)(2,1)S(1)}, bf16[512,256]{1,0:T(8,128)(2,1)S(1)}, u32[]{:S(2)}, u32[]{:S(2)}) collective-permute-start(bf16[512,256]{1,0:T(8,128)(2,1)S(1)} %get-tuple-element.28), channel_id=1, source_target_pairs={{0,1},{1,2},{2,3},{3,0},{4,5},{5,6},{6,7},{7,4},{8,9},{9,10},{10,1... | collective-permute-start | bytes 786440 | tf_op jit(solution)/shard_map/ppermute | solution.py:319
  70.6 28.0 %collective-permute-start.2 = (bf16[512,256]{1,0:T(8,128)(2,1)S(1)}, bf16[512,256]{1,0:T(8,128)(2,1)S(1)}, u32[]{:S(2)}, u32[]{:S(2)}) collective-permute-start(bf16[512,256]{1,0:T(8,128)(2,1)S(1)} %get-tuple-element.29), channel_id=1, source_target_pairs={{0,2},{1,3},{2,0},{3,1},{4,6},{5,7},{6,4},{7,5},{8,10},{9,11},{10,... | collective-permute-start | bytes 786440 | tf_op jit(solution)/shard_map/ppermute | solution.py:319
  73.1 25.6 %collective-permute-start.3 = (bf16[512,256]{1,0:T(8,128)(2,1)S(1)}, bf16[512,256]{1,0:T(8,128)(2,1)S(1)}, u32[]{:S(2)}, u32[]{:S(2)}) collective-permute-start(bf16[512,256]{1,0:T(8,128)(2,1)S(1)} %get-tuple-element.30), channel_id=1, source_target_pairs={{0,3},{1,0},{2,1},{3,2},{4,7},{5,4},{6,5},{7,6},{8,11},{9,8},{10,9... | collective-permute-start | bytes 786440 | tf_op jit(solution)/shard_map/ppermute | solution.py:319
  98.8 5.4 %collective-permute-start.4 = (bf16[128,256]{1,0:T(8,128)(2,1)S(1)}, bf16[128,256]{1,0:T(8,128)(2,1)S(1)}, u32[]{:S(2)}, u32[]{:S(2)}) collective-permute-start(bf16[128,256]{1,0:T(8,128)(2,1)S(1)} %get-tuple-element.32), channel_id=1, source_target_pairs={{0,32},{32,64},{64,96},{96,0},{1,33},{33,65},{65,97},{97,1},{2,34}... | collective-permute-start | bytes 196616 | tf_op jit(solution)/shard_map/ppermute | solution.py:319
  100.3 5.3 %collective-permute-start.5 = (bf16[128,256]{1,0:T(8,128)(2,1)S(1)}, bf16[128,256]{1,0:T(8,128)(2,1)S(1)}, u32[]{:S(2)}, u32[]{:S(2)}) collective-permute-start(bf16[128,256]{1,0:T(8,128)(2,1)S(1)} %get-tuple-element.33), channel_id=1, source_target_pairs={{0,64},{32,96},{64,0},{96,32},{1,65},{33,97},{65,1},{97,33},{2,66}... | collective-permute-start | bytes 196616 | tf_op jit(solution)/shard_map/ppermute | solution.py:319
  103.3 3.6 %collective-permute-start.6 = (bf16[128,256]{1,0:T(8,128)(2,1)S(1)}, bf16[128,256]{1,0:T(8,128)(2,1)S(1)}, u32[]{:S(2)}, u32[]{:S(2)}) collective-permute-start(bf16[128,256]{1,0:T(8,128)(2,1)S(1)} %get-tuple-element.34), channel_id=1, source_target_pairs={{0,96},{32,0},{64,32},{96,64},{1,97},{33,1},{65,33},{97,65},{2,98}... | collective-permute-start | bytes 196616 | tf_op jit(solution)/shard_map/ppermute | solution.py:319
  106.9 5.0 %collective-permute-start.7 = (bf16[32,256]{1,0:T(8,128)(2,1)S(1)}, bf16[32,256]{1,0:T(8,128)(2,1)S(1)}, u32[]{:S(2)}, u32[]{:S(2)}) collective-permute-start(bf16[32,256]{1,0:T(8,128)(2,1)S(1)} %get-tuple-element.36), channel_id=1, source_target_pairs={{0,8},{8,16},{16,24},{24,0},{1,9},{9,17},{17,25},{25,1},{2,10},{10... | collective-permute-start | bytes 49160 | tf_op jit(solution)/shard_map/ppermute | solution.py:319
  108.2 4.1 %collective-permute-start.8 = (bf16[32,256]{1,0:T(8,128)(2,1)S(1)}, bf16[32,256]{1,0:T(8,128)(2,1)S(1)}, u32[]{:S(2)}, u32[]{:S(2)}) collective-permute-start(bf16[32,256]{1,0:T(8,128)(2,1)S(1)} %get-tuple-element.37), channel_id=1, source_target_pairs={{0,16},{8,24},{16,0},{24,8},{1,17},{9,25},{17,1},{25,9},{2,18},{10... | collective-permute-start | bytes 49160 | tf_op jit(solution)/shard_map/ppermute | solution.py:319
  110.7 2.9 %collective-permute-start.9 = (bf16[32,256]{1,0:T(8,128)(2,1)S(1)}, bf16[32,256]{1,0:T(8,128)(2,1)S(1)}, u32[]{:S(2)}, u32[]{:S(2)}) collective-permute-start(bf16[32,256]{1,0:T(8,128)(2,1)S(1)} %get-tuple-element.38), channel_id=1, source_target_pairs={{0,24},{8,0},{16,8},{24,16},{1,25},{9,1},{17,9},{25,17},{2,26},{10... | collective-permute-start | bytes 49160 | tf_op jit(solution)/shard_map/ppermute | solution.py:319
  113.6 2.2 %copy-start.1 = (bf16[4,8,256,256]{3,2,1,0:T(8,128)(2,1)S(1)}, bf16[4,8,256,256]{3,2,1,0:T(8,128)(2,1)}, u32[]{:S(2)}) copy-start(bf16[4,8,256,256]{3,2,1,0:T(8,128)(2,1)} %copy-done) | copy-start | bytes 12582916
  116.4 3.2 %collective-permute-start.12 = (bf16[32,256]{1,0:T(8,128)(2,1)S(1)}, bf16[32,256]{1,0:T(8,128)(2,1)S(1)}, u32[]{:S(2)}, u32[]{:S(2)}) collective-permute-start(bf16[32,256]{1,0:T(8,128)(2,1)S(1)} %shard_map.107.refs_0_), channel_id=1, source_target_pairs={{0,24},{8,0},{16,8},{24,16},{1,25},{9,1},{17,9},{25,17},{2,26},{10... | collective-permute-start | bytes 49160 | tf_op jit(solution)/shard_map/ppermute | solution.py:319
  118.7 4.1 %collective-permute-start.11 = (bf16[32,256]{1,0:T(8,128)(2,1)S(1)}, bf16[32,256]{1,0:T(8,128)(2,1)S(1)}, u32[]{:S(2)}, u32[]{:S(2)}) collective-permute-start(bf16[32,256]{1,0:T(8,128)(2,1)S(1)} %shard_map.107.refs_0_), channel_id=1, source_target_pairs={{0,16},{8,24},{16,0},{24,8},{1,17},{9,25},{17,1},{25,9},{2,18},{10... | collective-permute-start | bytes 49160 | tf_op jit(solution)/shard_map/ppermute | solution.py:319
  118.7 4.1 %collective-permute-start.10 = (bf16[32,256]{1,0:T(8,128)(2,1)S(1)}, bf16[32,256]{1,0:T(8,128)(2,1)S(1)}, u32[]{:S(2)}, u32[]{:S(2)}) collective-permute-start(bf16[32,256]{1,0:T(8,128)(2,1)S(1)} %shard_map.107.refs_0_), channel_id=1, source_target_pairs={{0,8},{8,16},{16,24},{24,0},{1,9},{9,17},{17,25},{25,1},{2,10},{10... | collective-permute-start | bytes 49160 | tf_op jit(solution)/shard_map/ppermute | solution.py:319
  122.8 4.1 %collective-permute-start.15 = (bf16[128,256]{1,0:T(8,128)(2,1)S(1)}, bf16[128,256]{1,0:T(8,128)(2,1)S(1)}, u32[]{:S(2)}, u32[]{:S(2)}) collective-permute-start(bf16[128,256]{1,0:T(8,128)(2,1)S(1)} %shard_map.108.refs_0_), channel_id=1, source_target_pairs={{0,96},{32,0},{64,32},{96,64},{1,97},{33,1},{65,33},{97,65},{2,98}... | collective-permute-start | bytes 196616 | tf_op jit(solution)/shard_map/ppermute | solution.py:319
  124.9 4.7 %collective-permute-start.14 = (bf16[128,256]{1,0:T(8,128)(2,1)S(1)}, bf16[128,256]{1,0:T(8,128)(2,1)S(1)}, u32[]{:S(2)}, u32[]{:S(2)}) collective-permute-start(bf16[128,256]{1,0:T(8,128)(2,1)S(1)} %shard_map.108.refs_0_), channel_id=1, source_target_pairs={{0,64},{32,96},{64,0},{96,32},{1,65},{33,97},{65,1},{97,33},{2,66}... | collective-permute-start | bytes 196616 | tf_op jit(solution)/shard_map/ppermute | solution.py:319
  124.9 5.0 %collective-permute-start.13 = (bf16[128,256]{1,0:T(8,128)(2,1)S(1)}, bf16[128,256]{1,0:T(8,128)(2,1)S(1)}, u32[]{:S(2)}, u32[]{:S(2)}) collective-permute-start(bf16[128,256]{1,0:T(8,128)(2,1)S(1)} %shard_map.108.refs_0_), channel_id=1, source_target_pairs={{0,32},{32,64},{64,96},{96,0},{1,33},{33,65},{65,97},{97,1},{2,34}... | collective-permute-start | bytes 196616 | tf_op jit(solution)/shard_map/ppermute | solution.py:319
  130.0 18.4 %copy-start.9 = (bf16[256,256]{1,0:T(8,128)(2,1)S(1)}, bf16[256,256]{1,0:T(8,128)(2,1)}, u32[]{:S(2)}) copy-start(bf16[256,256]{1,0:T(8,128)(2,1)} %skip.1) | copy-start | bytes 393220
  130.0 18.4 %copy-start.13 = (s32[1,2048]{1,0:T(1,128)S(1)}, s32[1,2048]{1,0:T(1,128)}, u32[]{:S(2)}) copy-start(s32[1,2048]{1,0:T(1,128)} %get-tuple-element.46.slots) | copy-start | bytes 24580
  130.0 17.8 %collective-permute-start.18 = (bf16[512,256]{1,0:T(8,128)(2,1)S(1)}, bf16[512,256]{1,0:T(8,128)(2,1)S(1)}, u32[]{:S(2)}, u32[]{:S(2)}) collective-permute-start(bf16[512,256]{1,0:T(8,128)(2,1)S(1)} %shard_map.109.m0), channel_id=1, source_target_pairs={{0,3},{1,0},{2,1},{3,2},{4,7},{5,4},{6,5},{7,6},{8,11},{9,8},{10,9... | collective-permute-start | bytes 786440 | tf_op jit(solution)/shard_map/ppermute | solution.py:319
  130.1 17.7 %collective-permute-start.17 = (bf16[512,256]{1,0:T(8,128)(2,1)S(1)}, bf16[512,256]{1,0:T(8,128)(2,1)S(1)}, u32[]{:S(2)}, u32[]{:S(2)}) collective-permute-start(bf16[512,256]{1,0:T(8,128)(2,1)S(1)} %shard_map.109.m0), channel_id=1, source_target_pairs={{0,2},{1,3},{2,0},{3,1},{4,6},{5,7},{6,4},{7,5},{8,10},{9,11},{10,... | collective-permute-start | bytes 786440 | tf_op jit(solution)/shard_map/ppermute | solution.py:319
  131.5 16.8 %collective-permute-start.16 = (bf16[512,256]{1,0:T(8,128)(2,1)S(1)}, bf16[512,256]{1,0:T(8,128)(2,1)S(1)}, u32[]{:S(2)}, u32[]{:S(2)}) collective-permute-start(bf16[512,256]{1,0:T(8,128)(2,1)S(1)} %shard_map.109.m0), channel_id=1, source_target_pairs={{0,1},{1,2},{2,3},{3,0},{4,5},{5,6},{6,7},{7,4},{8,9},{9,10},{10,1... | collective-permute-start | bytes 786440 | tf_op jit(solution)/shard_map/ppermute | solution.py:319
  136.8 2.0 %copy-start.14 = (bf16[2048,1024]{1,0:T(8,128)(2,1)}, bf16[2048,1024]{1,0:T(8,128)(2,1)S(1)}, u32[]{:S(2)}) copy-start(bf16[2048,1024]{1,0:T(8,128)(2,1)S(1)} %get-tuple-element.44.wave_yz) | copy-start | bytes 12582916
  138.8 1.4 copy-start.16
  140.1 14.5 %collective-permute-start.19 = (bf16[512,256]{1,0:T(8,128)(2,1)S(1)}, bf16[512,256]{1,0:T(8,128)(2,1)S(1)}, u32[]{:S(2)}, u32[]{:S(2)}) collective-permute-start(bf16[512,256]{1,0:T(8,128)(2,1)S(1)} %shard_map.109.m0), channel_id=1, source_target_pairs={{0,4},{4,0},{1,5},{5,1},{2,6},{6,2},{3,7},{7,3},{8,12},{12,8},{9,1... | collective-permute-start | bytes 786440 | tf_op jit(solution)/shard_map/ppermute | solution.py:330
  147.8 6.9 %collective-permute-start.22 = (bf16[512,256]{1,0:T(8,128)(2,1)S(1)}, bf16[512,256]{1,0:T(8,128)(2,1)S(1)}, u32[]{:S(2)}, u32[]{:S(2)}) collective-permute-start(bf16[512,256]{1,0:T(8,128)(2,1)S(1)} %collective-permute-done.18.m3), channel_id=1, source_target_pairs={{0,4},{4,0},{1,5},{5,1},{2,6},{6,2},{3,7},{7,3},{8,12},{12,8},{9,1... | collective-permute-start | bytes 786440 | tf_op jit(solution)/shard_map/ppermute | solution.py:330
  147.8 6.9 %collective-permute-start.21 = (bf16[512,256]{1,0:T(8,128)(2,1)S(1)}, bf16[512,256]{1,0:T(8,128)(2,1)S(1)}, u32[]{:S(2)}, u32[]{:S(2)}) collective-permute-start(bf16[512,256]{1,0:T(8,128)(2,1)S(1)} %collective-permute-done.17.m2), channel_id=1, source_target_pairs={{0,4},{4,0},{1,5},{5,1},{2,6},{6,2},{3,7},{7,3},{8,12},{12,8},{9,1... | collective-permute-start | bytes 786440 | tf_op jit(solution)/shard_map/ppermute | solution.py:330
  148.3 6.4 %collective-permute-start.20 = (bf16[512,256]{1,0:T(8,128)(2,1)S(1)}, bf16[512,256]{1,0:T(8,128)(2,1)}, u32[]{:S(2)}, u32[]{:S(2)}) collective-permute-start(bf16[512,256]{1,0:T(8,128)(2,1)S(1)} %collective-permute-done.16.m1), channel_id=1, source_target_pairs={{0,4},{4,0},{1,5},{5,1},{2,6},{6,2},{3,7},{7,3},{8,12},{12,8},{9,1... | collective-permute-start | bytes 786440 | tf_op jit(solution)/shard_map/ppermute | solution.py:330
  148.4 6.3 %copy-start.10 = (bf16[256,256]{1,0:T(8,128)(2,1)S(1)}, bf16[256,256]{1,0:T(8,128)(2,1)}, u32[]{:S(2)}) copy-start(bf16[256,256]{1,0:T(8,128)(2,1)} %hidden_weight.1) | copy-start | bytes 393220
  148.4 6.3 %copy-start.11 = (bf16[256,256]{1,0:T(8,128)(2,1)S(1)}, bf16[256,256]{1,0:T(8,128)(2,1)}, u32[]{:S(2)}) copy-start(bf16[256,256]{1,0:T(8,128)(2,1)} %output_weight.1) | copy-start | bytes 393220
  148.4 6.3 %copy-start.12 = (f32[2048]{0:T(1024)S(1)}, f32[2048]{0:T(1024)}, u32[]{:S(2)}) copy-start(f32[2048]{0:T(1024)} %param.14) | copy-start | bytes 24580
  148.4 6.3 %copy-start.15 = (bf16[2048,1024]{1,0:T(8,128)(2,1)S(1)}, bf16[2048,1024]{1,0:T(8,128)(2,1)}, u32[]{:S(2)}) copy-start(bf16[2048,1024]{1,0:T(8,128)(2,1)} %copy-done.14) | copy-start | bytes 12582916
  148.5 6.3 %copy-start.17 = (bf16[2048,512]{1,0:T(8,128)(2,1)S(1)}, bf16[2048,512]{1,0:T(8,128)(2,1)}, u32[]{:S(2)}) copy-start(bf16[2048,512]{1,0:T(8,128)(2,1)} %copy-done.16) | copy-start | bytes 6291460

commit v5 on v4

--- a/solution.py
+++ b/solution.py
@@ -1,7 +1,8 @@
-import math
+import functools
 
 import jax
 import jax.numpy as jnp
+import numpy as np
 from jax import lax
 from jax.experimental import pallas as pl
 from jax.experimental.pallas import tpu as pltpu
@@ -13,6 +14,7 @@
 F32 = jnp.float32
 BF16 = jnp.bfloat16
 VMEM = pl.BlockSpec(memory_space=pltpu.VMEM)
+SMEM = pl.BlockSpec(memory_space=pltpu.SMEM)
 
 
 def iota(shape, dim):
@@ -32,12 +34,12 @@
     return jnp.transpose(jnp.broadcast_to(row, (lanes, n)))
 
 
-def call(body, outs, ins, scratch=(), limit=20, flops=1000000):
+def call(body, outs, ins, scratch=(), limit=20, flops=1000000, scalars=0):
     single = not isinstance(outs, (tuple, list))
     fn = pl.pallas_call(
         body,
         out_shape=outs,
-        in_specs=[VMEM] * len(ins),
+        in_specs=[VMEM] * (len(ins) - scalars) + [SMEM] * scalars,
         out_specs=VMEM if single else [VMEM] * len(outs),
         scratch_shapes=list(scratch),
         compiler_params=pltpu.CompilerParams(vmem_limit_bytes=limit * 2**20),
@@ -100,43 +102,55 @@
     return x, y, lax.bitwise_and(cell, 63)
 
 
-def spectrum_body(message, tile, cell, table_x, table_y, table_z, out, ys, yz, xs):
+def device_at(where):
+    d = where[0]
+    return d // 32, d // 8 % 4, d // 4 % 2, d % 4
+
+
+def bits(value, low, mask):
+    return lax.bitwise_and(lax.shift_right_logical(value, low), mask)
+
+
+def spectrum_body(message, tile, cell, basis, where, out, xy, away):
     points = message.shape[0]
+    at_z, at_y, core, at_b = device_at(where)
+    core = 1 - core if away else core
+    r = iota((256, 16), 0)
+    wide, near, last, j4 = bits(r, 6, 3), bits(r, 4, 3), bits(r, 2, 3), bits(r, 0, 3)
+    shift_x = near + core * (wide - near)
+    shift_y = wide + near - shift_x
+    mode_x = 4 * bits(at_z + shift_x, 0, 3) + bits(at_y + last, 0, 3)
+    mode_y = 4 * bits(at_b + shift_y, 0, 3) + j4
+    mode_z = 8 * core + iota((8, 16), 0)
     x, y, z = positions(tile[...], cell[...])
-
-    def values(table, at):
-        hot = (at == iota((64, points), 0)).astype(BF16)
-        both = mm(table[...], hot)
-        half = both.shape[0] // 2
-        return both[:half] + both[half:]
-
-    xs[...] = values(table_x, x)
-    ys[...] = values(table_y, y)
-    zs = values(table_z, z)
+    row = lax.bitwise_and(iota((128, points), 0), 63)
+
+    def values(mode, at):
+        pick = (mode == iota(mode.shape, 1)).astype(BF16)
+        table = mm(pick, basis[...]).astype(BF16)
+        return mm(table, (at == row).astype(BF16))
+
+    xy[...] = values(mode_x, x) * values(mode_y, y)
+    zs = values(mode_z, z)
 
     def some(s, carry):
-        for j in range(4):
-            yz[j * 8 : j * 8 + 8, :] = zs * ys[pl.ds(s * 4 + j, 1), :]
-        rows = [(xs[i : i + 1, :] * yz[...]).astype(BF16) for i in range(16)]
-        part = mm(jnp.concatenate(rows, axis=0), message[...])
-        out[pl.ds(s * 512, 512), :] = part.astype(BF16)
+        rows = [(xy[pl.ds(s * 64 + i, 1), :] * zs).astype(F32) for i in range(64)]
+        wave = jnp.concatenate(rows, axis=0).astype(BF16)
+        out[pl.ds(s * 512, 512), :] = mm(wave, message[...]).astype(BF16)
         return carry
 
     lax.fori_loop(0, 4, some, 0)
 
 
-def spectrum(message, tile, cell, table_x, table_y, table_z):
+def spectrum(message, tile, cell, basis, where, away):
     points = message.shape[0]
     return call(
-        spectrum_body,
+        functools.partial(spectrum_body, away=away),
         jax.ShapeDtypeStruct((2048, 256), BF16),
-        (message, tile, cell, table_x, table_y, table_z),
-        (
-            pltpu.VMEM((16, points), F32),
-            pltpu.VMEM((32, points), F32),
-            pltpu.VMEM((16, points), F32),
-        ),
+        (message, tile, cell, basis, where),
+        (pltpu.VMEM((256, points), F32),),
         flops=2 * 2048 * 2048 * 256,
+        scalars=1,
     )
 
 
@@ -251,7 +265,26 @@
     lax.fori_loop(0, out.shape[0] // 256, some, 0)
 
 
-def waves_body(tile, cell, wide_x, wide_y, wide_z, out_x, out_yz, spots):
+def waves_body(tile, cell, basis, where, out_p, out_qz, spots, wide_p, wide_q, wide_z):
+    at_z, at_y, at_core, at_b = device_at(where)
+    lane = iota((16, 1024), 1)
+    outer, last, j4 = bits(lane, 7, 3), bits(lane, 5, 3), bits(lane, 3, 3)
+    mode_x = 4 * bits(at_z - outer, 0, 3) + bits(at_y - last, 0, 3)
+    mode_y = 4 * bits(at_b - outer, 0, 3) + j4
+    lane = iota((16, 256), 1)
+    mode_z = 8 * lax.bitwise_xor(bits(lane, 7, 1), at_core) + bits(lane, 0, 7)
+
+    def table(mode):
+        return mm(basis[...], (mode == iota(mode.shape, 0)).astype(BF16))
+
+    straight = lax.bitwise_xor(bits(iota((128, 1024), 1), 9, 1), at_core) == 0
+    factor = table(mode_x)
+    wide_p[0:128, :] = jnp.where(straight, factor, 0.0).astype(BF16)
+    wide_q[0:128, :] = jnp.where(straight, 0.0, factor).astype(BF16)
+    factor = table(mode_y)
+    wide_p[128:256, :] = jnp.where(straight, 0.0, factor).astype(BF16)
+    wide_q[128:256, :] = jnp.where(straight, factor, 0.0).astype(BF16)
+    wide_z[...] = table(mode_z).astype(BF16)
     x, y, z = positions(tile[...], cell[...])
     spots[0:1, :] = x
     spots[1:2, :] = y
@@ -261,25 +294,26 @@
     def some(step, carry):
         at = step * 128
 
-        def values(which, table):
+        def hot(which):
             col = as_column(spots[which : which + 1, pl.ds(at, 128)], 128)
-            return mm((col == lane).astype(BF16), table[...])
-
-        out_x[pl.ds(at, 128), :] = values(0, wide_x).astype(BF16)
-        vy = values(1, wide_y)
-        vz = values(2, wide_z)
+            return (col == lane).astype(BF16)
+
+        xy = jnp.concatenate([hot(0), hot(1)], axis=1)
+        out_p[pl.ds(at, 128), :] = mm(xy, wide_p[...]).astype(BF16)
+        q = mm(xy, wide_q[...])
+        vz = mm(hot(2), wide_z[...])
         for h in range(2):
-            for s in range(4):
-                yz = vy[:, s * 128 : s * 128 + 128] * vz[:, h * 128 : h * 128 + 128]
-                to = (h * 4 + s) * 128
-                out_yz[pl.ds(at, 128), to : to + 128] = yz.astype(BF16)
-        return carry
-
-    lax.fori_loop(0, out_x.shape[0] // 128, some, 0)
+            for o in range(4):
+                to = (h * 4 + o) * 128
+                qz = q[:, to : to + 128] * vz[:, h * 128 : h * 128 + 128]
+                out_qz[pl.ds(at, 128), to : to + 128] = qz.astype(BF16)
+        return carry
+
+    lax.fori_loop(0, out_p.shape[0] // 128, some, 0)
 
 
 def decode_body(
-    m0, m1, m2, m3, m4, m5, m6, m7, wave_x, wave_yz, base, read, hidden_weight, output_weight, out
+    m0, m1, m2, m3, m4, m5, m6, m7, wave_p, wave_qz, base, read, hidden_weight, output_weight, out
 ):
     modes = (m0, m1, m2, m3, m4, m5, m6, m7)
 
@@ -287,8 +321,12 @@
         at = step * 256
         total = base[pl.ds(at, 256), :]
         for q in range(8):
-            yz = wave_yz[pl.ds(at, 256), q * 128 : q * 128 + 128]
-            wave = [yz * wave_x[pl.ds(at, 256), i * 128 : i * 128 + 128] for i in range(4)]
+            qz = wave_qz[pl.ds(at, 256), q * 128 : q * 128 + 128]
+            lane = q // 4 * 512
+            wave = [
+                qz * wave_p[pl.ds(at, 256), lane + i * 128 : lane + i * 128 + 128]
+                for i in range(4)
+            ]
             total = total + mm(jnp.concatenate(wave, axis=1), modes[q][...])
         value = jax.nn.gelu(total).astype(BF16).astype(F32)
         scale = jnp.concatenate(
@@ -299,30 +337,37 @@
         out[pl.ds(at, 256), :] = mm(hidden, output_weight[...]).astype(BF16)
         return carry
 
-    lax.fori_loop(0, out.shape[0] // 256, some, 0)
-
-
-def basis_table(mode, position):
-    half = M // 2
-    frequency = jnp.where(mode < half, mode, mode - half + 1).astype(F32)
-    phase = 2.0 * math.pi * frequency * position.astype(F32) / G
-    wave = jnp.where(mode < half, jnp.cos(phase), jnp.sin(phase))
-    return wave * jnp.where(mode == 0, math.sqrt(1.0 / G), math.sqrt(2.0 / G))
-
-
-def two_terms(table):
-    high = lax.reduce_precision(table, 8, 7)
-    return jnp.concatenate([high, table - high], axis=0).astype(BF16)
-
-
-def around(shard, axis, s):
-    return lax.ppermute(shard, axis, [(i, (i + s) % 4) for i in range(4)])
-
-
-def from_others(pieces, axis):
+    lax.fori_loop(0, out.shape[0] // 256, some, 0, unroll=2)
+
+
+def basis_terms():
+    mode = np.arange(M)[:, None]
+    frequency = np.where(mode < M // 2, mode, mode - M // 2 + 1)
+    phase = 2.0 * np.pi * frequency * np.arange(G)[None, :] / G
+    wave = np.where(mode < M // 2, np.cos(phase), np.sin(phase))
+    wave = wave * np.where(mode == 0, np.sqrt(1.0 / G), np.sqrt(2.0 / G))
+    high = wave.astype(np.float32).astype(jnp.bfloat16)
+    low = (wave - high.astype(np.float64)).astype(np.float32).astype(jnp.bfloat16)
+    return np.concatenate([high, low], axis=1)
+
+
+def around(shard, stage, s):
+    if stage == "y":
+        return lax.ppermute(shard, "y", [(i, (i + s) % 4) for i in range(4)])
+    pairs = []
+    for z in range(4):
+        for core in range(2):
+            for b in range(4):
+                along_b = (core == 0) == (stage == "wide")
+                to = (z, (b + s) % 4) if along_b else ((z + s) % 4, b)
+                pairs.append(((z * 2 + core) * 4 + b, (to[0] * 2 + core) * 4 + to[1]))
+    return lax.ppermute(shard, ("z", "core", "ba"), pairs)
+
+
+def from_others(pieces, stage):
     got = [pieces[0]]
     for s in (1, 2, 3):
-        got.append(around(pieces[s], axis, s))
+        got.append(around(pieces[s], stage, s))
     return tuple(got)
 
 
@@ -346,32 +391,12 @@
     everyone = ("z", "y", "core", "ba")
     devices = lax.axis_size(everyone)
     shape = jax.ShapeDtypeStruct
-    at_z, at_y, at_core, at_b = (lax.axis_index(a) for a in everyone)
+    where = lax.axis_index(everyone).astype(jnp.int32).reshape(1)
     tile = tile_ids.reshape(1, points)
     cell = cell_ids.reshape(1, points)
-    grid = jnp.arange(G, dtype=jnp.int32)
-
-    def mode_x(i, sign):
-        return 4 * ((at_z + sign * (i // 4)) % 4) + (at_y + sign * (i % 4)) % 4
-
-    def mode_y(s, j, sign):
-        return 4 * ((at_b + sign * s) % 4) + j
-
-    i16 = jnp.arange(16, dtype=jnp.int32)
-    k8 = jnp.arange(8, dtype=jnp.int32)
-    to_x = two_terms(basis_table(mode_x(i16, 1)[:, None], grid[None, :]))
-    to_y = two_terms(basis_table(mode_y(i16 // 4, i16 % 4, 1)[:, None], grid[None, :]))
-    other_z = two_terms(basis_table((8 * (1 - at_core) + k8)[:, None], grid[None, :]))
-    own_z = two_terms(basis_table((8 * at_core + k8)[:, None], grid[None, :]))
-    lane = jnp.arange(512, dtype=jnp.int32)
-    wide_x = two_terms(basis_table(mode_x(lane // 32, -1)[None, :], grid[:, None]))
-    wide_y = two_terms(
-        basis_table(mode_y(lane // 128, lane // 8 % 4, -1)[None, :], grid[:, None])
-    )
-    lane = lane[:256]
-    wide_z = two_terms(
-        basis_table((8 * ((at_core + lane // 128) % 2) + lane % 8)[None, :], grid[:, None])
-    )
+    terms = basis_terms()
+    basis = jnp.asarray(terms)
+    basis_tall = jnp.asarray(np.ascontiguousarray(terms.T))
 
     send, slots, message = call(
         spread_body,
@@ -385,18 +410,24 @@
         limit=60,
     )
     recv = lax.all_to_all(send, everyone, 0, 0, tiled=True)
-    away = spectrum(message, tile, cell, to_x, to_y, other_z)
-    near = spectrum(message, tile, cell, to_x, to_y, own_z)
-    wave_x, wave_yz = call(
+    away = spectrum(message, tile, cell, basis, where, True)
+    near = spectrum(message, tile, cell, basis, where, False)
+    wave_p, wave_qz = call(
         waves_body,
-        (shape((points, 512), BF16), shape((points, 1024), BF16)),
-        (tile, cell, wide_x, wide_y, wide_z),
-        (pltpu.VMEM((8, points), jnp.int32),),
+        (shape((points, 1024), BF16), shape((points, 1024), BF16)),
+        (tile, cell, basis_tall, where),
+        (
+            pltpu.VMEM((8, points), jnp.int32),
+            pltpu.VMEM((256, 1024), BF16),
+            pltpu.VMEM((256, 1024), BF16),
+            pltpu.VMEM((128, 256), BF16),
+        ),
         flops=10**9,
+        scalars=1,
     )
     parts = add_and_cut((near, swapped(away)))
-    parts = add_and_cut(from_others(parts, "ba"))
-    parts = add_and_cut(from_others(parts, "z"))
+    parts = add_and_cut(from_others(parts, "wide"))
+    parts = add_and_cut(from_others(parts, "near"))
     latent, places = call(
         collect_body,
         (shape((2048, width), BF16), shape((1024, 128), BF16)),
@@ -421,8 +452,8 @@
     )(latent, places, spectral_weight)
     mixed = call(mix_body, shape((32, width), BF16), from_others(parts, "y") + (weight,), ())
     line = joined(from_others((mixed,) * 4, "y"))
-    plane = joined(from_others((line,) * 4, "z"))
-    modes = from_others((plane,) * 4, "ba")
+    plane = joined(from_others((line,) * 4, "near"))
+    modes = from_others((plane,) * 4, "wide")
     modes = modes + tuple(swapped(m) for m in modes)
 
     returned = lax.all_to_all(back, everyone, 0, 0, tiled=True)
@@ -437,7 +468,7 @@
         decode_body,
         shape((points, width), BF16),
         modes
-        + (wave_x, wave_yz, base, read_weight.reshape(1, points), hidden_weight, output_weight),
+        + (wave_p, wave_qz, base, read_weight.reshape(1, points), hidden_weight, output_weight),
         (),
         limit=32,
         flops=2 * 4096 * 2048 * 256,

time: 166 us -> 166 us (level)
  Pallas kernels: 52.8 us -> 59.4 us
  waiting for transfers between devices: 53.3 us -> 49.5 us
  local copies, waits for them, and re-layouts: 9.75 us -> 7.22 us
  starting transfers between devices: 47.5 us -> 49.5 us
  other arithmetic: 1.89 us -> 0 us
    ppermute x18, waiting for transfers between devices: 35.2 us -> 27.8 us  [the longest x12 22.6 us: around(): return lax.ppermute(shard, ('z', 'core', 'ba'), pairs)]
    pallas_call x13, Pallas kernels: 45.7 us -> 52.5 us  [call(): return fn(*ins)]
    all_to_all x1, waiting for transfers between devices: 18.1 us -> 21.7 us  [per_device(): recv = lax.all_to_all(send, everyone, 0, 0, tiled=True)]
    ppermute x5, starting transfers between devices: 9.33 us -> 11.9 us  [swapped(): return lax.ppermute(shard, 'core', [(0, 1), (1, 0)])]
    unnamed x36, local copies, waits for them, and re-layouts: 9.75 us -> 7.22 us
  transfers between devices with their start and end apart: 25 -> 25, of which waited for: 11 -> 12; matrix products, arithmetic and copies ran while one was open for 1% -> 0% of each run, Pallas kernels for 20% -> 22%
where the time goes in v5:
time: 166 us
  Pallas kernels  59.4 us (36%)
  starting transfers between devices  49.5 us (30%)
  waiting for transfers between devices  49.5 us (30%)
  local copies, waits for them, and re-layouts  7.22 us (4%)
    pallas_call x13, Pallas kernels, call(): return fn(*ins)  52.5 us
    ppermute x12, waiting for transfers between devices, around(): return lax.ppermute(shard, ('z', 'core', 'ba'), pairs)  22.6 us
    all_to_all x1, waiting for transfers between devices, per_device(): recv = lax.all_to_all(send, everyone, 0, 0, tiled=True)  21.7 us
    ppermute x12, starting transfers between devices, around(): return lax.ppermute(shard, ('z', 'core', 'ba'), pairs)  15.2 us
    ppermute x5, starting transfers between devices, swapped(): return lax.ppermute(shard, 'core', [(0, 1), (1, 0)])  11.9 us
    all_to_all x1, starting transfers between devices, per_device(): recv = lax.all_to_all(send, everyone, 0, 0, tiled=True)  11.5 us
    unnamed x36, local copies, waits for them, and re-layouts  7.22 us
    ppermute x6, starting transfers between devices, around(): return lax.ppermute(shard, 'y', [(i, (i + s) % 4) for i in range(4)])  7.1 us
  transfers between devices with their start and end apart: 25, of which 12 were waited for; matrix products, arithmetic and copies ran while one was open for 0% of the time, Pallas kernels for 22%

profile of v5, /device:TPU:1, one launch (start us, length us, event | category | flops | bytes accessed | tf_op | source)
XLA Modules:
  0.0 166.0 jit_solution(8616312649764396895)
XLA Ops:
  0.0 9.4 %shard_map.118 = (bf16[128,56,128]{2,1,0:T(8,128)(2,1)}, s32[1,2048]{1,0:T(1,128)}, bf16[2048,256]{1,0:T(8,128)(2,1)}) custom-call(bf16[2048,256]{1,0:T(8,128)(2,1)} %feat.1, s32[1,2048]{1,0:T(1,128)} %bitcast.7, s32[1,2048]{1,0:T(1,128)} %bitcast.11, f32[1,2048]{1,0:T(1,128)} %bitcast.16, bf16[256,256]{1,0:T(8,128)(2,1)} %weight.2), custom_call_target="tpu_custom_call" | custom-call | flops 1000000 | bytes 4000000 | tf_op jit(solution)/shard_map/pallas_call | solution.py:48
  9.5 0.0 copy-start.13
  9.5 11.5 %all-to-all-start = ((bf16[128,56,128]{2,1,0:T(8,128)(2,1)}), bf16[128,56,128]{2,1,0:T(8,128)(2,1)S(1)}, u32[]{:S(2)}, u32[]{:S(2)}) async-start(bf16[128,56,128]{2,1,0:T(8,128)(2,1)} %get-tuple-element.39), calls=%async_computation | async-start | bytes 3670016 | tf_op jit(solution)/shard_map/all_to_all | solution.py:412
  21.0 5.2 %shard_map.120 = bf16[2048,256]{1,0:T(8,128)(2,1)} custom-call(bf16[2048,256]{1,0:T(8,128)(2,1)S(1)} %copy-done.5, s32[1,2048]{1,0:T(1,128)S(1)} %bitcast.8, s32[1,2048]{1,0:T(1,128)S(1)} %bitcast.12, bf16[16,128]{1,0:T(8,128)(2,1)S(1)} %copy-done.13, s32[1]{0:T(128)} %bitcast.3.where), custom_call_target="tpu_custom_call" | custom-call | flops 2147483648 | bytes 4000000 | tf_op jit(solution)/shard_map/pallas_call | solution.py:48
  26.2 1.1 collective-permute-start
  27.2 21.7 %all-to-all-done.recv = bf16[128,56,128]{2,1,0:T(8,128)(2,1)S(1)} async-done(((bf16[128,56,128]{2,1,0:T(8,128)(2,1)}), bf16[128,56,128]{2,1,0:T(8,128)(2,1)S(1)}, u32[]{:S(2)}, u32[]{:S(2)}) %all-to-all-start) | async-done | bytes 1835040 | tf_op jit(solution)/shard_map/all_to_all | solution.py:412
  48.9 5.9 %shard_map.124 = (bf16[2048,256]{1,0:T(8,128)(2,1)S(1)}, bf16[1024,128]{1,0:T(8,128)(2,1)S(1)}) custom-call(bf16[128,56,128]{2,1,0:T(8,128)(2,1)S(1)} %all-to-all-done.recv), custom_call_target="tpu_custom_call" | custom-call | flops 3221225472 | bytes 4000000 | tf_op jit(solution)/shard_map/pallas_call | solution.py:48
  54.9 7.0 %reply.1 = (bf16[128,24,256]{2,1,0:T(8,128)(2,1)}, bf16[4,8,256,256]{3,2,1,0:T(8,128)(2,1)S(1)}) custom-call(bf16[2048,256]{1,0:T(8,128)(2,1)S(1)} %get-tuple-element.40.latent, bf16[1024,128]{1,0:T(8,128)(2,1)S(1)} %get-tuple-element.41.places, bf16[4,8,256,256]{3,2,1,0:T(8,128)(2,1)S(1)} %copy-done.4), custom_call_target="tpu_custom_call" | custom-call | flops 3221225472 | bytes 4000000 | tf_op jit(solution)/shard_map/reply/pallas_call | solution.py:438
  61.9 2.0 %copy-done = bf16[4,8,256,256]{3,2,1,0:T(8,128)(2,1)} copy-done((bf16[4,8,256,256]{3,2,1,0:T(8,128)(2,1)}, bf16[4,8,256,256]{3,2,1,0:T(8,128)(2,1)S(1)}, u32[]{:S(2)}) %copy-start) | copy-done | bytes 4194328
  63.8 3.8 %all-to-all-start.1 = ((bf16[128,24,256]{2,1,0:T(8,128)(2,1)}), bf16[128,24,256]{2,1,0:T(8,128)(2,1)S(1)}, u32[]{:S(2)}, u32[]{:S(2)}) async-start(bf16[128,24,256]{2,1,0:T(8,128)(2,1)} %get-tuple-element.45), calls=%async_computation.1 | async-start | bytes 3145728 | tf_op jit(solution)/shard_map/all_to_all | solution.py:459
  67.6 0.0 copy-start.6
  67.6 1.2 copy-done.6
  68.8 4.2 %shard_map.119.refs_0_ = bf16[2048,256]{1,0:T(8,128)(2,1)S(1)} custom-call(bf16[2048,256]{1,0:T(8,128)(2,1)S(1)} %copy-done.6, s32[1,2048]{1,0:T(1,128)S(1)} %bitcast.9, s32[1,2048]{1,0:T(1,128)S(1)} %bitcast.13, bf16[16,128]{1,0:T(8,128)(2,1)S(1)} %copy-done.13, s32[1]{0:T(128)} %bitcast.3.where), custom_call_target="tpu_custom_call" | custom-call | flops 2147483648 | bytes 4000000 | tf_op jit(solution)/shard_map/pallas_call | solution.py:48
  73.0 0.0 collective-permute-done.refs_1_
  73.0 0.2 shard_map.121
  73.3 1.7 %collective-permute-start.1 = (bf16[512,256]{1,0:T(8,128)(2,1)S(1)}, bf16[512,256]{1,0:T(8,128)(2,1)S(1)}, u32[]{:S(2)}, u32[]{:S(2)}) collective-permute-start(bf16[512,256]{1,0:T(8,128)(2,1)S(1)} %get-tuple-element.28), channel_id=1, source_target_pairs={{0,1},{1,2},{2,3},{3,0},{4,36},{5,37},{6,38},{7,39},{32,33},{33,34... | collective-permute-start | bytes 786440 | tf_op jit(solution)/shard_map/ppermute | solution.py:364
  74.9 2.9 %collective-permute-start.2 = (bf16[512,256]{1,0:T(8,128)(2,1)S(1)}, bf16[512,256]{1,0:T(8,128)(2,1)S(1)}, u32[]{:S(2)}, u32[]{:S(2)}) collective-permute-start(bf16[512,256]{1,0:T(8,128)(2,1)S(1)} %get-tuple-element.29), channel_id=1, source_target_pairs={{0,2},{1,3},{2,0},{3,1},{4,68},{5,69},{6,70},{7,71},{32,34},{33,35... | collective-permute-start | bytes 786440 | tf_op jit(solution)/shard_map/ppermute | solution.py:364
  77.9 0.9 collective-permute-start.3
  78.8 13.1 %collective-permute-done.1.refs_1_ = bf16[512,256]{1,0:T(8,128)(2,1)S(1)} collective-permute-done((bf16[512,256]{1,0:T(8,128)(2,1)S(1)}, bf16[512,256]{1,0:T(8,128)(2,1)S(1)}, u32[]{:S(2)}, u32[]{:S(2)}) %collective-permute-start.1) | collective-permute-done | bytes 262176 | tf_op jit(solution)/shard_map/ppermute | solution.py:364
  91.8 2.9 %collective-permute-done.2.refs_2_ = bf16[512,256]{1,0:T(8,128)(2,1)S(1)} collective-permute-done((bf16[512,256]{1,0:T(8,128)(2,1)S(1)}, bf16[512,256]{1,0:T(8,128)(2,1)S(1)}, u32[]{:S(2)}, u32[]{:S(2)}) %collective-permute-start.2) | collective-permute-done | bytes 262176 | tf_op jit(solution)/shard_map/ppermute | solution.py:364
  94.8 0.1 shard_map.122
  94.9 1.2 collective-permute-start.4
  96.2 2.4 %collective-permute-start.5 = (bf16[128,256]{1,0:T(8,128)(2,1)S(1)}, bf16[128,256]{1,0:T(8,128)(2,1)S(1)}, u32[]{:S(2)}, u32[]{:S(2)}) collective-permute-start(bf16[128,256]{1,0:T(8,128)(2,1)S(1)} %get-tuple-element.33), channel_id=1, source_target_pairs={{0,64},{1,65},{2,66},{3,67},{4,6},{5,7},{6,4},{7,5},{32,96},{33,97... | collective-permute-start | bytes 196616 | tf_op jit(solution)/shard_map/ppermute | solution.py:364
  98.6 0.9 collective-permute-start.6
  99.5 1.7 %collective-permute-done.5.refs_2_ = bf16[128,256]{1,0:T(8,128)(2,1)S(1)} collective-permute-done((bf16[128,256]{1,0:T(8,128)(2,1)S(1)}, bf16[128,256]{1,0:T(8,128)(2,1)S(1)}, u32[]{:S(2)}, u32[]{:S(2)}) %collective-permute-start.5) | collective-permute-done | bytes 65568 | tf_op jit(solution)/shard_map/ppermute | solution.py:364
  101.3 0.5 collective-permute-done.6.refs_3_
  101.8 0.7 collective-permute-start.7
  102.4 2.3 %collective-permute-start.8 = (bf16[32,256]{1,0:T(8,128)(2,1)S(1)}, bf16[32,256]{1,0:T(8,128)(2,1)S(1)}, u32[]{:S(2)}, u32[]{:S(2)}) collective-permute-start(bf16[32,256]{1,0:T(8,128)(2,1)S(1)} %get-tuple-element.37), channel_id=1, source_target_pairs={{0,16},{8,24},{16,0},{24,8},{1,17},{9,25},{17,1},{25,9},{2,18},{10... | collective-permute-start | bytes 49160 | tf_op jit(solution)/shard_map/ppermute | solution.py:356
  104.8 1.2 collective-permute-start.9
  105.9 0.0 collective-permute-done.7.b
  105.9 0.6 collective-permute-done.8.c
  106.5 1.1 collective-permute-done.9.d
  107.7 0.7 shard_map.125.refs_0_
  108.3 2.3 %collective-permute-start.12 = (bf16[32,256]{1,0:T(8,128)(2,1)S(1)}, bf16[32,256]{1,0:T(8,128)(2,1)S(1)}, u32[]{:S(2)}, u32[]{:S(2)}) collective-permute-start(bf16[32,256]{1,0:T(8,128)(2,1)S(1)} %shard_map.125.refs_0_), channel_id=1, source_target_pairs={{0,24},{8,0},{16,8},{24,16},{1,25},{9,1},{17,9},{25,17},{2,26},{10... | collective-permute-start | bytes 49160 | tf_op jit(solution)/shard_map/ppermute | solution.py:356
  110.6 0.1 collective-permute-start.11
  110.7 0.6 collective-permute-start.10
  111.2 0.2 collective-permute-done.12.refs_3_
  111.4 3.2 %collective-permute-done.11.refs_2_ = bf16[32,256]{1,0:T(8,128)(2,1)S(1)} collective-permute-done((bf16[32,256]{1,0:T(8,128)(2,1)S(1)}, bf16[32,256]{1,0:T(8,128)(2,1)S(1)}, u32[]{:S(2)}, u32[]{:S(2)}) %collective-permute-start.11) | collective-permute-done | bytes 16416 | tf_op jit(solution)/shard_map/ppermute | solution.py:356
  114.7 0.0 collective-permute-done.10.refs_1_
  114.7 0.0 copy-start.7
  114.7 2.2 %collective-permute-start.15 = (bf16[128,256]{1,0:T(8,128)(2,1)S(1)}, bf16[128,256]{1,0:T(8,128)(2,1)S(1)}, u32[]{:S(2)}, u32[]{:S(2)}) collective-permute-start(bf16[128,256]{1,0:T(8,128)(2,1)S(1)} %shard_map.126.refs_0_), channel_id=1, source_target_pairs={{0,96},{1,97},{2,98},{3,99},{4,7},{5,4},{6,5},{7,6},{32,0},{33,1},... | collective-permute-start | bytes 196616 | tf_op jit(solution)/shard_map/ppermute | solution.py:364
  116.9 0.1 collective-permute-start.14
  116.9 0.6 collective-permute-start.13
  117.5 1.2 collective-permute-done.15.refs_3_
  118.8 2.8 %collective-permute-done.14.refs_2_ = bf16[128,256]{1,0:T(8,128)(2,1)S(1)} collective-permute-done((bf16[128,256]{1,0:T(8,128)(2,1)S(1)}, bf16[128,256]{1,0:T(8,128)(2,1)S(1)}, u32[]{:S(2)}, u32[]{:S(2)}) %collective-permute-start.14) | collective-permute-done | bytes 65568 | tf_op jit(solution)/shard_map/ppermute | solution.py:364
  121.6 0.4 collective-permute-done.13.refs_1_
  122.0 0.5 collective-permute-start.18
  122.5 1.7 %collective-permute-start.17 = (bf16[512,256]{1,0:T(8,128)(2,1)S(1)}, bf16[512,256]{1,0:T(8,128)(2,1)S(1)}, u32[]{:S(2)}, u32[]{:S(2)}) collective-permute-start(bf16[512,256]{1,0:T(8,128)(2,1)S(1)} %shard_map.127.m0), channel_id=1, source_target_pairs={{0,2},{1,3},{2,0},{3,1},{4,68},{5,69},{6,70},{7,71},{32,34},{33,35... | collective-permute-start | bytes 786440 | tf_op jit(solution)/shard_map/ppermute | solution.py:364
  124.2 0.0 collective-permute-start.16
  124.2 6.8 %shard_map.128 = (bf16[2048,1024]{1,0:T(8,128)(2,1)S(1)}, bf16[2048,1024]{1,0:T(8,128)(2,1)S(1)}) custom-call(s32[1,2048]{1,0:T(1,128)S(1)} %bitcast.10, s32[1,2048]{1,0:T(1,128)S(1)} %bitcast.14, bf16[128,16]{1,0:T(8,128)(2,1)S(1)} %copy-done.12, s32[1]{0:T(128)} %bitcast.3.where), custom_call_target="tpu_custom_call" | custom-call | flops 1000000000 | bytes 4000000 | tf_op jit(solution)/shard_map/pallas_call | solution.py:48
  131.0 2.0 %copy-done.14 = bf16[2048,1024]{1,0:T(8,128)(2,1)} copy-done((bf16[2048,1024]{1,0:T(8,128)(2,1)}, bf16[2048,1024]{1,0:T(8,128)(2,1)S(1)}, u32[]{:S(2)}) %copy-start.14) | copy-done | bytes 4194328
  133.0 2.0 %copy-done.16 = bf16[2048,1024]{1,0:T(8,128)(2,1)} copy-done((bf16[2048,1024]{1,0:T(8,128)(2,1)}, bf16[2048,1024]{1,0:T(8,128)(2,1)S(1)}, u32[]{:S(2)}) %copy-start.16) | copy-done | bytes 4194328
  135.0 10.3 %collective-permute-start.19 = (bf16[512,256]{1,0:T(8,128)(2,1)S(1)}, bf16[512,256]{1,0:T(8,128)(2,1)S(1)}, u32[]{:S(2)}, u32[]{:S(2)}) collective-permute-start(bf16[512,256]{1,0:T(8,128)(2,1)S(1)} %shard_map.127.m0), channel_id=1, source_target_pairs={{0,4},{4,0},{1,5},{5,1},{2,6},{6,2},{3,7},{7,3},{8,12},{12,8},{9,1... | collective-permute-start | bytes 786440 | tf_op jit(solution)/shard_map/ppermute | solution.py:375
  145.3 0.0 collective-permute-start.22
  145.3 0.0 collective-permute-done.17.m2
  145.3 0.5 collective-permute-start.21
  145.8 0.1 collective-permute-start.20
  145.9 0.0 all-to-all-done.1
  145.9 0.0 copy-start.8
  145.9 0.0 copy-start.9
  145.9 0.0 copy-start.10
  145.9 6.2 %shard_map.129.base = f32[2048,256]{1,0:T(8,128)S(1)} custom-call(bf16[3072,256]{1,0:T(8,128)(2,1)S(1)} %bitcast.6, s32[1,2048]{1,0:T(1,128)S(1)} %copy-done.11, bf16[256,256]{1,0:T(8,128)(2,1)S(1)} %copy-done.7), custom_call_target="tpu_custom_call" | custom-call | flops 3221225472 | bytes 4000000 | tf_op jit(solution)/shard_map/pallas_call | solution.py:48
  152.1 0.0 collective-permute-done.19.m4
  152.2 13.7 %shard_map.130 = bf16[2048,256]{1,0:T(8,128)(2,1)} custom-call(bf16[512,256]{1,0:T(8,128)(2,1)S(1)} %shard_map.127.m0, bf16[512,256]{1,0:T(8,128)(2,1)S(1)} %collective-permute-done.16.m1, bf16[512,256]{1,0:T(8,128)(2,1)S(1)} %collective-permute-done.17.m2, bf16[512,256]{1,0:T(8,128)(2,1)S(1)} %collective-permute-done.18.m3, ...), custom_call_target="tpu_custom_call" | custom-call | flops 4294967296 | bytes 4000000 | tf_op jit(solution)/shard_map/pallas_call | solution.py:48
  (36 shorter events, 0.1 us)
Async XLA Ops:
  9.4 11.5 %copy-start.2 = (s32[2048,1]{0,1:T(1,128)S(1)}, s32[2048,1]{0,1:T(1,128)}, u32[]{:S(2)}) copy-start(s32[2048,1]{0,1:T(1,128)} %param.13) | copy-start | bytes 24580
  9.5 11.5 %copy-start.3 = (s32[2048]{0:T(1024)S(1)}, s32[2048]{0:T(1024)}, u32[]{:S(2)}) copy-start(s32[2048]{0:T(1024)} %param.14) | copy-start | bytes 24580
  9.5 11.5 %copy-start.5 = (bf16[2048,256]{1,0:T(8,128)(2,1)S(1)}, bf16[2048,256]{1,0:T(8,128)(2,1)}, u32[]{:S(2)}) copy-start(bf16[2048,256]{1,0:T(8,128)(2,1)} %get-tuple-element.26.message) | copy-start | bytes 3145732
  9.5 11.5 %copy-start.13 = (bf16[16,128]{1,0:T(8,128)(2,1)S(1)}, bf16[16,128]{1,0:T(8,128)(2,1)}, u32[]{:S(2)}) copy-start(bf16[16,128]{1,0:T(8,128)(2,1)} %constant.26.clone.basis) | copy-start | bytes 12292
  9.5 39.4 %all-to-all-start = ((bf16[128,56,128]{2,1,0:T(8,128)(2,1)}), bf16[128,56,128]{2,1,0:T(8,128)(2,1)S(1)}, u32[]{:S(2)}, u32[]{:S(2)}) async-start(bf16[128,56,128]{2,1,0:T(8,128)(2,1)} %get-tuple-element.39), calls=%async_computation | async-start | bytes 3670016 | tf_op jit(solution)/shard_map/all_to_all | solution.py:412
  26.2 46.8 %collective-permute-start = (bf16[2048,256]{1,0:T(8,128)(2,1)}, bf16[2048,256]{1,0:T(8,128)(2,1)S(1)}, u32[]{:S(2)}, u32[]{:S(2)}) collective-permute-start(bf16[2048,256]{1,0:T(8,128)(2,1)} %shard_map.120), channel_id=1, source_target_pairs={{0,4},{4,0},{1,5},{5,1},{2,6},{6,2},{3,7},{7,3},{8,12},{12,8},{9,1... | collective-permute-start | bytes 3145736 | tf_op jit(solution)/shard_map/ppermute | solution.py:375
  48.9 5.9 %copy-start.4 = (bf16[4,8,256,256]{3,2,1,0:T(8,128)(2,1)S(1)}, bf16[4,8,256,256]{3,2,1,0:T(8,128)(2,1)}, u32[]{:S(2)}) copy-start(bf16[4,8,256,256]{3,2,1,0:T(8,128)(2,1)} %weight.3) | copy-start | bytes 12582916
  61.9 2.0 %copy-start = (bf16[4,8,256,256]{3,2,1,0:T(8,128)(2,1)}, bf16[4,8,256,256]{3,2,1,0:T(8,128)(2,1)S(1)}, u32[]{:S(2)}) copy-start(bf16[4,8,256,256]{3,2,1,0:T(8,128)(2,1)S(1)} %get-tuple-element.42.weight) | copy-start | bytes 12582916
  63.8 82.1 %all-to-all-start.1 = ((bf16[128,24,256]{2,1,0:T(8,128)(2,1)}), bf16[128,24,256]{2,1,0:T(8,128)(2,1)S(1)}, u32[]{:S(2)}, u32[]{:S(2)}) async-start(bf16[128,24,256]{2,1,0:T(8,128)(2,1)} %get-tuple-element.45), calls=%async_computation.1 | async-start | bytes 3145728 | tf_op jit(solution)/shard_map/all_to_all | solution.py:459
  67.6 1.2 copy-start.6
  68.8 38.8 %copy-start.1 = (bf16[4,8,256,256]{3,2,1,0:T(8,128)(2,1)S(1)}, bf16[4,8,256,256]{3,2,1,0:T(8,128)(2,1)}, u32[]{:S(2)}) copy-start(bf16[4,8,256,256]{3,2,1,0:T(8,128)(2,1)} %copy-done) | copy-start | bytes 12582916
  73.3 18.6 %collective-permute-start.1 = (bf16[512,256]{1,0:T(8,128)(2,1)S(1)}, bf16[512,256]{1,0:T(8,128)(2,1)S(1)}, u32[]{:S(2)}, u32[]{:S(2)}) collective-permute-start(bf16[512,256]{1,0:T(8,128)(2,1)S(1)} %get-tuple-element.28), channel_id=1, source_target_pairs={{0,1},{1,2},{2,3},{3,0},{4,36},{5,37},{6,38},{7,39},{32,33},{33,34... | collective-permute-start | bytes 786440 | tf_op jit(solution)/shard_map/ppermute | solution.py:364
  74.9 19.8 %collective-permute-start.2 = (bf16[512,256]{1,0:T(8,128)(2,1)S(1)}, bf16[512,256]{1,0:T(8,128)(2,1)S(1)}, u32[]{:S(2)}, u32[]{:S(2)}) collective-permute-start(bf16[512,256]{1,0:T(8,128)(2,1)S(1)} %get-tuple-element.29), channel_id=1, source_target_pairs={{0,2},{1,3},{2,0},{3,1},{4,68},{5,69},{6,70},{7,71},{32,34},{33,35... | collective-permute-start | bytes 786440 | tf_op jit(solution)/shard_map/ppermute | solution.py:364
  77.9 16.9 %collective-permute-start.3 = (bf16[512,256]{1,0:T(8,128)(2,1)S(1)}, bf16[512,256]{1,0:T(8,128)(2,1)S(1)}, u32[]{:S(2)}, u32[]{:S(2)}) collective-permute-start(bf16[512,256]{1,0:T(8,128)(2,1)S(1)} %get-tuple-element.30), channel_id=1, source_target_pairs={{0,3},{1,0},{2,1},{3,2},{4,100},{5,101},{6,102},{7,103},{32,35},{3... | collective-permute-start | bytes 786440 | tf_op jit(solution)/shard_map/ppermute | solution.py:364
  94.9 4.6 %collective-permute-start.4 = (bf16[128,256]{1,0:T(8,128)(2,1)S(1)}, bf16[128,256]{1,0:T(8,128)(2,1)S(1)}, u32[]{:S(2)}, u32[]{:S(2)}) collective-permute-start(bf16[128,256]{1,0:T(8,128)(2,1)S(1)} %get-tuple-element.32), channel_id=1, source_target_pairs={{0,32},{1,33},{2,34},{3,35},{4,5},{5,6},{6,7},{7,4},{32,64},{33,65... | collective-permute-start | bytes 196616 | tf_op jit(solution)/shard_map/ppermute | solution.py:364
  96.2 5.1 %collective-permute-start.5 = (bf16[128,256]{1,0:T(8,128)(2,1)S(1)}, bf16[128,256]{1,0:T(8,128)(2,1)S(1)}, u32[]{:S(2)}, u32[]{:S(2)}) collective-permute-start(bf16[128,256]{1,0:T(8,128)(2,1)S(1)} %get-tuple-element.33), channel_id=1, source_target_pairs={{0,64},{1,65},{2,66},{3,67},{4,6},{5,7},{6,4},{7,5},{32,96},{33,97... | collective-permute-start | bytes 196616 | tf_op jit(solution)/shard_map/ppermute | solution.py:364
  98.6 3.1 %collective-permute-start.6 = (bf16[128,256]{1,0:T(8,128)(2,1)S(1)}, bf16[128,256]{1,0:T(8,128)(2,1)S(1)}, u32[]{:S(2)}, u32[]{:S(2)}) collective-permute-start(bf16[128,256]{1,0:T(8,128)(2,1)S(1)} %get-tuple-element.34), channel_id=1, source_target_pairs={{0,96},{1,97},{2,98},{3,99},{4,7},{5,4},{6,5},{7,6},{32,0},{33,1},... | collective-permute-start | bytes 196616 | tf_op jit(solution)/shard_map/ppermute | solution.py:364
  101.8 4.2 %collective-permute-start.7 = (bf16[32,256]{1,0:T(8,128)(2,1)S(1)}, bf16[32,256]{1,0:T(8,128)(2,1)S(1)}, u32[]{:S(2)}, u32[]{:S(2)}) collective-permute-start(bf16[32,256]{1,0:T(8,128)(2,1)S(1)} %get-tuple-element.36), channel_id=1, source_target_pairs={{0,8},{8,16},{16,24},{24,0},{1,9},{9,17},{17,25},{25,1},{2,10},{10... | collective-permute-start | bytes 49160 | tf_op jit(solution)/shard_map/ppermute | solution.py:356
  102.4 4.1 %collective-permute-start.8 = (bf16[32,256]{1,0:T(8,128)(2,1)S(1)}, bf16[32,256]{1,0:T(8,128)(2,1)S(1)}, u32[]{:S(2)}, u32[]{:S(2)}) collective-permute-start(bf16[32,256]{1,0:T(8,128)(2,1)S(1)} %get-tuple-element.37), channel_id=1, source_target_pairs={{0,16},{8,24},{16,0},{24,8},{1,17},{9,25},{17,1},{25,9},{2,18},{10... | collective-permute-start | bytes 49160 | tf_op jit(solution)/shard_map/ppermute | solution.py:356
  104.8 2.9 %collective-permute-start.9 = (bf16[32,256]{1,0:T(8,128)(2,1)S(1)}, bf16[32,256]{1,0:T(8,128)(2,1)S(1)}, u32[]{:S(2)}, u32[]{:S(2)}) collective-permute-start(bf16[32,256]{1,0:T(8,128)(2,1)S(1)} %get-tuple-element.38), channel_id=1, source_target_pairs={{0,24},{8,0},{16,8},{24,16},{1,25},{9,1},{17,9},{25,17},{2,26},{10... | collective-permute-start | bytes 49160 | tf_op jit(solution)/shard_map/ppermute | solution.py:356
  107.7 16.6 %copy-start.12 = (bf16[128,16]{1,0:T(8,128)(2,1)S(1)}, bf16[128,16]{1,0:T(8,128)(2,1)}, u32[]{:S(2)}) copy-start(bf16[128,16]{1,0:T(8,128)(2,1)} %constant.27.clone.basis) | copy-start | bytes 12292
  108.3 3.1 %collective-permute-start.12 = (bf16[32,256]{1,0:T(8,128)(2,1)S(1)}, bf16[32,256]{1,0:T(8,128)(2,1)S(1)}, u32[]{:S(2)}, u32[]{:S(2)}) collective-permute-start(bf16[32,256]{1,0:T(8,128)(2,1)S(1)} %shard_map.125.refs_0_), channel_id=1, source_target_pairs={{0,24},{8,0},{16,8},{24,16},{1,25},{9,1},{17,9},{25,17},{2,26},{10... | collective-permute-start | bytes 49160 | tf_op jit(solution)/shard_map/ppermute | solution.py:356
  110.6 4.1 %collective-permute-start.11 = (bf16[32,256]{1,0:T(8,128)(2,1)S(1)}, bf16[32,256]{1,0:T(8,128)(2,1)S(1)}, u32[]{:S(2)}, u32[]{:S(2)}) collective-permute-start(bf16[32,256]{1,0:T(8,128)(2,1)S(1)} %shard_map.125.refs_0_), channel_id=1, source_target_pairs={{0,16},{8,24},{16,0},{24,8},{1,17},{9,25},{17,1},{25,9},{2,18},{10... | collective-permute-start | bytes 49160 | tf_op jit(solution)/shard_map/ppermute | solution.py:356
  110.7 4.0 %collective-permute-start.10 = (bf16[32,256]{1,0:T(8,128)(2,1)S(1)}, bf16[32,256]{1,0:T(8,128)(2,1)S(1)}, u32[]{:S(2)}, u32[]{:S(2)}) collective-permute-start(bf16[32,256]{1,0:T(8,128)(2,1)S(1)} %shard_map.125.refs_0_), channel_id=1, source_target_pairs={{0,8},{8,16},{16,24},{24,0},{1,9},{9,17},{17,25},{25,1},{2,10},{10... | collective-permute-start | bytes 49160 | tf_op jit(solution)/shard_map/ppermute | solution.py:356
  114.7 31.2 %copy-start.7 = (bf16[256,256]{1,0:T(8,128)(2,1)S(1)}, bf16[256,256]{1,0:T(8,128)(2,1)}, u32[]{:S(2)}) copy-start(bf16[256,256]{1,0:T(8,128)(2,1)} %skip.1) | copy-start | bytes 393220
  114.7 31.2 %copy-start.11 = (s32[1,2048]{1,0:T(1,128)S(1)}, s32[1,2048]{1,0:T(1,128)}, u32[]{:S(2)}) copy-start(s32[1,2048]{1,0:T(1,128)} %get-tuple-element.46.slots) | copy-start | bytes 24580
  114.7 4.1 %collective-permute-start.15 = (bf16[128,256]{1,0:T(8,128)(2,1)S(1)}, bf16[128,256]{1,0:T(8,128)(2,1)S(1)}, u32[]{:S(2)}, u32[]{:S(2)}) collective-permute-start(bf16[128,256]{1,0:T(8,128)(2,1)S(1)} %shard_map.126.refs_0_), channel_id=1, source_target_pairs={{0,96},{1,97},{2,98},{3,99},{4,7},{5,4},{6,5},{7,6},{32,0},{33,1},... | collective-permute-start | bytes 196616 | tf_op jit(solution)/shard_map/ppermute | solution.py:364
  116.9 4.7 %collective-permute-start.14 = (bf16[128,256]{1,0:T(8,128)(2,1)S(1)}, bf16[128,256]{1,0:T(8,128)(2,1)S(1)}, u32[]{:S(2)}, u32[]{:S(2)}) collective-permute-start(bf16[128,256]{1,0:T(8,128)(2,1)S(1)} %shard_map.126.refs_0_), channel_id=1, source_target_pairs={{0,64},{1,65},{2,66},{3,67},{4,6},{5,7},{6,4},{7,5},{32,96},{33,97... | collective-permute-start | bytes 196616 | tf_op jit(solution)/shard_map/ppermute | solution.py:364
  116.9 5.0 %collective-permute-start.13 = (bf16[128,256]{1,0:T(8,128)(2,1)S(1)}, bf16[128,256]{1,0:T(8,128)(2,1)S(1)}, u32[]{:S(2)}, u32[]{:S(2)}) collective-permute-start(bf16[128,256]{1,0:T(8,128)(2,1)S(1)} %shard_map.126.refs_0_), channel_id=1, source_target_pairs={{0,32},{1,33},{2,34},{3,35},{4,5},{5,6},{6,7},{7,4},{32,64},{33,65... | collective-permute-start | bytes 196616 | tf_op jit(solution)/shard_map/ppermute | solution.py:364
  122.0 23.3 %collective-permute-start.18 = (bf16[512,256]{1,0:T(8,128)(2,1)S(1)}, bf16[512,256]{1,0:T(8,128)(2,1)S(1)}, u32[]{:S(2)}, u32[]{:S(2)}) collective-permute-start(bf16[512,256]{1,0:T(8,128)(2,1)S(1)} %shard_map.127.m0), channel_id=1, source_target_pairs={{0,3},{1,0},{2,1},{3,2},{4,100},{5,101},{6,102},{7,103},{32,35},{3... | collective-permute-start | bytes 786440 | tf_op jit(solution)/shard_map/ppermute | solution.py:364
  122.5 22.8 %collective-permute-start.17 = (bf16[512,256]{1,0:T(8,128)(2,1)S(1)}, bf16[512,256]{1,0:T(8,128)(2,1)S(1)}, u32[]{:S(2)}, u32[]{:S(2)}) collective-permute-start(bf16[512,256]{1,0:T(8,128)(2,1)S(1)} %shard_map.127.m0), channel_id=1, source_target_pairs={{0,2},{1,3},{2,0},{3,1},{4,68},{5,69},{6,70},{7,71},{32,34},{33,35... | collective-permute-start | bytes 786440 | tf_op jit(solution)/shard_map/ppermute | solution.py:364
  124.2 21.6 %collective-permute-start.16 = (bf16[512,256]{1,0:T(8,128)(2,1)S(1)}, bf16[512,256]{1,0:T(8,128)(2,1)S(1)}, u32[]{:S(2)}, u32[]{:S(2)}) collective-permute-start(bf16[512,256]{1,0:T(8,128)(2,1)S(1)} %shard_map.127.m0), channel_id=1, source_target_pairs={{0,1},{1,2},{2,3},{3,0},{4,36},{5,37},{6,38},{7,39},{32,33},{33,34... | collective-permute-start | bytes 786440 | tf_op jit(solution)/shard_map/ppermute | solution.py:364
  131.0 2.0 %copy-start.14 = (bf16[2048,1024]{1,0:T(8,128)(2,1)}, bf16[2048,1024]{1,0:T(8,128)(2,1)S(1)}, u32[]{:S(2)}) copy-start(bf16[2048,1024]{1,0:T(8,128)(2,1)S(1)} %get-tuple-element.43.wave_p) | copy-start | bytes 12582916
  133.0 2.0 %copy-start.16 = (bf16[2048,1024]{1,0:T(8,128)(2,1)}, bf16[2048,1024]{1,0:T(8,128)(2,1)S(1)}, u32[]{:S(2)}) copy-start(bf16[2048,1024]{1,0:T(8,128)(2,1)S(1)} %get-tuple-element.44.wave_qz) | copy-start | bytes 12582916
  135.0 17.1 %collective-permute-start.19 = (bf16[512,256]{1,0:T(8,128)(2,1)S(1)}, bf16[512,256]{1,0:T(8,128)(2,1)S(1)}, u32[]{:S(2)}, u32[]{:S(2)}) collective-permute-start(bf16[512,256]{1,0:T(8,128)(2,1)S(1)} %shard_map.127.m0), channel_id=1, source_target_pairs={{0,4},{4,0},{1,5},{5,1},{2,6},{6,2},{3,7},{7,3},{8,12},{12,8},{9,1... | collective-permute-start | bytes 786440 | tf_op jit(solution)/shard_map/ppermute | solution.py:375
  145.3 6.9 %collective-permute-start.22 = (bf16[512,256]{1,0:T(8,128)(2,1)S(1)}, bf16[512,256]{1,0:T(8,128)(2,1)S(1)}, u32[]{:S(2)}, u32[]{:S(2)}) collective-permute-start(bf16[512,256]{1,0:T(8,128)(2,1)S(1)} %collective-permute-done.18.m3), channel_id=1, source_target_pairs={{0,4},{4,0},{1,5},{5,1},{2,6},{6,2},{3,7},{7,3},{8,12},{12,8},{9,1... | collective-permute-start | bytes 786440 | tf_op jit(solution)/shard_map/ppermute | solution.py:375
  145.3 6.9 %collective-permute-start.21 = (bf16[512,256]{1,0:T(8,128)(2,1)S(1)}, bf16[512,256]{1,0:T(8,128)(2,1)S(1)}, u32[]{:S(2)}, u32[]{:S(2)}) collective-permute-start(bf16[512,256]{1,0:T(8,128)(2,1)S(1)} %collective-permute-done.17.m2), channel_id=1, source_target_pairs={{0,4},{4,0},{1,5},{5,1},{2,6},{6,2},{3,7},{7,3},{8,12},{12,8},{9,1... | collective-permute-start | bytes 786440 | tf_op jit(solution)/shard_map/ppermute | solution.py:375
  145.8 6.4 %collective-permute-start.20 = (bf16[512,256]{1,0:T(8,128)(2,1)S(1)}, bf16[512,256]{1,0:T(8,128)(2,1)}, u32[]{:S(2)}, u32[]{:S(2)}) collective-permute-start(bf16[512,256]{1,0:T(8,128)(2,1)S(1)} %collective-permute-done.16.m1), channel_id=1, source_target_pairs={{0,4},{4,0},{1,5},{5,1},{2,6},{6,2},{3,7},{7,3},{8,12},{12,8},{9,1... | collective-permute-start | bytes 786440 | tf_op jit(solution)/shard_map/ppermute | solution.py:375
  145.9 6.3 %copy-start.8 = (bf16[256,256]{1,0:T(8,128)(2,1)S(1)}, bf16[256,256]{1,0:T(8,128)(2,1)}, u32[]{:S(2)}) copy-start(bf16[256,256]{1,0:T(8,128)(2,1)} %hidden_weight.1) | copy-start | bytes 393220
  145.9 6.3 %copy-start.9 = (bf16[256,256]{1,0:T(8,128)(2,1)S(1)}, bf16[256,256]{1,0:T(8,128)(2,1)}, u32[]{:S(2)}) copy-start(bf16[256,256]{1,0:T(8,128)(2,1)} %output_weight.1) | copy-start | bytes 393220
  145.9 6.3 %copy-start.10 = (f32[2048]{0:T(1024)S(1)}, f32[2048]{0:T(1024)}, u32[]{:S(2)}) copy-start(f32[2048]{0:T(1024)} %param.16) | copy-start | bytes 24580
  145.9 6.3 %copy-start.15 = (bf16[2048,1024]{1,0:T(8,128)(2,1)S(1)}, bf16[2048,1024]{1,0:T(8,128)(2,1)}, u32[]{:S(2)}) copy-start(bf16[2048,1024]{1,0:T(8,128)(2,1)} %copy-done.14) | copy-start | bytes 12582916
  145.9 6.3 %copy-start.17 = (bf16[2048,1024]{1,0:T(8,128)(2,1)S(1)}, bf16[2048,1024]{1,0:T(8,128)(2,1)}, u32[]{:S(2)}) copy-start(bf16[2048,1024]{1,0:T(8,128)(2,1)} %copy-done.16) | copy-start | bytes 12582916

commit v6 on v5

--- a/solution.py
+++ b/solution.py
@@ -48,10 +48,14 @@
     return fn(*ins)
 
 
-def spread_body(feat, tile, cell, spread, weight, send, slots, message, rank_row):
-    devices = send.shape[0]
-    points = feat.shape[0]
+def spread_body(
+    feat, tile, cell, spread, weight, send, slots, message, rank_row, local, place, built, loads, saves
+):
+    devices = built.shape[0]
+    points = local.shape[0]
     cap = 24
+    load = pltpu.make_async_copy(feat, local, loads)
+    load.start()
     upper = (iota((256, 256), 0) < iota((256, 256), 1)).astype(BF16)
     ones = jnp.ones((256, 128), BF16)
     used = jnp.zeros((devices, 256), F32)
@@ -65,20 +69,32 @@
         rank = jnp.sum(hot * before, axis=0, keepdims=True).astype(jnp.int32)
         rank_row[:, at : at + 256] = rank
         slots[:, at : at + 256] = tile[:, at : at + 256] * cap + rank
-    for at in range(0, points, 128):
-        product = mm(feat[at : at + 128, :], weight[...])
-        scale = as_column(spread[:, at : at + 128], 128)
+    load.wait()
+    lane = iota((128, 128), 1)
+
+    def weigh(step, carry):
+        at = step * 128
+        product = mm(local[pl.ds(at, 128), :], weight[...])
+        scale = as_column(spread[:, pl.ds(at, 128)], 128)
         scale = jnp.concatenate([scale, scale], axis=1)
-        message[at : at + 128, :] = (scale * product).astype(BF16)
+        message[pl.ds(at, 128), :] = (scale * product).astype(BF16)
+        group = as_column(lax.shift_right_logical(rank_row[:, pl.ds(at, 128)], 3), 128)
+        where = as_column(cell[:, pl.ds(at, 128)], 128)
+        high_part = lax.shift_right_logical(where, 6).astype(F32)
+        low_part = lax.bitwise_and(where, 63).astype(F32)
+        both = jnp.where(lane == 2 * group, high_part, 0.0)
+        both = jnp.where(lane == 2 * group + 1, low_part, both)
+        place[pl.ds(at, 128), :] = both.astype(BF16)
+        return carry
+
+    lax.fori_loop(0, points // 128, weigh, 0, unroll=2)
     rank = rank_row[...]
-    group = lax.shift_right_logical(rank, 3)
     low = tile[...] * 8 + lax.bitwise_and(rank, 7)
-    high_part = lax.shift_right_logical(cell[...], 6).astype(F32)
-    low_part = lax.bitwise_and(cell[...], 63).astype(F32)
-    lane = iota((128, points), 0)
-    where = jnp.where(lane == 2 * group, high_part, 0.0)
-    where = jnp.where(lane == 2 * group + 1, low_part, where).astype(BF16)
     slot = slots[...]
+
+    def save(step):
+        rows = pl.ds(step * 16, 16)
+        return pltpu.make_async_copy(built.at[rows], send.at[rows], saves.at[step])
 
     def fill(step, carry):
         base = step * 16
@@ -87,13 +103,16 @@
         left = rows[:, :128].reshape(16, cap, 128).astype(BF16)
         right = rows[:, 128:].reshape(16, cap, 128).astype(BF16)
         hot8 = (low - base * 8 == iota((128, points), 0)).astype(BF16)
-        placing = mm_nt(hot8, where).reshape(16, 8, 128).astype(BF16)
-        send[pl.ds(base, 16), 0:cap, :] = left
-        send[pl.ds(base, 16), cap : 2 * cap, :] = right
-        send[pl.ds(base, 16), 2 * cap :, :] = placing
+        placing = mm(hot8, place[...]).reshape(16, 8, 128).astype(BF16)
+        built[pl.ds(base, 16), 0:cap, :] = left
+        built[pl.ds(base, 16), cap : 2 * cap, :] = right
+        built[pl.ds(base, 16), 2 * cap :, :] = placing
+        save(step).start()
         return carry
 
     lax.fori_loop(0, devices // 16, fill, 0)
+    for step in range(devices // 16):
+        save(step).wait()
 
 
 def positions(tile, cell):
@@ -201,7 +220,7 @@
         return carry
 
     lax.fori_loop(0, 8, unpack, 0)
-    tile = 256
+    tile = 512
 
     def total(step, carry):
         at = step * tile
@@ -250,19 +269,19 @@
         out[j * 8 : j * 8 + 8, :] = mixed.astype(BF16)
 
 
-def own_body(returned, slots, skip, out):
+def own_body(returned, slots, skip, part, out):
     def some(step, carry):
-        at = step * 256
+        at = step * 512
         hot = []
-        for part in range(2):
-            slot = as_column(slots[:, pl.ds(at + part * 128, 128)], 128)
+        for p in range(4):
+            slot = as_column(slots[:, pl.ds(at + p * 128, 128)], 128)
             one = [(slot == iota((128, 128), 1) + 128 * k).astype(BF16) for k in range(24)]
             hot.append(jnp.concatenate(one, axis=1))
         own = mm(jnp.concatenate(hot, axis=0), returned[...]).astype(BF16)
-        out[pl.ds(at, 256), :] = mm(own, skip[...])
-        return carry
-
-    lax.fori_loop(0, out.shape[0] // 256, some, 0)
+        out[pl.ds(at, 512), :] = mm(own, skip[...]) + part[pl.ds(at, 512), :]
+        return carry
+
+    lax.fori_loop(0, out.shape[0] // 512, some, 0)
 
 
 def waves_body(tile, cell, basis, where, out_p, out_qz, spots, wide_p, wide_q, wide_z):
@@ -312,32 +331,47 @@
     lax.fori_loop(0, out_p.shape[0] // 128, some, 0)
 
 
+def wave_of(wave_p, wave_qz, at, rows, h, o):
+    qz = wave_qz[pl.ds(at, rows), (h * 4 + o) * 128 : (h * 4 + o) * 128 + 128]
+    wave = [
+        qz * wave_p[pl.ds(at, rows), h * 512 + i * 128 : h * 512 + i * 128 + 128]
+        for i in range(4)
+    ]
+    return jnp.concatenate(wave, axis=1)
+
+
+def begin_body(near, far, wave_p, wave_qz, out):
+    def some(step, carry):
+        at = step * 512
+        total = mm(wave_of(wave_p, wave_qz, at, 512, 0, 0), near[...])
+        out[pl.ds(at, 512), :] = total + mm(wave_of(wave_p, wave_qz, at, 512, 1, 0), far[...])
+        return carry
+
+    lax.fori_loop(0, out.shape[0] // 512, some, 0)
+
+
 def decode_body(
-    m0, m1, m2, m3, m4, m5, m6, m7, wave_p, wave_qz, base, read, hidden_weight, output_weight, out
+    m1, m2, m3, m5, m6, m7, wave_p, wave_qz, base, read, hidden_weight, output_weight, out
 ):
-    modes = (m0, m1, m2, m3, m4, m5, m6, m7)
+    modes = ((m1, m2, m3), (m5, m6, m7))
 
     def some(step, carry):
-        at = step * 256
-        total = base[pl.ds(at, 256), :]
-        for q in range(8):
-            qz = wave_qz[pl.ds(at, 256), q * 128 : q * 128 + 128]
-            lane = q // 4 * 512
-            wave = [
-                qz * wave_p[pl.ds(at, 256), lane + i * 128 : lane + i * 128 + 128]
-                for i in range(4)
-            ]
-            total = total + mm(jnp.concatenate(wave, axis=1), modes[q][...])
+        at = step * 512
+        total = base[pl.ds(at, 512), :]
+        for h in range(2):
+            for o in range(3):
+                wave = wave_of(wave_p, wave_qz, at, 512, h, o + 1)
+                total = total + mm(wave, modes[h][o][...])
         value = jax.nn.gelu(total).astype(BF16).astype(F32)
         scale = jnp.concatenate(
-            [as_column(read[:, pl.ds(at + 128 * part, 128)], 128) for part in range(2)], axis=0
+            [as_column(read[:, pl.ds(at + 128 * part, 128)], 128) for part in range(4)], axis=0
         )
         gathered = (jnp.concatenate([scale, scale], axis=1) * value).astype(BF16)
         hidden = jax.nn.gelu(mm(gathered, hidden_weight[...])).astype(BF16)
-        out[pl.ds(at, 256), :] = mm(hidden, output_weight[...]).astype(BF16)
-        return carry
-
-    lax.fori_loop(0, out.shape[0] // 256, some, 0, unroll=2)
+        out[pl.ds(at, 512), :] = mm(hidden, output_weight[...]).astype(BF16)
+        return carry
+
+    lax.fori_loop(0, out.shape[0] // 512, some, 0)
 
 
 def basis_terms():
@@ -398,17 +432,27 @@
     basis = jnp.asarray(terms)
     basis_tall = jnp.asarray(np.ascontiguousarray(terms.T))
 
-    send, slots, message = call(
+    anywhere = pl.BlockSpec(memory_space=pl.ANY)
+    send, slots, message = pl.pallas_call(
         spread_body,
-        (
+        out_shape=(
             shape((devices, 56, 128), BF16),
             shape((1, points), jnp.int32),
             shape((points, width), BF16),
         ),
-        (features, tile, cell, spread_weight.reshape(1, points), message_weight),
-        (pltpu.VMEM((1, points), jnp.int32),),
-        limit=60,
-    )
+        in_specs=[anywhere, VMEM, VMEM, VMEM, VMEM],
+        out_specs=[anywhere, VMEM, VMEM],
+        scratch_shapes=[
+            pltpu.VMEM((1, points), jnp.int32),
+            pltpu.VMEM((points, width), BF16),
+            pltpu.VMEM((points, 128), BF16),
+            pltpu.VMEM((devices, 56, 128), BF16),
+            pltpu.SemaphoreType.DMA(()),
+            pltpu.SemaphoreType.DMA((devices // 16,)),
+        ],
+        name="spread",
+        compiler_params=pltpu.CompilerParams(vmem_limit_bytes=60 * 2**20),
+    )(features, tile, cell, spread_weight.reshape(1, points), message_weight)
     recv = lax.all_to_all(send, everyone, 0, 0, tiled=True)
     away = spectrum(message, tile, cell, basis, where, True)
     near = spectrum(message, tile, cell, basis, where, False)
@@ -441,7 +485,7 @@
             shape((devices, 24, width), BF16),
             shape(spectral_weight.shape, BF16),
         ),
-        in_specs=[VMEM, VMEM, pl.BlockSpec(memory_space=pl.ANY)],
+        in_specs=[VMEM, VMEM, anywhere],
         out_specs=[VMEM, VMEM],
         scratch_shapes=[pltpu.SemaphoreType.DMA(())],
         name="reply",
@@ -457,17 +501,25 @@
     modes = modes + tuple(swapped(m) for m in modes)
 
     returned = lax.all_to_all(back, everyone, 0, 0, tiled=True)
+    part = call(
+        begin_body,
+        shape((points, width), F32),
+        (modes[0], modes[4], wave_p, wave_qz),
+        (),
+        flops=2 * 1024 * 2048 * 256,
+    )
     base = call(
         own_body,
         shape((points, width), F32),
-        (returned.reshape(devices * 24, width), slots, skip_weight),
+        (returned.reshape(devices * 24, width), slots, skip_weight, part),
         (),
         flops=2 * 3072 * 2048 * 256,
     )
     return call(
         decode_body,
         shape((points, width), BF16),
-        modes
+        modes[1:4]
+        + modes[5:]
         + (wave_p, wave_qz, base, read_weight.reshape(1, points), hidden_weight, output_weight),
         (),
         limit=32,

time: 166 us -> 164 us (0.988)
  Pallas kernels: 59.4 us -> 56.9 us
  starting transfers between devices: 49.5 us -> 51.9 us
    pallas_call x13, Pallas kernels: 52.5 us -> 38.6 us  [call(): return fn(*ins)]
    pallas_call x0 -> x1, Pallas kernels: none -> 11.3 us  [per_device(): pl.pallas_call(spread_body, out_shape=(shape((devices, 56, 128), BF16), s...]
    ppermute x12, starting transfers between devices: 15.2 us -> 17.1 us  [around(): return lax.ppermute(shard, ('z', 'core', 'ba'), pairs)]
  transfers between devices with their start and end apart: 25 -> 25, of which waited for: 12 -> 13; matrix products, arithmetic and copies ran while one was open for 0% -> 0% of each run, Pallas kernels for 22% -> 23%
where the time goes in v6:
time: 164 us; the launch traced here: 163 us
  Pallas kernels  56.9 us (35%)
  starting transfers between devices  51.9 us (32%)
  waiting for transfers between devices  48 us (29%)
  local copies, waits for them, and re-layouts  6 us (4%)
    pallas_call x13, Pallas kernels, call(): return fn(*ins)  38.6 us
    ppermute x12, waiting for transfers between devices, around(): return lax.ppermute(shard, ('z', 'core', 'ba'), pairs)  22.1 us
    all_to_all x1, waiting for transfers between devices, per_device(): recv = lax.all_to_all(send, everyone, 0, 0, tiled=True)  21.7 us
    ppermute x12, starting transfers between devices, around(): return lax.ppermute(shard, ('z', 'core', 'ba'), pairs)  17.1 us
    all_to_all x1, starting transfers between devices, per_device(): recv = lax.all_to_all(send, everyone, 0, 0, tiled=True)  11.5 us
    pallas_call x1, Pallas kernels, per_device(): pl.pallas_call(spread_body, out_shape=(shape((devices, 56, 128), BF16), s...  11.3 us
    ppermute x5, starting transfers between devices, swapped(): return lax.ppermute(shard, 'core', [(0, 1), (1, 0)])  10.8 us
    ppermute x6, starting transfers between devices, around(): return lax.ppermute(shard, 'y', [(i, (i + s) % 4) for i in range(4)])  7.62 us
  transfers between devices with their start and end apart: 25, of which 13 were waited for; matrix products, arithmetic and copies ran while one was open for 0% of the time, Pallas kernels for 23%

profile of v6, /device:TPU:1, one launch (start us, length us, event | category | flops | bytes accessed | tf_op | source)
XLA Modules:
  0.0 163.2 jit_solution(5952294870970366009)
XLA Ops:
  0.0 11.3 %spread.1 = (bf16[128,56,128]{2,1,0:T(8,128)(2,1)}, s32[1,2048]{1,0:T(1,128)}, bf16[2048,256]{1,0:T(8,128)(2,1)}) custom-call(bf16[2048,256]{1,0:T(8,128)(2,1)} %feat.1, s32[1,2048]{1,0:T(1,128)} %bitcast.6, s32[1,2048]{1,0:T(1,128)} %bitcast.10, f32[1,2048]{1,0:T(1,128)} %bitcast.15, bf16[256,256]{1,0:T(8,128)(2,1)} %weight.2), custom_call_target="tpu_custom_call" | custom-call | tf_op jit(solution)/shard_map/spread/pallas_call | solution.py:436
  11.3 0.0 copy-start.6
  11.3 0.0 copy-start.7
  11.3 0.0 copy-start.9
  11.4 0.0 copy-start.17
  11.4 11.5 %all-to-all-start = ((bf16[128,56,128]{2,1,0:T(8,128)(2,1)}), bf16[128,56,128]{2,1,0:T(8,128)(2,1)S(1)}, u32[]{:S(2)}, u32[]{:S(2)}) async-start(bf16[128,56,128]{2,1,0:T(8,128)(2,1)} %get-tuple-element.39), calls=%async_computation | async-start | bytes 3670016 | tf_op jit(solution)/shard_map/all_to_all | solution.py:456
  22.9 5.2 %shard_map.119 = bf16[2048,256]{1,0:T(8,128)(2,1)} custom-call(bf16[2048,256]{1,0:T(8,128)(2,1)S(1)} %copy-done.9, s32[1,2048]{1,0:T(1,128)S(1)} %bitcast.7, s32[1,2048]{1,0:T(1,128)S(1)} %bitcast.11, bf16[16,128]{1,0:T(8,128)(2,1)S(1)} %copy-done.17, s32[1]{0:T(128)} %bitcast.3.where), custom_call_target="tpu_custom_call" | custom-call | flops 2147483648 | bytes 4000000 | tf_op jit(solution)/shard_map/pallas_call | solution.py:48
  28.1 1.1 collective-permute-start
  29.1 21.7 %all-to-all-done.recv = bf16[128,56,128]{2,1,0:T(8,128)(2,1)S(1)} async-done(((bf16[128,56,128]{2,1,0:T(8,128)(2,1)}), bf16[128,56,128]{2,1,0:T(8,128)(2,1)S(1)}, u32[]{:S(2)}, u32[]{:S(2)}) %all-to-all-start) | async-done | bytes 1835040 | tf_op jit(solution)/shard_map/all_to_all | solution.py:456
  50.8 5.2 %shard_map.123 = (bf16[2048,256]{1,0:T(8,128)(2,1)S(1)}, bf16[1024,128]{1,0:T(8,128)(2,1)S(1)}) custom-call(bf16[128,56,128]{2,1,0:T(8,128)(2,1)S(1)} %all-to-all-done.recv), custom_call_target="tpu_custom_call" | custom-call | flops 3221225472 | bytes 4000000 | tf_op jit(solution)/shard_map/pallas_call | solution.py:48
  56.0 7.0 %reply.1 = (bf16[128,24,256]{2,1,0:T(8,128)(2,1)}, bf16[4,8,256,256]{3,2,1,0:T(8,128)(2,1)S(1)}) custom-call(bf16[2048,256]{1,0:T(8,128)(2,1)S(1)} %get-tuple-element.40.latent, bf16[1024,128]{1,0:T(8,128)(2,1)S(1)} %get-tuple-element.41.places, bf16[4,8,256,256]{3,2,1,0:T(8,128)(2,1)S(1)} %copy-done.8), custom_call_target="tpu_custom_call" | custom-call | flops 3221225472 | bytes 4000000 | tf_op jit(solution)/shard_map/reply/pallas_call | solution.py:482
  63.0 2.0 %copy-done = bf16[4,8,256,256]{3,2,1,0:T(8,128)(2,1)} copy-done((bf16[4,8,256,256]{3,2,1,0:T(8,128)(2,1)}, bf16[4,8,256,256]{3,2,1,0:T(8,128)(2,1)S(1)}, u32[]{:S(2)}) %copy-start) | copy-done | bytes 4194328
  65.0 4.9 %all-to-all-start.1 = ((bf16[128,24,256]{2,1,0:T(8,128)(2,1)}), bf16[128,24,256]{2,1,0:T(8,128)(2,1)}, u32[]{:S(2)}, u32[]{:S(2)}) async-start(bf16[128,24,256]{2,1,0:T(8,128)(2,1)} %get-tuple-element.45), calls=%async_computation.1 | async-start | bytes 3145728 | tf_op jit(solution)/shard_map/all_to_all | solution.py:503
  69.9 4.2 %shard_map.118.refs_0_ = bf16[2048,256]{1,0:T(8,128)(2,1)S(1)} custom-call(bf16[2048,256]{1,0:T(8,128)(2,1)S(1)} %copy-done.10, s32[1,2048]{1,0:T(1,128)S(1)} %bitcast.8, s32[1,2048]{1,0:T(1,128)S(1)} %bitcast.12, bf16[16,128]{1,0:T(8,128)(2,1)S(1)} %copy-done.17, s32[1]{0:T(128)} %bitcast.3.where), custom_call_target="tpu_custom_call" | custom-call | flops 2147483648 | bytes 4000000 | tf_op jit(solution)/shard_map/pallas_call | solution.py:48
  74.1 0.0 collective-permute-done.refs_1_
  74.1 0.3 shard_map.120
  74.4 1.7 %collective-permute-start.1 = (bf16[512,256]{1,0:T(8,128)(2,1)S(1)}, bf16[512,256]{1,0:T(8,128)(2,1)S(1)}, u32[]{:S(2)}, u32[]{:S(2)}) collective-permute-start(bf16[512,256]{1,0:T(8,128)(2,1)S(1)} %get-tuple-element.28), channel_id=1, source_target_pairs={{0,1},{1,2},{2,3},{3,0},{4,36},{5,37},{6,38},{7,39},{32,33},{33,34... | collective-permute-start | bytes 786440 | tf_op jit(solution)/shard_map/ppermute | solution.py:398
  76.1 2.9 %collective-permute-start.2 = (bf16[512,256]{1,0:T(8,128)(2,1)S(1)}, bf16[512,256]{1,0:T(8,128)(2,1)S(1)}, u32[]{:S(2)}, u32[]{:S(2)}) collective-permute-start(bf16[512,256]{1,0:T(8,128)(2,1)S(1)} %get-tuple-element.29), channel_id=1, source_target_pairs={{0,2},{1,3},{2,0},{3,1},{4,68},{5,69},{6,70},{7,71},{32,34},{33,35... | collective-permute-start | bytes 786440 | tf_op jit(solution)/shard_map/ppermute | solution.py:398
  79.0 0.9 collective-permute-start.3
  79.9 13.8 %collective-permute-done.1.refs_1_ = bf16[512,256]{1,0:T(8,128)(2,1)S(1)} collective-permute-done((bf16[512,256]{1,0:T(8,128)(2,1)S(1)}, bf16[512,256]{1,0:T(8,128)(2,1)S(1)}, u32[]{:S(2)}, u32[]{:S(2)}) %collective-permute-start.1) | collective-permute-done | bytes 262176 | tf_op jit(solution)/shard_map/ppermute | solution.py:398
  93.7 3.0 %collective-permute-done.2.refs_2_ = bf16[512,256]{1,0:T(8,128)(2,1)S(1)} collective-permute-done((bf16[512,256]{1,0:T(8,128)(2,1)S(1)}, bf16[512,256]{1,0:T(8,128)(2,1)S(1)}, u32[]{:S(2)}, u32[]{:S(2)}) %collective-permute-start.2) | collective-permute-done | bytes 262176 | tf_op jit(solution)/shard_map/ppermute | solution.py:398
  96.8 0.1 shard_map.121
  96.9 1.0 collective-permute-start.4
  97.9 2.6 %collective-permute-start.5 = (bf16[128,256]{1,0:T(8,128)(2,1)S(1)}, bf16[128,256]{1,0:T(8,128)(2,1)S(1)}, u32[]{:S(2)}, u32[]{:S(2)}) collective-permute-start(bf16[128,256]{1,0:T(8,128)(2,1)S(1)} %get-tuple-element.33), channel_id=1, source_target_pairs={{0,64},{1,65},{2,66},{3,67},{4,6},{5,7},{6,4},{7,5},{32,96},{33,97... | collective-permute-start | bytes 196616 | tf_op jit(solution)/shard_map/ppermute | solution.py:398
  100.5 0.9 collective-permute-start.6
  101.5 0.0 collective-permute-done.4.refs_1_
  101.5 1.7 %collective-permute-done.5.refs_2_ = bf16[128,256]{1,0:T(8,128)(2,1)S(1)} collective-permute-done((bf16[128,256]{1,0:T(8,128)(2,1)S(1)}, bf16[128,256]{1,0:T(8,128)(2,1)S(1)}, u32[]{:S(2)}, u32[]{:S(2)}) %collective-permute-start.5) | collective-permute-done | bytes 65568 | tf_op jit(solution)/shard_map/ppermute | solution.py:398
  103.2 0.5 collective-permute-done.6.refs_3_
  103.7 0.6 collective-permute-start.7
  104.3 2.3 %collective-permute-start.8 = (bf16[32,256]{1,0:T(8,128)(2,1)S(1)}, bf16[32,256]{1,0:T(8,128)(2,1)S(1)}, u32[]{:S(2)}, u32[]{:S(2)}) collective-permute-start(bf16[32,256]{1,0:T(8,128)(2,1)S(1)} %get-tuple-element.37), channel_id=1, source_target_pairs={{0,16},{8,24},{16,0},{24,8},{1,17},{9,25},{17,1},{25,9},{2,18},{10... | collective-permute-start | bytes 49160 | tf_op jit(solution)/shard_map/ppermute | solution.py:390
  106.7 1.2 collective-permute-start.9
  107.8 0.0 collective-permute-done.7.b
  107.8 0.6 collective-permute-done.8.c
  108.4 1.1 collective-permute-done.9.d
  109.6 0.7 shard_map.124.refs_0_
  110.2 0.6 collective-permute-start.10
  110.8 2.9 %collective-permute-start.11 = (bf16[32,256]{1,0:T(8,128)(2,1)S(1)}, bf16[32,256]{1,0:T(8,128)(2,1)S(1)}, u32[]{:S(2)}, u32[]{:S(2)}) collective-permute-start(bf16[32,256]{1,0:T(8,128)(2,1)S(1)} %shard_map.124.refs_0_), channel_id=1, source_target_pairs={{0,16},{8,24},{16,0},{24,8},{1,17},{9,25},{17,1},{25,9},{2,18},{10... | collective-permute-start | bytes 49160 | tf_op jit(solution)/shard_map/ppermute | solution.py:390
  113.7 0.0 collective-permute-start.12
  113.7 0.5 collective-permute-done.10.refs_1_
  114.2 0.8 collective-permute-done.11.refs_2_
  115.0 1.3 collective-permute-done.12.refs_3_
  116.3 0.3 collective-permute-start.13
  116.6 3.3 %collective-permute-start.14 = (bf16[128,256]{1,0:T(8,128)(2,1)S(1)}, bf16[128,256]{1,0:T(8,128)(2,1)S(1)}, u32[]{:S(2)}, u32[]{:S(2)}) collective-permute-start(bf16[128,256]{1,0:T(8,128)(2,1)S(1)} %shard_map.125.refs_0_), channel_id=1, source_target_pairs={{0,64},{1,65},{2,66},{3,67},{4,6},{5,7},{6,4},{7,5},{32,96},{33,97... | collective-permute-start | bytes 196616 | tf_op jit(solution)/shard_map/ppermute | solution.py:398
  119.9 0.1 collective-permute-start.15
  119.9 0.7 collective-permute-done.13.refs_1_
  120.6 1.6 %collective-permute-done.14.refs_2_ = bf16[128,256]{1,0:T(8,128)(2,1)S(1)} collective-permute-done((bf16[128,256]{1,0:T(8,128)(2,1)S(1)}, bf16[128,256]{1,0:T(8,128)(2,1)S(1)}, u32[]{:S(2)}, u32[]{:S(2)}) %collective-permute-start.14) | collective-permute-done | bytes 65568 | tf_op jit(solution)/shard_map/ppermute | solution.py:398
  122.2 0.8 collective-permute-done.15.refs_3_
  123.0 0.1 collective-permute-start.16
  123.1 1.3 collective-permute-start.17
  124.4 2.0 %collective-permute-start.18 = (bf16[512,256]{1,0:T(8,128)(2,1)S(1)}, bf16[512,256]{1,0:T(8,128)(2,1)S(1)}, u32[]{:S(2)}, u32[]{:S(2)}) collective-permute-start(bf16[512,256]{1,0:T(8,128)(2,1)S(1)} %shard_map.126.near), channel_id=1, source_target_pairs={{0,3},{1,0},{2,1},{3,2},{4,100},{5,101},{6,102},{7,103},{32,35},{3... | collective-permute-start | bytes 786440 | tf_op jit(solution)/shard_map/ppermute | solution.py:398
  126.4 8.9 %collective-permute-start.22 = (bf16[512,256]{1,0:T(8,128)(2,1)S(1)}, bf16[512,256]{1,0:T(8,128)(2,1)S(1)}, u32[]{:S(2)}, u32[]{:S(2)}) collective-permute-start(bf16[512,256]{1,0:T(8,128)(2,1)S(1)} %shard_map.126.near), channel_id=1, source_target_pairs={{0,4},{4,0},{1,5},{5,1},{2,6},{6,2},{3,7},{7,3},{8,12},{12,8},{9,1... | collective-permute-start | bytes 786440 | tf_op jit(solution)/shard_map/ppermute | solution.py:409
  135.2 6.8 %shard_map.127 = (bf16[2048,1024]{1,0:T(8,128)(2,1)S(1)}, bf16[2048,1024]{1,0:T(8,128)(2,1)S(1)}) custom-call(s32[1,2048]{1,0:T(1,128)S(1)} %bitcast.9, s32[1,2048]{1,0:T(1,128)S(1)} %bitcast.13, bf16[128,16]{1,0:T(8,128)(2,1)S(1)} %copy-done.16, s32[1]{0:T(128)} %bitcast.3.where), custom_call_target="tpu_custom_call" | custom-call | flops 1000000000 | bytes 4000000 | tf_op jit(solution)/shard_map/pallas_call | solution.py:48
  142.0 0.0 collective-permute-done.16.m1
  142.0 0.1 collective-permute-start.19
  142.1 0.5 collective-permute-start.20
  142.6 0.2 collective-permute-start.21
  142.9 1.8 %shard_map.128.part = f32[2048,256]{1,0:T(8,128)S(1)} custom-call(bf16[512,256]{1,0:T(8,128)(2,1)S(1)} %shard_map.126.near, bf16[512,256]{1,0:T(8,128)(2,1)S(1)} %collective-permute-done.22.far, bf16[2048,1024]{1,0:T(8,128)(2,1)S(1)} %get-tuple-element.43.wave_p, bf16[2048,1024]{1,0:T(8,128)(2,1)S(1)} %get-tuple-element.44.wave_qz), custom_call_target="tpu_custom_call" | custom-call | flops 1073741824 | bytes 4000000 | tf_op jit(solution)/shard_map/pallas_call | solution.py:48
  144.7 2.0 %copy-done.2 = bf16[2048,1024]{1,0:T(8,128)(2,1)} copy-done((bf16[2048,1024]{1,0:T(8,128)(2,1)}, bf16[2048,1024]{1,0:T(8,128)(2,1)S(1)}, u32[]{:S(2)}) %copy-start.2) | copy-done | bytes 4194328
  146.6 2.0 %copy-done.4 = bf16[2048,1024]{1,0:T(8,128)(2,1)} copy-done((bf16[2048,1024]{1,0:T(8,128)(2,1)}, bf16[2048,1024]{1,0:T(8,128)(2,1)S(1)}, u32[]{:S(2)}) %copy-start.4) | copy-done | bytes 4194328
  148.7 0.0 copy-start.12
  148.7 0.0 copy-start.13
  148.7 0.0 copy-start.14
  148.7 6.4 %shard_map.129.base = f32[2048,256]{1,0:T(8,128)S(1)} custom-call(bf16[3072,256]{1,0:T(8,128)(2,1)} %bitcast.4.returned, s32[1,2048]{1,0:T(1,128)S(1)} %copy-done.15, bf16[256,256]{1,0:T(8,128)(2,1)S(1)} %copy-done.11, f32[2048,256]{1,0:T(8,128)S(1)} %shard_map.128.part), custom_call_target="tpu_custom_call" | custom-call | flops 3221225472 | bytes 4000000 | tf_op jit(solution)/shard_map/pallas_call | solution.py:48
  155.2 8.0 %shard_map.130 = bf16[2048,256]{1,0:T(8,128)(2,1)} custom-call(bf16[512,256]{1,0:T(8,128)(2,1)S(1)} %collective-permute-done.16.m1, bf16[512,256]{1,0:T(8,128)(2,1)S(1)} %collective-permute-done.17.m2, bf16[512,256]{1,0:T(8,128)(2,1)S(1)} %collective-permute-done.18.m3, bf16[512,256]{1,0:T(8,128)(2,1)S(1)} %collective-permute-done.19.m5, ...), custom_call_target="tpu_custom_call" | custom-call | flops 4294967296 | bytes 4000000 | tf_op jit(solution)/shard_map/pallas_call | solution.py:48
  (37 shorter events, 0.1 us)
Async XLA Ops:
  11.3 11.6 %copy-start.6 = (s32[2048,1]{0,1:T(1,128)S(1)}, s32[2048,1]{0,1:T(1,128)}, u32[]{:S(2)}) copy-start(s32[2048,1]{0,1:T(1,128)} %param.13) | copy-start | bytes 24580
  11.3 11.6 %copy-start.7 = (s32[2048]{0:T(1024)S(1)}, s32[2048]{0:T(1024)}, u32[]{:S(2)}) copy-start(s32[2048]{0:T(1024)} %param.14) | copy-start | bytes 24580
  11.3 11.6 %copy-start.9 = (bf16[2048,256]{1,0:T(8,128)(2,1)S(1)}, bf16[2048,256]{1,0:T(8,128)(2,1)}, u32[]{:S(2)}) copy-start(bf16[2048,256]{1,0:T(8,128)(2,1)} %get-tuple-element.26.message) | copy-start | bytes 3145732
  11.4 11.6 %copy-start.17 = (bf16[16,128]{1,0:T(8,128)(2,1)S(1)}, bf16[16,128]{1,0:T(8,128)(2,1)}, u32[]{:S(2)}) copy-start(bf16[16,128]{1,0:T(8,128)(2,1)} %constant.26.clone.basis) | copy-start | bytes 12292
  11.4 39.5 %all-to-all-start = ((bf16[128,56,128]{2,1,0:T(8,128)(2,1)}), bf16[128,56,128]{2,1,0:T(8,128)(2,1)S(1)}, u32[]{:S(2)}, u32[]{:S(2)}) async-start(bf16[128,56,128]{2,1,0:T(8,128)(2,1)} %get-tuple-element.39), calls=%async_computation | async-start | bytes 3670016 | tf_op jit(solution)/shard_map/all_to_all | solution.py:456
  28.1 46.0 %collective-permute-start = (bf16[2048,256]{1,0:T(8,128)(2,1)}, bf16[2048,256]{1,0:T(8,128)(2,1)S(1)}, u32[]{:S(2)}, u32[]{:S(2)}) collective-permute-start(bf16[2048,256]{1,0:T(8,128)(2,1)} %shard_map.119), channel_id=1, source_target_pairs={{0,4},{4,0},{1,5},{5,1},{2,6},{6,2},{3,7},{7,3},{8,12},{12,8},{9,1... | collective-permute-start | bytes 3145736 | tf_op jit(solution)/shard_map/ppermute | solution.py:409
  50.8 5.2 %copy-start.8 = (bf16[4,8,256,256]{3,2,1,0:T(8,128)(2,1)S(1)}, bf16[4,8,256,256]{3,2,1,0:T(8,128)(2,1)}, u32[]{:S(2)}) copy-start(bf16[4,8,256,256]{3,2,1,0:T(8,128)(2,1)} %weight.3) | copy-start | bytes 12582916
  63.0 2.0 %copy-start = (bf16[4,8,256,256]{3,2,1,0:T(8,128)(2,1)}, bf16[4,8,256,256]{3,2,1,0:T(8,128)(2,1)S(1)}, u32[]{:S(2)}) copy-start(bf16[4,8,256,256]{3,2,1,0:T(8,128)(2,1)S(1)} %get-tuple-element.42.weight) | copy-start | bytes 12582916
  65.0 4.9 %copy-start.10 = (bf16[2048,256]{1,0:T(8,128)(2,1)S(1)}, bf16[2048,256]{1,0:T(8,128)(2,1)}, u32[]{:S(2)}) copy-start(bf16[2048,256]{1,0:T(8,128)(2,1)} %get-tuple-element.26.message) | copy-start | bytes 3145732
  65.0 83.6 %all-to-all-start.1 = ((bf16[128,24,256]{2,1,0:T(8,128)(2,1)}), bf16[128,24,256]{2,1,0:T(8,128)(2,1)}, u32[]{:S(2)}, u32[]{:S(2)}) async-start(bf16[128,24,256]{2,1,0:T(8,128)(2,1)} %get-tuple-element.45), calls=%async_computation.1 | async-start | bytes 3145728 | tf_op jit(solution)/shard_map/all_to_all | solution.py:503
  69.9 39.6 %copy-start.1 = (bf16[4,8,256,256]{3,2,1,0:T(8,128)(2,1)S(1)}, bf16[4,8,256,256]{3,2,1,0:T(8,128)(2,1)}, u32[]{:S(2)}) copy-start(bf16[4,8,256,256]{3,2,1,0:T(8,128)(2,1)} %copy-done) | copy-start | bytes 12582916
  74.4 19.4 %collective-permute-start.1 = (bf16[512,256]{1,0:T(8,128)(2,1)S(1)}, bf16[512,256]{1,0:T(8,128)(2,1)S(1)}, u32[]{:S(2)}, u32[]{:S(2)}) collective-permute-start(bf16[512,256]{1,0:T(8,128)(2,1)S(1)} %get-tuple-element.28), channel_id=1, source_target_pairs={{0,1},{1,2},{2,3},{3,0},{4,36},{5,37},{6,38},{7,39},{32,33},{33,34... | collective-permute-start | bytes 786440 | tf_op jit(solution)/shard_map/ppermute | solution.py:398
  76.1 20.7 %collective-permute-start.2 = (bf16[512,256]{1,0:T(8,128)(2,1)S(1)}, bf16[512,256]{1,0:T(8,128)(2,1)S(1)}, u32[]{:S(2)}, u32[]{:S(2)}) collective-permute-start(bf16[512,256]{1,0:T(8,128)(2,1)S(1)} %get-tuple-element.29), channel_id=1, source_target_pairs={{0,2},{1,3},{2,0},{3,1},{4,68},{5,69},{6,70},{7,71},{32,34},{33,35... | collective-permute-start | bytes 786440 | tf_op jit(solution)/shard_map/ppermute | solution.py:398
  79.0 17.8 %collective-permute-start.3 = (bf16[512,256]{1,0:T(8,128)(2,1)S(1)}, bf16[512,256]{1,0:T(8,128)(2,1)S(1)}, u32[]{:S(2)}, u32[]{:S(2)}) collective-permute-start(bf16[512,256]{1,0:T(8,128)(2,1)S(1)} %get-tuple-element.30), channel_id=1, source_target_pairs={{0,3},{1,0},{2,1},{3,2},{4,100},{5,101},{6,102},{7,103},{32,35},{3... | collective-permute-start | bytes 786440 | tf_op jit(solution)/shard_map/ppermute | solution.py:398
  96.9 4.6 %collective-permute-start.4 = (bf16[128,256]{1,0:T(8,128)(2,1)S(1)}, bf16[128,256]{1,0:T(8,128)(2,1)S(1)}, u32[]{:S(2)}, u32[]{:S(2)}) collective-permute-start(bf16[128,256]{1,0:T(8,128)(2,1)S(1)} %get-tuple-element.32), channel_id=1, source_target_pairs={{0,32},{1,33},{2,34},{3,35},{4,5},{5,6},{6,7},{7,4},{32,64},{33,65... | collective-permute-start | bytes 196616 | tf_op jit(solution)/shard_map/ppermute | solution.py:398
  97.9 5.2 %collective-permute-start.5 = (bf16[128,256]{1,0:T(8,128)(2,1)S(1)}, bf16[128,256]{1,0:T(8,128)(2,1)S(1)}, u32[]{:S(2)}, u32[]{:S(2)}) collective-permute-start(bf16[128,256]{1,0:T(8,128)(2,1)S(1)} %get-tuple-element.33), channel_id=1, source_target_pairs={{0,64},{1,65},{2,66},{3,67},{4,6},{5,7},{6,4},{7,5},{32,96},{33,97... | collective-permute-start | bytes 196616 | tf_op jit(solution)/shard_map/ppermute | solution.py:398
  100.5 3.1 %collective-permute-start.6 = (bf16[128,256]{1,0:T(8,128)(2,1)S(1)}, bf16[128,256]{1,0:T(8,128)(2,1)S(1)}, u32[]{:S(2)}, u32[]{:S(2)}) collective-permute-start(bf16[128,256]{1,0:T(8,128)(2,1)S(1)} %get-tuple-element.34), channel_id=1, source_target_pairs={{0,96},{1,97},{2,98},{3,99},{4,7},{5,4},{6,5},{7,6},{32,0},{33,1},... | collective-permute-start | bytes 196616 | tf_op jit(solution)/shard_map/ppermute | solution.py:398
  103.7 4.2 %collective-permute-start.7 = (bf16[32,256]{1,0:T(8,128)(2,1)S(1)}, bf16[32,256]{1,0:T(8,128)(2,1)S(1)}, u32[]{:S(2)}, u32[]{:S(2)}) collective-permute-start(bf16[32,256]{1,0:T(8,128)(2,1)S(1)} %get-tuple-element.36), channel_id=1, source_target_pairs={{0,8},{8,16},{16,24},{24,0},{1,9},{9,17},{17,25},{25,1},{2,10},{10... | collective-permute-start | bytes 49160 | tf_op jit(solution)/shard_map/ppermute | solution.py:390
  104.3 4.1 %collective-permute-start.8 = (bf16[32,256]{1,0:T(8,128)(2,1)S(1)}, bf16[32,256]{1,0:T(8,128)(2,1)S(1)}, u32[]{:S(2)}, u32[]{:S(2)}) collective-permute-start(bf16[32,256]{1,0:T(8,128)(2,1)S(1)} %get-tuple-element.37), channel_id=1, source_target_pairs={{0,16},{8,24},{16,0},{24,8},{1,17},{9,25},{17,1},{25,9},{2,18},{10... | collective-permute-start | bytes 49160 | tf_op jit(solution)/shard_map/ppermute | solution.py:390
  106.7 2.9 %collective-permute-start.9 = (bf16[32,256]{1,0:T(8,128)(2,1)S(1)}, bf16[32,256]{1,0:T(8,128)(2,1)S(1)}, u32[]{:S(2)}, u32[]{:S(2)}) collective-permute-start(bf16[32,256]{1,0:T(8,128)(2,1)S(1)} %get-tuple-element.38), channel_id=1, source_target_pairs={{0,24},{8,0},{16,8},{24,16},{1,25},{9,1},{17,9},{25,17},{2,26},{10... | collective-permute-start | bytes 49160 | tf_op jit(solution)/shard_map/ppermute | solution.py:390
  109.6 25.7 %copy-start.16 = (bf16[128,16]{1,0:T(8,128)(2,1)S(1)}, bf16[128,16]{1,0:T(8,128)(2,1)}, u32[]{:S(2)}) copy-start(bf16[128,16]{1,0:T(8,128)(2,1)} %constant.27.clone.basis) | copy-start | bytes 12292
  110.2 4.0 %collective-permute-start.10 = (bf16[32,256]{1,0:T(8,128)(2,1)S(1)}, bf16[32,256]{1,0:T(8,128)(2,1)S(1)}, u32[]{:S(2)}, u32[]{:S(2)}) collective-permute-start(bf16[32,256]{1,0:T(8,128)(2,1)S(1)} %shard_map.124.refs_0_), channel_id=1, source_target_pairs={{0,8},{8,16},{16,24},{24,0},{1,9},{9,17},{17,25},{25,1},{2,10},{10... | collective-permute-start | bytes 49160 | tf_op jit(solution)/shard_map/ppermute | solution.py:390
  110.8 4.2 %collective-permute-start.11 = (bf16[32,256]{1,0:T(8,128)(2,1)S(1)}, bf16[32,256]{1,0:T(8,128)(2,1)S(1)}, u32[]{:S(2)}, u32[]{:S(2)}) collective-permute-start(bf16[32,256]{1,0:T(8,128)(2,1)S(1)} %shard_map.124.refs_0_), channel_id=1, source_target_pairs={{0,16},{8,24},{16,0},{24,8},{1,17},{9,25},{17,1},{25,9},{2,18},{10... | collective-permute-start | bytes 49160 | tf_op jit(solution)/shard_map/ppermute | solution.py:390
  113.7 2.6 %collective-permute-start.12 = (bf16[32,256]{1,0:T(8,128)(2,1)S(1)}, bf16[32,256]{1,0:T(8,128)(2,1)S(1)}, u32[]{:S(2)}, u32[]{:S(2)}) collective-permute-start(bf16[32,256]{1,0:T(8,128)(2,1)S(1)} %shard_map.124.refs_0_), channel_id=1, source_target_pairs={{0,24},{8,0},{16,8},{24,16},{1,25},{9,1},{17,9},{25,17},{2,26},{10... | collective-permute-start | bytes 49160 | tf_op jit(solution)/shard_map/ppermute | solution.py:390
  116.3 4.3 %collective-permute-start.13 = (bf16[128,256]{1,0:T(8,128)(2,1)S(1)}, bf16[128,256]{1,0:T(8,128)(2,1)S(1)}, u32[]{:S(2)}, u32[]{:S(2)}) collective-permute-start(bf16[128,256]{1,0:T(8,128)(2,1)S(1)} %shard_map.125.refs_0_), channel_id=1, source_target_pairs={{0,32},{1,33},{2,34},{3,35},{4,5},{5,6},{6,7},{7,4},{32,64},{33,65... | collective-permute-start | bytes 196616 | tf_op jit(solution)/shard_map/ppermute | solution.py:398
  116.6 5.6 %collective-permute-start.14 = (bf16[128,256]{1,0:T(8,128)(2,1)S(1)}, bf16[128,256]{1,0:T(8,128)(2,1)S(1)}, u32[]{:S(2)}, u32[]{:S(2)}) collective-permute-start(bf16[128,256]{1,0:T(8,128)(2,1)S(1)} %shard_map.125.refs_0_), channel_id=1, source_target_pairs={{0,64},{1,65},{2,66},{3,67},{4,6},{5,7},{6,4},{7,5},{32,96},{33,97... | collective-permute-start | bytes 196616 | tf_op jit(solution)/shard_map/ppermute | solution.py:398
  119.9 3.1 %collective-permute-start.15 = (bf16[128,256]{1,0:T(8,128)(2,1)S(1)}, bf16[128,256]{1,0:T(8,128)(2,1)S(1)}, u32[]{:S(2)}, u32[]{:S(2)}) collective-permute-start(bf16[128,256]{1,0:T(8,128)(2,1)S(1)} %shard_map.125.refs_0_), channel_id=1, source_target_pairs={{0,96},{1,97},{2,98},{3,99},{4,7},{5,4},{6,5},{7,6},{32,0},{33,1},... | collective-permute-start | bytes 196616 | tf_op jit(solution)/shard_map/ppermute | solution.py:398
  123.0 19.0 %collective-permute-start.16 = (bf16[512,256]{1,0:T(8,128)(2,1)S(1)}, bf16[512,256]{1,0:T(8,128)(2,1)S(1)}, u32[]{:S(2)}, u32[]{:S(2)}) collective-permute-start(bf16[512,256]{1,0:T(8,128)(2,1)S(1)} %shard_map.126.near), channel_id=1, source_target_pairs={{0,1},{1,2},{2,3},{3,0},{4,36},{5,37},{6,38},{7,39},{32,33},{33,34... | collective-permute-start | bytes 786440 | tf_op jit(solution)/shard_map/ppermute | solution.py:398
  123.1 19.0 %collective-permute-start.17 = (bf16[512,256]{1,0:T(8,128)(2,1)S(1)}, bf16[512,256]{1,0:T(8,128)(2,1)S(1)}, u32[]{:S(2)}, u32[]{:S(2)}) collective-permute-start(bf16[512,256]{1,0:T(8,128)(2,1)S(1)} %shard_map.126.near), channel_id=1, source_target_pairs={{0,2},{1,3},{2,0},{3,1},{4,68},{5,69},{6,70},{7,71},{32,34},{33,35... | collective-permute-start | bytes 786440 | tf_op jit(solution)/shard_map/ppermute | solution.py:398
  124.4 18.2 %collective-permute-start.18 = (bf16[512,256]{1,0:T(8,128)(2,1)S(1)}, bf16[512,256]{1,0:T(8,128)(2,1)S(1)}, u32[]{:S(2)}, u32[]{:S(2)}) collective-permute-start(bf16[512,256]{1,0:T(8,128)(2,1)S(1)} %shard_map.126.near), channel_id=1, source_target_pairs={{0,3},{1,0},{2,1},{3,2},{4,100},{5,101},{6,102},{7,103},{32,35},{3... | collective-permute-start | bytes 786440 | tf_op jit(solution)/shard_map/ppermute | solution.py:398
  126.4 16.5 %collective-permute-start.22 = (bf16[512,256]{1,0:T(8,128)(2,1)S(1)}, bf16[512,256]{1,0:T(8,128)(2,1)S(1)}, u32[]{:S(2)}, u32[]{:S(2)}) collective-permute-start(bf16[512,256]{1,0:T(8,128)(2,1)S(1)} %shard_map.126.near), channel_id=1, source_target_pairs={{0,4},{4,0},{1,5},{5,1},{2,6},{6,2},{3,7},{7,3},{8,12},{12,8},{9,1... | collective-permute-start | bytes 786440 | tf_op jit(solution)/shard_map/ppermute | solution.py:409
  142.0 13.1 %collective-permute-start.19 = (bf16[512,256]{1,0:T(8,128)(2,1)S(1)}, bf16[512,256]{1,0:T(8,128)(2,1)S(1)}, u32[]{:S(2)}, u32[]{:S(2)}) collective-permute-start(bf16[512,256]{1,0:T(8,128)(2,1)S(1)} %collective-permute-done.16.m1), channel_id=1, source_target_pairs={{0,4},{4,0},{1,5},{5,1},{2,6},{6,2},{3,7},{7,3},{8,12},{12,8},{9,1... | collective-permute-start | bytes 786440 | tf_op jit(solution)/shard_map/ppermute | solution.py:409
  142.1 13.0 %collective-permute-start.20 = (bf16[512,256]{1,0:T(8,128)(2,1)S(1)}, bf16[512,256]{1,0:T(8,128)(2,1)S(1)}, u32[]{:S(2)}, u32[]{:S(2)}) collective-permute-start(bf16[512,256]{1,0:T(8,128)(2,1)S(1)} %collective-permute-done.17.m2), channel_id=1, source_target_pairs={{0,4},{4,0},{1,5},{5,1},{2,6},{6,2},{3,7},{7,3},{8,12},{12,8},{9,1... | collective-permute-start | bytes 786440 | tf_op jit(solution)/shard_map/ppermute | solution.py:409
  142.6 12.5 %collective-permute-start.21 = (bf16[512,256]{1,0:T(8,128)(2,1)S(1)}, bf16[512,256]{1,0:T(8,128)(2,1)}, u32[]{:S(2)}, u32[]{:S(2)}) collective-permute-start(bf16[512,256]{1,0:T(8,128)(2,1)S(1)} %collective-permute-done.18.m3), channel_id=1, source_target_pairs={{0,4},{4,0},{1,5},{5,1},{2,6},{6,2},{3,7},{7,3},{8,12},{12,8},{9,1... | collective-permute-start | bytes 786440 | tf_op jit(solution)/shard_map/ppermute | solution.py:409
  142.9 5.8 %copy-start.11 = (bf16[256,256]{1,0:T(8,128)(2,1)S(1)}, bf16[256,256]{1,0:T(8,128)(2,1)}, u32[]{:S(2)}) copy-start(bf16[256,256]{1,0:T(8,128)(2,1)} %skip.1) | copy-start | bytes 393220
  142.9 5.8 %copy-start.15 = (s32[1,2048]{1,0:T(1,128)S(1)}, s32[1,2048]{1,0:T(1,128)}, u32[]{:S(2)}) copy-start(s32[1,2048]{1,0:T(1,128)} %get-tuple-element.46.slots) | copy-start | bytes 24580
  144.7 2.0 %copy-start.2 = (bf16[2048,1024]{1,0:T(8,128)(2,1)}, bf16[2048,1024]{1,0:T(8,128)(2,1)S(1)}, u32[]{:S(2)}) copy-start(bf16[2048,1024]{1,0:T(8,128)(2,1)S(1)} %get-tuple-element.43.wave_p) | copy-start | bytes 12582916
  146.6 2.0 %copy-start.4 = (bf16[2048,1024]{1,0:T(8,128)(2,1)}, bf16[2048,1024]{1,0:T(8,128)(2,1)S(1)}, u32[]{:S(2)}) copy-start(bf16[2048,1024]{1,0:T(8,128)(2,1)S(1)} %get-tuple-element.44.wave_qz) | copy-start | bytes 12582916
  148.6 6.5 %copy-start.3 = (bf16[2048,1024]{1,0:T(8,128)(2,1)S(1)}, bf16[2048,1024]{1,0:T(8,128)(2,1)}, u32[]{:S(2)}) copy-start(bf16[2048,1024]{1,0:T(8,128)(2,1)} %copy-done.2) | copy-start | bytes 12582916
  148.7 6.5 %copy-start.5 = (bf16[2048,1024]{1,0:T(8,128)(2,1)S(1)}, bf16[2048,1024]{1,0:T(8,128)(2,1)}, u32[]{:S(2)}) copy-start(bf16[2048,1024]{1,0:T(8,128)(2,1)} %copy-done.4) | copy-start | bytes 12582916
  148.7 6.5 %copy-start.12 = (bf16[256,256]{1,0:T(8,128)(2,1)S(1)}, bf16[256,256]{1,0:T(8,128)(2,1)}, u32[]{:S(2)}) copy-start(bf16[256,256]{1,0:T(8,128)(2,1)} %hidden_weight.1) | copy-start | bytes 393220
  148.7 6.5 %copy-start.13 = (bf16[256,256]{1,0:T(8,128)(2,1)S(1)}, bf16[256,256]{1,0:T(8,128)(2,1)}, u32[]{:S(2)}) copy-start(bf16[256,256]{1,0:T(8,128)(2,1)} %output_weight.1) | copy-start | bytes 393220
  148.7 6.5 %copy-start.14 = (f32[2048]{0:T(1024)S(1)}, f32[2048]{0:T(1024)}, u32[]{:S(2)}) copy-start(f32[2048]{0:T(1024)} %param.16) | copy-start | bytes 24580

commit v7 on v6

--- a/solution.py
+++ b/solution.py
@@ -49,13 +49,11 @@
 
 
 def spread_body(
-    feat, tile, cell, spread, weight, send, slots, message, rank_row, local, place, built, loads, saves
+    feat, tile, cell, spread, weight, send, slots, sent, rank_row, message, place, built, saves
 ):
     devices = built.shape[0]
-    points = local.shape[0]
+    points = message.shape[0]
     cap = 24
-    load = pltpu.make_async_copy(feat, local, loads)
-    load.start()
     upper = (iota((256, 256), 0) < iota((256, 256), 1)).astype(BF16)
     ones = jnp.ones((256, 128), BF16)
     used = jnp.zeros((devices, 256), F32)
@@ -69,12 +67,11 @@
         rank = jnp.sum(hot * before, axis=0, keepdims=True).astype(jnp.int32)
         rank_row[:, at : at + 256] = rank
         slots[:, at : at + 256] = tile[:, at : at + 256] * cap + rank
-    load.wait()
     lane = iota((128, 128), 1)
 
     def weigh(step, carry):
         at = step * 128
-        product = mm(local[pl.ds(at, 128), :], weight[...])
+        product = mm(feat[pl.ds(at, 128), :], weight[...])
         scale = as_column(spread[:, pl.ds(at, 128)], 128)
         scale = jnp.concatenate([scale, scale], axis=1)
         message[pl.ds(at, 128), :] = (scale * product).astype(BF16)
@@ -88,6 +85,8 @@
         return carry
 
     lax.fori_loop(0, points // 128, weigh, 0, unroll=2)
+    save_message = pltpu.make_async_copy(message, sent, saves.at[devices // 16])
+    save_message.start()
     rank = rank_row[...]
     low = tile[...] * 8 + lax.bitwise_and(rank, 7)
     slot = slots[...]
@@ -111,6 +110,7 @@
         return carry
 
     lax.fori_loop(0, devices // 16, fill, 0)
+    save_message.wait()
     for step in range(devices // 16):
         save(step).wait()
 
@@ -234,9 +234,7 @@
     lax.fori_loop(0, latent.shape[0] // tile, total, 0)
 
 
-def reply_body(latent, places, weight, out, held, done):
-    copy = pltpu.make_async_copy(weight, held, done)
-    copy.start()
+def reply_body(latent, places, weight, out, built, saves):
     lane = iota((128, 128), 0)
     column = iota((128, 128), 1)
 
@@ -251,11 +249,17 @@
         got = mm(jnp.concatenate(tall, axis=0), latent[...])
         for g in range(3):
             piece = got[g * 128 : g * 128 + 128].reshape(16, 8, 256).astype(BF16)
-            out[pl.ds(step * 16, 16), g * 8 : g * 8 + 8, :] = piece
-        return carry
+            built[pl.ds(step * 16, 16), g * 8 : g * 8 + 8, :] = piece
+        save(step).start()
+        return carry
+
+    def save(step):
+        rows = pl.ds(step * 16, 16)
+        return pltpu.make_async_copy(built.at[rows], out.at[rows], saves.at[step])
 
     lax.fori_loop(0, 8, back, 0)
-    copy.wait()
+    for step in range(8):
+        save(step).wait()
 
 
 def mix_body(a, b, c, d, weight, out):
@@ -269,7 +273,7 @@
         out[j * 8 : j * 8 + 8, :] = mixed.astype(BF16)
 
 
-def own_body(returned, slots, skip, part, out):
+def own_body(returned, slots, skip, out):
     def some(step, carry):
         at = step * 512
         hot = []
@@ -278,7 +282,7 @@
             one = [(slot == iota((128, 128), 1) + 128 * k).astype(BF16) for k in range(24)]
             hot.append(jnp.concatenate(one, axis=1))
         own = mm(jnp.concatenate(hot, axis=0), returned[...]).astype(BF16)
-        out[pl.ds(at, 512), :] = mm(own, skip[...]) + part[pl.ds(at, 512), :]
+        out[pl.ds(at, 512), :] = mm(own, skip[...])
         return carry
 
     lax.fori_loop(0, out.shape[0] // 512, some, 0)
@@ -340,10 +344,11 @@
     return jnp.concatenate(wave, axis=1)
 
 
-def begin_body(near, far, wave_p, wave_qz, out):
+def begin_body(near, far, wave_p, wave_qz, base, out):
     def some(step, carry):
         at = step * 512
-        total = mm(wave_of(wave_p, wave_qz, at, 512, 0, 0), near[...])
+        total = base[pl.ds(at, 512), :]
+        total = total + mm(wave_of(wave_p, wave_qz, at, 512, 0, 0), near[...])
         out[pl.ds(at, 512), :] = total + mm(wave_of(wave_p, wave_qz, at, 512, 1, 0), far[...])
         return carry
 
@@ -440,15 +445,14 @@
             shape((1, points), jnp.int32),
             shape((points, width), BF16),
         ),
-        in_specs=[anywhere, VMEM, VMEM, VMEM, VMEM],
-        out_specs=[anywhere, VMEM, VMEM],
+        in_specs=[VMEM] * 5,
+        out_specs=[anywhere, VMEM, anywhere],
         scratch_shapes=[
             pltpu.VMEM((1, points), jnp.int32),
             pltpu.VMEM((points, width), BF16),
             pltpu.VMEM((points, 128), BF16),
             pltpu.VMEM((devices, 56, 128), BF16),
-            pltpu.SemaphoreType.DMA(()),
-            pltpu.SemaphoreType.DMA((devices // 16,)),
+            pltpu.SemaphoreType.DMA((devices // 16 + 1,)),
         ],
         name="spread",
         compiler_params=pltpu.CompilerParams(vmem_limit_bytes=60 * 2**20),
@@ -479,41 +483,43 @@
         (pltpu.VMEM((3072, width), BF16), pltpu.VMEM((8, 8, 128), jnp.int32)),
         flops=2 * 3072 * 2048 * 256,
     )
-    back, weight = pl.pallas_call(
+    back = pl.pallas_call(
         reply_body,
-        out_shape=(
-            shape((devices, 24, width), BF16),
-            shape(spectral_weight.shape, BF16),
-        ),
+        out_shape=shape((devices, 24, width), BF16),
         in_specs=[VMEM, VMEM, anywhere],
-        out_specs=[VMEM, VMEM],
-        scratch_shapes=[pltpu.SemaphoreType.DMA(())],
+        out_specs=anywhere,
+        scratch_shapes=[
+            pltpu.VMEM((devices, 24, width), BF16),
+            pltpu.SemaphoreType.DMA((8,)),
+        ],
         name="reply",
         compiler_params=pltpu.CompilerParams(vmem_limit_bytes=20 * 2**20),
         cost_estimate=pl.CostEstimate(
             flops=2 * 3072 * 2048 * 256, transcendentals=0, bytes_accessed=4000000
         ),
     )(latent, places, spectral_weight)
-    mixed = call(mix_body, shape((32, width), BF16), from_others(parts, "y") + (weight,), ())
+    mixed = call(
+        mix_body, shape((32, width), BF16), from_others(parts, "y") + (spectral_weight,), ()
+    )
     line = joined(from_others((mixed,) * 4, "y"))
     plane = joined(from_others((line,) * 4, "near"))
     modes = from_others((plane,) * 4, "wide")
     modes = modes + tuple(swapped(m) for m in modes)
 
     returned = lax.all_to_all(back, everyone, 0, 0, tiled=True)
-    part = call(
-        begin_body,
-        shape((points, width), F32),
-        (modes[0], modes[4], wave_p, wave_qz),
-        (),
-        flops=2 * 1024 * 2048 * 256,
-    )
     base = call(
         own_body,
         shape((points, width), F32),
-        (returned.reshape(devices * 24, width), slots, skip_weight, part),
+        (returned.reshape(devices * 24, width), slots, skip_weight),
         (),
         flops=2 * 3072 * 2048 * 256,
+    )
+    base = call(
+        begin_body,
+        shape((points, width), F32),
+        (modes[0], modes[4], wave_p, wave_qz, base),
+        (),
+        flops=2 * 1024 * 2048 * 256,
     )
     return call(
         decode_body,

time: 164 us -> 158 us (0.963)
  Pallas kernels: 56.9 us -> 54 us
    unnamed x36 -> x34, local copies, waits for them, and re-layouts: 6 us -> 5.26 us
  transfers between devices with their start and end apart: 25 -> 25, of which waited for: 13 -> 13; matrix products, arithmetic and copies ran while one was open for 0% -> 0% of each run, Pallas kernels for 23% -> 22%
where the time goes in v7:
time: 158 us
  Pallas kernels  54 us (34%)
  starting transfers between devices  50.8 us (32%)
  waiting for transfers between devices  47.2 us (30%)
  local copies, waits for them, and re-layouts  5.26 us (3%)
    pallas_call x13, Pallas kernels, call(): return fn(*ins)  37.2 us
    all_to_all x1, waiting for transfers between devices, per_device(): recv = lax.all_to_all(send, everyone, 0, 0, tiled=True)  21.7 us
    ppermute x12, waiting for transfers between devices, around(): return lax.ppermute(shard, ('z', 'core', 'ba'), pairs)  21.2 us
    ppermute x12, starting transfers between devices, around(): return lax.ppermute(shard, ('z', 'core', 'ba'), pairs)  17.3 us
    all_to_all x1, starting transfers between devices, per_device(): recv = lax.all_to_all(send, everyone, 0, 0, tiled=True)  11.5 us
    ppermute x5, starting transfers between devices, swapped(): return lax.ppermute(shard, 'core', [(0, 1), (1, 0)])  10.6 us
    pallas_call x1, Pallas kernels, per_device(): pl.pallas_call(spread_body, out_shape=(shape((devices, 56, 128), BF16), s...  10.5 us
    ppermute x6, starting transfers between devices, around(): return lax.ppermute(shard, 'y', [(i, (i + s) % 4) for i in range(4)])  7.63 us
  transfers between devices with their start and end apart: 25, of which 13 were waited for; matrix products, arithmetic and copies ran while one was open for 0% of the time, Pallas kernels for 22%

profile of v7, /device:TPU:1, one launch (start us, length us, event | category | flops | bytes accessed | tf_op | source)
XLA Modules:
  0.0 157.6 jit_solution(5596786845971661069)
XLA Ops:
  0.0 10.5 %spread.1 = (bf16[128,56,128]{2,1,0:T(8,128)(2,1)}, s32[1,2048]{1,0:T(1,128)}, bf16[2048,256]{1,0:T(8,128)(2,1)}) custom-call(bf16[2048,256]{1,0:T(8,128)(2,1)} %feat.1, s32[1,2048]{1,0:T(1,128)} %bitcast.7, s32[1,2048]{1,0:T(1,128)} %bitcast.11, f32[1,2048]{1,0:T(1,128)} %bitcast.16, bf16[256,256]{1,0:T(8,128)(2,1)} %weight.3), custom_call_target="tpu_custom_call" | custom-call | tf_op jit(solution)/shard_map/spread/pallas_call | solution.py:441
  10.5 0.0 copy-start.6
  10.5 0.0 copy-start.7
  10.6 0.0 copy-start.8
  10.6 0.0 copy-start.16
  10.6 11.5 %all-to-all-start = ((bf16[128,56,128]{2,1,0:T(8,128)(2,1)}), bf16[128,56,128]{2,1,0:T(8,128)(2,1)S(1)}, u32[]{:S(2)}, u32[]{:S(2)}) async-start(bf16[128,56,128]{2,1,0:T(8,128)(2,1)} %get-tuple-element.39), calls=%async_computation | async-start | bytes 3670016 | tf_op jit(solution)/shard_map/all_to_all | solution.py:460
  22.1 5.1 %shard_map.119 = bf16[2048,256]{1,0:T(8,128)(2,1)} custom-call(bf16[2048,256]{1,0:T(8,128)(2,1)S(1)} %copy-done.8, s32[1,2048]{1,0:T(1,128)S(1)} %bitcast.8, s32[1,2048]{1,0:T(1,128)S(1)} %bitcast.12, bf16[16,128]{1,0:T(8,128)(2,1)S(1)} %copy-done.16, s32[1]{0:T(128)} %bitcast.3.where), custom_call_target="tpu_custom_call" | custom-call | flops 2147483648 | bytes 4000000 | tf_op jit(solution)/shard_map/pallas_call | solution.py:48
  27.3 1.1 collective-permute-start
  28.3 21.7 %all-to-all-done.recv = bf16[128,56,128]{2,1,0:T(8,128)(2,1)S(1)} async-done(((bf16[128,56,128]{2,1,0:T(8,128)(2,1)}), bf16[128,56,128]{2,1,0:T(8,128)(2,1)S(1)}, u32[]{:S(2)}, u32[]{:S(2)}) %all-to-all-start) | async-done | bytes 1835040 | tf_op jit(solution)/shard_map/all_to_all | solution.py:460
  50.0 5.2 %shard_map.127 = (bf16[2048,256]{1,0:T(8,128)(2,1)S(1)}, bf16[1024,128]{1,0:T(8,128)(2,1)S(1)}) custom-call(bf16[128,56,128]{2,1,0:T(8,128)(2,1)S(1)} %all-to-all-done.recv), custom_call_target="tpu_custom_call" | custom-call | flops 3221225472 | bytes 4000000 | tf_op jit(solution)/shard_map/pallas_call | solution.py:48
  55.3 6.3 %reply.1 = bf16[128,24,256]{2,1,0:T(8,128)(2,1)} custom-call(bf16[2048,256]{1,0:T(8,128)(2,1)S(1)} %get-tuple-element.40.latent, bf16[1024,128]{1,0:T(8,128)(2,1)S(1)} %get-tuple-element.41.places, bf16[4,8,256,256]{3,2,1,0:T(8,128)(2,1)S(1)} %copy-done.4), custom_call_target="tpu_custom_call" | custom-call | flops 3221225472 | bytes 4000000 | tf_op jit(solution)/shard_map/reply/pallas_call | solution.py:486
  61.6 3.8 %all-to-all-start.1 = ((bf16[128,24,256]{2,1,0:T(8,128)(2,1)}), bf16[128,24,256]{2,1,0:T(8,128)(2,1)S(1)}, u32[]{:S(2)}, u32[]{:S(2)}) async-start(bf16[128,24,256]{2,1,0:T(8,128)(2,1)} %reply.1), calls=%async_computation.1 | async-start | bytes 3145728 | tf_op jit(solution)/shard_map/all_to_all | solution.py:509
  65.4 0.0 copy-start.9
  65.4 1.2 copy-done.9
  66.6 4.1 %shard_map.118.refs_0_ = bf16[2048,256]{1,0:T(8,128)(2,1)S(1)} custom-call(bf16[2048,256]{1,0:T(8,128)(2,1)S(1)} %copy-done.9, s32[1,2048]{1,0:T(1,128)S(1)} %bitcast.9, s32[1,2048]{1,0:T(1,128)S(1)} %bitcast.13, bf16[16,128]{1,0:T(8,128)(2,1)S(1)} %copy-done.16, s32[1]{0:T(128)} %bitcast.3.where), custom_call_target="tpu_custom_call" | custom-call | flops 2147483648 | bytes 4000000 | tf_op jit(solution)/shard_map/pallas_call | solution.py:48
  70.8 0.2 shard_map.120
  71.0 1.7 %collective-permute-start.1 = (bf16[512,256]{1,0:T(8,128)(2,1)S(1)}, bf16[512,256]{1,0:T(8,128)(2,1)S(1)}, u32[]{:S(2)}, u32[]{:S(2)}) collective-permute-start(bf16[512,256]{1,0:T(8,128)(2,1)S(1)} %get-tuple-element.26), channel_id=1, source_target_pairs={{0,1},{1,2},{2,3},{3,0},{4,36},{5,37},{6,38},{7,39},{32,33},{33,34... | collective-permute-start | bytes 786440 | tf_op jit(solution)/shard_map/ppermute | solution.py:403
  72.7 2.9 %collective-permute-start.2 = (bf16[512,256]{1,0:T(8,128)(2,1)S(1)}, bf16[512,256]{1,0:T(8,128)(2,1)S(1)}, u32[]{:S(2)}, u32[]{:S(2)}) collective-permute-start(bf16[512,256]{1,0:T(8,128)(2,1)S(1)} %get-tuple-element.27), channel_id=1, source_target_pairs={{0,2},{1,3},{2,0},{3,1},{4,68},{5,69},{6,70},{7,71},{32,34},{33,35... | collective-permute-start | bytes 786440 | tf_op jit(solution)/shard_map/ppermute | solution.py:403
  75.6 0.9 collective-permute-start.3
  76.6 13.1 %collective-permute-done.1.refs_1_ = bf16[512,256]{1,0:T(8,128)(2,1)S(1)} collective-permute-done((bf16[512,256]{1,0:T(8,128)(2,1)S(1)}, bf16[512,256]{1,0:T(8,128)(2,1)S(1)}, u32[]{:S(2)}, u32[]{:S(2)}) %collective-permute-start.1) | collective-permute-done | bytes 262176 | tf_op jit(solution)/shard_map/ppermute | solution.py:403
  89.6 2.9 %collective-permute-done.2.refs_2_ = bf16[512,256]{1,0:T(8,128)(2,1)S(1)} collective-permute-done((bf16[512,256]{1,0:T(8,128)(2,1)S(1)}, bf16[512,256]{1,0:T(8,128)(2,1)S(1)}, u32[]{:S(2)}, u32[]{:S(2)}) %collective-permute-start.2) | collective-permute-done | bytes 262176 | tf_op jit(solution)/shard_map/ppermute | solution.py:403
  92.5 0.0 collective-permute-done.3.refs_3_
  92.6 0.1 shard_map.121
  92.7 1.2 collective-permute-start.4
  93.9 2.4 %collective-permute-start.5 = (bf16[128,256]{1,0:T(8,128)(2,1)S(1)}, bf16[128,256]{1,0:T(8,128)(2,1)S(1)}, u32[]{:S(2)}, u32[]{:S(2)}) collective-permute-start(bf16[128,256]{1,0:T(8,128)(2,1)S(1)} %get-tuple-element.31), channel_id=1, source_target_pairs={{0,64},{1,65},{2,66},{3,67},{4,6},{5,7},{6,4},{7,5},{32,96},{33,97... | collective-permute-start | bytes 196616 | tf_op jit(solution)/shard_map/ppermute | solution.py:403
  96.4 0.9 collective-permute-start.6
  97.3 0.0 collective-permute-done.4.refs_1_
  97.3 1.7 %collective-permute-done.5.refs_2_ = bf16[128,256]{1,0:T(8,128)(2,1)S(1)} collective-permute-done((bf16[128,256]{1,0:T(8,128)(2,1)S(1)}, bf16[128,256]{1,0:T(8,128)(2,1)S(1)}, u32[]{:S(2)}, u32[]{:S(2)}) %collective-permute-start.5) | collective-permute-done | bytes 65568 | tf_op jit(solution)/shard_map/ppermute | solution.py:403
  99.0 0.5 collective-permute-done.6.refs_3_
  99.5 0.7 collective-permute-start.7
  100.2 2.3 %collective-permute-start.8 = (bf16[32,256]{1,0:T(8,128)(2,1)S(1)}, bf16[32,256]{1,0:T(8,128)(2,1)S(1)}, u32[]{:S(2)}, u32[]{:S(2)}) collective-permute-start(bf16[32,256]{1,0:T(8,128)(2,1)S(1)} %get-tuple-element.35), channel_id=1, source_target_pairs={{0,16},{8,24},{16,0},{24,8},{1,17},{9,25},{17,1},{25,9},{2,18},{10... | collective-permute-start | bytes 49160 | tf_op jit(solution)/shard_map/ppermute | solution.py:395
  102.5 1.2 collective-permute-start.9
  103.7 0.6 collective-permute-done.8.c
  104.3 1.1 collective-permute-done.9.d
  105.4 0.7 shard_map.123.refs_0_
  106.1 0.6 collective-permute-start.10
  106.7 2.9 %collective-permute-start.11 = (bf16[32,256]{1,0:T(8,128)(2,1)S(1)}, bf16[32,256]{1,0:T(8,128)(2,1)S(1)}, u32[]{:S(2)}, u32[]{:S(2)}) collective-permute-start(bf16[32,256]{1,0:T(8,128)(2,1)S(1)} %shard_map.123.refs_0_), channel_id=1, source_target_pairs={{0,16},{8,24},{16,0},{24,8},{1,17},{9,25},{17,1},{25,9},{2,18},{10... | collective-permute-start | bytes 49160 | tf_op jit(solution)/shard_map/ppermute | solution.py:395
  109.5 0.0 collective-permute-start.12
  109.5 0.5 collective-permute-done.10.refs_1_
  110.1 0.8 collective-permute-done.11.refs_2_
  110.8 1.3 collective-permute-done.12.refs_3_
  112.1 0.4 collective-permute-start.13
  112.6 3.2 %collective-permute-start.14 = (bf16[128,256]{1,0:T(8,128)(2,1)S(1)}, bf16[128,256]{1,0:T(8,128)(2,1)S(1)}, u32[]{:S(2)}, u32[]{:S(2)}) collective-permute-start(bf16[128,256]{1,0:T(8,128)(2,1)S(1)} %shard_map.124.refs_0_), channel_id=1, source_target_pairs={{0,64},{1,65},{2,66},{3,67},{4,6},{5,7},{6,4},{7,5},{32,96},{33,97... | collective-permute-start | bytes 196616 | tf_op jit(solution)/shard_map/ppermute | solution.py:403
  115.8 0.1 collective-permute-start.15
  115.9 0.7 collective-permute-done.13.refs_1_
  116.5 1.6 %collective-permute-done.14.refs_2_ = bf16[128,256]{1,0:T(8,128)(2,1)S(1)} collective-permute-done((bf16[128,256]{1,0:T(8,128)(2,1)S(1)}, bf16[128,256]{1,0:T(8,128)(2,1)S(1)}, u32[]{:S(2)}, u32[]{:S(2)}) %collective-permute-start.14) | collective-permute-done | bytes 65568 | tf_op jit(solution)/shard_map/ppermute | solution.py:403
  118.1 0.8 collective-permute-done.15.refs_3_
  118.9 0.1 collective-permute-start.16
  119.0 1.3 collective-permute-start.17
  120.3 2.0 %collective-permute-start.18 = (bf16[512,256]{1,0:T(8,128)(2,1)S(1)}, bf16[512,256]{1,0:T(8,128)(2,1)S(1)}, u32[]{:S(2)}, u32[]{:S(2)}) collective-permute-start(bf16[512,256]{1,0:T(8,128)(2,1)S(1)} %shard_map.125.near), channel_id=1, source_target_pairs={{0,3},{1,0},{2,1},{3,2},{4,100},{5,101},{6,102},{7,103},{32,35},{3... | collective-permute-start | bytes 786440 | tf_op jit(solution)/shard_map/ppermute | solution.py:403
  122.3 6.8 %shard_map.126 = (bf16[2048,1024]{1,0:T(8,128)(2,1)S(1)}, bf16[2048,1024]{1,0:T(8,128)(2,1)S(1)}) custom-call(s32[1,2048]{1,0:T(1,128)S(1)} %bitcast.10, s32[1,2048]{1,0:T(1,128)S(1)} %bitcast.14, bf16[128,16]{1,0:T(8,128)(2,1)S(1)} %copy-done.15, s32[1]{0:T(128)} %bitcast.3.where), custom_call_target="tpu_custom_call" | custom-call | flops 1000000000 | bytes 4000000 | tf_op jit(solution)/shard_map/pallas_call | solution.py:48
  129.1 1.9 %copy-done = bf16[2048,1024]{1,0:T(8,128)(2,1)} copy-done((bf16[2048,1024]{1,0:T(8,128)(2,1)}, bf16[2048,1024]{1,0:T(8,128)(2,1)S(1)}, u32[]{:S(2)}) %copy-start) | copy-done | bytes 4194328
  131.1 2.0 %copy-done.2 = bf16[2048,1024]{1,0:T(8,128)(2,1)} copy-done((bf16[2048,1024]{1,0:T(8,128)(2,1)}, bf16[2048,1024]{1,0:T(8,128)(2,1)S(1)}, u32[]{:S(2)}) %copy-start.2) | copy-done | bytes 4194328
  133.1 8.9 %collective-permute-start.22 = (bf16[512,256]{1,0:T(8,128)(2,1)S(1)}, bf16[512,256]{1,0:T(8,128)(2,1)S(1)}, u32[]{:S(2)}, u32[]{:S(2)}) collective-permute-start(bf16[512,256]{1,0:T(8,128)(2,1)S(1)} %shard_map.125.near), channel_id=1, source_target_pairs={{0,4},{4,0},{1,5},{5,1},{2,6},{6,2},{3,7},{7,3},{8,12},{12,8},{9,1... | collective-permute-start | bytes 786440 | tf_op jit(solution)/shard_map/ppermute | solution.py:414
  142.0 0.0 collective-permute-start.19
  142.0 0.0 collective-permute-done.17.m2
  142.0 0.5 collective-permute-start.20
  142.5 0.1 collective-permute-start.21
  142.6 4.8 %shard_map.128.base = f32[2048,256]{1,0:T(8,128)S(1)} custom-call(bf16[3072,256]{1,0:T(8,128)(2,1)S(1)} %bitcast.6, s32[1,2048]{1,0:T(1,128)S(1)} %copy-done.14, bf16[256,256]{1,0:T(8,128)(2,1)S(1)} %copy-done.10), custom_call_target="tpu_custom_call" | custom-call | flops 3221225472 | bytes 4000000 | tf_op jit(solution)/shard_map/pallas_call | solution.py:48
  147.5 0.0 copy-start.11
  147.5 0.0 copy-start.12
  147.5 0.0 copy-start.13
  147.5 1.8 %shard_map.129.base = f32[2048,256]{1,0:T(8,128)S(1)} custom-call(bf16[512,256]{1,0:T(8,128)(2,1)S(1)} %shard_map.125.near, bf16[512,256]{1,0:T(8,128)(2,1)S(1)} %collective-permute-done.22.far, bf16[2048,1024]{1,0:T(8,128)(2,1)S(1)} %copy-done.1, bf16[2048,1024]{1,0:T(8,128)(2,1)S(1)} %copy-done.3, f32[2048,256]{1,0:T(8,128)S(1)} %shard_map.128.base), custom_call_target="tpu_custom_call" | custom-call | flops 1073741824 | bytes 4000000 | tf_op jit(solution)/shard_map/pallas_call | solution.py:48
  149.4 8.2 %shard_map.130 = bf16[2048,256]{1,0:T(8,128)(2,1)} custom-call(bf16[512,256]{1,0:T(8,128)(2,1)S(1)} %collective-permute-done.16.m1, bf16[512,256]{1,0:T(8,128)(2,1)S(1)} %collective-permute-done.17.m2, bf16[512,256]{1,0:T(8,128)(2,1)S(1)} %collective-permute-done.18.m3, bf16[512,256]{1,0:T(8,128)(2,1)S(1)} %collective-permute-done.19.m5, ...), custom_call_target="tpu_custom_call" | custom-call | flops 4294967296 | bytes 4000000 | tf_op jit(solution)/shard_map/pallas_call | solution.py:48
  (35 shorter events, 0.1 us)
Async XLA Ops:
  10.5 11.6 %copy-start.6 = (s32[2048,1]{0,1:T(1,128)S(1)}, s32[2048,1]{0,1:T(1,128)}, u32[]{:S(2)}) copy-start(s32[2048,1]{0,1:T(1,128)} %param.13) | copy-start | bytes 24580
  10.5 11.6 %copy-start.7 = (s32[2048]{0:T(1024)S(1)}, s32[2048]{0:T(1024)}, u32[]{:S(2)}) copy-start(s32[2048]{0:T(1024)} %param.14) | copy-start | bytes 24580
  10.6 11.5 %copy-start.8 = (bf16[2048,256]{1,0:T(8,128)(2,1)S(1)}, bf16[2048,256]{1,0:T(8,128)(2,1)}, u32[]{:S(2)}) copy-start(bf16[2048,256]{1,0:T(8,128)(2,1)} %get-tuple-element.24.message) | copy-start | bytes 3145732
  10.6 11.5 %copy-start.16 = (bf16[16,128]{1,0:T(8,128)(2,1)S(1)}, bf16[16,128]{1,0:T(8,128)(2,1)}, u32[]{:S(2)}) copy-start(bf16[16,128]{1,0:T(8,128)(2,1)} %constant.26.clone.basis) | copy-start | bytes 12292
  10.6 39.4 %all-to-all-start = ((bf16[128,56,128]{2,1,0:T(8,128)(2,1)}), bf16[128,56,128]{2,1,0:T(8,128)(2,1)S(1)}, u32[]{:S(2)}, u32[]{:S(2)}) async-start(bf16[128,56,128]{2,1,0:T(8,128)(2,1)} %get-tuple-element.39), calls=%async_computation | async-start | bytes 3670016 | tf_op jit(solution)/shard_map/all_to_all | solution.py:460
  27.3 43.5 %collective-permute-start = (bf16[2048,256]{1,0:T(8,128)(2,1)}, bf16[2048,256]{1,0:T(8,128)(2,1)S(1)}, u32[]{:S(2)}, u32[]{:S(2)}) collective-permute-start(bf16[2048,256]{1,0:T(8,128)(2,1)} %shard_map.119), channel_id=1, source_target_pairs={{0,4},{4,0},{1,5},{5,1},{2,6},{6,2},{3,7},{7,3},{8,12},{12,8},{9,1... | collective-permute-start | bytes 3145736 | tf_op jit(solution)/shard_map/ppermute | solution.py:414
  50.0 5.2 %copy-start.4 = (bf16[4,8,256,256]{3,2,1,0:T(8,128)(2,1)S(1)}, bf16[4,8,256,256]{3,2,1,0:T(8,128)(2,1)}, u32[]{:S(2)}) copy-start(bf16[4,8,256,256]{3,2,1,0:T(8,128)(2,1)} %weight.5) | copy-start | bytes 12582916
  61.6 81.0 %all-to-all-start.1 = ((bf16[128,24,256]{2,1,0:T(8,128)(2,1)}), bf16[128,24,256]{2,1,0:T(8,128)(2,1)S(1)}, u32[]{:S(2)}, u32[]{:S(2)}) async-start(bf16[128,24,256]{2,1,0:T(8,128)(2,1)} %reply.1), calls=%async_computation.1 | async-start | bytes 3145728 | tf_op jit(solution)/shard_map/all_to_all | solution.py:509
  65.4 1.2 copy-start.9
  66.6 38.8 %copy-start.5 = (bf16[4,8,256,256]{3,2,1,0:T(8,128)(2,1)S(1)}, bf16[4,8,256,256]{3,2,1,0:T(8,128)(2,1)}, u32[]{:S(2)}) copy-start(bf16[4,8,256,256]{3,2,1,0:T(8,128)(2,1)} %weight.5) | copy-start | bytes 12582916
  71.0 18.6 %collective-permute-start.1 = (bf16[512,256]{1,0:T(8,128)(2,1)S(1)}, bf16[512,256]{1,0:T(8,128)(2,1)S(1)}, u32[]{:S(2)}, u32[]{:S(2)}) collective-permute-start(bf16[512,256]{1,0:T(8,128)(2,1)S(1)} %get-tuple-element.26), channel_id=1, source_target_pairs={{0,1},{1,2},{2,3},{3,0},{4,36},{5,37},{6,38},{7,39},{32,33},{33,34... | collective-permute-start | bytes 786440 | tf_op jit(solution)/shard_map/ppermute | solution.py:403
  72.7 19.8 %collective-permute-start.2 = (bf16[512,256]{1,0:T(8,128)(2,1)S(1)}, bf16[512,256]{1,0:T(8,128)(2,1)S(1)}, u32[]{:S(2)}, u32[]{:S(2)}) collective-permute-start(bf16[512,256]{1,0:T(8,128)(2,1)S(1)} %get-tuple-element.27), channel_id=1, source_target_pairs={{0,2},{1,3},{2,0},{3,1},{4,68},{5,69},{6,70},{7,71},{32,34},{33,35... | collective-permute-start | bytes 786440 | tf_op jit(solution)/shard_map/ppermute | solution.py:403
  75.6 16.9 %collective-permute-start.3 = (bf16[512,256]{1,0:T(8,128)(2,1)S(1)}, bf16[512,256]{1,0:T(8,128)(2,1)S(1)}, u32[]{:S(2)}, u32[]{:S(2)}) collective-permute-start(bf16[512,256]{1,0:T(8,128)(2,1)S(1)} %get-tuple-element.28), channel_id=1, source_target_pairs={{0,3},{1,0},{2,1},{3,2},{4,100},{5,101},{6,102},{7,103},{32,35},{3... | collective-permute-start | bytes 786440 | tf_op jit(solution)/shard_map/ppermute | solution.py:403
  92.7 4.6 %collective-permute-start.4 = (bf16[128,256]{1,0:T(8,128)(2,1)S(1)}, bf16[128,256]{1,0:T(8,128)(2,1)S(1)}, u32[]{:S(2)}, u32[]{:S(2)}) collective-permute-start(bf16[128,256]{1,0:T(8,128)(2,1)S(1)} %get-tuple-element.30), channel_id=1, source_target_pairs={{0,32},{1,33},{2,34},{3,35},{4,5},{5,6},{6,7},{7,4},{32,64},{33,65... | collective-permute-start | bytes 196616 | tf_op jit(solution)/shard_map/ppermute | solution.py:403
  93.9 5.1 %collective-permute-start.5 = (bf16[128,256]{1,0:T(8,128)(2,1)S(1)}, bf16[128,256]{1,0:T(8,128)(2,1)S(1)}, u32[]{:S(2)}, u32[]{:S(2)}) collective-permute-start(bf16[128,256]{1,0:T(8,128)(2,1)S(1)} %get-tuple-element.31), channel_id=1, source_target_pairs={{0,64},{1,65},{2,66},{3,67},{4,6},{5,7},{6,4},{7,5},{32,96},{33,97... | collective-permute-start | bytes 196616 | tf_op jit(solution)/shard_map/ppermute | solution.py:403
  96.4 3.1 %collective-permute-start.6 = (bf16[128,256]{1,0:T(8,128)(2,1)S(1)}, bf16[128,256]{1,0:T(8,128)(2,1)S(1)}, u32[]{:S(2)}, u32[]{:S(2)}) collective-permute-start(bf16[128,256]{1,0:T(8,128)(2,1)S(1)} %get-tuple-element.32), channel_id=1, source_target_pairs={{0,96},{1,97},{2,98},{3,99},{4,7},{5,4},{6,5},{7,6},{32,0},{33,1},... | collective-permute-start | bytes 196616 | tf_op jit(solution)/shard_map/ppermute | solution.py:403
  99.5 4.2 %collective-permute-start.7 = (bf16[32,256]{1,0:T(8,128)(2,1)S(1)}, bf16[32,256]{1,0:T(8,128)(2,1)S(1)}, u32[]{:S(2)}, u32[]{:S(2)}) collective-permute-start(bf16[32,256]{1,0:T(8,128)(2,1)S(1)} %get-tuple-element.34), channel_id=1, source_target_pairs={{0,8},{8,16},{16,24},{24,0},{1,9},{9,17},{17,25},{25,1},{2,10},{10... | collective-permute-start | bytes 49160 | tf_op jit(solution)/shard_map/ppermute | solution.py:395
  100.2 4.1 %collective-permute-start.8 = (bf16[32,256]{1,0:T(8,128)(2,1)S(1)}, bf16[32,256]{1,0:T(8,128)(2,1)S(1)}, u32[]{:S(2)}, u32[]{:S(2)}) collective-permute-start(bf16[32,256]{1,0:T(8,128)(2,1)S(1)} %get-tuple-element.35), channel_id=1, source_target_pairs={{0,16},{8,24},{16,0},{24,8},{1,17},{9,25},{17,1},{25,9},{2,18},{10... | collective-permute-start | bytes 49160 | tf_op jit(solution)/shard_map/ppermute | solution.py:395
  102.5 2.9 %collective-permute-start.9 = (bf16[32,256]{1,0:T(8,128)(2,1)S(1)}, bf16[32,256]{1,0:T(8,128)(2,1)S(1)}, u32[]{:S(2)}, u32[]{:S(2)}) collective-permute-start(bf16[32,256]{1,0:T(8,128)(2,1)S(1)} %get-tuple-element.36), channel_id=1, source_target_pairs={{0,24},{8,0},{16,8},{24,16},{1,25},{9,1},{17,9},{25,17},{2,26},{10... | collective-permute-start | bytes 49160 | tf_op jit(solution)/shard_map/ppermute | solution.py:395
  105.4 16.9 %copy-start.15 = (bf16[128,16]{1,0:T(8,128)(2,1)S(1)}, bf16[128,16]{1,0:T(8,128)(2,1)}, u32[]{:S(2)}) copy-start(bf16[128,16]{1,0:T(8,128)(2,1)} %constant.27.clone.basis) | copy-start | bytes 12292
  106.1 4.0 %collective-permute-start.10 = (bf16[32,256]{1,0:T(8,128)(2,1)S(1)}, bf16[32,256]{1,0:T(8,128)(2,1)S(1)}, u32[]{:S(2)}, u32[]{:S(2)}) collective-permute-start(bf16[32,256]{1,0:T(8,128)(2,1)S(1)} %shard_map.123.refs_0_), channel_id=1, source_target_pairs={{0,8},{8,16},{16,24},{24,0},{1,9},{9,17},{17,25},{25,1},{2,10},{10... | collective-permute-start | bytes 49160 | tf_op jit(solution)/shard_map/ppermute | solution.py:395
  106.7 4.2 %collective-permute-start.11 = (bf16[32,256]{1,0:T(8,128)(2,1)S(1)}, bf16[32,256]{1,0:T(8,128)(2,1)S(1)}, u32[]{:S(2)}, u32[]{:S(2)}) collective-permute-start(bf16[32,256]{1,0:T(8,128)(2,1)S(1)} %shard_map.123.refs_0_), channel_id=1, source_target_pairs={{0,16},{8,24},{16,0},{24,8},{1,17},{9,25},{17,1},{25,9},{2,18},{10... | collective-permute-start | bytes 49160 | tf_op jit(solution)/shard_map/ppermute | solution.py:395
  109.5 2.6 %collective-permute-start.12 = (bf16[32,256]{1,0:T(8,128)(2,1)S(1)}, bf16[32,256]{1,0:T(8,128)(2,1)S(1)}, u32[]{:S(2)}, u32[]{:S(2)}) collective-permute-start(bf16[32,256]{1,0:T(8,128)(2,1)S(1)} %shard_map.123.refs_0_), channel_id=1, source_target_pairs={{0,24},{8,0},{16,8},{24,16},{1,25},{9,1},{17,9},{25,17},{2,26},{10... | collective-permute-start | bytes 49160 | tf_op jit(solution)/shard_map/ppermute | solution.py:395
  112.1 30.5 %copy-start.10 = (bf16[256,256]{1,0:T(8,128)(2,1)S(1)}, bf16[256,256]{1,0:T(8,128)(2,1)}, u32[]{:S(2)}) copy-start(bf16[256,256]{1,0:T(8,128)(2,1)} %skip.1) | copy-start | bytes 393220
  112.1 30.5 %copy-start.14 = (s32[1,2048]{1,0:T(1,128)S(1)}, s32[1,2048]{1,0:T(1,128)}, u32[]{:S(2)}) copy-start(s32[1,2048]{1,0:T(1,128)} %get-tuple-element.42.slots) | copy-start | bytes 24580
  112.1 4.4 %collective-permute-start.13 = (bf16[128,256]{1,0:T(8,128)(2,1)S(1)}, bf16[128,256]{1,0:T(8,128)(2,1)S(1)}, u32[]{:S(2)}, u32[]{:S(2)}) collective-permute-start(bf16[128,256]{1,0:T(8,128)(2,1)S(1)} %shard_map.124.refs_0_), channel_id=1, source_target_pairs={{0,32},{1,33},{2,34},{3,35},{4,5},{5,6},{6,7},{7,4},{32,64},{33,65... | collective-permute-start | bytes 196616 | tf_op jit(solution)/shard_map/ppermute | solution.py:403
  112.6 5.5 %collective-permute-start.14 = (bf16[128,256]{1,0:T(8,128)(2,1)S(1)}, bf16[128,256]{1,0:T(8,128)(2,1)S(1)}, u32[]{:S(2)}, u32[]{:S(2)}) collective-permute-start(bf16[128,256]{1,0:T(8,128)(2,1)S(1)} %shard_map.124.refs_0_), channel_id=1, source_target_pairs={{0,64},{1,65},{2,66},{3,67},{4,6},{5,7},{6,4},{7,5},{32,96},{33,97... | collective-permute-start | bytes 196616 | tf_op jit(solution)/shard_map/ppermute | solution.py:403
  115.8 3.1 %collective-permute-start.15 = (bf16[128,256]{1,0:T(8,128)(2,1)S(1)}, bf16[128,256]{1,0:T(8,128)(2,1)S(1)}, u32[]{:S(2)}, u32[]{:S(2)}) collective-permute-start(bf16[128,256]{1,0:T(8,128)(2,1)S(1)} %shard_map.124.refs_0_), channel_id=1, source_target_pairs={{0,96},{1,97},{2,98},{3,99},{4,7},{5,4},{6,5},{7,6},{32,0},{33,1},... | collective-permute-start | bytes 196616 | tf_op jit(solution)/shard_map/ppermute | solution.py:403
  118.9 23.1 %collective-permute-start.16 = (bf16[512,256]{1,0:T(8,128)(2,1)S(1)}, bf16[512,256]{1,0:T(8,128)(2,1)S(1)}, u32[]{:S(2)}, u32[]{:S(2)}) collective-permute-start(bf16[512,256]{1,0:T(8,128)(2,1)S(1)} %shard_map.125.near), channel_id=1, source_target_pairs={{0,1},{1,2},{2,3},{3,0},{4,36},{5,37},{6,38},{7,39},{32,33},{33,34... | collective-permute-start | bytes 786440 | tf_op jit(solution)/shard_map/ppermute | solution.py:403
  119.0 23.0 %collective-permute-start.17 = (bf16[512,256]{1,0:T(8,128)(2,1)S(1)}, bf16[512,256]{1,0:T(8,128)(2,1)S(1)}, u32[]{:S(2)}, u32[]{:S(2)}) collective-permute-start(bf16[512,256]{1,0:T(8,128)(2,1)S(1)} %shard_map.125.near), channel_id=1, source_target_pairs={{0,2},{1,3},{2,0},{3,1},{4,68},{5,69},{6,70},{7,71},{32,34},{33,35... | collective-permute-start | bytes 786440 | tf_op jit(solution)/shard_map/ppermute | solution.py:403
  120.3 22.2 %collective-permute-start.18 = (bf16[512,256]{1,0:T(8,128)(2,1)S(1)}, bf16[512,256]{1,0:T(8,128)(2,1)S(1)}, u32[]{:S(2)}, u32[]{:S(2)}) collective-permute-start(bf16[512,256]{1,0:T(8,128)(2,1)S(1)} %shard_map.125.near), channel_id=1, source_target_pairs={{0,3},{1,0},{2,1},{3,2},{4,100},{5,101},{6,102},{7,103},{32,35},{3... | collective-permute-start | bytes 786440 | tf_op jit(solution)/shard_map/ppermute | solution.py:403
  129.1 2.0 %copy-start = (bf16[2048,1024]{1,0:T(8,128)(2,1)}, bf16[2048,1024]{1,0:T(8,128)(2,1)S(1)}, u32[]{:S(2)}) copy-start(bf16[2048,1024]{1,0:T(8,128)(2,1)S(1)} %get-tuple-element.37.wave_p) | copy-start | bytes 12582916
  131.0 2.0 %copy-start.2 = (bf16[2048,1024]{1,0:T(8,128)(2,1)}, bf16[2048,1024]{1,0:T(8,128)(2,1)S(1)}, u32[]{:S(2)}) copy-start(bf16[2048,1024]{1,0:T(8,128)(2,1)S(1)} %get-tuple-element.38.wave_qz) | copy-start | bytes 12582916
  133.1 14.4 %collective-permute-start.22 = (bf16[512,256]{1,0:T(8,128)(2,1)S(1)}, bf16[512,256]{1,0:T(8,128)(2,1)S(1)}, u32[]{:S(2)}, u32[]{:S(2)}) collective-permute-start(bf16[512,256]{1,0:T(8,128)(2,1)S(1)} %shard_map.125.near), channel_id=1, source_target_pairs={{0,4},{4,0},{1,5},{5,1},{2,6},{6,2},{3,7},{7,3},{8,12},{12,8},{9,1... | collective-permute-start | bytes 786440 | tf_op jit(solution)/shard_map/ppermute | solution.py:414
  142.0 7.4 %collective-permute-start.19 = (bf16[512,256]{1,0:T(8,128)(2,1)S(1)}, bf16[512,256]{1,0:T(8,128)(2,1)S(1)}, u32[]{:S(2)}, u32[]{:S(2)}) collective-permute-start(bf16[512,256]{1,0:T(8,128)(2,1)S(1)} %collective-permute-done.16.m1), channel_id=1, source_target_pairs={{0,4},{4,0},{1,5},{5,1},{2,6},{6,2},{3,7},{7,3},{8,12},{12,8},{9,1... | collective-permute-start | bytes 786440 | tf_op jit(solution)/shard_map/ppermute | solution.py:414
  142.0 7.4 %collective-permute-start.20 = (bf16[512,256]{1,0:T(8,128)(2,1)S(1)}, bf16[512,256]{1,0:T(8,128)(2,1)S(1)}, u32[]{:S(2)}, u32[]{:S(2)}) collective-permute-start(bf16[512,256]{1,0:T(8,128)(2,1)S(1)} %collective-permute-done.17.m2), channel_id=1, source_target_pairs={{0,4},{4,0},{1,5},{5,1},{2,6},{6,2},{3,7},{7,3},{8,12},{12,8},{9,1... | collective-permute-start | bytes 786440 | tf_op jit(solution)/shard_map/ppermute | solution.py:414
  142.5 6.9 %collective-permute-start.21 = (bf16[512,256]{1,0:T(8,128)(2,1)S(1)}, bf16[512,256]{1,0:T(8,128)(2,1)}, u32[]{:S(2)}, u32[]{:S(2)}) collective-permute-start(bf16[512,256]{1,0:T(8,128)(2,1)S(1)} %collective-permute-done.18.m3), channel_id=1, source_target_pairs={{0,4},{4,0},{1,5},{5,1},{2,6},{6,2},{3,7},{7,3},{8,12},{12,8},{9,1... | collective-permute-start | bytes 786440 | tf_op jit(solution)/shard_map/ppermute | solution.py:414
  142.6 4.9 %copy-start.1 = (bf16[2048,1024]{1,0:T(8,128)(2,1)S(1)}, bf16[2048,1024]{1,0:T(8,128)(2,1)}, u32[]{:S(2)}) copy-start(bf16[2048,1024]{1,0:T(8,128)(2,1)} %copy-done) | copy-start | bytes 12582916
  142.6 4.9 %copy-start.3 = (bf16[2048,1024]{1,0:T(8,128)(2,1)S(1)}, bf16[2048,1024]{1,0:T(8,128)(2,1)}, u32[]{:S(2)}) copy-start(bf16[2048,1024]{1,0:T(8,128)(2,1)} %copy-done.2) | copy-start | bytes 12582916
  147.5 1.9 %copy-start.11 = (bf16[256,256]{1,0:T(8,128)(2,1)S(1)}, bf16[256,256]{1,0:T(8,128)(2,1)}, u32[]{:S(2)}) copy-start(bf16[256,256]{1,0:T(8,128)(2,1)} %hidden_weight.1) | copy-start | bytes 393220
  147.5 1.9 %copy-start.12 = (bf16[256,256]{1,0:T(8,128)(2,1)S(1)}, bf16[256,256]{1,0:T(8,128)(2,1)}, u32[]{:S(2)}) copy-start(bf16[256,256]{1,0:T(8,128)(2,1)} %output_weight.1) | copy-start | bytes 393220
  147.5 1.9 %copy-start.13 = (f32[2048]{0:T(1024)S(1)}, f32[2048]{0:T(1024)}, u32[]{:S(2)}) copy-start(f32[2048]{0:T(1024)} %param.16) | copy-start | bytes 24580

commit v8 on v7

--- a/solution.py
+++ b/solution.py
@@ -85,33 +85,36 @@
         return carry
 
     lax.fori_loop(0, points // 128, weigh, 0, unroll=2)
-    save_message = pltpu.make_async_copy(message, sent, saves.at[devices // 16])
+    save_message = pltpu.make_async_copy(message, sent, saves.at[4])
     save_message.start()
     rank = rank_row[...]
     low = tile[...] * 8 + lax.bitwise_and(rank, 7)
     slot = slots[...]
 
+    many = 32
+    steps = devices // many
+
     def save(step):
-        rows = pl.ds(step * 16, 16)
+        rows = pl.ds(step * many, many)
         return pltpu.make_async_copy(built.at[rows], send.at[rows], saves.at[step])
 
     def fill(step, carry):
-        base = step * 16
-        hot = (slot - base * cap == iota((16 * cap, points), 0)).astype(BF16)
+        base = step * many
+        hot = (slot - base * cap == iota((many * cap, points), 0)).astype(BF16)
         rows = mm(hot, message[...])
-        left = rows[:, :128].reshape(16, cap, 128).astype(BF16)
-        right = rows[:, 128:].reshape(16, cap, 128).astype(BF16)
-        hot8 = (low - base * 8 == iota((128, points), 0)).astype(BF16)
-        placing = mm(hot8, place[...]).reshape(16, 8, 128).astype(BF16)
-        built[pl.ds(base, 16), 0:cap, :] = left
-        built[pl.ds(base, 16), cap : 2 * cap, :] = right
-        built[pl.ds(base, 16), 2 * cap :, :] = placing
+        left = rows[:, :128].reshape(many, cap, 128).astype(BF16)
+        right = rows[:, 128:].reshape(many, cap, 128).astype(BF16)
+        hot8 = (low - base * 8 == iota((many * 8, points), 0)).astype(BF16)
+        placing = mm(hot8, place[...]).reshape(many, 8, 128).astype(BF16)
+        built[pl.ds(base, many), 0:cap, :] = left
+        built[pl.ds(base, many), cap : 2 * cap, :] = right
+        built[pl.ds(base, many), 2 * cap :, :] = placing
         save(step).start()
         return carry
 
-    lax.fori_loop(0, devices // 16, fill, 0)
+    lax.fori_loop(0, steps, fill, 0)
     save_message.wait()
-    for step in range(devices // 16):
+    for step in range(steps):
         save(step).wait()
 
 
@@ -236,10 +239,12 @@
 
 def reply_body(latent, places, weight, out, built, saves):
     lane = iota((128, 128), 0)
-    column = iota((128, 128), 1)
+    column = iota((256, 128), 1)
+
+    many = 32
 
     def back(step, carry):
-        place = places[pl.ds(step * 128, 128), :]
+        place = places[pl.ds(step * many * 8, many * 8), :]
         tall = []
         for g in range(3):
             pick = jnp.where(lane == 2 * g, 64.0, jnp.where(lane == 2 * g + 1, 1.0, 0.0))
@@ -248,17 +253,18 @@
             tall.append(jnp.concatenate(hot, axis=1))
         got = mm(jnp.concatenate(tall, axis=0), latent[...])
         for g in range(3):
-            piece = got[g * 128 : g * 128 + 128].reshape(16, 8, 256).astype(BF16)
-            built[pl.ds(step * 16, 16), g * 8 : g * 8 + 8, :] = piece
+            piece = got[g * many * 8 : (g + 1) * many * 8]
+            piece = piece.reshape(many, 8, 256).astype(BF16)
+            built[pl.ds(step * many, many), g * 8 : g * 8 + 8, :] = piece
         save(step).start()
         return carry
 
     def save(step):
-        rows = pl.ds(step * 16, 16)
+        rows = pl.ds(step * many, many)
         return pltpu.make_async_copy(built.at[rows], out.at[rows], saves.at[step])
 
-    lax.fori_loop(0, 8, back, 0)
-    for step in range(8):
+    lax.fori_loop(0, 4, back, 0)
+    for step in range(4):
         save(step).wait()
 
 
@@ -356,7 +362,7 @@
 
 
 def decode_body(
-    m1, m2, m3, m5, m6, m7, wave_p, wave_qz, base, read, hidden_weight, output_weight, out
+    m1, m2, m3, m5, m6, m7, wave_p, wave_qz, base, read, hidden_weight, output_weight, out, built, saves
 ):
     modes = ((m1, m2, m3), (m5, m6, m7))
 
@@ -373,10 +379,17 @@
         )
         gathered = (jnp.concatenate([scale, scale], axis=1) * value).astype(BF16)
         hidden = jax.nn.gelu(mm(gathered, hidden_weight[...])).astype(BF16)
-        out[pl.ds(at, 512), :] = mm(hidden, output_weight[...]).astype(BF16)
-        return carry
-
-    lax.fori_loop(0, out.shape[0] // 512, some, 0)
+        built[pl.ds(at, 512), :] = mm(hidden, output_weight[...]).astype(BF16)
+        save(step).start()
+        return carry
+
+    def save(step):
+        rows = pl.ds(step * 512, 512)
+        return pltpu.make_async_copy(built.at[rows], out.at[rows], saves.at[step])
+
+    lax.fori_loop(0, 4, some, 0)
+    for step in range(4):
+        save(step).wait()
 
 
 def basis_terms():
@@ -452,7 +465,7 @@
             pltpu.VMEM((points, width), BF16),
             pltpu.VMEM((points, 128), BF16),
             pltpu.VMEM((devices, 56, 128), BF16),
-            pltpu.SemaphoreType.DMA((devices // 16 + 1,)),
+            pltpu.SemaphoreType.DMA((5,)),
         ],
         name="spread",
         compiler_params=pltpu.CompilerParams(vmem_limit_bytes=60 * 2**20),
@@ -490,7 +503,7 @@
         out_specs=anywhere,
         scratch_shapes=[
             pltpu.VMEM((devices, 24, width), BF16),
-            pltpu.SemaphoreType.DMA((8,)),
+            pltpu.SemaphoreType.DMA((4,)),
         ],
         name="reply",
         compiler_params=pltpu.CompilerParams(vmem_limit_bytes=20 * 2**20),
@@ -521,16 +534,21 @@
         (),
         flops=2 * 1024 * 2048 * 256,
     )
-    return call(
+    arrays = modes[1:4] + modes[5:]
+    arrays = arrays + (wave_p, wave_qz, base, read_weight.reshape(1, points))
+    arrays = arrays + (hidden_weight, output_weight)
+    return pl.pallas_call(
         decode_body,
-        shape((points, width), BF16),
-        modes[1:4]
-        + modes[5:]
-        + (wave_p, wave_qz, base, read_weight.reshape(1, points), hidden_weight, output_weight),
-        (),
-        limit=32,
-        flops=2 * 4096 * 2048 * 256,
-    )
+        out_shape=shape((points, width), BF16),
+        in_specs=[VMEM] * len(arrays),
+        out_specs=anywhere,
+        scratch_shapes=[pltpu.VMEM((points, width), BF16), pltpu.SemaphoreType.DMA((4,))],
+        name="decode",
+        compiler_params=pltpu.CompilerParams(vmem_limit_bytes=32 * 2**20),
+        cost_estimate=pl.CostEstimate(
+            flops=2 * 4096 * 2048 * 256, transcendentals=0, bytes_accessed=4000000
+        ),
+    )(*arrays)
 
 
 def solution(mesh):

time: 158 us -> 156 us (0.987)
  Pallas kernels: 54 us -> 52.1 us
    pallas_call x13 -> x12, Pallas kernels: 37.2 us -> 29 us  [call(): return fn(*ins)]
    pallas_call x0 -> x1, Pallas kernels: none -> 7.97 us  [per_device(): pl.pallas_call(decode_body, out_shape=shape((points, width), BF16), in_sp...]
where the time goes in v8:
time: 156 us
  Pallas kernels  52.1 us (33%)
  starting transfers between devices  50.6 us (32%)
  waiting for transfers between devices  47.2 us (30%)
  local copies, waits for them, and re-layouts  5.26 us (3%)
    pallas_call x12, Pallas kernels, call(): return fn(*ins)  29 us
    all_to_all x1, waiting for transfers between devices, per_device(): recv = lax.all_to_all(send, everyone, 0, 0, tiled=True)  21.7 us
    ppermute x12, waiting for transfers between devices, around(): return lax.ppermute(shard, ('z', 'core', 'ba'), pairs)  21.2 us
    ppermute x12, starting transfers between devices, around(): return lax.ppermute(shard, ('z', 'core', 'ba'), pairs)  17.3 us
    all_to_all x1, starting transfers between devices, per_device(): recv = lax.all_to_all(send, everyone, 0, 0, tiled=True)  11.5 us
    ppermute x5, starting transfers between devices, swapped(): return lax.ppermute(shard, 'core', [(0, 1), (1, 0)])  10.6 us
    pallas_call x1, Pallas kernels, per_device(): pl.pallas_call(spread_body, out_shape=(shape((devices, 56, 128), BF16), s...  9.84 us
    pallas_call x1, Pallas kernels, per_device(): pl.pallas_call(decode_body, out_shape=shape((points, width), BF16), in_sp...  7.97 us
  transfers between devices with their start and end apart: 25, of which 13 were waited for; matrix products, arithmetic and copies ran while one was open for 0% of the time, Pallas kernels for 22%

profile of v8, /device:TPU:1, one launch (start us, length us, event | category | flops | bytes accessed | tf_op | source)
XLA Modules:
  0.0 155.7 jit_solution(1824345014518063841)
XLA Ops:
  0.0 9.8 %spread.1 = (bf16[128,56,128]{2,1,0:T(8,128)(2,1)}, s32[1,2048]{1,0:T(1,128)}, bf16[2048,256]{1,0:T(8,128)(2,1)}) custom-call(bf16[2048,256]{1,0:T(8,128)(2,1)} %feat.1, s32[1,2048]{1,0:T(1,128)} %bitcast.7, s32[1,2048]{1,0:T(1,128)} %bitcast.11, f32[1,2048]{1,0:T(1,128)} %bitcast.16, bf16[256,256]{1,0:T(8,128)(2,1)} %weight.3), custom_call_target="tpu_custom_call" | custom-call | tf_op jit(solution)/shard_map/spread/pallas_call | solution.py:454
  9.8 0.0 copy-start.6
  9.9 0.0 copy-start.7
  9.9 0.0 copy-start.8
  9.9 0.0 copy-start.16
  9.9 11.5 %all-to-all-start = ((bf16[128,56,128]{2,1,0:T(8,128)(2,1)}), bf16[128,56,128]{2,1,0:T(8,128)(2,1)S(1)}, u32[]{:S(2)}, u32[]{:S(2)}) async-start(bf16[128,56,128]{2,1,0:T(8,128)(2,1)} %get-tuple-element.39), calls=%async_computation | async-start | bytes 3670016 | tf_op jit(solution)/shard_map/all_to_all | solution.py:473
  21.4 5.1 %shard_map.119 = bf16[2048,256]{1,0:T(8,128)(2,1)} custom-call(bf16[2048,256]{1,0:T(8,128)(2,1)S(1)} %copy-done.8, s32[1,2048]{1,0:T(1,128)S(1)} %bitcast.8, s32[1,2048]{1,0:T(1,128)S(1)} %bitcast.12, bf16[16,128]{1,0:T(8,128)(2,1)S(1)} %copy-done.16, s32[1]{0:T(128)} %bitcast.3.where), custom_call_target="tpu_custom_call" | custom-call | flops 2147483648 | bytes 4000000 | tf_op jit(solution)/shard_map/pallas_call | solution.py:48
  26.6 1.1 collective-permute-start
  27.6 21.7 %all-to-all-done.recv = bf16[128,56,128]{2,1,0:T(8,128)(2,1)S(1)} async-done(((bf16[128,56,128]{2,1,0:T(8,128)(2,1)}), bf16[128,56,128]{2,1,0:T(8,128)(2,1)S(1)}, u32[]{:S(2)}, u32[]{:S(2)}) %all-to-all-start) | async-done | bytes 1835040 | tf_op jit(solution)/shard_map/all_to_all | solution.py:473
  49.3 5.2 %shard_map.127 = (bf16[2048,256]{1,0:T(8,128)(2,1)S(1)}, bf16[1024,128]{1,0:T(8,128)(2,1)S(1)}) custom-call(bf16[128,56,128]{2,1,0:T(8,128)(2,1)S(1)} %all-to-all-done.recv), custom_call_target="tpu_custom_call" | custom-call | flops 3221225472 | bytes 4000000 | tf_op jit(solution)/shard_map/pallas_call | solution.py:48
  54.6 5.3 %reply.1 = bf16[128,24,256]{2,1,0:T(8,128)(2,1)} custom-call(bf16[2048,256]{1,0:T(8,128)(2,1)S(1)} %get-tuple-element.40.latent, bf16[1024,128]{1,0:T(8,128)(2,1)S(1)} %get-tuple-element.41.places, bf16[4,8,256,256]{3,2,1,0:T(8,128)(2,1)S(1)} %copy-done.4), custom_call_target="tpu_custom_call" | custom-call | flops 3221225472 | bytes 4000000 | tf_op jit(solution)/shard_map/reply/pallas_call | solution.py:499
  59.9 3.8 %all-to-all-start.1 = ((bf16[128,24,256]{2,1,0:T(8,128)(2,1)}), bf16[128,24,256]{2,1,0:T(8,128)(2,1)S(1)}, u32[]{:S(2)}, u32[]{:S(2)}) async-start(bf16[128,24,256]{2,1,0:T(8,128)(2,1)} %reply.1), calls=%async_computation.1 | async-start | bytes 3145728 | tf_op jit(solution)/shard_map/all_to_all | solution.py:522
  63.7 0.0 copy-start.9
  63.7 1.2 copy-done.9
  64.9 4.1 %shard_map.118.refs_0_ = bf16[2048,256]{1,0:T(8,128)(2,1)S(1)} custom-call(bf16[2048,256]{1,0:T(8,128)(2,1)S(1)} %copy-done.9, s32[1,2048]{1,0:T(1,128)S(1)} %bitcast.9, s32[1,2048]{1,0:T(1,128)S(1)} %bitcast.13, bf16[16,128]{1,0:T(8,128)(2,1)S(1)} %copy-done.16, s32[1]{0:T(128)} %bitcast.3.where), custom_call_target="tpu_custom_call" | custom-call | flops 2147483648 | bytes 4000000 | tf_op jit(solution)/shard_map/pallas_call | solution.py:48
  69.0 0.0 collective-permute-done.refs_1_
  69.1 0.2 shard_map.120
  69.3 1.7 %collective-permute-start.1 = (bf16[512,256]{1,0:T(8,128)(2,1)S(1)}, bf16[512,256]{1,0:T(8,128)(2,1)S(1)}, u32[]{:S(2)}, u32[]{:S(2)}) collective-permute-start(bf16[512,256]{1,0:T(8,128)(2,1)S(1)} %get-tuple-element.26), channel_id=1, source_target_pairs={{0,1},{1,2},{2,3},{3,0},{4,36},{5,37},{6,38},{7,39},{32,33},{33,34... | collective-permute-start | bytes 786440 | tf_op jit(solution)/shard_map/ppermute | solution.py:416
  71.0 2.9 %collective-permute-start.2 = (bf16[512,256]{1,0:T(8,128)(2,1)S(1)}, bf16[512,256]{1,0:T(8,128)(2,1)S(1)}, u32[]{:S(2)}, u32[]{:S(2)}) collective-permute-start(bf16[512,256]{1,0:T(8,128)(2,1)S(1)} %get-tuple-element.27), channel_id=1, source_target_pairs={{0,2},{1,3},{2,0},{3,1},{4,68},{5,69},{6,70},{7,71},{32,34},{33,35... | collective-permute-start | bytes 786440 | tf_op jit(solution)/shard_map/ppermute | solution.py:416
  73.9 0.9 collective-permute-start.3
  74.8 13.1 %collective-permute-done.1.refs_1_ = bf16[512,256]{1,0:T(8,128)(2,1)S(1)} collective-permute-done((bf16[512,256]{1,0:T(8,128)(2,1)S(1)}, bf16[512,256]{1,0:T(8,128)(2,1)S(1)}, u32[]{:S(2)}, u32[]{:S(2)}) %collective-permute-start.1) | collective-permute-done | bytes 262176 | tf_op jit(solution)/shard_map/ppermute | solution.py:416
  87.9 2.9 %collective-permute-done.2.refs_2_ = bf16[512,256]{1,0:T(8,128)(2,1)S(1)} collective-permute-done((bf16[512,256]{1,0:T(8,128)(2,1)S(1)}, bf16[512,256]{1,0:T(8,128)(2,1)S(1)}, u32[]{:S(2)}, u32[]{:S(2)}) %collective-permute-start.2) | collective-permute-done | bytes 262176 | tf_op jit(solution)/shard_map/ppermute | solution.py:416
  90.8 0.1 shard_map.121
  91.0 1.2 collective-permute-start.4
  92.2 2.4 %collective-permute-start.5 = (bf16[128,256]{1,0:T(8,128)(2,1)S(1)}, bf16[128,256]{1,0:T(8,128)(2,1)S(1)}, u32[]{:S(2)}, u32[]{:S(2)}) collective-permute-start(bf16[128,256]{1,0:T(8,128)(2,1)S(1)} %get-tuple-element.31), channel_id=1, source_target_pairs={{0,64},{1,65},{2,66},{3,67},{4,6},{5,7},{6,4},{7,5},{32,96},{33,97... | collective-permute-start | bytes 196616 | tf_op jit(solution)/shard_map/ppermute | solution.py:416
  94.7 0.9 collective-permute-start.6
  95.6 1.7 %collective-permute-done.5.refs_2_ = bf16[128,256]{1,0:T(8,128)(2,1)S(1)} collective-permute-done((bf16[128,256]{1,0:T(8,128)(2,1)S(1)}, bf16[128,256]{1,0:T(8,128)(2,1)S(1)}, u32[]{:S(2)}, u32[]{:S(2)}) %collective-permute-start.5) | collective-permute-done | bytes 65568 | tf_op jit(solution)/shard_map/ppermute | solution.py:416
  97.3 0.5 collective-permute-done.6.refs_3_
  97.8 0.7 collective-permute-start.7
  98.5 2.3 %collective-permute-start.8 = (bf16[32,256]{1,0:T(8,128)(2,1)S(1)}, bf16[32,256]{1,0:T(8,128)(2,1)S(1)}, u32[]{:S(2)}, u32[]{:S(2)}) collective-permute-start(bf16[32,256]{1,0:T(8,128)(2,1)S(1)} %get-tuple-element.35), channel_id=1, source_target_pairs={{0,16},{8,24},{16,0},{24,8},{1,17},{9,25},{17,1},{25,9},{2,18},{10... | collective-permute-start | bytes 49160 | tf_op jit(solution)/shard_map/ppermute | solution.py:408
  100.8 1.2 collective-permute-start.9
  102.0 0.6 collective-permute-done.8.c
  102.6 1.1 collective-permute-done.9.d
  103.7 0.7 shard_map.123.refs_0_
  104.4 0.4 collective-permute-start.10
  104.8 2.9 %collective-permute-start.11 = (bf16[32,256]{1,0:T(8,128)(2,1)S(1)}, bf16[32,256]{1,0:T(8,128)(2,1)S(1)}, u32[]{:S(2)}, u32[]{:S(2)}) collective-permute-start(bf16[32,256]{1,0:T(8,128)(2,1)S(1)} %shard_map.123.refs_0_), channel_id=1, source_target_pairs={{0,16},{8,24},{16,0},{24,8},{1,17},{9,25},{17,1},{25,9},{2,18},{10... | collective-permute-start | bytes 49160 | tf_op jit(solution)/shard_map/ppermute | solution.py:408
  107.6 0.0 collective-permute-start.12
  107.7 0.5 collective-permute-done.10.refs_1_
  108.2 0.8 collective-permute-done.11.refs_2_
  108.9 1.3 collective-permute-done.12.refs_3_
  110.3 0.4 collective-permute-start.13
  110.7 3.2 %collective-permute-start.14 = (bf16[128,256]{1,0:T(8,128)(2,1)S(1)}, bf16[128,256]{1,0:T(8,128)(2,1)S(1)}, u32[]{:S(2)}, u32[]{:S(2)}) collective-permute-start(bf16[128,256]{1,0:T(8,128)(2,1)S(1)} %shard_map.124.refs_0_), channel_id=1, source_target_pairs={{0,64},{1,65},{2,66},{3,67},{4,6},{5,7},{6,4},{7,5},{32,96},{33,97... | collective-permute-start | bytes 196616 | tf_op jit(solution)/shard_map/ppermute | solution.py:416
  113.9 0.1 collective-permute-start.15
  114.0 0.7 collective-permute-done.13.refs_1_
  114.6 1.6 %collective-permute-done.14.refs_2_ = bf16[128,256]{1,0:T(8,128)(2,1)S(1)} collective-permute-done((bf16[128,256]{1,0:T(8,128)(2,1)S(1)}, bf16[128,256]{1,0:T(8,128)(2,1)S(1)}, u32[]{:S(2)}, u32[]{:S(2)}) %collective-permute-start.14) | collective-permute-done | bytes 65568 | tf_op jit(solution)/shard_map/ppermute | solution.py:416
  116.2 0.8 collective-permute-done.15.refs_3_
  117.0 0.1 collective-permute-start.16
  117.1 1.3 collective-permute-start.17
  118.4 2.0 %collective-permute-start.18 = (bf16[512,256]{1,0:T(8,128)(2,1)S(1)}, bf16[512,256]{1,0:T(8,128)(2,1)S(1)}, u32[]{:S(2)}, u32[]{:S(2)}) collective-permute-start(bf16[512,256]{1,0:T(8,128)(2,1)S(1)} %shard_map.125.near), channel_id=1, source_target_pairs={{0,3},{1,0},{2,1},{3,2},{4,100},{5,101},{6,102},{7,103},{32,35},{3... | collective-permute-start | bytes 786440 | tf_op jit(solution)/shard_map/ppermute | solution.py:416
  120.4 6.8 %shard_map.126 = (bf16[2048,1024]{1,0:T(8,128)(2,1)S(1)}, bf16[2048,1024]{1,0:T(8,128)(2,1)S(1)}) custom-call(s32[1,2048]{1,0:T(1,128)S(1)} %bitcast.10, s32[1,2048]{1,0:T(1,128)S(1)} %bitcast.14, bf16[128,16]{1,0:T(8,128)(2,1)S(1)} %copy-done.15, s32[1]{0:T(128)} %bitcast.3.where), custom_call_target="tpu_custom_call" | custom-call | flops 1000000000 | bytes 4000000 | tf_op jit(solution)/shard_map/pallas_call | solution.py:48
  127.2 1.9 %copy-done = bf16[2048,1024]{1,0:T(8,128)(2,1)} copy-done((bf16[2048,1024]{1,0:T(8,128)(2,1)}, bf16[2048,1024]{1,0:T(8,128)(2,1)S(1)}, u32[]{:S(2)}) %copy-start) | copy-done | bytes 4194328
  129.2 2.0 %copy-done.2 = bf16[2048,1024]{1,0:T(8,128)(2,1)} copy-done((bf16[2048,1024]{1,0:T(8,128)(2,1)}, bf16[2048,1024]{1,0:T(8,128)(2,1)S(1)}, u32[]{:S(2)}) %copy-start.2) | copy-done | bytes 4194328
  131.2 8.9 %collective-permute-start.22 = (bf16[512,256]{1,0:T(8,128)(2,1)S(1)}, bf16[512,256]{1,0:T(8,128)(2,1)S(1)}, u32[]{:S(2)}, u32[]{:S(2)}) collective-permute-start(bf16[512,256]{1,0:T(8,128)(2,1)S(1)} %shard_map.125.near), channel_id=1, source_target_pairs={{0,4},{4,0},{1,5},{5,1},{2,6},{6,2},{3,7},{7,3},{8,12},{12,8},{9,1... | collective-permute-start | bytes 786440 | tf_op jit(solution)/shard_map/ppermute | solution.py:427
  140.1 0.0 collective-permute-start.19
  140.1 0.0 collective-permute-done.17.m2
  140.1 0.5 collective-permute-start.20
  140.6 0.1 collective-permute-start.21
  140.7 0.0 all-to-all-done.1
  140.7 4.8 %shard_map.128.base = f32[2048,256]{1,0:T(8,128)S(1)} custom-call(bf16[3072,256]{1,0:T(8,128)(2,1)S(1)} %bitcast.6, s32[1,2048]{1,0:T(1,128)S(1)} %copy-done.14, bf16[256,256]{1,0:T(8,128)(2,1)S(1)} %copy-done.10), custom_call_target="tpu_custom_call" | custom-call | flops 3221225472 | bytes 4000000 | tf_op jit(solution)/shard_map/pallas_call | solution.py:48
  145.6 0.0 copy-start.11
  145.6 0.0 copy-start.12
  145.6 0.0 copy-start.13
  145.6 1.8 %shard_map.129.base = f32[2048,256]{1,0:T(8,128)S(1)} custom-call(bf16[512,256]{1,0:T(8,128)(2,1)S(1)} %shard_map.125.near, bf16[512,256]{1,0:T(8,128)(2,1)S(1)} %collective-permute-done.22.far, bf16[2048,1024]{1,0:T(8,128)(2,1)S(1)} %copy-done.1, bf16[2048,1024]{1,0:T(8,128)(2,1)S(1)} %copy-done.3, f32[2048,256]{1,0:T(8,128)S(1)} %shard_map.128.base), custom_call_target="tpu_custom_call" | custom-call | flops 1073741824 | bytes 4000000 | tf_op jit(solution)/shard_map/pallas_call | solution.py:48
  147.5 8.0 %decode.1 = bf16[2048,256]{1,0:T(8,128)(2,1)} custom-call(bf16[512,256]{1,0:T(8,128)(2,1)S(1)} %collective-permute-done.16.m1, bf16[512,256]{1,0:T(8,128)(2,1)S(1)} %collective-permute-done.17.m2, bf16[512,256]{1,0:T(8,128)(2,1)S(1)} %collective-permute-done.18.m3, bf16[512,256]{1,0:T(8,128)(2,1)S(1)} %collective-permute-done.19.m5, ...), custom_call_target="tpu_custom_call" | custom-call | flops 4294967296 | bytes 4000000 | tf_op jit(solution)/shard_map/decode/pallas_call | solution.py:540
  (35 shorter events, 0.1 us)
Async XLA Ops:
  9.8 11.6 %copy-start.6 = (s32[2048,1]{0,1:T(1,128)S(1)}, s32[2048,1]{0,1:T(1,128)}, u32[]{:S(2)}) copy-start(s32[2048,1]{0,1:T(1,128)} %param.13) | copy-start | bytes 24580
  9.9 11.6 %copy-start.7 = (s32[2048]{0:T(1024)S(1)}, s32[2048]{0:T(1024)}, u32[]{:S(2)}) copy-start(s32[2048]{0:T(1024)} %param.14) | copy-start | bytes 24580
  9.9 11.5 %copy-start.8 = (bf16[2048,256]{1,0:T(8,128)(2,1)S(1)}, bf16[2048,256]{1,0:T(8,128)(2,1)}, u32[]{:S(2)}) copy-start(bf16[2048,256]{1,0:T(8,128)(2,1)} %get-tuple-element.24.message) | copy-start | bytes 3145732
  9.9 11.5 %copy-start.16 = (bf16[16,128]{1,0:T(8,128)(2,1)S(1)}, bf16[16,128]{1,0:T(8,128)(2,1)}, u32[]{:S(2)}) copy-start(bf16[16,128]{1,0:T(8,128)(2,1)} %constant.26.clone.basis) | copy-start | bytes 12292
  9.9 39.4 %all-to-all-start = ((bf16[128,56,128]{2,1,0:T(8,128)(2,1)}), bf16[128,56,128]{2,1,0:T(8,128)(2,1)S(1)}, u32[]{:S(2)}, u32[]{:S(2)}) async-start(bf16[128,56,128]{2,1,0:T(8,128)(2,1)} %get-tuple-element.39), calls=%async_computation | async-start | bytes 3670016 | tf_op jit(solution)/shard_map/all_to_all | solution.py:473
  26.6 42.5 %collective-permute-start = (bf16[2048,256]{1,0:T(8,128)(2,1)}, bf16[2048,256]{1,0:T(8,128)(2,1)S(1)}, u32[]{:S(2)}, u32[]{:S(2)}) collective-permute-start(bf16[2048,256]{1,0:T(8,128)(2,1)} %shard_map.119), channel_id=1, source_target_pairs={{0,4},{4,0},{1,5},{5,1},{2,6},{6,2},{3,7},{7,3},{8,12},{12,8},{9,1... | collective-permute-start | bytes 3145736 | tf_op jit(solution)/shard_map/ppermute | solution.py:427
  49.3 5.2 %copy-start.4 = (bf16[4,8,256,256]{3,2,1,0:T(8,128)(2,1)S(1)}, bf16[4,8,256,256]{3,2,1,0:T(8,128)(2,1)}, u32[]{:S(2)}) copy-start(bf16[4,8,256,256]{3,2,1,0:T(8,128)(2,1)} %weight.5) | copy-start | bytes 12582916
  59.9 80.9 %all-to-all-start.1 = ((bf16[128,24,256]{2,1,0:T(8,128)(2,1)}), bf16[128,24,256]{2,1,0:T(8,128)(2,1)S(1)}, u32[]{:S(2)}, u32[]{:S(2)}) async-start(bf16[128,24,256]{2,1,0:T(8,128)(2,1)} %reply.1), calls=%async_computation.1 | async-start | bytes 3145728 | tf_op jit(solution)/shard_map/all_to_all | solution.py:522
  63.7 1.2 copy-start.9
  64.9 38.8 %copy-start.5 = (bf16[4,8,256,256]{3,2,1,0:T(8,128)(2,1)S(1)}, bf16[4,8,256,256]{3,2,1,0:T(8,128)(2,1)}, u32[]{:S(2)}) copy-start(bf16[4,8,256,256]{3,2,1,0:T(8,128)(2,1)} %weight.5) | copy-start | bytes 12582916
  69.3 18.6 %collective-permute-start.1 = (bf16[512,256]{1,0:T(8,128)(2,1)S(1)}, bf16[512,256]{1,0:T(8,128)(2,1)S(1)}, u32[]{:S(2)}, u32[]{:S(2)}) collective-permute-start(bf16[512,256]{1,0:T(8,128)(2,1)S(1)} %get-tuple-element.26), channel_id=1, source_target_pairs={{0,1},{1,2},{2,3},{3,0},{4,36},{5,37},{6,38},{7,39},{32,33},{33,34... | collective-permute-start | bytes 786440 | tf_op jit(solution)/shard_map/ppermute | solution.py:416
  71.0 19.8 %collective-permute-start.2 = (bf16[512,256]{1,0:T(8,128)(2,1)S(1)}, bf16[512,256]{1,0:T(8,128)(2,1)S(1)}, u32[]{:S(2)}, u32[]{:S(2)}) collective-permute-start(bf16[512,256]{1,0:T(8,128)(2,1)S(1)} %get-tuple-element.27), channel_id=1, source_target_pairs={{0,2},{1,3},{2,0},{3,1},{4,68},{5,69},{6,70},{7,71},{32,34},{33,35... | collective-permute-start | bytes 786440 | tf_op jit(solution)/shard_map/ppermute | solution.py:416
  73.9 16.9 %collective-permute-start.3 = (bf16[512,256]{1,0:T(8,128)(2,1)S(1)}, bf16[512,256]{1,0:T(8,128)(2,1)S(1)}, u32[]{:S(2)}, u32[]{:S(2)}) collective-permute-start(bf16[512,256]{1,0:T(8,128)(2,1)S(1)} %get-tuple-element.28), channel_id=1, source_target_pairs={{0,3},{1,0},{2,1},{3,2},{4,100},{5,101},{6,102},{7,103},{32,35},{3... | collective-permute-start | bytes 786440 | tf_op jit(solution)/shard_map/ppermute | solution.py:416
  91.0 4.6 %collective-permute-start.4 = (bf16[128,256]{1,0:T(8,128)(2,1)S(1)}, bf16[128,256]{1,0:T(8,128)(2,1)S(1)}, u32[]{:S(2)}, u32[]{:S(2)}) collective-permute-start(bf16[128,256]{1,0:T(8,128)(2,1)S(1)} %get-tuple-element.30), channel_id=1, source_target_pairs={{0,32},{1,33},{2,34},{3,35},{4,5},{5,6},{6,7},{7,4},{32,64},{33,65... | collective-permute-start | bytes 196616 | tf_op jit(solution)/shard_map/ppermute | solution.py:416
  92.2 5.1 %collective-permute-start.5 = (bf16[128,256]{1,0:T(8,128)(2,1)S(1)}, bf16[128,256]{1,0:T(8,128)(2,1)S(1)}, u32[]{:S(2)}, u32[]{:S(2)}) collective-permute-start(bf16[128,256]{1,0:T(8,128)(2,1)S(1)} %get-tuple-element.31), channel_id=1, source_target_pairs={{0,64},{1,65},{2,66},{3,67},{4,6},{5,7},{6,4},{7,5},{32,96},{33,97... | collective-permute-start | bytes 196616 | tf_op jit(solution)/shard_map/ppermute | solution.py:416
  94.7 3.1 %collective-permute-start.6 = (bf16[128,256]{1,0:T(8,128)(2,1)S(1)}, bf16[128,256]{1,0:T(8,128)(2,1)S(1)}, u32[]{:S(2)}, u32[]{:S(2)}) collective-permute-start(bf16[128,256]{1,0:T(8,128)(2,1)S(1)} %get-tuple-element.32), channel_id=1, source_target_pairs={{0,96},{1,97},{2,98},{3,99},{4,7},{5,4},{6,5},{7,6},{32,0},{33,1},... | collective-permute-start | bytes 196616 | tf_op jit(solution)/shard_map/ppermute | solution.py:416
  97.8 4.2 %collective-permute-start.7 = (bf16[32,256]{1,0:T(8,128)(2,1)S(1)}, bf16[32,256]{1,0:T(8,128)(2,1)S(1)}, u32[]{:S(2)}, u32[]{:S(2)}) collective-permute-start(bf16[32,256]{1,0:T(8,128)(2,1)S(1)} %get-tuple-element.34), channel_id=1, source_target_pairs={{0,8},{8,16},{16,24},{24,0},{1,9},{9,17},{17,25},{25,1},{2,10},{10... | collective-permute-start | bytes 49160 | tf_op jit(solution)/shard_map/ppermute | solution.py:408
  98.5 4.1 %collective-permute-start.8 = (bf16[32,256]{1,0:T(8,128)(2,1)S(1)}, bf16[32,256]{1,0:T(8,128)(2,1)S(1)}, u32[]{:S(2)}, u32[]{:S(2)}) collective-permute-start(bf16[32,256]{1,0:T(8,128)(2,1)S(1)} %get-tuple-element.35), channel_id=1, source_target_pairs={{0,16},{8,24},{16,0},{24,8},{1,17},{9,25},{17,1},{25,9},{2,18},{10... | collective-permute-start | bytes 49160 | tf_op jit(solution)/shard_map/ppermute | solution.py:408
  100.8 2.9 %collective-permute-start.9 = (bf16[32,256]{1,0:T(8,128)(2,1)S(1)}, bf16[32,256]{1,0:T(8,128)(2,1)S(1)}, u32[]{:S(2)}, u32[]{:S(2)}) collective-permute-start(bf16[32,256]{1,0:T(8,128)(2,1)S(1)} %get-tuple-element.36), channel_id=1, source_target_pairs={{0,24},{8,0},{16,8},{24,16},{1,25},{9,1},{17,9},{25,17},{2,26},{10... | collective-permute-start | bytes 49160 | tf_op jit(solution)/shard_map/ppermute | solution.py:408
  103.7 16.7 %copy-start.15 = (bf16[128,16]{1,0:T(8,128)(2,1)S(1)}, bf16[128,16]{1,0:T(8,128)(2,1)}, u32[]{:S(2)}) copy-start(bf16[128,16]{1,0:T(8,128)(2,1)} %constant.27.clone.basis) | copy-start | bytes 12292
  104.4 3.8 %collective-permute-start.10 = (bf16[32,256]{1,0:T(8,128)(2,1)S(1)}, bf16[32,256]{1,0:T(8,128)(2,1)S(1)}, u32[]{:S(2)}, u32[]{:S(2)}) collective-permute-start(bf16[32,256]{1,0:T(8,128)(2,1)S(1)} %shard_map.123.refs_0_), channel_id=1, source_target_pairs={{0,8},{8,16},{16,24},{24,0},{1,9},{9,17},{17,25},{25,1},{2,10},{10... | collective-permute-start | bytes 49160 | tf_op jit(solution)/shard_map/ppermute | solution.py:408
  104.8 4.2 %collective-permute-start.11 = (bf16[32,256]{1,0:T(8,128)(2,1)S(1)}, bf16[32,256]{1,0:T(8,128)(2,1)S(1)}, u32[]{:S(2)}, u32[]{:S(2)}) collective-permute-start(bf16[32,256]{1,0:T(8,128)(2,1)S(1)} %shard_map.123.refs_0_), channel_id=1, source_target_pairs={{0,16},{8,24},{16,0},{24,8},{1,17},{9,25},{17,1},{25,9},{2,18},{10... | collective-permute-start | bytes 49160 | tf_op jit(solution)/shard_map/ppermute | solution.py:408
  107.6 2.6 %collective-permute-start.12 = (bf16[32,256]{1,0:T(8,128)(2,1)S(1)}, bf16[32,256]{1,0:T(8,128)(2,1)S(1)}, u32[]{:S(2)}, u32[]{:S(2)}) collective-permute-start(bf16[32,256]{1,0:T(8,128)(2,1)S(1)} %shard_map.123.refs_0_), channel_id=1, source_target_pairs={{0,24},{8,0},{16,8},{24,16},{1,25},{9,1},{17,9},{25,17},{2,26},{10... | collective-permute-start | bytes 49160 | tf_op jit(solution)/shard_map/ppermute | solution.py:408
  110.2 30.5 %copy-start.10 = (bf16[256,256]{1,0:T(8,128)(2,1)S(1)}, bf16[256,256]{1,0:T(8,128)(2,1)}, u32[]{:S(2)}) copy-start(bf16[256,256]{1,0:T(8,128)(2,1)} %skip.1) | copy-start | bytes 393220
  110.2 30.5 %copy-start.14 = (s32[1,2048]{1,0:T(1,128)S(1)}, s32[1,2048]{1,0:T(1,128)}, u32[]{:S(2)}) copy-start(s32[1,2048]{1,0:T(1,128)} %get-tuple-element.42.slots) | copy-start | bytes 24580
  110.3 4.4 %collective-permute-start.13 = (bf16[128,256]{1,0:T(8,128)(2,1)S(1)}, bf16[128,256]{1,0:T(8,128)(2,1)S(1)}, u32[]{:S(2)}, u32[]{:S(2)}) collective-permute-start(bf16[128,256]{1,0:T(8,128)(2,1)S(1)} %shard_map.124.refs_0_), channel_id=1, source_target_pairs={{0,32},{1,33},{2,34},{3,35},{4,5},{5,6},{6,7},{7,4},{32,64},{33,65... | collective-permute-start | bytes 196616 | tf_op jit(solution)/shard_map/ppermute | solution.py:416
  110.7 5.5 %collective-permute-start.14 = (bf16[128,256]{1,0:T(8,128)(2,1)S(1)}, bf16[128,256]{1,0:T(8,128)(2,1)S(1)}, u32[]{:S(2)}, u32[]{:S(2)}) collective-permute-start(bf16[128,256]{1,0:T(8,128)(2,1)S(1)} %shard_map.124.refs_0_), channel_id=1, source_target_pairs={{0,64},{1,65},{2,66},{3,67},{4,6},{5,7},{6,4},{7,5},{32,96},{33,97... | collective-permute-start | bytes 196616 | tf_op jit(solution)/shard_map/ppermute | solution.py:416
  113.9 3.1 %collective-permute-start.15 = (bf16[128,256]{1,0:T(8,128)(2,1)S(1)}, bf16[128,256]{1,0:T(8,128)(2,1)S(1)}, u32[]{:S(2)}, u32[]{:S(2)}) collective-permute-start(bf16[128,256]{1,0:T(8,128)(2,1)S(1)} %shard_map.124.refs_0_), channel_id=1, source_target_pairs={{0,96},{1,97},{2,98},{3,99},{4,7},{5,4},{6,5},{7,6},{32,0},{33,1},... | collective-permute-start | bytes 196616 | tf_op jit(solution)/shard_map/ppermute | solution.py:416
  117.0 23.1 %collective-permute-start.16 = (bf16[512,256]{1,0:T(8,128)(2,1)S(1)}, bf16[512,256]{1,0:T(8,128)(2,1)S(1)}, u32[]{:S(2)}, u32[]{:S(2)}) collective-permute-start(bf16[512,256]{1,0:T(8,128)(2,1)S(1)} %shard_map.125.near), channel_id=1, source_target_pairs={{0,1},{1,2},{2,3},{3,0},{4,36},{5,37},{6,38},{7,39},{32,33},{33,34... | collective-permute-start | bytes 786440 | tf_op jit(solution)/shard_map/ppermute | solution.py:416
  117.1 23.0 %collective-permute-start.17 = (bf16[512,256]{1,0:T(8,128)(2,1)S(1)}, bf16[512,256]{1,0:T(8,128)(2,1)S(1)}, u32[]{:S(2)}, u32[]{:S(2)}) collective-permute-start(bf16[512,256]{1,0:T(8,128)(2,1)S(1)} %shard_map.125.near), channel_id=1, source_target_pairs={{0,2},{1,3},{2,0},{3,1},{4,68},{5,69},{6,70},{7,71},{32,34},{33,35... | collective-permute-start | bytes 786440 | tf_op jit(solution)/shard_map/ppermute | solution.py:416
  118.4 22.2 %collective-permute-start.18 = (bf16[512,256]{1,0:T(8,128)(2,1)S(1)}, bf16[512,256]{1,0:T(8,128)(2,1)S(1)}, u32[]{:S(2)}, u32[]{:S(2)}) collective-permute-start(bf16[512,256]{1,0:T(8,128)(2,1)S(1)} %shard_map.125.near), channel_id=1, source_target_pairs={{0,3},{1,0},{2,1},{3,2},{4,100},{5,101},{6,102},{7,103},{32,35},{3... | collective-permute-start | bytes 786440 | tf_op jit(solution)/shard_map/ppermute | solution.py:416
  127.2 2.0 %copy-start = (bf16[2048,1024]{1,0:T(8,128)(2,1)}, bf16[2048,1024]{1,0:T(8,128)(2,1)S(1)}, u32[]{:S(2)}) copy-start(bf16[2048,1024]{1,0:T(8,128)(2,1)S(1)} %get-tuple-element.37.wave_p) | copy-start | bytes 12582916
  129.2 2.0 %copy-start.2 = (bf16[2048,1024]{1,0:T(8,128)(2,1)}, bf16[2048,1024]{1,0:T(8,128)(2,1)S(1)}, u32[]{:S(2)}) copy-start(bf16[2048,1024]{1,0:T(8,128)(2,1)S(1)} %get-tuple-element.38.wave_qz) | copy-start | bytes 12582916
  131.2 14.4 %collective-permute-start.22 = (bf16[512,256]{1,0:T(8,128)(2,1)S(1)}, bf16[512,256]{1,0:T(8,128)(2,1)S(1)}, u32[]{:S(2)}, u32[]{:S(2)}) collective-permute-start(bf16[512,256]{1,0:T(8,128)(2,1)S(1)} %shard_map.125.near), channel_id=1, source_target_pairs={{0,4},{4,0},{1,5},{5,1},{2,6},{6,2},{3,7},{7,3},{8,12},{12,8},{9,1... | collective-permute-start | bytes 786440 | tf_op jit(solution)/shard_map/ppermute | solution.py:427
  140.1 7.4 %collective-permute-start.19 = (bf16[512,256]{1,0:T(8,128)(2,1)S(1)}, bf16[512,256]{1,0:T(8,128)(2,1)S(1)}, u32[]{:S(2)}, u32[]{:S(2)}) collective-permute-start(bf16[512,256]{1,0:T(8,128)(2,1)S(1)} %collective-permute-done.16.m1), channel_id=1, source_target_pairs={{0,4},{4,0},{1,5},{5,1},{2,6},{6,2},{3,7},{7,3},{8,12},{12,8},{9,1... | collective-permute-start | bytes 786440 | tf_op jit(solution)/shard_map/ppermute | solution.py:427
  140.1 7.4 %collective-permute-start.20 = (bf16[512,256]{1,0:T(8,128)(2,1)S(1)}, bf16[512,256]{1,0:T(8,128)(2,1)S(1)}, u32[]{:S(2)}, u32[]{:S(2)}) collective-permute-start(bf16[512,256]{1,0:T(8,128)(2,1)S(1)} %collective-permute-done.17.m2), channel_id=1, source_target_pairs={{0,4},{4,0},{1,5},{5,1},{2,6},{6,2},{3,7},{7,3},{8,12},{12,8},{9,1... | collective-permute-start | bytes 786440 | tf_op jit(solution)/shard_map/ppermute | solution.py:427
  140.6 6.9 %collective-permute-start.21 = (bf16[512,256]{1,0:T(8,128)(2,1)S(1)}, bf16[512,256]{1,0:T(8,128)(2,1)}, u32[]{:S(2)}, u32[]{:S(2)}) collective-permute-start(bf16[512,256]{1,0:T(8,128)(2,1)S(1)} %collective-permute-done.18.m3), channel_id=1, source_target_pairs={{0,4},{4,0},{1,5},{5,1},{2,6},{6,2},{3,7},{7,3},{8,12},{12,8},{9,1... | collective-permute-start | bytes 786440 | tf_op jit(solution)/shard_map/ppermute | solution.py:427
  140.7 4.9 %copy-start.1 = (bf16[2048,1024]{1,0:T(8,128)(2,1)S(1)}, bf16[2048,1024]{1,0:T(8,128)(2,1)}, u32[]{:S(2)}) copy-start(bf16[2048,1024]{1,0:T(8,128)(2,1)} %copy-done) | copy-start | bytes 12582916
  140.7 4.9 %copy-start.3 = (bf16[2048,1024]{1,0:T(8,128)(2,1)S(1)}, bf16[2048,1024]{1,0:T(8,128)(2,1)}, u32[]{:S(2)}) copy-start(bf16[2048,1024]{1,0:T(8,128)(2,1)} %copy-done.2) | copy-start | bytes 12582916
  145.6 1.9 %copy-start.11 = (bf16[256,256]{1,0:T(8,128)(2,1)S(1)}, bf16[256,256]{1,0:T(8,128)(2,1)}, u32[]{:S(2)}) copy-start(bf16[256,256]{1,0:T(8,128)(2,1)} %hidden_weight.1) | copy-start | bytes 393220
  145.6 1.9 %copy-start.12 = (bf16[256,256]{1,0:T(8,128)(2,1)S(1)}, bf16[256,256]{1,0:T(8,128)(2,1)}, u32[]{:S(2)}) copy-start(bf16[256,256]{1,0:T(8,128)(2,1)} %output_weight.1) | copy-start | bytes 393220
  145.6 1.9 %copy-start.13 = (f32[2048]{0:T(1024)S(1)}, f32[2048]{0:T(1024)}, u32[]{:S(2)}) copy-start(f32[2048]{0:T(1024)} %param.16) | copy-start | bytes 24580

commit v9 on v8

--- a/solution.py
+++ b/solution.py
@@ -49,8 +49,29 @@
 
 
 def spread_body(
-    feat, tile, cell, spread, weight, send, slots, sent, rank_row, message, place, built, saves
+    tile,
+    far_feat,
+    far_cell,
+    far_spread,
+    far_weight,
+    send,
+    slots,
+    sent,
+    rank_row,
+    message,
+    place,
+    built,
+    feat,
+    cell,
+    spread,
+    weight,
+    saves,
+    loads,
 ):
+    pairs = ((far_feat, feat), (far_weight, weight), (far_spread, spread), (far_cell, cell))
+    copies = [pltpu.make_async_copy(a, b, loads.at[i]) for i, (a, b) in enumerate(pairs)]
+    for copy in copies:
+        copy.start()
     devices = built.shape[0]
     points = message.shape[0]
     cap = 24
@@ -67,6 +88,8 @@
         rank = jnp.sum(hot * before, axis=0, keepdims=True).astype(jnp.int32)
         rank_row[:, at : at + 256] = rank
         slots[:, at : at + 256] = tile[:, at : at + 256] * cap + rank
+    for copy in copies:
+        copy.wait()
     lane = iota((128, 128), 1)
 
     def weigh(step, carry):
@@ -458,18 +481,23 @@
             shape((1, points), jnp.int32),
             shape((points, width), BF16),
         ),
-        in_specs=[VMEM] * 5,
+        in_specs=[VMEM] + [anywhere] * 4,
         out_specs=[anywhere, VMEM, anywhere],
         scratch_shapes=[
             pltpu.VMEM((1, points), jnp.int32),
             pltpu.VMEM((points, width), BF16),
             pltpu.VMEM((points, 128), BF16),
             pltpu.VMEM((devices, 56, 128), BF16),
+            pltpu.VMEM((points, width), BF16),
+            pltpu.VMEM((1, points), jnp.int32),
+            pltpu.VMEM((1, points), F32),
+            pltpu.VMEM((width, width), BF16),
             pltpu.SemaphoreType.DMA((5,)),
+            pltpu.SemaphoreType.DMA((4,)),
         ],
         name="spread",
         compiler_params=pltpu.CompilerParams(vmem_limit_bytes=60 * 2**20),
-    )(features, tile, cell, spread_weight.reshape(1, points), message_weight)
+    )(tile, features, cell, spread_weight.reshape(1, points), message_weight)
     recv = lax.all_to_all(send, everyone, 0, 0, tiled=True)
     away = spectrum(message, tile, cell, basis, where, True)
     near = spectrum(message, tile, cell, basis, where, False)

time: 156 us -> 156 us (level)
  no operation moved by 1% of the time
where the time goes in v9:
time: 156 us
  Pallas kernels  52.3 us (34%)
  starting transfers between devices  50.6 us (32%)
  waiting for transfers between devices  47.2 us (30%)
  local copies, waits for them, and re-layouts  5.26 us (3%)
    pallas_call x12, Pallas kernels, call(): return fn(*ins)  29 us
    all_to_all x1, waiting for transfers between devices, per_device(): recv = lax.all_to_all(send, everyone, 0, 0, tiled=True)  21.7 us
    ppermute x12, waiting for transfers between devices, around(): return lax.ppermute(shard, ('z', 'core', 'ba'), pairs)  21.2 us
    ppermute x12, starting transfers between devices, around(): return lax.ppermute(shard, ('z', 'core', 'ba'), pairs)  17.3 us
    all_to_all x1, starting transfers between devices, per_device(): recv = lax.all_to_all(send, everyone, 0, 0, tiled=True)  11.5 us
    ppermute x5, starting transfers between devices, swapped(): return lax.ppermute(shard, 'core', [(0, 1), (1, 0)])  10.6 us
    pallas_call x1, Pallas kernels, per_device(): pl.pallas_call(spread_body, out_shape=(shape((devices, 56, 128), BF16), s...  10 us
    pallas_call x1, Pallas kernels, per_device(): pl.pallas_call(decode_body, out_shape=shape((points, width), BF16), in_sp...  7.97 us
  transfers between devices with their start and end apart: 25, of which 13 were waited for; matrix products, arithmetic and copies ran while one was open for 0% of the time, Pallas kernels for 22%

profile of v9, /device:TPU:1, one launch (start us, length us, event | category | flops | bytes accessed | tf_op | source)
XLA Modules:
  0.0 155.9 jit_solution(3634352121913885854)
XLA Ops:
  0.0 10.0 %spread.1 = (bf16[128,56,128]{2,1,0:T(8,128)(2,1)}, s32[1,2048]{1,0:T(1,128)}, bf16[2048,256]{1,0:T(8,128)(2,1)}) custom-call(s32[1,2048]{1,0:T(1,128)} %bitcast.7, bf16[2048,256]{1,0:T(8,128)(2,1)} %far_feat.1, s32[1,2048]{1,0:T(1,128)} %bitcast.11, f32[1,2048]{1,0:T(1,128)} %bitcast.16, bf16[256,256]{1,0:T(8,128)(2,1)} %far_weight.1), custom_call_target="tpu_custom_call" | custom-call | tf_op jit(solution)/shard_map/spread/pallas_call | solution.py:477
  10.0 0.0 copy-start.6
  10.1 0.0 copy-start.7
  10.1 0.0 copy-start.8
  10.1 0.0 copy-start.16
  10.1 11.5 %all-to-all-start = ((bf16[128,56,128]{2,1,0:T(8,128)(2,1)}), bf16[128,56,128]{2,1,0:T(8,128)(2,1)S(1)}, u32[]{:S(2)}, u32[]{:S(2)}) async-start(bf16[128,56,128]{2,1,0:T(8,128)(2,1)} %get-tuple-element.39), calls=%async_computation | async-start | bytes 3670016 | tf_op jit(solution)/shard_map/all_to_all | solution.py:501
  21.6 5.1 %shard_map.119 = bf16[2048,256]{1,0:T(8,128)(2,1)} custom-call(bf16[2048,256]{1,0:T(8,128)(2,1)S(1)} %copy-done.8, s32[1,2048]{1,0:T(1,128)S(1)} %bitcast.8, s32[1,2048]{1,0:T(1,128)S(1)} %bitcast.12, bf16[16,128]{1,0:T(8,128)(2,1)S(1)} %copy-done.16, s32[1]{0:T(128)} %bitcast.3.where), custom_call_target="tpu_custom_call" | custom-call | flops 2147483648 | bytes 4000000 | tf_op jit(solution)/shard_map/pallas_call | solution.py:48
  26.8 1.1 collective-permute-start
  27.8 21.7 %all-to-all-done.recv = bf16[128,56,128]{2,1,0:T(8,128)(2,1)S(1)} async-done(((bf16[128,56,128]{2,1,0:T(8,128)(2,1)}), bf16[128,56,128]{2,1,0:T(8,128)(2,1)S(1)}, u32[]{:S(2)}, u32[]{:S(2)}) %all-to-all-start) | async-done | bytes 1835040 | tf_op jit(solution)/shard_map/all_to_all | solution.py:501
  49.5 5.2 %shard_map.127 = (bf16[2048,256]{1,0:T(8,128)(2,1)S(1)}, bf16[1024,128]{1,0:T(8,128)(2,1)S(1)}) custom-call(bf16[128,56,128]{2,1,0:T(8,128)(2,1)S(1)} %all-to-all-done.recv), custom_call_target="tpu_custom_call" | custom-call | flops 3221225472 | bytes 4000000 | tf_op jit(solution)/shard_map/pallas_call | solution.py:48
  54.8 5.3 %reply.1 = bf16[128,24,256]{2,1,0:T(8,128)(2,1)} custom-call(bf16[2048,256]{1,0:T(8,128)(2,1)S(1)} %get-tuple-element.40.latent, bf16[1024,128]{1,0:T(8,128)(2,1)S(1)} %get-tuple-element.41.places, bf16[4,8,256,256]{3,2,1,0:T(8,128)(2,1)S(1)} %copy-done.4), custom_call_target="tpu_custom_call" | custom-call | flops 3221225472 | bytes 4000000 | tf_op jit(solution)/shard_map/reply/pallas_call | solution.py:527
  60.1 3.8 %all-to-all-start.1 = ((bf16[128,24,256]{2,1,0:T(8,128)(2,1)}), bf16[128,24,256]{2,1,0:T(8,128)(2,1)S(1)}, u32[]{:S(2)}, u32[]{:S(2)}) async-start(bf16[128,24,256]{2,1,0:T(8,128)(2,1)} %reply.1), calls=%async_computation.1 | async-start | bytes 3145728 | tf_op jit(solution)/shard_map/all_to_all | solution.py:550
  63.9 0.0 copy-start.9
  63.9 1.2 copy-done.9
  65.1 4.1 %shard_map.118.refs_0_ = bf16[2048,256]{1,0:T(8,128)(2,1)S(1)} custom-call(bf16[2048,256]{1,0:T(8,128)(2,1)S(1)} %copy-done.9, s32[1,2048]{1,0:T(1,128)S(1)} %bitcast.9, s32[1,2048]{1,0:T(1,128)S(1)} %bitcast.13, bf16[16,128]{1,0:T(8,128)(2,1)S(1)} %copy-done.16, s32[1]{0:T(128)} %bitcast.3.where), custom_call_target="tpu_custom_call" | custom-call | flops 2147483648 | bytes 4000000 | tf_op jit(solution)/shard_map/pallas_call | solution.py:48
  69.3 0.2 shard_map.120
  69.5 1.7 %collective-permute-start.1 = (bf16[512,256]{1,0:T(8,128)(2,1)S(1)}, bf16[512,256]{1,0:T(8,128)(2,1)S(1)}, u32[]{:S(2)}, u32[]{:S(2)}) collective-permute-start(bf16[512,256]{1,0:T(8,128)(2,1)S(1)} %get-tuple-element.26), channel_id=1, source_target_pairs={{0,1},{1,2},{2,3},{3,0},{4,36},{5,37},{6,38},{7,39},{32,33},{33,34... | collective-permute-start | bytes 786440 | tf_op jit(solution)/shard_map/ppermute | solution.py:439
  71.2 2.9 %collective-permute-start.2 = (bf16[512,256]{1,0:T(8,128)(2,1)S(1)}, bf16[512,256]{1,0:T(8,128)(2,1)S(1)}, u32[]{:S(2)}, u32[]{:S(2)}) collective-permute-start(bf16[512,256]{1,0:T(8,128)(2,1)S(1)} %get-tuple-element.27), channel_id=1, source_target_pairs={{0,2},{1,3},{2,0},{3,1},{4,68},{5,69},{6,70},{7,71},{32,34},{33,35... | collective-permute-start | bytes 786440 | tf_op jit(solution)/shard_map/ppermute | solution.py:439
  74.1 0.9 collective-permute-start.3
  75.0 13.1 %collective-permute-done.1.refs_1_ = bf16[512,256]{1,0:T(8,128)(2,1)S(1)} collective-permute-done((bf16[512,256]{1,0:T(8,128)(2,1)S(1)}, bf16[512,256]{1,0:T(8,128)(2,1)S(1)}, u32[]{:S(2)}, u32[]{:S(2)}) %collective-permute-start.1) | collective-permute-done | bytes 262176 | tf_op jit(solution)/shard_map/ppermute | solution.py:439
  88.1 2.9 %collective-permute-done.2.refs_2_ = bf16[512,256]{1,0:T(8,128)(2,1)S(1)} collective-permute-done((bf16[512,256]{1,0:T(8,128)(2,1)S(1)}, bf16[512,256]{1,0:T(8,128)(2,1)S(1)}, u32[]{:S(2)}, u32[]{:S(2)}) %collective-permute-start.2) | collective-permute-done | bytes 262176 | tf_op jit(solution)/shard_map/ppermute | solution.py:439
  91.0 0.1 shard_map.121
  91.2 1.2 collective-permute-start.4
  92.4 2.4 %collective-permute-start.5 = (bf16[128,256]{1,0:T(8,128)(2,1)S(1)}, bf16[128,256]{1,0:T(8,128)(2,1)S(1)}, u32[]{:S(2)}, u32[]{:S(2)}) collective-permute-start(bf16[128,256]{1,0:T(8,128)(2,1)S(1)} %get-tuple-element.31), channel_id=1, source_target_pairs={{0,64},{1,65},{2,66},{3,67},{4,6},{5,7},{6,4},{7,5},{32,96},{33,97... | collective-permute-start | bytes 196616 | tf_op jit(solution)/shard_map/ppermute | solution.py:439
  94.9 0.9 collective-permute-start.6
  95.8 0.0 collective-permute-done.4.refs_1_
  95.8 1.7 %collective-permute-done.5.refs_2_ = bf16[128,256]{1,0:T(8,128)(2,1)S(1)} collective-permute-done((bf16[128,256]{1,0:T(8,128)(2,1)S(1)}, bf16[128,256]{1,0:T(8,128)(2,1)S(1)}, u32[]{:S(2)}, u32[]{:S(2)}) %collective-permute-start.5) | collective-permute-done | bytes 65568 | tf_op jit(solution)/shard_map/ppermute | solution.py:439
  97.5 0.5 collective-permute-done.6.refs_3_
  98.0 0.7 collective-permute-start.7
  98.7 2.3 %collective-permute-start.8 = (bf16[32,256]{1,0:T(8,128)(2,1)S(1)}, bf16[32,256]{1,0:T(8,128)(2,1)S(1)}, u32[]{:S(2)}, u32[]{:S(2)}) collective-permute-start(bf16[32,256]{1,0:T(8,128)(2,1)S(1)} %get-tuple-element.35), channel_id=1, source_target_pairs={{0,16},{8,24},{16,0},{24,8},{1,17},{9,25},{17,1},{25,9},{2,18},{10... | collective-permute-start | bytes 49160 | tf_op jit(solution)/shard_map/ppermute | solution.py:431
  101.0 1.2 collective-permute-start.9
  102.2 0.6 collective-permute-done.8.c
  102.8 1.1 collective-permute-done.9.d
  103.9 0.7 shard_map.123.refs_0_
  104.6 0.4 collective-permute-start.10
  105.0 2.9 %collective-permute-start.11 = (bf16[32,256]{1,0:T(8,128)(2,1)S(1)}, bf16[32,256]{1,0:T(8,128)(2,1)S(1)}, u32[]{:S(2)}, u32[]{:S(2)}) collective-permute-start(bf16[32,256]{1,0:T(8,128)(2,1)S(1)} %shard_map.123.refs_0_), channel_id=1, source_target_pairs={{0,16},{8,24},{16,0},{24,8},{1,17},{9,25},{17,1},{25,9},{2,18},{10... | collective-permute-start | bytes 49160 | tf_op jit(solution)/shard_map/ppermute | solution.py:431
  107.8 0.0 collective-permute-start.12
  107.9 0.5 collective-permute-done.10.refs_1_
  108.4 0.8 collective-permute-done.11.refs_2_
  109.1 1.3 collective-permute-done.12.refs_3_
  110.5 0.4 collective-permute-start.13
  110.9 3.2 %collective-permute-start.14 = (bf16[128,256]{1,0:T(8,128)(2,1)S(1)}, bf16[128,256]{1,0:T(8,128)(2,1)S(1)}, u32[]{:S(2)}, u32[]{:S(2)}) collective-permute-start(bf16[128,256]{1,0:T(8,128)(2,1)S(1)} %shard_map.124.refs_0_), channel_id=1, source_target_pairs={{0,64},{1,65},{2,66},{3,67},{4,6},{5,7},{6,4},{7,5},{32,96},{33,97... | collective-permute-start | bytes 196616 | tf_op jit(solution)/shard_map/ppermute | solution.py:439
  114.1 0.1 collective-permute-start.15
  114.2 0.7 collective-permute-done.13.refs_1_
  114.9 1.6 %collective-permute-done.14.refs_2_ = bf16[128,256]{1,0:T(8,128)(2,1)S(1)} collective-permute-done((bf16[128,256]{1,0:T(8,128)(2,1)S(1)}, bf16[128,256]{1,0:T(8,128)(2,1)S(1)}, u32[]{:S(2)}, u32[]{:S(2)}) %collective-permute-start.14) | collective-permute-done | bytes 65568 | tf_op jit(solution)/shard_map/ppermute | solution.py:439
  116.4 0.8 collective-permute-done.15.refs_3_
  117.2 0.1 collective-permute-start.16
  117.3 1.3 collective-permute-start.17
  118.6 2.0 %collective-permute-start.18 = (bf16[512,256]{1,0:T(8,128)(2,1)S(1)}, bf16[512,256]{1,0:T(8,128)(2,1)S(1)}, u32[]{:S(2)}, u32[]{:S(2)}) collective-permute-start(bf16[512,256]{1,0:T(8,128)(2,1)S(1)} %shard_map.125.near), channel_id=1, source_target_pairs={{0,3},{1,0},{2,1},{3,2},{4,100},{5,101},{6,102},{7,103},{32,35},{3... | collective-permute-start | bytes 786440 | tf_op jit(solution)/shard_map/ppermute | solution.py:439
  120.6 6.8 %shard_map.126 = (bf16[2048,1024]{1,0:T(8,128)(2,1)S(1)}, bf16[2048,1024]{1,0:T(8,128)(2,1)S(1)}) custom-call(s32[1,2048]{1,0:T(1,128)S(1)} %bitcast.10, s32[1,2048]{1,0:T(1,128)S(1)} %bitcast.14, bf16[128,16]{1,0:T(8,128)(2,1)S(1)} %copy-done.15, s32[1]{0:T(128)} %bitcast.3.where), custom_call_target="tpu_custom_call" | custom-call | flops 1000000000 | bytes 4000000 | tf_op jit(solution)/shard_map/pallas_call | solution.py:48
  127.4 1.9 %copy-done = bf16[2048,1024]{1,0:T(8,128)(2,1)} copy-done((bf16[2048,1024]{1,0:T(8,128)(2,1)}, bf16[2048,1024]{1,0:T(8,128)(2,1)S(1)}, u32[]{:S(2)}) %copy-start) | copy-done | bytes 4194328
  129.4 2.0 %copy-done.2 = bf16[2048,1024]{1,0:T(8,128)(2,1)} copy-done((bf16[2048,1024]{1,0:T(8,128)(2,1)}, bf16[2048,1024]{1,0:T(8,128)(2,1)S(1)}, u32[]{:S(2)}) %copy-start.2) | copy-done | bytes 4194328
  131.4 8.9 %collective-permute-start.22 = (bf16[512,256]{1,0:T(8,128)(2,1)S(1)}, bf16[512,256]{1,0:T(8,128)(2,1)S(1)}, u32[]{:S(2)}, u32[]{:S(2)}) collective-permute-start(bf16[512,256]{1,0:T(8,128)(2,1)S(1)} %shard_map.125.near), channel_id=1, source_target_pairs={{0,4},{4,0},{1,5},{5,1},{2,6},{6,2},{3,7},{7,3},{8,12},{12,8},{9,1... | collective-permute-start | bytes 786440 | tf_op jit(solution)/shard_map/ppermute | solution.py:450
  140.3 0.0 collective-permute-done.16.m1
  140.3 0.0 collective-permute-start.19
  140.3 0.0 collective-permute-done.17.m2
  140.3 0.5 collective-permute-start.20
  140.8 0.1 collective-permute-start.21
  140.9 4.8 %shard_map.128.base = f32[2048,256]{1,0:T(8,128)S(1)} custom-call(bf16[3072,256]{1,0:T(8,128)(2,1)S(1)} %bitcast.6, s32[1,2048]{1,0:T(1,128)S(1)} %copy-done.14, bf16[256,256]{1,0:T(8,128)(2,1)S(1)} %copy-done.10), custom_call_target="tpu_custom_call" | custom-call | flops 3221225472 | bytes 4000000 | tf_op jit(solution)/shard_map/pallas_call | solution.py:48
  145.8 0.0 copy-start.11
  145.8 0.0 copy-start.12
  145.8 0.0 copy-start.13
  145.8 1.8 %shard_map.129.base = f32[2048,256]{1,0:T(8,128)S(1)} custom-call(bf16[512,256]{1,0:T(8,128)(2,1)S(1)} %shard_map.125.near, bf16[512,256]{1,0:T(8,128)(2,1)S(1)} %collective-permute-done.22.far, bf16[2048,1024]{1,0:T(8,128)(2,1)S(1)} %copy-done.1, bf16[2048,1024]{1,0:T(8,128)(2,1)S(1)} %copy-done.3, f32[2048,256]{1,0:T(8,128)S(1)} %shard_map.128.base), custom_call_target="tpu_custom_call" | custom-call | flops 1073741824 | bytes 4000000 | tf_op jit(solution)/shard_map/pallas_call | solution.py:48
  147.7 8.0 %decode.1 = bf16[2048,256]{1,0:T(8,128)(2,1)} custom-call(bf16[512,256]{1,0:T(8,128)(2,1)S(1)} %collective-permute-done.16.m1, bf16[512,256]{1,0:T(8,128)(2,1)S(1)} %collective-permute-done.17.m2, bf16[512,256]{1,0:T(8,128)(2,1)S(1)} %collective-permute-done.18.m3, bf16[512,256]{1,0:T(8,128)(2,1)S(1)} %collective-permute-done.19.m5, ...), custom_call_target="tpu_custom_call" | custom-call | flops 4294967296 | bytes 4000000 | tf_op jit(solution)/shard_map/decode/pallas_call | solution.py:568
  (35 shorter events, 0.1 us)
Async XLA Ops:
  10.0 11.6 %copy-start.6 = (s32[2048,1]{0,1:T(1,128)S(1)}, s32[2048,1]{0,1:T(1,128)}, u32[]{:S(2)}) copy-start(s32[2048,1]{0,1:T(1,128)} %param.13) | copy-start | bytes 24580
  10.1 11.6 %copy-start.7 = (s32[2048]{0:T(1024)S(1)}, s32[2048]{0:T(1024)}, u32[]{:S(2)}) copy-start(s32[2048]{0:T(1024)} %param.14) | copy-start | bytes 24580
  10.1 11.6 %copy-start.8 = (bf16[2048,256]{1,0:T(8,128)(2,1)S(1)}, bf16[2048,256]{1,0:T(8,128)(2,1)}, u32[]{:S(2)}) copy-start(bf16[2048,256]{1,0:T(8,128)(2,1)} %get-tuple-element.24.message) | copy-start | bytes 3145732
  10.1 11.6 %copy-start.16 = (bf16[16,128]{1,0:T(8,128)(2,1)S(1)}, bf16[16,128]{1,0:T(8,128)(2,1)}, u32[]{:S(2)}) copy-start(bf16[16,128]{1,0:T(8,128)(2,1)} %constant.26.clone.basis) | copy-start | bytes 12292
  10.1 39.5 %all-to-all-start = ((bf16[128,56,128]{2,1,0:T(8,128)(2,1)}), bf16[128,56,128]{2,1,0:T(8,128)(2,1)S(1)}, u32[]{:S(2)}, u32[]{:S(2)}) async-start(bf16[128,56,128]{2,1,0:T(8,128)(2,1)} %get-tuple-element.39), calls=%async_computation | async-start | bytes 3670016 | tf_op jit(solution)/shard_map/all_to_all | solution.py:501
  26.8 42.5 %collective-permute-start = (bf16[2048,256]{1,0:T(8,128)(2,1)}, bf16[2048,256]{1,0:T(8,128)(2,1)S(1)}, u32[]{:S(2)}, u32[]{:S(2)}) collective-permute-start(bf16[2048,256]{1,0:T(8,128)(2,1)} %shard_map.119), channel_id=1, source_target_pairs={{0,4},{4,0},{1,5},{5,1},{2,6},{6,2},{3,7},{7,3},{8,12},{12,8},{9,1... | collective-permute-start | bytes 3145736 | tf_op jit(solution)/shard_map/ppermute | solution.py:450
  49.5 5.2 %copy-start.4 = (bf16[4,8,256,256]{3,2,1,0:T(8,128)(2,1)S(1)}, bf16[4,8,256,256]{3,2,1,0:T(8,128)(2,1)}, u32[]{:S(2)}) copy-start(bf16[4,8,256,256]{3,2,1,0:T(8,128)(2,1)} %weight.3) | copy-start | bytes 12582916
  60.1 80.9 %all-to-all-start.1 = ((bf16[128,24,256]{2,1,0:T(8,128)(2,1)}), bf16[128,24,256]{2,1,0:T(8,128)(2,1)S(1)}, u32[]{:S(2)}, u32[]{:S(2)}) async-start(bf16[128,24,256]{2,1,0:T(8,128)(2,1)} %reply.1), calls=%async_computation.1 | async-start | bytes 3145728 | tf_op jit(solution)/shard_map/all_to_all | solution.py:550
  63.9 1.2 copy-start.9
  65.1 38.8 %copy-start.5 = (bf16[4,8,256,256]{3,2,1,0:T(8,128)(2,1)S(1)}, bf16[4,8,256,256]{3,2,1,0:T(8,128)(2,1)}, u32[]{:S(2)}) copy-start(bf16[4,8,256,256]{3,2,1,0:T(8,128)(2,1)} %weight.3) | copy-start | bytes 12582916
  69.5 18.6 %collective-permute-start.1 = (bf16[512,256]{1,0:T(8,128)(2,1)S(1)}, bf16[512,256]{1,0:T(8,128)(2,1)S(1)}, u32[]{:S(2)}, u32[]{:S(2)}) collective-permute-start(bf16[512,256]{1,0:T(8,128)(2,1)S(1)} %get-tuple-element.26), channel_id=1, source_target_pairs={{0,1},{1,2},{2,3},{3,0},{4,36},{5,37},{6,38},{7,39},{32,33},{33,34... | collective-permute-start | bytes 786440 | tf_op jit(solution)/shard_map/ppermute | solution.py:439
  71.2 19.8 %collective-permute-start.2 = (bf16[512,256]{1,0:T(8,128)(2,1)S(1)}, bf16[512,256]{1,0:T(8,128)(2,1)S(1)}, u32[]{:S(2)}, u32[]{:S(2)}) collective-permute-start(bf16[512,256]{1,0:T(8,128)(2,1)S(1)} %get-tuple-element.27), channel_id=1, source_target_pairs={{0,2},{1,3},{2,0},{3,1},{4,68},{5,69},{6,70},{7,71},{32,34},{33,35... | collective-permute-start | bytes 786440 | tf_op jit(solution)/shard_map/ppermute | solution.py:439
  74.1 16.9 %collective-permute-start.3 = (bf16[512,256]{1,0:T(8,128)(2,1)S(1)}, bf16[512,256]{1,0:T(8,128)(2,1)S(1)}, u32[]{:S(2)}, u32[]{:S(2)}) collective-permute-start(bf16[512,256]{1,0:T(8,128)(2,1)S(1)} %get-tuple-element.28), channel_id=1, source_target_pairs={{0,3},{1,0},{2,1},{3,2},{4,100},{5,101},{6,102},{7,103},{32,35},{3... | collective-permute-start | bytes 786440 | tf_op jit(solution)/shard_map/ppermute | solution.py:439
  91.2 4.6 %collective-permute-start.4 = (bf16[128,256]{1,0:T(8,128)(2,1)S(1)}, bf16[128,256]{1,0:T(8,128)(2,1)S(1)}, u32[]{:S(2)}, u32[]{:S(2)}) collective-permute-start(bf16[128,256]{1,0:T(8,128)(2,1)S(1)} %get-tuple-element.30), channel_id=1, source_target_pairs={{0,32},{1,33},{2,34},{3,35},{4,5},{5,6},{6,7},{7,4},{32,64},{33,65... | collective-permute-start | bytes 196616 | tf_op jit(solution)/shard_map/ppermute | solution.py:439
  92.4 5.1 %collective-permute-start.5 = (bf16[128,256]{1,0:T(8,128)(2,1)S(1)}, bf16[128,256]{1,0:T(8,128)(2,1)S(1)}, u32[]{:S(2)}, u32[]{:S(2)}) collective-permute-start(bf16[128,256]{1,0:T(8,128)(2,1)S(1)} %get-tuple-element.31), channel_id=1, source_target_pairs={{0,64},{1,65},{2,66},{3,67},{4,6},{5,7},{6,4},{7,5},{32,96},{33,97... | collective-permute-start | bytes 196616 | tf_op jit(solution)/shard_map/ppermute | solution.py:439
  94.9 3.1 %collective-permute-start.6 = (bf16[128,256]{1,0:T(8,128)(2,1)S(1)}, bf16[128,256]{1,0:T(8,128)(2,1)S(1)}, u32[]{:S(2)}, u32[]{:S(2)}) collective-permute-start(bf16[128,256]{1,0:T(8,128)(2,1)S(1)} %get-tuple-element.32), channel_id=1, source_target_pairs={{0,96},{1,97},{2,98},{3,99},{4,7},{5,4},{6,5},{7,6},{32,0},{33,1},... | collective-permute-start | bytes 196616 | tf_op jit(solution)/shard_map/ppermute | solution.py:439
  98.0 4.2 %collective-permute-start.7 = (bf16[32,256]{1,0:T(8,128)(2,1)S(1)}, bf16[32,256]{1,0:T(8,128)(2,1)S(1)}, u32[]{:S(2)}, u32[]{:S(2)}) collective-permute-start(bf16[32,256]{1,0:T(8,128)(2,1)S(1)} %get-tuple-element.34), channel_id=1, source_target_pairs={{0,8},{8,16},{16,24},{24,0},{1,9},{9,17},{17,25},{25,1},{2,10},{10... | collective-permute-start | bytes 49160 | tf_op jit(solution)/shard_map/ppermute | solution.py:431
  98.7 4.1 %collective-permute-start.8 = (bf16[32,256]{1,0:T(8,128)(2,1)S(1)}, bf16[32,256]{1,0:T(8,128)(2,1)S(1)}, u32[]{:S(2)}, u32[]{:S(2)}) collective-permute-start(bf16[32,256]{1,0:T(8,128)(2,1)S(1)} %get-tuple-element.35), channel_id=1, source_target_pairs={{0,16},{8,24},{16,0},{24,8},{1,17},{9,25},{17,1},{25,9},{2,18},{10... | collective-permute-start | bytes 49160 | tf_op jit(solution)/shard_map/ppermute | solution.py:431
  101.0 2.9 %collective-permute-start.9 = (bf16[32,256]{1,0:T(8,128)(2,1)S(1)}, bf16[32,256]{1,0:T(8,128)(2,1)S(1)}, u32[]{:S(2)}, u32[]{:S(2)}) collective-permute-start(bf16[32,256]{1,0:T(8,128)(2,1)S(1)} %get-tuple-element.36), channel_id=1, source_target_pairs={{0,24},{8,0},{16,8},{24,16},{1,25},{9,1},{17,9},{25,17},{2,26},{10... | collective-permute-start | bytes 49160 | tf_op jit(solution)/shard_map/ppermute | solution.py:431
  103.9 16.7 %copy-start.15 = (bf16[128,16]{1,0:T(8,128)(2,1)S(1)}, bf16[128,16]{1,0:T(8,128)(2,1)}, u32[]{:S(2)}) copy-start(bf16[128,16]{1,0:T(8,128)(2,1)} %constant.27.clone.basis) | copy-start | bytes 12292
  104.6 3.8 %collective-permute-start.10 = (bf16[32,256]{1,0:T(8,128)(2,1)S(1)}, bf16[32,256]{1,0:T(8,128)(2,1)S(1)}, u32[]{:S(2)}, u32[]{:S(2)}) collective-permute-start(bf16[32,256]{1,0:T(8,128)(2,1)S(1)} %shard_map.123.refs_0_), channel_id=1, source_target_pairs={{0,8},{8,16},{16,24},{24,0},{1,9},{9,17},{17,25},{25,1},{2,10},{10... | collective-permute-start | bytes 49160 | tf_op jit(solution)/shard_map/ppermute | solution.py:431
  105.0 4.2 %collective-permute-start.11 = (bf16[32,256]{1,0:T(8,128)(2,1)S(1)}, bf16[32,256]{1,0:T(8,128)(2,1)S(1)}, u32[]{:S(2)}, u32[]{:S(2)}) collective-permute-start(bf16[32,256]{1,0:T(8,128)(2,1)S(1)} %shard_map.123.refs_0_), channel_id=1, source_target_pairs={{0,16},{8,24},{16,0},{24,8},{1,17},{9,25},{17,1},{25,9},{2,18},{10... | collective-permute-start | bytes 49160 | tf_op jit(solution)/shard_map/ppermute | solution.py:431
  107.8 2.6 %collective-permute-start.12 = (bf16[32,256]{1,0:T(8,128)(2,1)S(1)}, bf16[32,256]{1,0:T(8,128)(2,1)S(1)}, u32[]{:S(2)}, u32[]{:S(2)}) collective-permute-start(bf16[32,256]{1,0:T(8,128)(2,1)S(1)} %shard_map.123.refs_0_), channel_id=1, source_target_pairs={{0,24},{8,0},{16,8},{24,16},{1,25},{9,1},{17,9},{25,17},{2,26},{10... | collective-permute-start | bytes 49160 | tf_op jit(solution)/shard_map/ppermute | solution.py:431
  110.4 30.5 %copy-start.10 = (bf16[256,256]{1,0:T(8,128)(2,1)S(1)}, bf16[256,256]{1,0:T(8,128)(2,1)}, u32[]{:S(2)}) copy-start(bf16[256,256]{1,0:T(8,128)(2,1)} %skip.1) | copy-start | bytes 393220
  110.4 30.5 %copy-start.14 = (s32[1,2048]{1,0:T(1,128)S(1)}, s32[1,2048]{1,0:T(1,128)}, u32[]{:S(2)}) copy-start(s32[1,2048]{1,0:T(1,128)} %get-tuple-element.42.slots) | copy-start | bytes 24580
  110.5 4.4 %collective-permute-start.13 = (bf16[128,256]{1,0:T(8,128)(2,1)S(1)}, bf16[128,256]{1,0:T(8,128)(2,1)S(1)}, u32[]{:S(2)}, u32[]{:S(2)}) collective-permute-start(bf16[128,256]{1,0:T(8,128)(2,1)S(1)} %shard_map.124.refs_0_), channel_id=1, source_target_pairs={{0,32},{1,33},{2,34},{3,35},{4,5},{5,6},{6,7},{7,4},{32,64},{33,65... | collective-permute-start | bytes 196616 | tf_op jit(solution)/shard_map/ppermute | solution.py:439
  110.9 5.5 %collective-permute-start.14 = (bf16[128,256]{1,0:T(8,128)(2,1)S(1)}, bf16[128,256]{1,0:T(8,128)(2,1)S(1)}, u32[]{:S(2)}, u32[]{:S(2)}) collective-permute-start(bf16[128,256]{1,0:T(8,128)(2,1)S(1)} %shard_map.124.refs_0_), channel_id=1, source_target_pairs={{0,64},{1,65},{2,66},{3,67},{4,6},{5,7},{6,4},{7,5},{32,96},{33,97... | collective-permute-start | bytes 196616 | tf_op jit(solution)/shard_map/ppermute | solution.py:439
  114.1 3.1 %collective-permute-start.15 = (bf16[128,256]{1,0:T(8,128)(2,1)S(1)}, bf16[128,256]{1,0:T(8,128)(2,1)S(1)}, u32[]{:S(2)}, u32[]{:S(2)}) collective-permute-start(bf16[128,256]{1,0:T(8,128)(2,1)S(1)} %shard_map.124.refs_0_), channel_id=1, source_target_pairs={{0,96},{1,97},{2,98},{3,99},{4,7},{5,4},{6,5},{7,6},{32,0},{33,1},... | collective-permute-start | bytes 196616 | tf_op jit(solution)/shard_map/ppermute | solution.py:439
  117.2 23.1 %collective-permute-start.16 = (bf16[512,256]{1,0:T(8,128)(2,1)S(1)}, bf16[512,256]{1,0:T(8,128)(2,1)S(1)}, u32[]{:S(2)}, u32[]{:S(2)}) collective-permute-start(bf16[512,256]{1,0:T(8,128)(2,1)S(1)} %shard_map.125.near), channel_id=1, source_target_pairs={{0,1},{1,2},{2,3},{3,0},{4,36},{5,37},{6,38},{7,39},{32,33},{33,34... | collective-permute-start | bytes 786440 | tf_op jit(solution)/shard_map/ppermute | solution.py:439
  117.3 23.0 %collective-permute-start.17 = (bf16[512,256]{1,0:T(8,128)(2,1)S(1)}, bf16[512,256]{1,0:T(8,128)(2,1)S(1)}, u32[]{:S(2)}, u32[]{:S(2)}) collective-permute-start(bf16[512,256]{1,0:T(8,128)(2,1)S(1)} %shard_map.125.near), channel_id=1, source_target_pairs={{0,2},{1,3},{2,0},{3,1},{4,68},{5,69},{6,70},{7,71},{32,34},{33,35... | collective-permute-start | bytes 786440 | tf_op jit(solution)/shard_map/ppermute | solution.py:439
  118.6 22.2 %collective-permute-start.18 = (bf16[512,256]{1,0:T(8,128)(2,1)S(1)}, bf16[512,256]{1,0:T(8,128)(2,1)S(1)}, u32[]{:S(2)}, u32[]{:S(2)}) collective-permute-start(bf16[512,256]{1,0:T(8,128)(2,1)S(1)} %shard_map.125.near), channel_id=1, source_target_pairs={{0,3},{1,0},{2,1},{3,2},{4,100},{5,101},{6,102},{7,103},{32,35},{3... | collective-permute-start | bytes 786440 | tf_op jit(solution)/shard_map/ppermute | solution.py:439
  127.4 2.0 %copy-start = (bf16[2048,1024]{1,0:T(8,128)(2,1)}, bf16[2048,1024]{1,0:T(8,128)(2,1)S(1)}, u32[]{:S(2)}) copy-start(bf16[2048,1024]{1,0:T(8,128)(2,1)S(1)} %get-tuple-element.37.wave_p) | copy-start | bytes 12582916
  129.4 2.0 %copy-start.2 = (bf16[2048,1024]{1,0:T(8,128)(2,1)}, bf16[2048,1024]{1,0:T(8,128)(2,1)S(1)}, u32[]{:S(2)}) copy-start(bf16[2048,1024]{1,0:T(8,128)(2,1)S(1)} %get-tuple-element.38.wave_qz) | copy-start | bytes 12582916
  131.4 14.4 %collective-permute-start.22 = (bf16[512,256]{1,0:T(8,128)(2,1)S(1)}, bf16[512,256]{1,0:T(8,128)(2,1)S(1)}, u32[]{:S(2)}, u32[]{:S(2)}) collective-permute-start(bf16[512,256]{1,0:T(8,128)(2,1)S(1)} %shard_map.125.near), channel_id=1, source_target_pairs={{0,4},{4,0},{1,5},{5,1},{2,6},{6,2},{3,7},{7,3},{8,12},{12,8},{9,1... | collective-permute-start | bytes 786440 | tf_op jit(solution)/shard_map/ppermute | solution.py:450
  140.3 7.4 %collective-permute-start.19 = (bf16[512,256]{1,0:T(8,128)(2,1)S(1)}, bf16[512,256]{1,0:T(8,128)(2,1)S(1)}, u32[]{:S(2)}, u32[]{:S(2)}) collective-permute-start(bf16[512,256]{1,0:T(8,128)(2,1)S(1)} %collective-permute-done.16.m1), channel_id=1, source_target_pairs={{0,4},{4,0},{1,5},{5,1},{2,6},{6,2},{3,7},{7,3},{8,12},{12,8},{9,1... | collective-permute-start | bytes 786440 | tf_op jit(solution)/shard_map/ppermute | solution.py:450
  140.3 7.4 %collective-permute-start.20 = (bf16[512,256]{1,0:T(8,128)(2,1)S(1)}, bf16[512,256]{1,0:T(8,128)(2,1)S(1)}, u32[]{:S(2)}, u32[]{:S(2)}) collective-permute-start(bf16[512,256]{1,0:T(8,128)(2,1)S(1)} %collective-permute-done.17.m2), channel_id=1, source_target_pairs={{0,4},{4,0},{1,5},{5,1},{2,6},{6,2},{3,7},{7,3},{8,12},{12,8},{9,1... | collective-permute-start | bytes 786440 | tf_op jit(solution)/shard_map/ppermute | solution.py:450
  140.8 6.9 %collective-permute-start.21 = (bf16[512,256]{1,0:T(8,128)(2,1)S(1)}, bf16[512,256]{1,0:T(8,128)(2,1)}, u32[]{:S(2)}, u32[]{:S(2)}) collective-permute-start(bf16[512,256]{1,0:T(8,128)(2,1)S(1)} %collective-permute-done.18.m3), channel_id=1, source_target_pairs={{0,4},{4,0},{1,5},{5,1},{2,6},{6,2},{3,7},{7,3},{8,12},{12,8},{9,1... | collective-permute-start | bytes 786440 | tf_op jit(solution)/shard_map/ppermute | solution.py:450
  140.9 4.9 %copy-start.1 = (bf16[2048,1024]{1,0:T(8,128)(2,1)S(1)}, bf16[2048,1024]{1,0:T(8,128)(2,1)}, u32[]{:S(2)}) copy-start(bf16[2048,1024]{1,0:T(8,128)(2,1)} %copy-done) | copy-start | bytes 12582916
  140.9 4.9 %copy-start.3 = (bf16[2048,1024]{1,0:T(8,128)(2,1)S(1)}, bf16[2048,1024]{1,0:T(8,128)(2,1)}, u32[]{:S(2)}) copy-start(bf16[2048,1024]{1,0:T(8,128)(2,1)} %copy-done.2) | copy-start | bytes 12582916
  145.8 1.9 %copy-start.11 = (bf16[256,256]{1,0:T(8,128)(2,1)S(1)}, bf16[256,256]{1,0:T(8,128)(2,1)}, u32[]{:S(2)}) copy-start(bf16[256,256]{1,0:T(8,128)(2,1)} %hidden_weight.1) | copy-start | bytes 393220
  145.8 1.9 %copy-start.12 = (bf16[256,256]{1,0:T(8,128)(2,1)S(1)}, bf16[256,256]{1,0:T(8,128)(2,1)}, u32[]{:S(2)}) copy-start(bf16[256,256]{1,0:T(8,128)(2,1)} %output_weight.1) | copy-start | bytes 393220
  145.8 1.9 %copy-start.13 = (f32[2048]{0:T(1024)S(1)}, f32[2048]{0:T(1024)}, u32[]{:S(2)}) copy-start(f32[2048]{0:T(1024)} %param.16) | copy-start | bytes 24580

commit v10 on v8

--- a/solution.py
+++ b/solution.py
@@ -133,16 +133,21 @@
     return lax.bitwise_and(lax.shift_right_logical(value, low), mask)
 
 
+def flipped(at, group):
+    low = bits(group, 0, 1)
+    return lax.bitwise_xor(at, lax.bitwise_xor(low, bits(group, 1, 1)) + 2 * low)
+
+
 def spectrum_body(message, tile, cell, basis, where, out, xy, away):
     points = message.shape[0]
     at_z, at_y, core, at_b = device_at(where)
     core = 1 - core if away else core
     r = iota((256, 16), 0)
     wide, near, last, j4 = bits(r, 6, 3), bits(r, 4, 3), bits(r, 2, 3), bits(r, 0, 3)
-    shift_x = near + core * (wide - near)
-    shift_y = wide + near - shift_x
-    mode_x = 4 * bits(at_z + shift_x, 0, 3) + bits(at_y + last, 0, 3)
-    mode_y = 4 * bits(at_b + shift_y, 0, 3) + j4
+    straight = jnp.full(r.shape, core, jnp.int32) == 0
+    turn_z, turn_b = flipped(at_z, near), flipped(at_b, near)
+    mode_x = 4 * jnp.where(straight, turn_z, bits(at_z + wide, 0, 3)) + flipped(at_y, last)
+    mode_y = 4 * jnp.where(straight, bits(at_b + wide, 0, 3), turn_b) + j4
     mode_z = 8 * core + iota((8, 16), 0)
     x, y, z = positions(tile[...], cell[...])
     row = lax.bitwise_and(iota((128, points), 0), 63)
@@ -176,20 +181,20 @@
     )
 
 
-def add_body(*refs):
-    count = len(refs) - 4
+def add_body(*refs, cuts):
+    count = len(refs) - cuts
     total = refs[0][...].astype(F32)
     for r in refs[1:count]:
         total = total + r[...].astype(F32)
-    rows = total.shape[0] // 4
-    for s in range(4):
+    rows = total.shape[0] // cuts
+    for s in range(cuts):
         refs[count + s][...] = total[s * rows : s * rows + rows].astype(BF16)
 
 
-def add_and_cut(parts):
+def add_and_cut(parts, cuts):
     rows, width = parts[0].shape
-    piece = jax.ShapeDtypeStruct((rows // 4, width), BF16)
-    return call(add_body, (piece,) * 4, parts, ())
+    piece = jax.ShapeDtypeStruct((rows // cuts, width), BF16)
+    return call(functools.partial(add_body, cuts=cuts), (piece,) * cuts, parts, ())
 
 
 def join_body(*refs):
@@ -201,6 +206,21 @@
 def joined(parts):
     rows, width = parts[0].shape
     return call(join_body, jax.ShapeDtypeStruct((rows * 4, width), BF16), parts, ())
+
+
+def total_cells(ids, rows, latent, first):
+    tile = 512
+
+    def total(step, carry):
+        at = step * tile
+        cells = iota((tile, 128), 0) + (at + first)
+        hot = [
+            (ids[i, g : g + 1, :] == cells).astype(BF16) for i in range(8) for g in range(3)
+        ]
+        latent[pl.ds(at, tile), :] = mm(jnp.concatenate(hot, axis=1), rows[...]).astype(BF16)
+        return carry
+
+    lax.fori_loop(0, latent.shape[0] // tile, total, 0)
 
 
 def collect_body(recv, latent, places, rows, ids):
@@ -223,35 +243,29 @@
         return carry
 
     lax.fori_loop(0, 8, unpack, 0)
-    tile = 512
-
-    def total(step, carry):
-        at = step * tile
-        cells = iota((tile, 128), 0) + at
-        hot = [
-            (ids[i, g : g + 1, :] == cells).astype(BF16) for i in range(8) for g in range(3)
-        ]
-        latent[pl.ds(at, tile), :] = mm(jnp.concatenate(hot, axis=1), rows[...]).astype(BF16)
-        return carry
-
-    lax.fori_loop(0, latent.shape[0] // tile, total, 0)
-
-
-def reply_body(latent, places, weight, out, built, saves):
+    total_cells(ids, rows, latent, 0)
+
+
+def collect_more_body(rows, ids, latent):
+    total_cells(ids, rows, latent, latent.shape[0])
+
+
+def reply_body(low, high, places, *refs, first):
+    out, built, saves = refs[-3:]
     lane = iota((128, 128), 0)
-    column = iota((256, 128), 1)
-
     many = 32
+    column = iota((many * 8, 128), 1)
 
     def back(step, carry):
-        place = places[pl.ds(step * many * 8, many * 8), :]
+        place = places[pl.ds((step + first) * many * 8, many * 8), :]
         tall = []
         for g in range(3):
             pick = jnp.where(lane == 2 * g, 64.0, jnp.where(lane == 2 * g + 1, 1.0, 0.0))
             cell = mm(place, pick.astype(BF16)).astype(jnp.int32)
             hot = [(cell == column + 128 * k).astype(BF16) for k in range(16)]
             tall.append(jnp.concatenate(hot, axis=1))
-        got = mm(jnp.concatenate(tall, axis=0), latent[...])
+        tall = jnp.concatenate(tall, axis=0)
+        got = mm(tall[:, :1024], low[...]) + mm(tall[:, 1024:], high[...])
         for g in range(3):
             piece = got[g * many * 8 : (g + 1) * many * 8]
             piece = piece.reshape(many, 8, 256).astype(BF16)
@@ -260,16 +274,36 @@
         return carry
 
     def save(step):
-        rows = pl.ds(step * many, many)
-        return pltpu.make_async_copy(built.at[rows], out.at[rows], saves.at[step])
-
-    lax.fori_loop(0, 4, back, 0)
-    for step in range(4):
+        source = built.at[pl.ds(step * many, many)]
+        target = out.at[pl.ds((step + first) * many, many)]
+        return pltpu.make_async_copy(source, target, saves.at[step])
+
+    lax.fori_loop(0, 2, back, 0)
+    for step in range(2):
         save(step).wait()
 
 
-def mix_body(a, b, c, d, weight, out):
-    spec = a[...].astype(F32) + b[...].astype(F32) + c[...].astype(F32) + d[...].astype(F32)
+def reply(low, high, places, before):
+    anywhere = pl.BlockSpec(memory_space=pl.ANY)
+    return pl.pallas_call(
+        functools.partial(reply_body, first=2 * (len(before) - 1)),
+        out_shape=jax.ShapeDtypeStruct((128, 24, 256), BF16),
+        in_specs=[VMEM, VMEM, VMEM] + [anywhere] * len(before),
+        out_specs=anywhere,
+        scratch_shapes=[
+            pltpu.VMEM((64, 24, 256), BF16),
+            pltpu.SemaphoreType.DMA((2,)),
+        ],
+        input_output_aliases={4: 0} if len(before) == 2 else {},
+        compiler_params=pltpu.CompilerParams(vmem_limit_bytes=20 * 2**20),
+        cost_estimate=pl.CostEstimate(
+            flops=3072 * 2048 * 256, transcendentals=0, bytes_accessed=4000000
+        ),
+    )(low, high, places, *before)
+
+
+def mix_body(a, b, weight, out):
+    spec = a[...].astype(F32) + b[...].astype(F32)
     spec = spec.astype(BF16)
     row = iota((8, 256), 0)
     for j in range(4):
@@ -412,6 +446,18 @@
             for b in range(4):
                 along_b = (core == 0) == (stage == "wide")
                 to = (z, (b + s) % 4) if along_b else ((z + s) % 4, b)
+                pairs.append(((z * 2 + core) * 4 + b, (to[0] * 2 + core) * 4 + to[1]))
+    return lax.ppermute(shard, ("z", "core", "ba"), pairs)
+
+
+def flip(shard, stage, turn):
+    if stage == "y":
+        return lax.ppermute(shard, "y", [(i, i ^ turn) for i in range(4)])
+    pairs = []
+    for z in range(4):
+        for core in range(2):
+            for b in range(4):
+                to = (z ^ turn, b) if core == 0 else (z, b ^ turn)
                 pairs.append(((z * 2 + core) * 4 + b, (to[0] * 2 + core) * 4 + to[1]))
     return lax.ppermute(shard, ("z", "core", "ba"), pairs)
 
@@ -486,33 +532,34 @@
         flops=10**9,
         scalars=1,
     )
-    parts = add_and_cut((near, swapped(away)))
-    parts = add_and_cut(from_others(parts, "wide"))
-    parts = add_and_cut(from_others(parts, "near"))
-    latent, places = call(
+    parts = add_and_cut((near, swapped(away)), 4)
+    keep, give = add_and_cut(from_others(parts, "wide"), 2)
+    keep, give = add_and_cut((keep, flip(give, "near", 1)), 2)
+    keep, give = add_and_cut((keep, flip(give, "near", 3)), 2)
+    keep, give = add_and_cut((keep, flip(give, "y", 1)), 2)
+    low, places, sorted_rows, ids = call(
         collect_body,
-        (shape((2048, width), BF16), shape((1024, 128), BF16)),
+        (
+            shape((1024, width), BF16),
+            shape((1024, 128), BF16),
+            shape((3072, width), BF16),
+            shape((8, 8, 128), jnp.int32),
+        ),
         (recv,),
-        (pltpu.VMEM((3072, width), BF16), pltpu.VMEM((8, 8, 128), jnp.int32)),
-        flops=2 * 3072 * 2048 * 256,
-    )
-    back = pl.pallas_call(
-        reply_body,
-        out_shape=shape((devices, 24, width), BF16),
-        in_specs=[VMEM, VMEM, anywhere],
-        out_specs=anywhere,
-        scratch_shapes=[
-            pltpu.VMEM((devices, 24, width), BF16),
-            pltpu.SemaphoreType.DMA((4,)),
-        ],
-        name="reply",
-        compiler_params=pltpu.CompilerParams(vmem_limit_bytes=20 * 2**20),
-        cost_estimate=pl.CostEstimate(
-            flops=2 * 3072 * 2048 * 256, transcendentals=0, bytes_accessed=4000000
-        ),
-    )(latent, places, spectral_weight)
+        (),
+        flops=3072 * 2048 * 256,
+    )
+    high = call(
+        collect_more_body,
+        shape((1024, width), BF16),
+        (sorted_rows, ids),
+        (),
+        flops=3072 * 2048 * 256,
+    )
+    back = reply(low, high, places, (spectral_weight,))
+    back = reply(low, high, places, (spectral_weight, back))
     mixed = call(
-        mix_body, shape((32, width), BF16), from_others(parts, "y") + (spectral_weight,), ()
+        mix_body, shape((32, width), BF16), (keep, flip(give, "y", 3), spectral_weight), ()
     )
     line = joined(from_others((mixed,) * 4, "y"))
     plane = joined(from_others((line,) * 4, "near"))

time: 156 us -> 160 us (1.026)
  waiting for transfers between devices: 47.2 us -> 52 us
  starting transfers between devices: 50.6 us -> 49 us
    ppermute x0 -> x4, waiting for transfers between devices: none -> 8.43 us  [the longest x2 4.53 us: flip(): return lax.ppermute(shard, ('z', 'core', 'ba'), pairs)]
    ppermute x0 -> x4, starting transfers between devices: none -> 6.78 us  [the longest x2 3.96 us: flip(): return lax.ppermute(shard, ('z', 'core', 'ba'), pairs)]
    ppermute x12 -> x9, starting transfers between devices: 17.3 us -> 12.5 us  [around(): return lax.ppermute(shard, ('z', 'core', 'ba'), pairs)]
    ppermute x6 -> x3, starting transfers between devices: 7.47 us -> 3.06 us  [around(): return lax.ppermute(shard, 'y', [(i, (i + s) % 4) for i in range(4)])]
    ppermute x12 -> x9, waiting for transfers between devices: 21.2 us -> 19.1 us  [around(): return lax.ppermute(shard, ('z', 'core', 'ba'), pairs)]
    ppermute x6 -> x3, waiting for transfers between devices: 4.28 us -> 2.84 us  [around(): return lax.ppermute(shard, 'y', [(i, (i + s) % 4) for i in range(4)])]
    pallas_call x1 -> x2, Pallas kernels: 5.27 us -> 6.02 us  [reply(): pl.pallas_call(functools.partial(reply_body, first=2 * (len(before) - 1))...]
    pallas_call x12 -> x15, Pallas kernels: 29 us -> 29.1 us  [call(): return fn(*ins)]
  transfers between devices with their start and end apart: 25 -> 23, of which waited for: 13 -> 12; matrix products, arithmetic and copies ran while one was open for 0% -> 0% of each run, Pallas kernels for 22% -> 22%
where the time goes in v10:
time: 160 us
  Pallas kernels  52.9 us (33%)
  waiting for transfers between devices  52 us (32%)
  starting transfers between devices  49 us (31%)
  local copies, waits for them, and re-layouts  5.48 us (3%)
    pallas_call x15, Pallas kernels, call(): return fn(*ins)  29.1 us
    all_to_all x1, waiting for transfers between devices, per_device(): recv = lax.all_to_all(send, everyone, 0, 0, tiled=True)  21.7 us
    ppermute x9, waiting for transfers between devices, around(): return lax.ppermute(shard, ('z', 'core', 'ba'), pairs)  19.1 us
    ppermute x9, starting transfers between devices, around(): return lax.ppermute(shard, ('z', 'core', 'ba'), pairs)  12.5 us
    all_to_all x1, starting transfers between devices, per_device(): recv = lax.all_to_all(send, everyone, 0, 0, tiled=True)  11.5 us
    ppermute x5, starting transfers between devices, swapped(): return lax.ppermute(shard, 'core', [(0, 1), (1, 0)])  11.3 us
    pallas_call x1, Pallas kernels, per_device(): pl.pallas_call(spread_body, out_shape=(shape((devices, 56, 128), BF16), s...  9.84 us
    pallas_call x1, Pallas kernels, per_device(): pl.pallas_call(decode_body, out_shape=shape((points, width), BF16), in_sp...  7.97 us
  transfers between devices with their start and end apart: 23, of which 12 were waited for; matrix products, arithmetic and copies ran while one was open for 0% of the time, Pallas kernels for 22%

profile of v10, /device:TPU:1, one launch (start us, length us, event | category | flops | bytes accessed | tf_op | source)
XLA Modules:
  0.0 159.9 jit_solution(10572140514321183311)
XLA Ops:
  0.0 9.8 %spread.1 = (bf16[128,56,128]{2,1,0:T(8,128)(2,1)}, s32[1,2048]{1,0:T(1,128)}, bf16[2048,256]{1,0:T(8,128)(2,1)}) custom-call(bf16[2048,256]{1,0:T(8,128)(2,1)} %feat.1, s32[1,2048]{1,0:T(1,128)} %bitcast.7, s32[1,2048]{1,0:T(1,128)} %bitcast.11, f32[1,2048]{1,0:T(1,128)} %bitcast.16, bf16[256,256]{1,0:T(8,128)(2,1)} %weight.2), custom_call_target="tpu_custom_call" | custom-call | tf_op jit(solution)/shard_map/spread/pallas_call | solution.py:500
  9.8 0.0 copy-start.6
  9.9 0.0 copy-start.7
  9.9 0.0 copy-start.8
  9.9 0.0 copy-start.16
  9.9 11.5 %all-to-all-start = ((bf16[128,56,128]{2,1,0:T(8,128)(2,1)}), bf16[128,56,128]{2,1,0:T(8,128)(2,1)S(1)}, u32[]{:S(2)}, u32[]{:S(2)}) async-start(bf16[128,56,128]{2,1,0:T(8,128)(2,1)} %get-tuple-element.41), calls=%async_computation | async-start | bytes 3670016 | tf_op jit(solution)/shard_map/all_to_all | solution.py:519
  21.4 5.2 %shard_map.119 = bf16[2048,256]{1,0:T(8,128)(2,1)} custom-call(bf16[2048,256]{1,0:T(8,128)(2,1)S(1)} %copy-done.8, s32[1,2048]{1,0:T(1,128)S(1)} %bitcast.8, s32[1,2048]{1,0:T(1,128)S(1)} %bitcast.12, bf16[16,128]{1,0:T(8,128)(2,1)S(1)} %copy-done.16, s32[1]{0:T(128)} %bitcast.3.where), custom_call_target="tpu_custom_call" | custom-call | flops 2147483648 | bytes 4000000 | tf_op jit(solution)/shard_map/pallas_call | solution.py:48
  26.6 1.1 collective-permute-start
  27.7 21.7 %all-to-all-done.recv = bf16[128,56,128]{2,1,0:T(8,128)(2,1)S(1)} async-done(((bf16[128,56,128]{2,1,0:T(8,128)(2,1)}), bf16[128,56,128]{2,1,0:T(8,128)(2,1)S(1)}, u32[]{:S(2)}, u32[]{:S(2)}) %all-to-all-start) | async-done | bytes 1835040 | tf_op jit(solution)/shard_map/all_to_all | solution.py:519
  49.3 3.2 %shard_map.129 = (bf16[1024,256]{1,0:T(8,128)(2,1)S(1)}, bf16[1024,128]{1,0:T(8,128)(2,1)S(1)}, bf16[3072,256]{1,0:T(8,128)(2,1)S(1)}, s32[8,8,128]{2,1,0:T(8,128)S(1)}) custom-call(bf16[128,56,128]{2,1,0:T(8,128)(2,1)S(1)} %all-to-all-done.recv), custom_call_target="tpu_custom_call" | custom-call | flops 1610612736 | bytes 4000000 | tf_op jit(solution)/shard_map/pallas_call | solution.py:48
  52.6 0.0 copy-start
  52.6 2.0 %shard_map.130.high = bf16[1024,256]{1,0:T(8,128)(2,1)S(1)} custom-call(bf16[3072,256]{1,0:T(8,128)(2,1)S(1)} %get-tuple-element.43.rows, s32[8,8,128]{2,1,0:T(8,128)S(1)} %get-tuple-element.44.ids), custom_call_target="tpu_custom_call" | custom-call | flops 1610612736 | bytes 4000000 | tf_op jit(solution)/shard_map/pallas_call | solution.py:48
  54.6 0.2 copy-done
  54.8 3.0 %shard_map.131.refs_1_ = bf16[128,24,256]{2,1,0:T(8,128)(2,1)} custom-call(bf16[1024,256]{1,0:T(8,128)(2,1)S(1)} %get-tuple-element.42.low, bf16[1024,256]{1,0:T(8,128)(2,1)S(1)} %shard_map.130.high, bf16[1024,128]{1,0:T(8,128)(2,1)S(1)} %get-tuple-element.45.places, bf16[4,8,256,256]{3,2,1,0:T(8,128)(2,1)S(1)} %copy-done), custom_call_target="tpu_custom_call" | custom-call | flops 1610612736 | bytes 4000000 | tf_op jit(solution)/shard_map/pallas_call | solution.py:288
  57.8 3.0 %shard_map.132 = bf16[128,24,256]{2,1,0:T(8,128)(2,1)} custom-call(bf16[1024,256]{1,0:T(8,128)(2,1)S(1)} %get-tuple-element.42.low, bf16[1024,256]{1,0:T(8,128)(2,1)S(1)} %shard_map.130.high, bf16[1024,128]{1,0:T(8,128)(2,1)S(1)} %get-tuple-element.45.places, bf16[4,8,256,256]{3,2,1,0:T(8,128)(2,1)S(1)} %copy-done, ...), custom_call_target="tpu_custom_call", output_to_operand_aliasing={{}: (4, {})} | custom-call | flops 1610612736 | bytes 4000000 | tf_op jit(solution)/shard_map/pallas_call | solution.py:288
  60.8 3.8 %all-to-all-start.1 = ((bf16[128,24,256]{2,1,0:T(8,128)(2,1)}), bf16[128,24,256]{2,1,0:T(8,128)(2,1)S(1)}, u32[]{:S(2)}, u32[]{:S(2)}) async-start(bf16[128,24,256]{2,1,0:T(8,128)(2,1)} %shard_map.132), calls=%async_computation.1 | async-start | bytes 3145728 | tf_op jit(solution)/shard_map/all_to_all | solution.py:569
  64.6 0.0 copy-start.9
  64.6 1.2 copy-done.9
  65.9 4.2 %shard_map.118.refs_0_ = bf16[2048,256]{1,0:T(8,128)(2,1)S(1)} custom-call(bf16[2048,256]{1,0:T(8,128)(2,1)S(1)} %copy-done.9, s32[1,2048]{1,0:T(1,128)S(1)} %bitcast.9, s32[1,2048]{1,0:T(1,128)S(1)} %bitcast.13, bf16[16,128]{1,0:T(8,128)(2,1)S(1)} %copy-done.16, s32[1]{0:T(128)} %bitcast.3.where), custom_call_target="tpu_custom_call" | custom-call | flops 2147483648 | bytes 4000000 | tf_op jit(solution)/shard_map/pallas_call | solution.py:48
  70.1 0.2 shard_map.120
  70.3 1.7 %collective-permute-start.1 = (bf16[512,256]{1,0:T(8,128)(2,1)S(1)}, bf16[512,256]{1,0:T(8,128)(2,1)S(1)}, u32[]{:S(2)}, u32[]{:S(2)}) collective-permute-start(bf16[512,256]{1,0:T(8,128)(2,1)S(1)} %get-tuple-element.28), channel_id=1, source_target_pairs={{0,1},{1,2},{2,3},{3,0},{4,36},{5,37},{6,38},{7,39},{32,33},{33,34... | collective-permute-start | bytes 786440 | tf_op jit(solution)/shard_map/ppermute | solution.py:450
  72.0 2.9 %collective-permute-start.2 = (bf16[512,256]{1,0:T(8,128)(2,1)S(1)}, bf16[512,256]{1,0:T(8,128)(2,1)S(1)}, u32[]{:S(2)}, u32[]{:S(2)}) collective-permute-start(bf16[512,256]{1,0:T(8,128)(2,1)S(1)} %get-tuple-element.29), channel_id=1, source_target_pairs={{0,2},{1,3},{2,0},{3,1},{4,68},{5,69},{6,70},{7,71},{32,34},{33,35... | collective-permute-start | bytes 786440 | tf_op jit(solution)/shard_map/ppermute | solution.py:450
  74.9 0.9 collective-permute-start.3
  75.8 13.0 %collective-permute-done.1.refs_1_ = bf16[512,256]{1,0:T(8,128)(2,1)S(1)} collective-permute-done((bf16[512,256]{1,0:T(8,128)(2,1)S(1)}, bf16[512,256]{1,0:T(8,128)(2,1)S(1)}, u32[]{:S(2)}, u32[]{:S(2)}) %collective-permute-start.1) | collective-permute-done | bytes 262176 | tf_op jit(solution)/shard_map/ppermute | solution.py:450
  88.9 2.9 %collective-permute-done.2.refs_2_ = bf16[512,256]{1,0:T(8,128)(2,1)S(1)} collective-permute-done((bf16[512,256]{1,0:T(8,128)(2,1)S(1)}, bf16[512,256]{1,0:T(8,128)(2,1)S(1)}, u32[]{:S(2)}, u32[]{:S(2)}) %collective-permute-start.2) | collective-permute-done | bytes 262176 | tf_op jit(solution)/shard_map/ppermute | solution.py:450
  91.8 0.0 collective-permute-done.3.refs_3_
  91.8 0.1 shard_map.121
  91.9 1.3 collective-permute-start.4
  93.2 2.6 %collective-permute-done.4.refs_1_ = bf16[256,256]{1,0:T(8,128)(2,1)S(1)} collective-permute-done((bf16[256,256]{1,0:T(8,128)(2,1)S(1)}, bf16[256,256]{1,0:T(8,128)(2,1)S(1)}, u32[]{:S(2)}, u32[]{:S(2)}) %collective-permute-start.4) | collective-permute-done | bytes 131104 | tf_op jit(solution)/shard_map/ppermute | solution.py:462
  95.9 2.7 %collective-permute-start.5 = (bf16[128,256]{1,0:T(8,128)(2,1)S(1)}, bf16[128,256]{1,0:T(8,128)(2,1)S(1)}, u32[]{:S(2)}, u32[]{:S(2)}) collective-permute-start(bf16[128,256]{1,0:T(8,128)(2,1)S(1)} %get-tuple-element.34), channel_id=1, source_target_pairs={{0,96},{1,97},{2,98},{3,99},{4,7},{5,6},{6,5},{7,4},{32,64},{33,65... | collective-permute-start | bytes 196616 | tf_op jit(solution)/shard_map/ppermute | solution.py:462
  98.6 1.9 %collective-permute-done.5.refs_1_ = bf16[128,256]{1,0:T(8,128)(2,1)S(1)} collective-permute-done((bf16[128,256]{1,0:T(8,128)(2,1)S(1)}, bf16[128,256]{1,0:T(8,128)(2,1)S(1)}, u32[]{:S(2)}, u32[]{:S(2)}) %collective-permute-start.5) | collective-permute-done | bytes 65568 | tf_op jit(solution)/shard_map/ppermute | solution.py:462
  100.5 0.9 collective-permute-start.6
  101.4 1.9 %collective-permute-done.6.refs_1_ = bf16[64,256]{1,0:T(8,128)(2,1)S(1)} collective-permute-done((bf16[64,256]{1,0:T(8,128)(2,1)S(1)}, bf16[64,256]{1,0:T(8,128)(2,1)S(1)}, u32[]{:S(2)}, u32[]{:S(2)}) %collective-permute-start.6) | collective-permute-done | bytes 32800 | tf_op jit(solution)/shard_map/ppermute | solution.py:455
  103.3 1.9 %collective-permute-start.7 = (bf16[32,256]{1,0:T(8,128)(2,1)S(1)}, bf16[32,256]{1,0:T(8,128)(2,1)S(1)}, u32[]{:S(2)}, u32[]{:S(2)}) collective-permute-start(bf16[32,256]{1,0:T(8,128)(2,1)S(1)} %get-tuple-element.38), channel_id=1, source_target_pairs={{0,24},{8,16},{16,8},{24,0},{1,25},{9,17},{17,9},{25,1},{2,26},{10... | collective-permute-start | bytes 49160 | tf_op jit(solution)/shard_map/ppermute | solution.py:455
  105.2 2.0 %collective-permute-done.7.b = bf16[32,256]{1,0:T(8,128)(2,1)S(1)} collective-permute-done((bf16[32,256]{1,0:T(8,128)(2,1)S(1)}, bf16[32,256]{1,0:T(8,128)(2,1)S(1)}, u32[]{:S(2)}, u32[]{:S(2)}) %collective-permute-start.7) | collective-permute-done | bytes 16416 | tf_op jit(solution)/shard_map/ppermute | solution.py:455
  107.2 0.7 shard_map.125.refs_0_
  107.9 1.8 %collective-permute-start.10 = (bf16[32,256]{1,0:T(8,128)(2,1)S(1)}, bf16[32,256]{1,0:T(8,128)(2,1)S(1)}, u32[]{:S(2)}, u32[]{:S(2)}) collective-permute-start(bf16[32,256]{1,0:T(8,128)(2,1)S(1)} %shard_map.125.refs_0_), channel_id=1, source_target_pairs={{0,24},{8,0},{16,8},{24,16},{1,25},{9,1},{17,9},{25,17},{2,26},{10... | collective-permute-start | bytes 49160 | tf_op jit(solution)/shard_map/ppermute | solution.py:442
  109.7 1.2 collective-permute-start.9
  110.9 0.0 collective-permute-done.10.refs_3_
  110.9 2.5 %collective-permute-done.8.refs_1_ = bf16[32,256]{1,0:T(8,128)(2,1)S(1)} collective-permute-done((bf16[32,256]{1,0:T(8,128)(2,1)S(1)}, bf16[32,256]{1,0:T(8,128)(2,1)S(1)}, u32[]{:S(2)}, u32[]{:S(2)}) %collective-permute-start.8) | collective-permute-done | bytes 16416 | tf_op jit(solution)/shard_map/ppermute | solution.py:442
  113.5 0.3 collective-permute-done.9.refs_2_
  113.8 0.0 collective-permute-start.11
  113.8 3.3 %collective-permute-start.12 = (bf16[128,256]{1,0:T(8,128)(2,1)S(1)}, bf16[128,256]{1,0:T(8,128)(2,1)S(1)}, u32[]{:S(2)}, u32[]{:S(2)}) collective-permute-start(bf16[128,256]{1,0:T(8,128)(2,1)S(1)} %shard_map.126.refs_0_), channel_id=1, source_target_pairs={{0,64},{1,65},{2,66},{3,67},{4,6},{5,7},{6,4},{7,5},{32,96},{33,97... | collective-permute-start | bytes 196616 | tf_op jit(solution)/shard_map/ppermute | solution.py:450
  117.1 1.0 collective-permute-done.11.refs_1_
  118.1 1.5 collective-permute-done.12.refs_2_
  119.6 0.6 collective-permute-done.13.refs_3_
  120.3 0.0 copy-start.10
  120.3 0.2 collective-permute-start.14
  120.5 1.8 %collective-permute-start.15 = (bf16[512,256]{1,0:T(8,128)(2,1)S(1)}, bf16[512,256]{1,0:T(8,128)(2,1)S(1)}, u32[]{:S(2)}, u32[]{:S(2)}) collective-permute-start(bf16[512,256]{1,0:T(8,128)(2,1)S(1)} %shard_map.127.near), channel_id=1, source_target_pairs={{0,2},{1,3},{2,0},{3,1},{4,68},{5,69},{6,70},{7,71},{32,34},{33,35... | collective-permute-start | bytes 786440 | tf_op jit(solution)/shard_map/ppermute | solution.py:450
  122.4 1.6 %collective-permute-start.16 = (bf16[512,256]{1,0:T(8,128)(2,1)S(1)}, bf16[512,256]{1,0:T(8,128)(2,1)S(1)}, u32[]{:S(2)}, u32[]{:S(2)}) collective-permute-start(bf16[512,256]{1,0:T(8,128)(2,1)S(1)} %shard_map.127.near), channel_id=1, source_target_pairs={{0,3},{1,0},{2,1},{3,2},{4,100},{5,101},{6,102},{7,103},{32,35},{3... | collective-permute-start | bytes 786440 | tf_op jit(solution)/shard_map/ppermute | solution.py:450
  124.0 6.8 %shard_map.128 = (bf16[2048,1024]{1,0:T(8,128)(2,1)S(1)}, bf16[2048,1024]{1,0:T(8,128)(2,1)S(1)}) custom-call(s32[1,2048]{1,0:T(1,128)S(1)} %bitcast.10, s32[1,2048]{1,0:T(1,128)S(1)} %bitcast.14, bf16[128,16]{1,0:T(8,128)(2,1)S(1)} %copy-done.15, s32[1]{0:T(128)} %bitcast.3.where), custom_call_target="tpu_custom_call" | custom-call | flops 1000000000 | bytes 4000000 | tf_op jit(solution)/shard_map/pallas_call | solution.py:48
  130.8 1.9 %copy-done.2 = bf16[2048,1024]{1,0:T(8,128)(2,1)} copy-done((bf16[2048,1024]{1,0:T(8,128)(2,1)}, bf16[2048,1024]{1,0:T(8,128)(2,1)S(1)}, u32[]{:S(2)}) %copy-start.2) | copy-done | bytes 4194328
  132.7 2.0 %copy-done.4 = bf16[2048,1024]{1,0:T(8,128)(2,1)} copy-done((bf16[2048,1024]{1,0:T(8,128)(2,1)}, bf16[2048,1024]{1,0:T(8,128)(2,1)S(1)}, u32[]{:S(2)}) %copy-start.4) | copy-done | bytes 4194328
  134.7 9.6 %collective-permute-start.20 = (bf16[512,256]{1,0:T(8,128)(2,1)S(1)}, bf16[512,256]{1,0:T(8,128)(2,1)S(1)}, u32[]{:S(2)}, u32[]{:S(2)}) collective-permute-start(bf16[512,256]{1,0:T(8,128)(2,1)S(1)} %shard_map.127.near), channel_id=1, source_target_pairs={{0,4},{4,0},{1,5},{5,1},{2,6},{6,2},{3,7},{7,3},{8,12},{12,8},{9,1... | collective-permute-start | bytes 786440 | tf_op jit(solution)/shard_map/ppermute | solution.py:473
  144.4 0.0 collective-permute-done.14.m1
  144.4 0.0 collective-permute-start.17
  144.4 0.5 collective-permute-start.18
  144.9 0.1 collective-permute-start.19
  145.0 4.8 %shard_map.133.base = f32[2048,256]{1,0:T(8,128)S(1)} custom-call(bf16[3072,256]{1,0:T(8,128)(2,1)S(1)} %bitcast.6, s32[1,2048]{1,0:T(1,128)S(1)} %copy-done.14, bf16[256,256]{1,0:T(8,128)(2,1)S(1)} %copy-done.10), custom_call_target="tpu_custom_call" | custom-call | flops 3221225472 | bytes 4000000 | tf_op jit(solution)/shard_map/pallas_call | solution.py:48
  149.9 0.0 copy-start.11
  149.9 0.0 copy-start.12
  149.9 0.0 copy-start.13
  149.9 1.8 %shard_map.134.base = f32[2048,256]{1,0:T(8,128)S(1)} custom-call(bf16[512,256]{1,0:T(8,128)(2,1)S(1)} %shard_map.127.near, bf16[512,256]{1,0:T(8,128)(2,1)S(1)} %collective-permute-done.20.far, bf16[2048,1024]{1,0:T(8,128)(2,1)S(1)} %copy-done.3, bf16[2048,1024]{1,0:T(8,128)(2,1)S(1)} %copy-done.5, f32[2048,256]{1,0:T(8,128)S(1)} %shard_map.133.base), custom_call_target="tpu_custom_call" | custom-call | flops 1073741824 | bytes 4000000 | tf_op jit(solution)/shard_map/pallas_call | solution.py:48
  151.8 8.0 %decode.1 = bf16[2048,256]{1,0:T(8,128)(2,1)} custom-call(bf16[512,256]{1,0:T(8,128)(2,1)S(1)} %collective-permute-done.14.m1, bf16[512,256]{1,0:T(8,128)(2,1)S(1)} %collective-permute-done.15.m2, bf16[512,256]{1,0:T(8,128)(2,1)S(1)} %collective-permute-done.16.m3, bf16[512,256]{1,0:T(8,128)(2,1)S(1)} %collective-permute-done.17.m5, ...), custom_call_target="tpu_custom_call" | custom-call | flops 4294967296 | bytes 4000000 | tf_op jit(solution)/shard_map/decode/pallas_call | solution.py:587
  (35 shorter events, 0.2 us)
Async XLA Ops:
  9.8 11.6 %copy-start.6 = (s32[2048,1]{0,1:T(1,128)S(1)}, s32[2048,1]{0,1:T(1,128)}, u32[]{:S(2)}) copy-start(s32[2048,1]{0,1:T(1,128)} %param.13) | copy-start | bytes 24580
  9.9 11.6 %copy-start.7 = (s32[2048]{0:T(1024)S(1)}, s32[2048]{0:T(1024)}, u32[]{:S(2)}) copy-start(s32[2048]{0:T(1024)} %param.14) | copy-start | bytes 24580
  9.9 11.5 %copy-start.8 = (bf16[2048,256]{1,0:T(8,128)(2,1)S(1)}, bf16[2048,256]{1,0:T(8,128)(2,1)}, u32[]{:S(2)}) copy-start(bf16[2048,256]{1,0:T(8,128)(2,1)} %get-tuple-element.26.message) | copy-start | bytes 3145732
  9.9 11.5 %copy-start.16 = (bf16[16,128]{1,0:T(8,128)(2,1)S(1)}, bf16[16,128]{1,0:T(8,128)(2,1)}, u32[]{:S(2)}) copy-start(bf16[16,128]{1,0:T(8,128)(2,1)} %constant.26.clone.basis) | copy-start | bytes 12292
  9.9 39.4 %all-to-all-start = ((bf16[128,56,128]{2,1,0:T(8,128)(2,1)}), bf16[128,56,128]{2,1,0:T(8,128)(2,1)S(1)}, u32[]{:S(2)}, u32[]{:S(2)}) async-start(bf16[128,56,128]{2,1,0:T(8,128)(2,1)} %get-tuple-element.41), calls=%async_computation | async-start | bytes 3670016 | tf_op jit(solution)/shard_map/all_to_all | solution.py:519
  26.6 43.4 %collective-permute-start = (bf16[2048,256]{1,0:T(8,128)(2,1)}, bf16[2048,256]{1,0:T(8,128)(2,1)S(1)}, u32[]{:S(2)}, u32[]{:S(2)}) collective-permute-start(bf16[2048,256]{1,0:T(8,128)(2,1)} %shard_map.119), channel_id=1, source_target_pairs={{0,4},{4,0},{1,5},{5,1},{2,6},{6,2},{3,7},{7,3},{8,12},{12,8},{9,1... | collective-permute-start | bytes 3145736 | tf_op jit(solution)/shard_map/ppermute | solution.py:473
  52.6 2.2 %copy-start = (bf16[4,8,256,256]{3,2,1,0:T(8,128)(2,1)S(1)}, bf16[4,8,256,256]{3,2,1,0:T(8,128)(2,1)}, u32[]{:S(2)}) copy-start(bf16[4,8,256,256]{3,2,1,0:T(8,128)(2,1)} %refs_0_.3) | copy-start | bytes 12582916
  60.8 84.2 %all-to-all-start.1 = ((bf16[128,24,256]{2,1,0:T(8,128)(2,1)}), bf16[128,24,256]{2,1,0:T(8,128)(2,1)S(1)}, u32[]{:S(2)}, u32[]{:S(2)}) async-start(bf16[128,24,256]{2,1,0:T(8,128)(2,1)} %shard_map.132), calls=%async_computation.1 | async-start | bytes 3145728 | tf_op jit(solution)/shard_map/all_to_all | solution.py:569
  64.6 1.2 copy-start.9
  65.9 41.4 %copy-start.1 = (bf16[4,8,256,256]{3,2,1,0:T(8,128)(2,1)S(1)}, bf16[4,8,256,256]{3,2,1,0:T(8,128)(2,1)}, u32[]{:S(2)}) copy-start(bf16[4,8,256,256]{3,2,1,0:T(8,128)(2,1)} %refs_0_.3) | copy-start | bytes 12582916
  70.3 18.6 %collective-permute-start.1 = (bf16[512,256]{1,0:T(8,128)(2,1)S(1)}, bf16[512,256]{1,0:T(8,128)(2,1)S(1)}, u32[]{:S(2)}, u32[]{:S(2)}) collective-permute-start(bf16[512,256]{1,0:T(8,128)(2,1)S(1)} %get-tuple-element.28), channel_id=1, source_target_pairs={{0,1},{1,2},{2,3},{3,0},{4,36},{5,37},{6,38},{7,39},{32,33},{33,34... | collective-permute-start | bytes 786440 | tf_op jit(solution)/shard_map/ppermute | solution.py:450
  72.0 19.8 %collective-permute-start.2 = (bf16[512,256]{1,0:T(8,128)(2,1)S(1)}, bf16[512,256]{1,0:T(8,128)(2,1)S(1)}, u32[]{:S(2)}, u32[]{:S(2)}) collective-permute-start(bf16[512,256]{1,0:T(8,128)(2,1)S(1)} %get-tuple-element.29), channel_id=1, source_target_pairs={{0,2},{1,3},{2,0},{3,1},{4,68},{5,69},{6,70},{7,71},{32,34},{33,35... | collective-permute-start | bytes 786440 | tf_op jit(solution)/shard_map/ppermute | solution.py:450
  74.9 16.9 %collective-permute-start.3 = (bf16[512,256]{1,0:T(8,128)(2,1)S(1)}, bf16[512,256]{1,0:T(8,128)(2,1)S(1)}, u32[]{:S(2)}, u32[]{:S(2)}) collective-permute-start(bf16[512,256]{1,0:T(8,128)(2,1)S(1)} %get-tuple-element.30), channel_id=1, source_target_pairs={{0,3},{1,0},{2,1},{3,2},{4,100},{5,101},{6,102},{7,103},{32,35},{3... | collective-permute-start | bytes 786440 | tf_op jit(solution)/shard_map/ppermute | solution.py:450
  91.9 3.9 %collective-permute-start.4 = (bf16[256,256]{1,0:T(8,128)(2,1)S(1)}, bf16[256,256]{1,0:T(8,128)(2,1)S(1)}, u32[]{:S(2)}, u32[]{:S(2)}) collective-permute-start(bf16[256,256]{1,0:T(8,128)(2,1)S(1)} %get-tuple-element.32), channel_id=1, source_target_pairs={{0,32},{1,33},{2,34},{3,35},{4,5},{5,4},{6,7},{7,6},{32,0},{33,1},... | collective-permute-start | bytes 393224 | tf_op jit(solution)/shard_map/ppermute | solution.py:462
  95.9 4.6 %collective-permute-start.5 = (bf16[128,256]{1,0:T(8,128)(2,1)S(1)}, bf16[128,256]{1,0:T(8,128)(2,1)S(1)}, u32[]{:S(2)}, u32[]{:S(2)}) collective-permute-start(bf16[128,256]{1,0:T(8,128)(2,1)S(1)} %get-tuple-element.34), channel_id=1, source_target_pairs={{0,96},{1,97},{2,98},{3,99},{4,7},{5,6},{6,5},{7,4},{32,64},{33,65... | collective-permute-start | bytes 196616 | tf_op jit(solution)/shard_map/ppermute | solution.py:462
  100.5 2.8 %collective-permute-start.6 = (bf16[64,256]{1,0:T(8,128)(2,1)S(1)}, bf16[64,256]{1,0:T(8,128)(2,1)S(1)}, u32[]{:S(2)}, u32[]{:S(2)}) collective-permute-start(bf16[64,256]{1,0:T(8,128)(2,1)S(1)} %get-tuple-element.36), channel_id=1, source_target_pairs={{0,8},{8,0},{16,24},{24,16},{1,9},{9,1},{17,25},{25,17},{2,10},{10... | collective-permute-start | bytes 98312 | tf_op jit(solution)/shard_map/ppermute | solution.py:455
  103.3 3.9 %collective-permute-start.7 = (bf16[32,256]{1,0:T(8,128)(2,1)S(1)}, bf16[32,256]{1,0:T(8,128)(2,1)S(1)}, u32[]{:S(2)}, u32[]{:S(2)}) collective-permute-start(bf16[32,256]{1,0:T(8,128)(2,1)S(1)} %get-tuple-element.38), channel_id=1, source_target_pairs={{0,24},{8,16},{16,8},{24,0},{1,25},{9,17},{17,9},{25,1},{2,26},{10... | collective-permute-start | bytes 49160 | tf_op jit(solution)/shard_map/ppermute | solution.py:455
  107.2 16.8 %copy-start.15 = (bf16[128,16]{1,0:T(8,128)(2,1)S(1)}, bf16[128,16]{1,0:T(8,128)(2,1)}, u32[]{:S(2)}) copy-start(bf16[128,16]{1,0:T(8,128)(2,1)} %constant.27.clone.basis) | copy-start | bytes 12292
  107.9 3.1 %collective-permute-start.10 = (bf16[32,256]{1,0:T(8,128)(2,1)S(1)}, bf16[32,256]{1,0:T(8,128)(2,1)S(1)}, u32[]{:S(2)}, u32[]{:S(2)}) collective-permute-start(bf16[32,256]{1,0:T(8,128)(2,1)S(1)} %shard_map.125.refs_0_), channel_id=1, source_target_pairs={{0,24},{8,0},{16,8},{24,16},{1,25},{9,1},{17,9},{25,17},{2,26},{10... | collective-permute-start | bytes 49160 | tf_op jit(solution)/shard_map/ppermute | solution.py:442
  109.7 3.8 %collective-permute-start.8 = (bf16[32,256]{1,0:T(8,128)(2,1)S(1)}, bf16[32,256]{1,0:T(8,128)(2,1)S(1)}, u32[]{:S(2)}, u32[]{:S(2)}) collective-permute-start(bf16[32,256]{1,0:T(8,128)(2,1)S(1)} %shard_map.125.refs_0_), channel_id=1, source_target_pairs={{0,8},{8,16},{16,24},{24,0},{1,9},{9,17},{17,25},{25,1},{2,10},{10... | collective-permute-start | bytes 49160 | tf_op jit(solution)/shard_map/ppermute | solution.py:442
  109.7 4.1 %collective-permute-start.9 = (bf16[32,256]{1,0:T(8,128)(2,1)S(1)}, bf16[32,256]{1,0:T(8,128)(2,1)S(1)}, u32[]{:S(2)}, u32[]{:S(2)}) collective-permute-start(bf16[32,256]{1,0:T(8,128)(2,1)S(1)} %shard_map.125.refs_0_), channel_id=1, source_target_pairs={{0,16},{8,24},{16,0},{24,8},{1,17},{9,25},{17,1},{25,9},{2,18},{10... | collective-permute-start | bytes 49160 | tf_op jit(solution)/shard_map/ppermute | solution.py:442
  113.8 4.3 %collective-permute-start.11 = (bf16[128,256]{1,0:T(8,128)(2,1)S(1)}, bf16[128,256]{1,0:T(8,128)(2,1)S(1)}, u32[]{:S(2)}, u32[]{:S(2)}) collective-permute-start(bf16[128,256]{1,0:T(8,128)(2,1)S(1)} %shard_map.126.refs_0_), channel_id=1, source_target_pairs={{0,32},{1,33},{2,34},{3,35},{4,5},{5,6},{6,7},{7,4},{32,64},{33,65... | collective-permute-start | bytes 196616 | tf_op jit(solution)/shard_map/ppermute | solution.py:450
  113.8 5.8 %collective-permute-start.12 = (bf16[128,256]{1,0:T(8,128)(2,1)S(1)}, bf16[128,256]{1,0:T(8,128)(2,1)S(1)}, u32[]{:S(2)}, u32[]{:S(2)}) collective-permute-start(bf16[128,256]{1,0:T(8,128)(2,1)S(1)} %shard_map.126.refs_0_), channel_id=1, source_target_pairs={{0,64},{1,65},{2,66},{3,67},{4,6},{5,7},{6,4},{7,5},{32,96},{33,97... | collective-permute-start | bytes 196616 | tf_op jit(solution)/shard_map/ppermute | solution.py:450
  117.1 3.1 %collective-permute-start.13 = (bf16[128,256]{1,0:T(8,128)(2,1)S(1)}, bf16[128,256]{1,0:T(8,128)(2,1)S(1)}, u32[]{:S(2)}, u32[]{:S(2)}) collective-permute-start(bf16[128,256]{1,0:T(8,128)(2,1)S(1)} %shard_map.126.refs_0_), channel_id=1, source_target_pairs={{0,96},{1,97},{2,98},{3,99},{4,7},{5,4},{6,5},{7,6},{32,0},{33,1},... | collective-permute-start | bytes 196616 | tf_op jit(solution)/shard_map/ppermute | solution.py:450
  120.3 24.7 %copy-start.10 = (bf16[256,256]{1,0:T(8,128)(2,1)S(1)}, bf16[256,256]{1,0:T(8,128)(2,1)}, u32[]{:S(2)}) copy-start(bf16[256,256]{1,0:T(8,128)(2,1)} %skip.1) | copy-start | bytes 393220
  120.3 24.7 %copy-start.14 = (s32[1,2048]{1,0:T(1,128)S(1)}, s32[1,2048]{1,0:T(1,128)}, u32[]{:S(2)}) copy-start(s32[1,2048]{1,0:T(1,128)} %get-tuple-element.46.slots) | copy-start | bytes 24580
  120.3 24.1 %collective-permute-start.14 = (bf16[512,256]{1,0:T(8,128)(2,1)S(1)}, bf16[512,256]{1,0:T(8,128)(2,1)S(1)}, u32[]{:S(2)}, u32[]{:S(2)}) collective-permute-start(bf16[512,256]{1,0:T(8,128)(2,1)S(1)} %shard_map.127.near), channel_id=1, source_target_pairs={{0,1},{1,2},{2,3},{3,0},{4,36},{5,37},{6,38},{7,39},{32,33},{33,34... | collective-permute-start | bytes 786440 | tf_op jit(solution)/shard_map/ppermute | solution.py:450
  120.5 23.9 %collective-permute-start.15 = (bf16[512,256]{1,0:T(8,128)(2,1)S(1)}, bf16[512,256]{1,0:T(8,128)(2,1)S(1)}, u32[]{:S(2)}, u32[]{:S(2)}) collective-permute-start(bf16[512,256]{1,0:T(8,128)(2,1)S(1)} %shard_map.127.near), channel_id=1, source_target_pairs={{0,2},{1,3},{2,0},{3,1},{4,68},{5,69},{6,70},{7,71},{32,34},{33,35... | collective-permute-start | bytes 786440 | tf_op jit(solution)/shard_map/ppermute | solution.py:450
  122.4 22.5 %collective-permute-start.16 = (bf16[512,256]{1,0:T(8,128)(2,1)S(1)}, bf16[512,256]{1,0:T(8,128)(2,1)S(1)}, u32[]{:S(2)}, u32[]{:S(2)}) collective-permute-start(bf16[512,256]{1,0:T(8,128)(2,1)S(1)} %shard_map.127.near), channel_id=1, source_target_pairs={{0,3},{1,0},{2,1},{3,2},{4,100},{5,101},{6,102},{7,103},{32,35},{3... | collective-permute-start | bytes 786440 | tf_op jit(solution)/shard_map/ppermute | solution.py:450
  130.8 2.0 %copy-start.2 = (bf16[2048,1024]{1,0:T(8,128)(2,1)}, bf16[2048,1024]{1,0:T(8,128)(2,1)S(1)}, u32[]{:S(2)}) copy-start(bf16[2048,1024]{1,0:T(8,128)(2,1)S(1)} %get-tuple-element.39.wave_p) | copy-start | bytes 12582916
  132.7 2.0 %copy-start.4 = (bf16[2048,1024]{1,0:T(8,128)(2,1)}, bf16[2048,1024]{1,0:T(8,128)(2,1)S(1)}, u32[]{:S(2)}) copy-start(bf16[2048,1024]{1,0:T(8,128)(2,1)S(1)} %get-tuple-element.40.wave_qz) | copy-start | bytes 12582916
  134.7 15.1 %collective-permute-start.20 = (bf16[512,256]{1,0:T(8,128)(2,1)S(1)}, bf16[512,256]{1,0:T(8,128)(2,1)S(1)}, u32[]{:S(2)}, u32[]{:S(2)}) collective-permute-start(bf16[512,256]{1,0:T(8,128)(2,1)S(1)} %shard_map.127.near), channel_id=1, source_target_pairs={{0,4},{4,0},{1,5},{5,1},{2,6},{6,2},{3,7},{7,3},{8,12},{12,8},{9,1... | collective-permute-start | bytes 786440 | tf_op jit(solution)/shard_map/ppermute | solution.py:473
  144.4 7.4 %collective-permute-start.17 = (bf16[512,256]{1,0:T(8,128)(2,1)S(1)}, bf16[512,256]{1,0:T(8,128)(2,1)S(1)}, u32[]{:S(2)}, u32[]{:S(2)}) collective-permute-start(bf16[512,256]{1,0:T(8,128)(2,1)S(1)} %collective-permute-done.14.m1), channel_id=1, source_target_pairs={{0,4},{4,0},{1,5},{5,1},{2,6},{6,2},{3,7},{7,3},{8,12},{12,8},{9,1... | collective-permute-start | bytes 786440 | tf_op jit(solution)/shard_map/ppermute | solution.py:473
  144.4 7.4 %collective-permute-start.18 = (bf16[512,256]{1,0:T(8,128)(2,1)S(1)}, bf16[512,256]{1,0:T(8,128)(2,1)S(1)}, u32[]{:S(2)}, u32[]{:S(2)}) collective-permute-start(bf16[512,256]{1,0:T(8,128)(2,1)S(1)} %collective-permute-done.15.m2), channel_id=1, source_target_pairs={{0,4},{4,0},{1,5},{5,1},{2,6},{6,2},{3,7},{7,3},{8,12},{12,8},{9,1... | collective-permute-start | bytes 786440 | tf_op jit(solution)/shard_map/ppermute | solution.py:473
  144.9 6.9 %collective-permute-start.19 = (bf16[512,256]{1,0:T(8,128)(2,1)S(1)}, bf16[512,256]{1,0:T(8,128)(2,1)}, u32[]{:S(2)}, u32[]{:S(2)}) collective-permute-start(bf16[512,256]{1,0:T(8,128)(2,1)S(1)} %collective-permute-done.16.m3), channel_id=1, source_target_pairs={{0,4},{4,0},{1,5},{5,1},{2,6},{6,2},{3,7},{7,3},{8,12},{12,8},{9,1... | collective-permute-start | bytes 786440 | tf_op jit(solution)/shard_map/ppermute | solution.py:473
  145.0 4.9 %copy-start.3 = (bf16[2048,1024]{1,0:T(8,128)(2,1)S(1)}, bf16[2048,1024]{1,0:T(8,128)(2,1)}, u32[]{:S(2)}) copy-start(bf16[2048,1024]{1,0:T(8,128)(2,1)} %copy-done.2) | copy-start | bytes 12582916
  145.0 4.9 %copy-start.5 = (bf16[2048,1024]{1,0:T(8,128)(2,1)S(1)}, bf16[2048,1024]{1,0:T(8,128)(2,1)}, u32[]{:S(2)}) copy-start(bf16[2048,1024]{1,0:T(8,128)(2,1)} %copy-done.4) | copy-start | bytes 12582916
  149.9 1.9 %copy-start.11 = (bf16[256,256]{1,0:T(8,128)(2,1)S(1)}, bf16[256,256]{1,0:T(8,128)(2,1)}, u32[]{:S(2)}) copy-start(bf16[256,256]{1,0:T(8,128)(2,1)} %hidden_weight.1) | copy-start | bytes 393220
  149.9 1.9 %copy-start.12 = (bf16[256,256]{1,0:T(8,128)(2,1)S(1)}, bf16[256,256]{1,0:T(8,128)(2,1)}, u32[]{:S(2)}) copy-start(bf16[256,256]{1,0:T(8,128)(2,1)} %output_weight.1) | copy-start | bytes 393220
  149.9 1.9 %copy-start.13 = (f32[2048]{0:T(1024)S(1)}, f32[2048]{0:T(1024)}, u32[]{:S(2)}) copy-start(f32[2048]{0:T(1024)} %param.16) | copy-start | bytes 24580

commit v11 on v8

--- a/solution.py
+++ b/solution.py
@@ -223,7 +223,7 @@
         return carry
 
     lax.fori_loop(0, 8, unpack, 0)
-    tile = 512
+    tile = 1024
 
     def total(step, carry):
         at = step * tile
@@ -281,17 +281,17 @@
 
 def own_body(returned, slots, skip, out):
     def some(step, carry):
-        at = step * 512
+        at = step * 1024
         hot = []
-        for p in range(4):
+        for p in range(8):
             slot = as_column(slots[:, pl.ds(at + p * 128, 128)], 128)
             one = [(slot == iota((128, 128), 1) + 128 * k).astype(BF16) for k in range(24)]
             hot.append(jnp.concatenate(one, axis=1))
         own = mm(jnp.concatenate(hot, axis=0), returned[...]).astype(BF16)
-        out[pl.ds(at, 512), :] = mm(own, skip[...])
-        return carry
-
-    lax.fori_loop(0, out.shape[0] // 512, some, 0)
+        out[pl.ds(at, 1024), :] = mm(own, skip[...])
+        return carry
+
+    lax.fori_loop(0, out.shape[0] // 1024, some, 0)
 
 
 def waves_body(tile, cell, basis, where, out_p, out_qz, spots, wide_p, wide_q, wide_z):
@@ -367,28 +367,28 @@
     modes = ((m1, m2, m3), (m5, m6, m7))
 
     def some(step, carry):
-        at = step * 512
-        total = base[pl.ds(at, 512), :]
+        at = step * 1024
+        total = base[pl.ds(at, 1024), :]
         for h in range(2):
             for o in range(3):
-                wave = wave_of(wave_p, wave_qz, at, 512, h, o + 1)
+                wave = wave_of(wave_p, wave_qz, at, 1024, h, o + 1)
                 total = total + mm(wave, modes[h][o][...])
         value = jax.nn.gelu(total).astype(BF16).astype(F32)
         scale = jnp.concatenate(
-            [as_column(read[:, pl.ds(at + 128 * part, 128)], 128) for part in range(4)], axis=0
+            [as_column(read[:, pl.ds(at + 128 * part, 128)], 128) for part in range(8)], axis=0
         )
         gathered = (jnp.concatenate([scale, scale], axis=1) * value).astype(BF16)
         hidden = jax.nn.gelu(mm(gathered, hidden_weight[...])).astype(BF16)
-        built[pl.ds(at, 512), :] = mm(hidden, output_weight[...]).astype(BF16)
+        built[pl.ds(at, 1024), :] = mm(hidden, output_weight[...]).astype(BF16)
         save(step).start()
         return carry
 
     def save(step):
-        rows = pl.ds(step * 512, 512)
+        rows = pl.ds(step * 1024, 1024)
         return pltpu.make_async_copy(built.at[rows], out.at[rows], saves.at[step])
 
-    lax.fori_loop(0, 4, some, 0)
-    for step in range(4):
+    lax.fori_loop(0, 2, some, 0)
+    for step in range(2):
         save(step).wait()
 
 
@@ -542,7 +542,7 @@
         out_shape=shape((points, width), BF16),
         in_specs=[VMEM] * len(arrays),
         out_specs=anywhere,
-        scratch_shapes=[pltpu.VMEM((points, width), BF16), pltpu.SemaphoreType.DMA((4,))],
+        scratch_shapes=[pltpu.VMEM((points, width), BF16), pltpu.SemaphoreType.DMA((2,))],
         name="decode",
         compiler_params=pltpu.CompilerParams(vmem_limit_bytes=32 * 2**20),
         cost_estimate=pl.CostEstimate(

time: 156 us -> 155 us (level)
  no operation moved by 1% of the time
where the time goes in v11:
time: 155 us; the launch traced here: 154 us
  starting transfers between devices  50.8 us (33%)
  Pallas kernels  50.7 us (33%)
  waiting for transfers between devices  47.2 us (30%)
  local copies, waits for them, and re-layouts  5.26 us (3%)
    pallas_call x12, Pallas kernels, call(): return fn(*ins)  28 us
    all_to_all x1, waiting for transfers between devices, per_device(): recv = lax.all_to_all(send, everyone, 0, 0, tiled=True)  21.7 us
    ppermute x12, waiting for transfers between devices, around(): return lax.ppermute(shard, ('z', 'core', 'ba'), pairs)  21.2 us
    ppermute x12, starting transfers between devices, around(): return lax.ppermute(shard, ('z', 'core', 'ba'), pairs)  17.3 us
    all_to_all x1, starting transfers between devices, per_device(): recv = lax.all_to_all(send, everyone, 0, 0, tiled=True)  11.5 us
    ppermute x5, starting transfers between devices, swapped(): return lax.ppermute(shard, 'core', [(0, 1), (1, 0)])  10.6 us
    pallas_call x1, Pallas kernels, per_device(): pl.pallas_call(spread_body, out_shape=(shape((devices, 56, 128), BF16), s...  9.84 us
    ppermute x6, starting transfers between devices, around(): return lax.ppermute(shard, 'y', [(i, (i + s) % 4) for i in range(4)])  7.65 us
  transfers between devices with their start and end apart: 25, of which 13 were waited for; matrix products, arithmetic and copies ran while one was open for 0% of the time, Pallas kernels for 22%

profile of v11, /device:TPU:1, one launch (start us, length us, event | category | flops | bytes accessed | tf_op | source)
XLA Modules:
  0.0 154.5 jit_solution(5935803456327680914)
XLA Ops:
  0.0 9.8 %spread.1 = (bf16[128,56,128]{2,1,0:T(8,128)(2,1)}, s32[1,2048]{1,0:T(1,128)}, bf16[2048,256]{1,0:T(8,128)(2,1)}) custom-call(bf16[2048,256]{1,0:T(8,128)(2,1)} %feat.1, s32[1,2048]{1,0:T(1,128)} %bitcast.7, s32[1,2048]{1,0:T(1,128)} %bitcast.11, f32[1,2048]{1,0:T(1,128)} %bitcast.16, bf16[256,256]{1,0:T(8,128)(2,1)} %weight.3), custom_call_target="tpu_custom_call" | custom-call | tf_op jit(solution)/shard_map/spread/pallas_call | solution.py:454
  9.8 0.0 copy-start.6
  9.9 0.0 copy-start.7
  9.9 0.0 copy-start.8
  9.9 0.0 copy-start.16
  9.9 11.5 %all-to-all-start = ((bf16[128,56,128]{2,1,0:T(8,128)(2,1)}), bf16[128,56,128]{2,1,0:T(8,128)(2,1)S(1)}, u32[]{:S(2)}, u32[]{:S(2)}) async-start(bf16[128,56,128]{2,1,0:T(8,128)(2,1)} %get-tuple-element.39), calls=%async_computation | async-start | bytes 3670016 | tf_op jit(solution)/shard_map/all_to_all | solution.py:473
  21.4 5.1 %shard_map.119 = bf16[2048,256]{1,0:T(8,128)(2,1)} custom-call(bf16[2048,256]{1,0:T(8,128)(2,1)S(1)} %copy-done.8, s32[1,2048]{1,0:T(1,128)S(1)} %bitcast.8, s32[1,2048]{1,0:T(1,128)S(1)} %bitcast.12, bf16[16,128]{1,0:T(8,128)(2,1)S(1)} %copy-done.16, s32[1]{0:T(128)} %bitcast.3.where), custom_call_target="tpu_custom_call" | custom-call | flops 2147483648 | bytes 4000000 | tf_op jit(solution)/shard_map/pallas_call | solution.py:48
  26.6 1.1 collective-permute-start
  27.6 21.7 %all-to-all-done.recv = bf16[128,56,128]{2,1,0:T(8,128)(2,1)S(1)} async-done(((bf16[128,56,128]{2,1,0:T(8,128)(2,1)}), bf16[128,56,128]{2,1,0:T(8,128)(2,1)S(1)}, u32[]{:S(2)}, u32[]{:S(2)}) %all-to-all-start) | async-done | bytes 1835040 | tf_op jit(solution)/shard_map/all_to_all | solution.py:473
  49.3 4.9 %shard_map.127 = (bf16[2048,256]{1,0:T(8,128)(2,1)S(1)}, bf16[1024,128]{1,0:T(8,128)(2,1)S(1)}) custom-call(bf16[128,56,128]{2,1,0:T(8,128)(2,1)S(1)} %all-to-all-done.recv), custom_call_target="tpu_custom_call" | custom-call | flops 3221225472 | bytes 4000000 | tf_op jit(solution)/shard_map/pallas_call | solution.py:48
  54.2 5.3 %reply.1 = bf16[128,24,256]{2,1,0:T(8,128)(2,1)} custom-call(bf16[2048,256]{1,0:T(8,128)(2,1)S(1)} %get-tuple-element.40.latent, bf16[1024,128]{1,0:T(8,128)(2,1)S(1)} %get-tuple-element.41.places, bf16[4,8,256,256]{3,2,1,0:T(8,128)(2,1)S(1)} %copy-done.4), custom_call_target="tpu_custom_call" | custom-call | flops 3221225472 | bytes 4000000 | tf_op jit(solution)/shard_map/reply/pallas_call | solution.py:499
  59.5 3.8 %all-to-all-start.1 = ((bf16[128,24,256]{2,1,0:T(8,128)(2,1)}), bf16[128,24,256]{2,1,0:T(8,128)(2,1)S(1)}, u32[]{:S(2)}, u32[]{:S(2)}) async-start(bf16[128,24,256]{2,1,0:T(8,128)(2,1)} %reply.1), calls=%async_computation.1 | async-start | bytes 3145728 | tf_op jit(solution)/shard_map/all_to_all | solution.py:522
  63.3 0.0 copy-start.9
  63.3 1.2 copy-done.9
  64.5 4.1 %shard_map.118.refs_0_ = bf16[2048,256]{1,0:T(8,128)(2,1)S(1)} custom-call(bf16[2048,256]{1,0:T(8,128)(2,1)S(1)} %copy-done.9, s32[1,2048]{1,0:T(1,128)S(1)} %bitcast.9, s32[1,2048]{1,0:T(1,128)S(1)} %bitcast.13, bf16[16,128]{1,0:T(8,128)(2,1)S(1)} %copy-done.16, s32[1]{0:T(128)} %bitcast.3.where), custom_call_target="tpu_custom_call" | custom-call | flops 2147483648 | bytes 4000000 | tf_op jit(solution)/shard_map/pallas_call | solution.py:48
  68.7 0.2 shard_map.120
  69.0 1.7 %collective-permute-start.1 = (bf16[512,256]{1,0:T(8,128)(2,1)S(1)}, bf16[512,256]{1,0:T(8,128)(2,1)S(1)}, u32[]{:S(2)}, u32[]{:S(2)}) collective-permute-start(bf16[512,256]{1,0:T(8,128)(2,1)S(1)} %get-tuple-element.26), channel_id=1, source_target_pairs={{0,1},{1,2},{2,3},{3,0},{4,36},{5,37},{6,38},{7,39},{32,33},{33,34... | collective-permute-start | bytes 786440 | tf_op jit(solution)/shard_map/ppermute | solution.py:416
  70.6 2.9 %collective-permute-start.2 = (bf16[512,256]{1,0:T(8,128)(2,1)S(1)}, bf16[512,256]{1,0:T(8,128)(2,1)S(1)}, u32[]{:S(2)}, u32[]{:S(2)}) collective-permute-start(bf16[512,256]{1,0:T(8,128)(2,1)S(1)} %get-tuple-element.27), channel_id=1, source_target_pairs={{0,2},{1,3},{2,0},{3,1},{4,68},{5,69},{6,70},{7,71},{32,34},{33,35... | collective-permute-start | bytes 786440 | tf_op jit(solution)/shard_map/ppermute | solution.py:416
  73.6 0.9 collective-permute-start.3
  74.5 13.0 %collective-permute-done.1.refs_1_ = bf16[512,256]{1,0:T(8,128)(2,1)S(1)} collective-permute-done((bf16[512,256]{1,0:T(8,128)(2,1)S(1)}, bf16[512,256]{1,0:T(8,128)(2,1)S(1)}, u32[]{:S(2)}, u32[]{:S(2)}) %collective-permute-start.1) | collective-permute-done | bytes 262176 | tf_op jit(solution)/shard_map/ppermute | solution.py:416
  87.5 2.9 %collective-permute-done.2.refs_2_ = bf16[512,256]{1,0:T(8,128)(2,1)S(1)} collective-permute-done((bf16[512,256]{1,0:T(8,128)(2,1)S(1)}, bf16[512,256]{1,0:T(8,128)(2,1)S(1)}, u32[]{:S(2)}, u32[]{:S(2)}) %collective-permute-start.2) | collective-permute-done | bytes 262176 | tf_op jit(solution)/shard_map/ppermute | solution.py:416
  90.5 0.0 collective-permute-done.3.refs_3_
  90.5 0.1 shard_map.121
  90.6 1.2 collective-permute-start.4
  91.9 2.4 %collective-permute-start.5 = (bf16[128,256]{1,0:T(8,128)(2,1)S(1)}, bf16[128,256]{1,0:T(8,128)(2,1)S(1)}, u32[]{:S(2)}, u32[]{:S(2)}) collective-permute-start(bf16[128,256]{1,0:T(8,128)(2,1)S(1)} %get-tuple-element.31), channel_id=1, source_target_pairs={{0,64},{1,65},{2,66},{3,67},{4,6},{5,7},{6,4},{7,5},{32,96},{33,97... | collective-permute-start | bytes 196616 | tf_op jit(solution)/shard_map/ppermute | solution.py:416
  94.3 0.9 collective-permute-start.6
  95.2 0.0 collective-permute-done.4.refs_1_
  95.2 1.7 %collective-permute-done.5.refs_2_ = bf16[128,256]{1,0:T(8,128)(2,1)S(1)} collective-permute-done((bf16[128,256]{1,0:T(8,128)(2,1)S(1)}, bf16[128,256]{1,0:T(8,128)(2,1)S(1)}, u32[]{:S(2)}, u32[]{:S(2)}) %collective-permute-start.5) | collective-permute-done | bytes 65568 | tf_op jit(solution)/shard_map/ppermute | solution.py:416
  97.0 0.5 collective-permute-done.6.refs_3_
  97.5 0.8 collective-permute-start.7
  98.3 2.3 %collective-permute-start.8 = (bf16[32,256]{1,0:T(8,128)(2,1)S(1)}, bf16[32,256]{1,0:T(8,128)(2,1)S(1)}, u32[]{:S(2)}, u32[]{:S(2)}) collective-permute-start(bf16[32,256]{1,0:T(8,128)(2,1)S(1)} %get-tuple-element.35), channel_id=1, source_target_pairs={{0,16},{8,24},{16,0},{24,8},{1,17},{9,25},{17,1},{25,9},{2,18},{10... | collective-permute-start | bytes 49160 | tf_op jit(solution)/shard_map/ppermute | solution.py:408
  100.7 1.2 collective-permute-start.9
  101.8 0.0 collective-permute-done.7.b
  101.8 0.6 collective-permute-done.8.c
  102.4 1.1 collective-permute-done.9.d
  103.5 0.7 shard_map.123.refs_0_
  104.2 0.4 collective-permute-start.10
  104.6 2.9 %collective-permute-start.11 = (bf16[32,256]{1,0:T(8,128)(2,1)S(1)}, bf16[32,256]{1,0:T(8,128)(2,1)S(1)}, u32[]{:S(2)}, u32[]{:S(2)}) collective-permute-start(bf16[32,256]{1,0:T(8,128)(2,1)S(1)} %shard_map.123.refs_0_), channel_id=1, source_target_pairs={{0,16},{8,24},{16,0},{24,8},{1,17},{9,25},{17,1},{25,9},{2,18},{10... | collective-permute-start | bytes 49160 | tf_op jit(solution)/shard_map/ppermute | solution.py:408
  107.5 0.0 collective-permute-start.12
  107.5 0.5 collective-permute-done.10.refs_1_
  108.0 0.8 collective-permute-done.11.refs_2_
  108.8 1.3 collective-permute-done.12.refs_3_
  110.1 0.4 collective-permute-start.13
  110.5 3.2 %collective-permute-start.14 = (bf16[128,256]{1,0:T(8,128)(2,1)S(1)}, bf16[128,256]{1,0:T(8,128)(2,1)S(1)}, u32[]{:S(2)}, u32[]{:S(2)}) collective-permute-start(bf16[128,256]{1,0:T(8,128)(2,1)S(1)} %shard_map.124.refs_0_), channel_id=1, source_target_pairs={{0,64},{1,65},{2,66},{3,67},{4,6},{5,7},{6,4},{7,5},{32,96},{33,97... | collective-permute-start | bytes 196616 | tf_op jit(solution)/shard_map/ppermute | solution.py:416
  113.7 0.1 collective-permute-start.15
  113.8 0.7 collective-permute-done.13.refs_1_
  114.5 1.6 %collective-permute-done.14.refs_2_ = bf16[128,256]{1,0:T(8,128)(2,1)S(1)} collective-permute-done((bf16[128,256]{1,0:T(8,128)(2,1)S(1)}, bf16[128,256]{1,0:T(8,128)(2,1)S(1)}, u32[]{:S(2)}, u32[]{:S(2)}) %collective-permute-start.14) | collective-permute-done | bytes 65568 | tf_op jit(solution)/shard_map/ppermute | solution.py:416
  116.1 0.8 collective-permute-done.15.refs_3_
  116.9 0.1 collective-permute-start.16
  117.0 1.3 collective-permute-start.17
  118.3 2.0 %collective-permute-start.18 = (bf16[512,256]{1,0:T(8,128)(2,1)S(1)}, bf16[512,256]{1,0:T(8,128)(2,1)S(1)}, u32[]{:S(2)}, u32[]{:S(2)}) collective-permute-start(bf16[512,256]{1,0:T(8,128)(2,1)S(1)} %shard_map.125.near), channel_id=1, source_target_pairs={{0,3},{1,0},{2,1},{3,2},{4,100},{5,101},{6,102},{7,103},{32,35},{3... | collective-permute-start | bytes 786440 | tf_op jit(solution)/shard_map/ppermute | solution.py:416
  120.3 6.8 %shard_map.126 = (bf16[2048,1024]{1,0:T(8,128)(2,1)S(1)}, bf16[2048,1024]{1,0:T(8,128)(2,1)S(1)}) custom-call(s32[1,2048]{1,0:T(1,128)S(1)} %bitcast.10, s32[1,2048]{1,0:T(1,128)S(1)} %bitcast.14, bf16[128,16]{1,0:T(8,128)(2,1)S(1)} %copy-done.15, s32[1]{0:T(128)} %bitcast.3.where), custom_call_target="tpu_custom_call" | custom-call | flops 1000000000 | bytes 4000000 | tf_op jit(solution)/shard_map/pallas_call | solution.py:48
  127.0 1.9 %copy-done = bf16[2048,1024]{1,0:T(8,128)(2,1)} copy-done((bf16[2048,1024]{1,0:T(8,128)(2,1)}, bf16[2048,1024]{1,0:T(8,128)(2,1)S(1)}, u32[]{:S(2)}) %copy-start) | copy-done | bytes 4194328
  129.0 2.0 %copy-done.2 = bf16[2048,1024]{1,0:T(8,128)(2,1)} copy-done((bf16[2048,1024]{1,0:T(8,128)(2,1)}, bf16[2048,1024]{1,0:T(8,128)(2,1)S(1)}, u32[]{:S(2)}) %copy-start.2) | copy-done | bytes 4194328
  131.0 8.9 %collective-permute-start.22 = (bf16[512,256]{1,0:T(8,128)(2,1)S(1)}, bf16[512,256]{1,0:T(8,128)(2,1)S(1)}, u32[]{:S(2)}, u32[]{:S(2)}) collective-permute-start(bf16[512,256]{1,0:T(8,128)(2,1)S(1)} %shard_map.125.near), channel_id=1, source_target_pairs={{0,4},{4,0},{1,5},{5,1},{2,6},{6,2},{3,7},{7,3},{8,12},{12,8},{9,1... | collective-permute-start | bytes 786440 | tf_op jit(solution)/shard_map/ppermute | solution.py:427
  139.9 0.0 collective-permute-start.19
  140.0 0.5 collective-permute-start.20
  140.5 0.1 collective-permute-start.21
  140.6 4.2 %shard_map.128.base = f32[2048,256]{1,0:T(8,128)S(1)} custom-call(bf16[3072,256]{1,0:T(8,128)(2,1)S(1)} %bitcast.6, s32[1,2048]{1,0:T(1,128)S(1)} %copy-done.14, bf16[256,256]{1,0:T(8,128)(2,1)S(1)} %copy-done.10), custom_call_target="tpu_custom_call" | custom-call | flops 3221225472 | bytes 4000000 | tf_op jit(solution)/shard_map/pallas_call | solution.py:48
  144.8 0.0 copy-start.11
  144.8 0.0 copy-start.12
  144.8 0.0 copy-start.13
  144.8 1.8 %shard_map.129.base = f32[2048,256]{1,0:T(8,128)S(1)} custom-call(bf16[512,256]{1,0:T(8,128)(2,1)S(1)} %shard_map.125.near, bf16[512,256]{1,0:T(8,128)(2,1)S(1)} %collective-permute-done.22.far, bf16[2048,1024]{1,0:T(8,128)(2,1)S(1)} %copy-done.1, bf16[2048,1024]{1,0:T(8,128)(2,1)S(1)} %copy-done.3, f32[2048,256]{1,0:T(8,128)S(1)} %shard_map.128.base), custom_call_target="tpu_custom_call" | custom-call | flops 1073741824 | bytes 4000000 | tf_op jit(solution)/shard_map/pallas_call | solution.py:48
  146.7 7.6 %decode.1 = bf16[2048,256]{1,0:T(8,128)(2,1)} custom-call(bf16[512,256]{1,0:T(8,128)(2,1)S(1)} %collective-permute-done.16.m1, bf16[512,256]{1,0:T(8,128)(2,1)S(1)} %collective-permute-done.17.m2, bf16[512,256]{1,0:T(8,128)(2,1)S(1)} %collective-permute-done.18.m3, bf16[512,256]{1,0:T(8,128)(2,1)S(1)} %collective-permute-done.19.m5, ...), custom_call_target="tpu_custom_call" | custom-call | flops 4294967296 | bytes 4000000 | tf_op jit(solution)/shard_map/decode/pallas_call | solution.py:540
  (35 shorter events, 0.1 us)
Async XLA Ops:
  9.8 11.6 %copy-start.6 = (s32[2048,1]{0,1:T(1,128)S(1)}, s32[2048,1]{0,1:T(1,128)}, u32[]{:S(2)}) copy-start(s32[2048,1]{0,1:T(1,128)} %param.13) | copy-start | bytes 24580
  9.9 11.6 %copy-start.7 = (s32[2048]{0:T(1024)S(1)}, s32[2048]{0:T(1024)}, u32[]{:S(2)}) copy-start(s32[2048]{0:T(1024)} %param.14) | copy-start | bytes 24580
  9.9 11.5 %copy-start.8 = (bf16[2048,256]{1,0:T(8,128)(2,1)S(1)}, bf16[2048,256]{1,0:T(8,128)(2,1)}, u32[]{:S(2)}) copy-start(bf16[2048,256]{1,0:T(8,128)(2,1)} %get-tuple-element.24.message) | copy-start | bytes 3145732
  9.9 11.5 %copy-start.16 = (bf16[16,128]{1,0:T(8,128)(2,1)S(1)}, bf16[16,128]{1,0:T(8,128)(2,1)}, u32[]{:S(2)}) copy-start(bf16[16,128]{1,0:T(8,128)(2,1)} %constant.26.clone.basis) | copy-start | bytes 12292
  9.9 39.4 %all-to-all-start = ((bf16[128,56,128]{2,1,0:T(8,128)(2,1)}), bf16[128,56,128]{2,1,0:T(8,128)(2,1)S(1)}, u32[]{:S(2)}, u32[]{:S(2)}) async-start(bf16[128,56,128]{2,1,0:T(8,128)(2,1)} %get-tuple-element.39), calls=%async_computation | async-start | bytes 3670016 | tf_op jit(solution)/shard_map/all_to_all | solution.py:473
  26.6 42.1 %collective-permute-start = (bf16[2048,256]{1,0:T(8,128)(2,1)}, bf16[2048,256]{1,0:T(8,128)(2,1)S(1)}, u32[]{:S(2)}, u32[]{:S(2)}) collective-permute-start(bf16[2048,256]{1,0:T(8,128)(2,1)} %shard_map.119), channel_id=1, source_target_pairs={{0,4},{4,0},{1,5},{5,1},{2,6},{6,2},{3,7},{7,3},{8,12},{12,8},{9,1... | collective-permute-start | bytes 3145736 | tf_op jit(solution)/shard_map/ppermute | solution.py:427
  49.3 4.9 %copy-start.4 = (bf16[4,8,256,256]{3,2,1,0:T(8,128)(2,1)S(1)}, bf16[4,8,256,256]{3,2,1,0:T(8,128)(2,1)}, u32[]{:S(2)}) copy-start(bf16[4,8,256,256]{3,2,1,0:T(8,128)(2,1)} %weight.5) | copy-start | bytes 12582916
  59.5 81.0 %all-to-all-start.1 = ((bf16[128,24,256]{2,1,0:T(8,128)(2,1)}), bf16[128,24,256]{2,1,0:T(8,128)(2,1)S(1)}, u32[]{:S(2)}, u32[]{:S(2)}) async-start(bf16[128,24,256]{2,1,0:T(8,128)(2,1)} %reply.1), calls=%async_computation.1 | async-start | bytes 3145728 | tf_op jit(solution)/shard_map/all_to_all | solution.py:522
  63.3 1.2 copy-start.9
  64.5 39.0 %copy-start.5 = (bf16[4,8,256,256]{3,2,1,0:T(8,128)(2,1)S(1)}, bf16[4,8,256,256]{3,2,1,0:T(8,128)(2,1)}, u32[]{:S(2)}) copy-start(bf16[4,8,256,256]{3,2,1,0:T(8,128)(2,1)} %weight.5) | copy-start | bytes 12582916
  69.0 18.6 %collective-permute-start.1 = (bf16[512,256]{1,0:T(8,128)(2,1)S(1)}, bf16[512,256]{1,0:T(8,128)(2,1)S(1)}, u32[]{:S(2)}, u32[]{:S(2)}) collective-permute-start(bf16[512,256]{1,0:T(8,128)(2,1)S(1)} %get-tuple-element.26), channel_id=1, source_target_pairs={{0,1},{1,2},{2,3},{3,0},{4,36},{5,37},{6,38},{7,39},{32,33},{33,34... | collective-permute-start | bytes 786440 | tf_op jit(solution)/shard_map/ppermute | solution.py:416
  70.6 19.8 %collective-permute-start.2 = (bf16[512,256]{1,0:T(8,128)(2,1)S(1)}, bf16[512,256]{1,0:T(8,128)(2,1)S(1)}, u32[]{:S(2)}, u32[]{:S(2)}) collective-permute-start(bf16[512,256]{1,0:T(8,128)(2,1)S(1)} %get-tuple-element.27), channel_id=1, source_target_pairs={{0,2},{1,3},{2,0},{3,1},{4,68},{5,69},{6,70},{7,71},{32,34},{33,35... | collective-permute-start | bytes 786440 | tf_op jit(solution)/shard_map/ppermute | solution.py:416
  73.6 16.9 %collective-permute-start.3 = (bf16[512,256]{1,0:T(8,128)(2,1)S(1)}, bf16[512,256]{1,0:T(8,128)(2,1)S(1)}, u32[]{:S(2)}, u32[]{:S(2)}) collective-permute-start(bf16[512,256]{1,0:T(8,128)(2,1)S(1)} %get-tuple-element.28), channel_id=1, source_target_pairs={{0,3},{1,0},{2,1},{3,2},{4,100},{5,101},{6,102},{7,103},{32,35},{3... | collective-permute-start | bytes 786440 | tf_op jit(solution)/shard_map/ppermute | solution.py:416
  90.6 4.6 %collective-permute-start.4 = (bf16[128,256]{1,0:T(8,128)(2,1)S(1)}, bf16[128,256]{1,0:T(8,128)(2,1)S(1)}, u32[]{:S(2)}, u32[]{:S(2)}) collective-permute-start(bf16[128,256]{1,0:T(8,128)(2,1)S(1)} %get-tuple-element.30), channel_id=1, source_target_pairs={{0,32},{1,33},{2,34},{3,35},{4,5},{5,6},{6,7},{7,4},{32,64},{33,65... | collective-permute-start | bytes 196616 | tf_op jit(solution)/shard_map/ppermute | solution.py:416
  91.9 5.1 %collective-permute-start.5 = (bf16[128,256]{1,0:T(8,128)(2,1)S(1)}, bf16[128,256]{1,0:T(8,128)(2,1)S(1)}, u32[]{:S(2)}, u32[]{:S(2)}) collective-permute-start(bf16[128,256]{1,0:T(8,128)(2,1)S(1)} %get-tuple-element.31), channel_id=1, source_target_pairs={{0,64},{1,65},{2,66},{3,67},{4,6},{5,7},{6,4},{7,5},{32,96},{33,97... | collective-permute-start | bytes 196616 | tf_op jit(solution)/shard_map/ppermute | solution.py:416
  94.3 3.1 %collective-permute-start.6 = (bf16[128,256]{1,0:T(8,128)(2,1)S(1)}, bf16[128,256]{1,0:T(8,128)(2,1)S(1)}, u32[]{:S(2)}, u32[]{:S(2)}) collective-permute-start(bf16[128,256]{1,0:T(8,128)(2,1)S(1)} %get-tuple-element.32), channel_id=1, source_target_pairs={{0,96},{1,97},{2,98},{3,99},{4,7},{5,4},{6,5},{7,6},{32,0},{33,1},... | collective-permute-start | bytes 196616 | tf_op jit(solution)/shard_map/ppermute | solution.py:416
  97.5 4.4 %collective-permute-start.7 = (bf16[32,256]{1,0:T(8,128)(2,1)S(1)}, bf16[32,256]{1,0:T(8,128)(2,1)S(1)}, u32[]{:S(2)}, u32[]{:S(2)}) collective-permute-start(bf16[32,256]{1,0:T(8,128)(2,1)S(1)} %get-tuple-element.34), channel_id=1, source_target_pairs={{0,8},{8,16},{16,24},{24,0},{1,9},{9,17},{17,25},{25,1},{2,10},{10... | collective-permute-start | bytes 49160 | tf_op jit(solution)/shard_map/ppermute | solution.py:408
  98.3 4.1 %collective-permute-start.8 = (bf16[32,256]{1,0:T(8,128)(2,1)S(1)}, bf16[32,256]{1,0:T(8,128)(2,1)S(1)}, u32[]{:S(2)}, u32[]{:S(2)}) collective-permute-start(bf16[32,256]{1,0:T(8,128)(2,1)S(1)} %get-tuple-element.35), channel_id=1, source_target_pairs={{0,16},{8,24},{16,0},{24,8},{1,17},{9,25},{17,1},{25,9},{2,18},{10... | collective-permute-start | bytes 49160 | tf_op jit(solution)/shard_map/ppermute | solution.py:408
  100.7 2.9 %collective-permute-start.9 = (bf16[32,256]{1,0:T(8,128)(2,1)S(1)}, bf16[32,256]{1,0:T(8,128)(2,1)S(1)}, u32[]{:S(2)}, u32[]{:S(2)}) collective-permute-start(bf16[32,256]{1,0:T(8,128)(2,1)S(1)} %get-tuple-element.36), channel_id=1, source_target_pairs={{0,24},{8,0},{16,8},{24,16},{1,25},{9,1},{17,9},{25,17},{2,26},{10... | collective-permute-start | bytes 49160 | tf_op jit(solution)/shard_map/ppermute | solution.py:408
  103.5 16.7 %copy-start.15 = (bf16[128,16]{1,0:T(8,128)(2,1)S(1)}, bf16[128,16]{1,0:T(8,128)(2,1)}, u32[]{:S(2)}) copy-start(bf16[128,16]{1,0:T(8,128)(2,1)} %constant.27.clone.basis) | copy-start | bytes 12292
  104.2 3.8 %collective-permute-start.10 = (bf16[32,256]{1,0:T(8,128)(2,1)S(1)}, bf16[32,256]{1,0:T(8,128)(2,1)S(1)}, u32[]{:S(2)}, u32[]{:S(2)}) collective-permute-start(bf16[32,256]{1,0:T(8,128)(2,1)S(1)} %shard_map.123.refs_0_), channel_id=1, source_target_pairs={{0,8},{8,16},{16,24},{24,0},{1,9},{9,17},{17,25},{25,1},{2,10},{10... | collective-permute-start | bytes 49160 | tf_op jit(solution)/shard_map/ppermute | solution.py:408
  104.6 4.2 %collective-permute-start.11 = (bf16[32,256]{1,0:T(8,128)(2,1)S(1)}, bf16[32,256]{1,0:T(8,128)(2,1)S(1)}, u32[]{:S(2)}, u32[]{:S(2)}) collective-permute-start(bf16[32,256]{1,0:T(8,128)(2,1)S(1)} %shard_map.123.refs_0_), channel_id=1, source_target_pairs={{0,16},{8,24},{16,0},{24,8},{1,17},{9,25},{17,1},{25,9},{2,18},{10... | collective-permute-start | bytes 49160 | tf_op jit(solution)/shard_map/ppermute | solution.py:408
  107.5 2.6 %collective-permute-start.12 = (bf16[32,256]{1,0:T(8,128)(2,1)S(1)}, bf16[32,256]{1,0:T(8,128)(2,1)S(1)}, u32[]{:S(2)}, u32[]{:S(2)}) collective-permute-start(bf16[32,256]{1,0:T(8,128)(2,1)S(1)} %shard_map.123.refs_0_), channel_id=1, source_target_pairs={{0,24},{8,0},{16,8},{24,16},{1,25},{9,1},{17,9},{25,17},{2,26},{10... | collective-permute-start | bytes 49160 | tf_op jit(solution)/shard_map/ppermute | solution.py:408
  110.1 30.5 %copy-start.10 = (bf16[256,256]{1,0:T(8,128)(2,1)S(1)}, bf16[256,256]{1,0:T(8,128)(2,1)}, u32[]{:S(2)}) copy-start(bf16[256,256]{1,0:T(8,128)(2,1)} %skip.1) | copy-start | bytes 393220
  110.1 30.5 %copy-start.14 = (s32[1,2048]{1,0:T(1,128)S(1)}, s32[1,2048]{1,0:T(1,128)}, u32[]{:S(2)}) copy-start(s32[1,2048]{1,0:T(1,128)} %get-tuple-element.42.slots) | copy-start | bytes 24580
  110.1 4.4 %collective-permute-start.13 = (bf16[128,256]{1,0:T(8,128)(2,1)S(1)}, bf16[128,256]{1,0:T(8,128)(2,1)S(1)}, u32[]{:S(2)}, u32[]{:S(2)}) collective-permute-start(bf16[128,256]{1,0:T(8,128)(2,1)S(1)} %shard_map.124.refs_0_), channel_id=1, source_target_pairs={{0,32},{1,33},{2,34},{3,35},{4,5},{5,6},{6,7},{7,4},{32,64},{33,65... | collective-permute-start | bytes 196616 | tf_op jit(solution)/shard_map/ppermute | solution.py:416
  110.5 5.5 %collective-permute-start.14 = (bf16[128,256]{1,0:T(8,128)(2,1)S(1)}, bf16[128,256]{1,0:T(8,128)(2,1)S(1)}, u32[]{:S(2)}, u32[]{:S(2)}) collective-permute-start(bf16[128,256]{1,0:T(8,128)(2,1)S(1)} %shard_map.124.refs_0_), channel_id=1, source_target_pairs={{0,64},{1,65},{2,66},{3,67},{4,6},{5,7},{6,4},{7,5},{32,96},{33,97... | collective-permute-start | bytes 196616 | tf_op jit(solution)/shard_map/ppermute | solution.py:416
  113.7 3.1 %collective-permute-start.15 = (bf16[128,256]{1,0:T(8,128)(2,1)S(1)}, bf16[128,256]{1,0:T(8,128)(2,1)S(1)}, u32[]{:S(2)}, u32[]{:S(2)}) collective-permute-start(bf16[128,256]{1,0:T(8,128)(2,1)S(1)} %shard_map.124.refs_0_), channel_id=1, source_target_pairs={{0,96},{1,97},{2,98},{3,99},{4,7},{5,4},{6,5},{7,6},{32,0},{33,1},... | collective-permute-start | bytes 196616 | tf_op jit(solution)/shard_map/ppermute | solution.py:416
  116.9 23.1 %collective-permute-start.16 = (bf16[512,256]{1,0:T(8,128)(2,1)S(1)}, bf16[512,256]{1,0:T(8,128)(2,1)S(1)}, u32[]{:S(2)}, u32[]{:S(2)}) collective-permute-start(bf16[512,256]{1,0:T(8,128)(2,1)S(1)} %shard_map.125.near), channel_id=1, source_target_pairs={{0,1},{1,2},{2,3},{3,0},{4,36},{5,37},{6,38},{7,39},{32,33},{33,34... | collective-permute-start | bytes 786440 | tf_op jit(solution)/shard_map/ppermute | solution.py:416
  117.0 23.0 %collective-permute-start.17 = (bf16[512,256]{1,0:T(8,128)(2,1)S(1)}, bf16[512,256]{1,0:T(8,128)(2,1)S(1)}, u32[]{:S(2)}, u32[]{:S(2)}) collective-permute-start(bf16[512,256]{1,0:T(8,128)(2,1)S(1)} %shard_map.125.near), channel_id=1, source_target_pairs={{0,2},{1,3},{2,0},{3,1},{4,68},{5,69},{6,70},{7,71},{32,34},{33,35... | collective-permute-start | bytes 786440 | tf_op jit(solution)/shard_map/ppermute | solution.py:416
  118.3 22.2 %collective-permute-start.18 = (bf16[512,256]{1,0:T(8,128)(2,1)S(1)}, bf16[512,256]{1,0:T(8,128)(2,1)S(1)}, u32[]{:S(2)}, u32[]{:S(2)}) collective-permute-start(bf16[512,256]{1,0:T(8,128)(2,1)S(1)} %shard_map.125.near), channel_id=1, source_target_pairs={{0,3},{1,0},{2,1},{3,2},{4,100},{5,101},{6,102},{7,103},{32,35},{3... | collective-permute-start | bytes 786440 | tf_op jit(solution)/shard_map/ppermute | solution.py:416
  127.0 2.0 %copy-start = (bf16[2048,1024]{1,0:T(8,128)(2,1)}, bf16[2048,1024]{1,0:T(8,128)(2,1)S(1)}, u32[]{:S(2)}) copy-start(bf16[2048,1024]{1,0:T(8,128)(2,1)S(1)} %get-tuple-element.37.wave_p) | copy-start | bytes 12582916
  129.0 2.0 %copy-start.2 = (bf16[2048,1024]{1,0:T(8,128)(2,1)}, bf16[2048,1024]{1,0:T(8,128)(2,1)S(1)}, u32[]{:S(2)}) copy-start(bf16[2048,1024]{1,0:T(8,128)(2,1)S(1)} %get-tuple-element.38.wave_qz) | copy-start | bytes 12582916
  131.0 13.8 %collective-permute-start.22 = (bf16[512,256]{1,0:T(8,128)(2,1)S(1)}, bf16[512,256]{1,0:T(8,128)(2,1)S(1)}, u32[]{:S(2)}, u32[]{:S(2)}) collective-permute-start(bf16[512,256]{1,0:T(8,128)(2,1)S(1)} %shard_map.125.near), channel_id=1, source_target_pairs={{0,4},{4,0},{1,5},{5,1},{2,6},{6,2},{3,7},{7,3},{8,12},{12,8},{9,1... | collective-permute-start | bytes 786440 | tf_op jit(solution)/shard_map/ppermute | solution.py:427
  139.9 6.7 %collective-permute-start.19 = (bf16[512,256]{1,0:T(8,128)(2,1)S(1)}, bf16[512,256]{1,0:T(8,128)(2,1)S(1)}, u32[]{:S(2)}, u32[]{:S(2)}) collective-permute-start(bf16[512,256]{1,0:T(8,128)(2,1)S(1)} %collective-permute-done.16.m1), channel_id=1, source_target_pairs={{0,4},{4,0},{1,5},{5,1},{2,6},{6,2},{3,7},{7,3},{8,12},{12,8},{9,1... | collective-permute-start | bytes 786440 | tf_op jit(solution)/shard_map/ppermute | solution.py:427
  140.0 6.7 %collective-permute-start.20 = (bf16[512,256]{1,0:T(8,128)(2,1)S(1)}, bf16[512,256]{1,0:T(8,128)(2,1)S(1)}, u32[]{:S(2)}, u32[]{:S(2)}) collective-permute-start(bf16[512,256]{1,0:T(8,128)(2,1)S(1)} %collective-permute-done.17.m2), channel_id=1, source_target_pairs={{0,4},{4,0},{1,5},{5,1},{2,6},{6,2},{3,7},{7,3},{8,12},{12,8},{9,1... | collective-permute-start | bytes 786440 | tf_op jit(solution)/shard_map/ppermute | solution.py:427
  140.5 6.2 %collective-permute-start.21 = (bf16[512,256]{1,0:T(8,128)(2,1)S(1)}, bf16[512,256]{1,0:T(8,128)(2,1)}, u32[]{:S(2)}, u32[]{:S(2)}) collective-permute-start(bf16[512,256]{1,0:T(8,128)(2,1)S(1)} %collective-permute-done.18.m3), channel_id=1, source_target_pairs={{0,4},{4,0},{1,5},{5,1},{2,6},{6,2},{3,7},{7,3},{8,12},{12,8},{9,1... | collective-permute-start | bytes 786440 | tf_op jit(solution)/shard_map/ppermute | solution.py:427
  140.6 4.2 %copy-start.1 = (bf16[2048,1024]{1,0:T(8,128)(2,1)S(1)}, bf16[2048,1024]{1,0:T(8,128)(2,1)}, u32[]{:S(2)}) copy-start(bf16[2048,1024]{1,0:T(8,128)(2,1)} %copy-done) | copy-start | bytes 12582916
  140.6 4.2 %copy-start.3 = (bf16[2048,1024]{1,0:T(8,128)(2,1)S(1)}, bf16[2048,1024]{1,0:T(8,128)(2,1)}, u32[]{:S(2)}) copy-start(bf16[2048,1024]{1,0:T(8,128)(2,1)} %copy-done.2) | copy-start | bytes 12582916
  144.8 1.9 %copy-start.11 = (bf16[256,256]{1,0:T(8,128)(2,1)S(1)}, bf16[256,256]{1,0:T(8,128)(2,1)}, u32[]{:S(2)}) copy-start(bf16[256,256]{1,0:T(8,128)(2,1)} %hidden_weight.1) | copy-start | bytes 393220
  144.8 1.9 %copy-start.12 = (bf16[256,256]{1,0:T(8,128)(2,1)S(1)}, bf16[256,256]{1,0:T(8,128)(2,1)}, u32[]{:S(2)}) copy-start(bf16[256,256]{1,0:T(8,128)(2,1)} %output_weight.1) | copy-start | bytes 393220
  144.8 1.9 %copy-start.13 = (f32[2048]{0:T(1024)S(1)}, f32[2048]{0:T(1024)}, u32[]{:S(2)}) copy-start(f32[2048]{0:T(1024)} %param.16) | copy-start | bytes 24580
